TPU v7x, 16 devices: a whole 2x2x2 slice. The times are simulated.
16 devices in a mesh: dp: 2 (over z), tp: 8 (over y, x, core).
Axes of the slice: x: 2, y: 2, z: 2, core: 2. Of those that a mesh axis runs over, the one named last changes fastest.
Arguments:
- hidden: bfloat16 [6, 1536, 2048], P('dp', 'tp'), parts along dimension 0
- grad_out: bfloat16 [6, 1536, 2048], P('dp', 'tp'), parts along dimension 0
- prefix_len: int32 [6], P('dp'), parts along dimension 0
- valid_len: int32 [6], P('dp'), parts along dimension 0
- attn_norm: bfloat16 [2048], replicated
- w_query: bfloat16 [2048, 2048], P(None, 'tp')
- w_key: bfloat16 [2048, 256], replicated
- w_value: bfloat16 [2048, 256], replicated
- w_out: bfloat16 [2048, 2048], P('tp')
- mlp_norm: bfloat16 [2048], replicated
- w_gate: bfloat16 [2048, 16384], P(None, 'tp')
- w_up: bfloat16 [2048, 16384], P(None, 'tp')
- w_down: bfloat16 [16384, 2048], P('tp')
Outputs:
- output 1: bfloat16 [6, 1536, 2048], P('dp', 'tp'), parts along dimension 0
- output 2: bfloat16 [6, 1536, 2048], P('dp', 'tp'), parts along dimension 0
- output 3: float32 [4096], P('dp'), parts along dimension 0
- output 4: float32 [4096, 2048], P('dp', 'tp'), parts along dimension 0
- output 5: float32 [4096, 256], P('dp'), parts along dimension 0
- output 6: float32 [4096, 256], P('dp'), parts along dimension 0
- output 7: float32 [4096, 2048], P(('dp', 'tp')), parts along dimension 0
- output 8: float32 [4096], P('dp'), parts along dimension 0
- output 9: float32 [4096, 16384], P('dp', 'tp'), parts along dimension 0
- output 10: float32 [4096, 16384], P('dp', 'tp'), parts along dimension 0
- output 11: float32 [32768, 2048], P(('dp', 'tp')), parts along dimension 0
There are 2 independent parts. A program takes and returns all parts, laid end to end along the dimension named above; an argument that names none is the same for every part.
All inputs are finite; a program needn't handle non-finite values.
Results may differ from a plain program's by a relative error of at most 0.02.
Values are sent between devices in bfloat16 or wider.
A program may use at most 1 GiB of HBM per device.

v0:
```python
import math
import jax
import jax.numpy as jnp
from jax import lax
from jax.sharding import PartitionSpec as P

NORM_EPS = 1e-6


def rms_norm(x_in, gain):
    x_f = x_in.astype(jnp.float32)
    inv_rms = lax.rsqrt(jnp.mean(x_f * x_f, axis=-1, keepdims=True) + NORM_EPS)
    return (x_f * inv_rms * (1.0 + gain)).astype(jnp.bfloat16)


def rope_tables(positions, head_dim):
    half_dim = head_dim // 2
    exponent = jnp.arange(half_dim, dtype=jnp.float32) * (2.0 / head_dim)
    inv_freq = jnp.exp(exponent * (-math.log(10000.0)))
    angles = positions.astype(jnp.float32)[:, None] * inv_freq[None, :]
    return jnp.cos(angles), jnp.sin(angles)


def apply_rope(x_f, cos_t, sin_t):
    half_dim = x_f.shape[-1] // 2
    first = x_f[..., :half_dim]
    second = x_f[..., half_dim:]
    return jnp.concatenate([first * cos_t - second * sin_t, second * cos_t + first * sin_t], axis=-1)


def attend(query, keys, values, prefix_len, valid_len, first_pos):
    scale = query.shape[-1] ** -0.5
    scores = jnp.einsum("crie,cle->cirl", query, keys, preferred_element_type=jnp.float32) * scale
    q_pos = first_pos + jnp.arange(query.shape[1])
    k_pos = jnp.arange(keys.shape[1])
    key_row = k_pos[None, None, :]
    visible = (key_row < valid_len[:, None, None]) & ((key_row < prefix_len[:, None, None]) | (key_row <= q_pos[None, :, None]))
    scores = jnp.where(visible[:, None, :, :], scores, -1e30)
    probs = jax.nn.softmax(scores, axis=-1).astype(jnp.bfloat16)
    return jnp.einsum("cirl,cle->crie", probs, values, preferred_element_type=jnp.float32).astype(jnp.bfloat16)


def gated_act(gate, upper):
    return (jax.nn.gelu(gate, approximate=True) * upper).astype(jnp.bfloat16)


def gather_seq(x_loc):
    return lax.all_gather(x_loc, "tp", axis=1, tiled=True)


def scatter_seq(x_part):
    return lax.psum_scatter(x_part, "tp", scatter_dimension=1, tiled=True)


def solution(mesh):
    tp_size = mesh.shape["tp"]
    act_spec = P("dp", "tp", None)
    in_specs = (act_spec, act_spec, P("dp"), P("dp"), P(None), P(None, "tp"), P(None, None), P(None, None), P("tp", None), P(None), P(None, "tp"), P(None, "tp"), P("tp", None))
    out_specs = (act_spec, act_spec, P("dp"), P("dp", "tp"), P("dp", None), P("dp", None), P(("dp", "tp"), None), P("dp"), P("dp", "tp"), P("dp", "tp"), P(("dp", "tp"), None))

    def local_layer(hidden, grad_out, prefix_len, valid_len, attn_norm, w_query, w_key, w_value, w_out, mlp_norm, w_gate, w_up, w_down):
        batch, shard_len, model_dim = hidden.shape
        head_dim = w_key.shape[1]
        local_heads = w_query.shape[1] // head_dim
        seq_len = shard_len * tp_size
        cos_t, sin_t = rope_tables(jnp.arange(seq_len), head_dim)

        def rope_heads(raw_proj):
            return apply_rope(raw_proj, cos_t[:, None, :], sin_t[:, None, :]).astype(jnp.bfloat16)

        def rope_single(raw_proj):
            return apply_rope(raw_proj, cos_t, sin_t).astype(jnp.bfloat16)

        def attend_here(q_in, k_in, v_in):
            return attend(q_in, k_in, v_in, prefix_len, valid_len, 0)

        normed, norm1_pull = jax.vjp(rms_norm, hidden, attn_norm.astype(jnp.float32))
        normed_all = gather_seq(normed)
        q_raw = jnp.einsum("bld,dn->bln", normed_all, w_query, preferred_element_type=jnp.float32).reshape(batch, seq_len, local_heads, head_dim)
        query, query_pull = jax.vjp(rope_heads, q_raw)
        k_raw = jnp.einsum("bld,de->ble", normed_all, w_key, preferred_element_type=jnp.float32)
        keys, key_pull = jax.vjp(rope_single, k_raw)
        values = jnp.einsum("bld,de->ble", normed_all, w_value, preferred_element_type=jnp.float32).astype(jnp.bfloat16)
        mixed, attn_pull = jax.vjp(attend_here, query, keys, values)
        w_out_heads = w_out.reshape(local_heads, head_dim, model_dim)
        attn_part = jnp.einsum("blhd,hde->ble", mixed, w_out_heads, preferred_element_type=jnp.float32).astype(jnp.bfloat16)
        attn_sum = scatter_seq(attn_part)
        resid = (hidden.astype(jnp.float32) + attn_sum.astype(jnp.float32)).astype(jnp.bfloat16)
        gated_in, norm2_pull = jax.vjp(rms_norm, resid, mlp_norm.astype(jnp.float32))
        gated_all = gather_seq(gated_in)
        gate = jnp.einsum("bld,df->blf", gated_all, w_gate, preferred_element_type=jnp.float32)
        upper = jnp.einsum("bld,df->blf", gated_all, w_up, preferred_element_type=jnp.float32)
        act, act_pull = jax.vjp(gated_act, gate, upper)
        mlp_part = jnp.einsum("blf,fd->bld", act, w_down, preferred_element_type=jnp.float32).astype(jnp.bfloat16)
        mlp_sum = scatter_seq(mlp_part)
        hidden_out = (resid.astype(jnp.float32) + mlp_sum.astype(jnp.float32)).astype(jnp.bfloat16)

        grad_all = gather_seq(grad_out)
        g_down = jnp.einsum("blf,bld->fd", act, grad_all, preferred_element_type=jnp.float32)
        d_act = jnp.einsum("bld,fd->blf", grad_all, w_down, preferred_element_type=jnp.float32).astype(jnp.bfloat16)
        d_gate, d_upper = act_pull(d_act)
        d_gate = d_gate.astype(jnp.bfloat16)
        d_upper = d_upper.astype(jnp.bfloat16)
        g_gate = jnp.einsum("bld,blf->df", gated_all, d_gate, preferred_element_type=jnp.float32)
        g_up = jnp.einsum("bld,blf->df", gated_all, d_upper, preferred_element_type=jnp.float32)
        d_gated_part = (jnp.einsum("blf,df->bld", d_gate, w_gate, preferred_element_type=jnp.float32)
                        + jnp.einsum("blf,df->bld", d_upper, w_up, preferred_element_type=jnp.float32)).astype(jnp.bfloat16)
        d_gated = scatter_seq(d_gated_part)
        d_resid_norm, g_mlp_norm_part = norm2_pull(d_gated)
        g_mlp_norm = lax.psum(g_mlp_norm_part, "tp")
        d_resid = (grad_out.astype(jnp.float32) + d_resid_norm.astype(jnp.float32)).astype(jnp.bfloat16)

        d_resid_all = gather_seq(d_resid)
        g_out = jnp.einsum("blhd,ble->hde", mixed, d_resid_all, preferred_element_type=jnp.float32).reshape(local_heads * head_dim, model_dim)
        d_mixed = jnp.einsum("ble,hde->blhd", d_resid_all, w_out_heads, preferred_element_type=jnp.float32).astype(jnp.bfloat16)
        d_query, d_keys, d_values = attn_pull(d_mixed)
        d_q_raw = query_pull(d_query)[0].astype(jnp.bfloat16).reshape(batch, seq_len, local_heads * head_dim)
        d_k_raw = key_pull(d_keys)[0].astype(jnp.bfloat16)
        g_query = jnp.einsum("bld,bln->dn", normed_all, d_q_raw, preferred_element_type=jnp.float32)
        g_key = lax.psum(jnp.einsum("bld,ble->de", normed_all, d_k_raw, preferred_element_type=jnp.float32), "tp")
        g_value = lax.psum(jnp.einsum("bld,ble->de", normed_all, d_values, preferred_element_type=jnp.float32), "tp")
        d_normed_part = (jnp.einsum("bln,dn->bld", d_q_raw, w_query, preferred_element_type=jnp.float32)
                         + jnp.einsum("ble,de->bld", d_k_raw, w_key, preferred_element_type=jnp.float32)
                         + jnp.einsum("ble,de->bld", d_values, w_value, preferred_element_type=jnp.float32)).astype(jnp.bfloat16)
        d_normed = scatter_seq(d_normed_part)
        d_hidden_norm, g_attn_norm_part = norm1_pull(d_normed)
        g_attn_norm = lax.psum(g_attn_norm_part, "tp")
        grad_hidden = (d_resid.astype(jnp.float32) + d_hidden_norm.astype(jnp.float32)).astype(jnp.bfloat16)
        return (hidden_out, grad_hidden, g_attn_norm, g_query, g_key, g_value, g_out, g_mlp_norm, g_gate, g_up, g_down)

    return jax.shard_map(local_layer, mesh=mesh, in_specs=in_specs, out_specs=out_specs, check_vma=False)
```

profile of v0, /device:TPU:0, one launch (start us, length us, event | category | flops | bytes accessed | tf_op | source)
XLA Modules:
  0.0 1511.7 jit_solution(949884504890575316)
XLA Ops:
  20.2 92.7 %all-gather.5.cloned.1.call-done = bf16[3,1536,2048]{2,1,0:T(8,128)(2,1)} async-done(((bf16[3,192,2048]{2,1,0:T(8,128)(2,1)}), bf16[3,1536,2048]{2,1,0:T(8,128)(2,1)}) %all-gather.5.cloned.1.call-update) | async-done | bytes 18874384 | tf_op jit(solution)/shard_map/all_gather | solution.py:48
  174.4 16.3 %fusion.66 = bf16[3,1536,256]{1,2,0:T(8,128)(2,1)S(1)} fusion(bf16[3,1536,256]{2,1,0:T(8,128)(2,1)S(1)} %convolution_convert_fusion.5, f32[3,1536]{1,0:T(4,128)S(1)} %fusion.106, f32[3,1536]{1,0:T(4,128)S(1)} %get-tuple-element.35, f32[3,1536,1536]{2,1,0:T(8,128)} %get-tuple-element.36, pred[1536,1536]{0,1:T(8,128)(4,1)S(1)} %copy-done.9, ...), kind=kOutput, calls=%fused_computation.99 | convolution fusion | flops 3674603520 | bytes 35435520 | tf_op jit(solution)/shard_map/jvp(cirl,cle->crie)/dot_general | solution.py:40
  202.3 119.1 %reduce-scatter.5.cloned.1.call-done = bf16[3,192,2048]{2,1,0:T(8,128)(2,1)} async-done(((bf16[3,1536,2048]{2,1,0:T(8,128)(2,1)}), bf16[3,192,2048]{2,1,0:T(8,128)(2,1)}) %reduce-scatter.5.cloned.1.call-update) | async-done | bytes 2359312 | tf_op jit(solution)/shard_map/reduce_scatter | solution.py:52
  327.5 90.6 %all-gather.9.cloned.1.call-done = bf16[3,1536,2048]{2,1,0:T(8,128)(2,1)} async-done(((bf16[3,192,2048]{2,1,0:T(8,128)(2,1)}), bf16[3,1536,2048]{2,1,0:T(8,128)(2,1)}) %all-gather.9.cloned.1.call-update) | async-done | bytes 18874384 | tf_op jit(solution)/shard_map/all_gather | solution.py:48
  418.1 46.6 %convolution_convert_fusion.1 = bf16[3,1536,2048]{2,1,0:T(8,128)(2,1)} fusion(bf16[3,1536,2048]{2,1,0:T(8,128)(2,1)} %all-gather.9.cloned.1.call-done, bf16[2048,2048]{1,0:T(8,128)(2,1)} %param.25), kind=kOutput, calls=%fused_computation.37 | convolution fusion | flops 38664142848 | bytes 46137344 | tf_op jit(solution)/shard_map/bld,fd->blf/dot_general | solution.py:100
  464.7 50.5 %all-gather.7.cloned.1.call-done = bf16[3,1536,2048]{2,1,0:T(8,128)(2,1)} async-done(((bf16[3,192,2048]{2,1,0:T(8,128)(2,1)}), bf16[3,1536,2048]{2,1,0:T(8,128)(2,1)}) %all-gather.7.cloned.1.call-update) | async-done | bytes 18874384 | tf_op jit(solution)/shard_map/all_gather | solution.py:48
  515.2 47.0 %fusion.25 = f32[3,1536,2048]{2,1,0:T(8,128)} fusion(bf16[3,1536,2048]{2,1,0:T(8,128)(2,1)} %all-gather.7.cloned.1.call-done, bf16[2048,2048]{1,0:T(8,128)(2,1)} %param.24), kind=kOutput, calls=%fused_computation.57 | convolution fusion | flops 38654705664 | bytes 65011712 | tf_op jit(solution)/shard_map/bld,df->blf/dot_general | solution.py:92
  562.2 77.4 %fusion.7 = (bf16[3,1536,2048]{2,1,0:T(8,128)(2,1)}, bf16[3,1536,2048]{2,1,0:T(8,128)(2,1)}, f32[3,1536,2048]{2,1,0:T(8,128)}) fusion(f32[3,1536,2048]{2,1,0:T(8,128)} %fusion.25, bf16[3,1536,2048]{2,1,0:T(8,128)(2,1)} %convolution_convert_fusion.1, bf16[3,1536,2048]{2,1,0:T(8,128)(2,1)} %all-gather.7.cloned.1.call-done, bf16[2048,2048]{1,0:T(8,128)(2,1)} %param.23), kind=kOutput, calls=%fused_computation.11 | convolution fusion | flops 38890635264 | bytes 159383552 | tf_op jit(solution)/shard_map/bld,df->blf/dot_general | solution.py:91
  639.6 47.5 %fusion.27 = f32[3,1536,2048]{2,1,0:T(8,128)} fusion(bf16[3,1536,2048]{2,1,0:T(8,128)(2,1)} %get-tuple-element.21, bf16[2048,2048]{1,0:T(8,128)(2,1)} %param.23), kind=kOutput, calls=%fused_computation.59 | convolution fusion | flops 38654705664 | bytes 65011712 | tf_op jit(solution)/shard_map/blf,df->bld/dot_general | solution.py:106
  687.1 54.3 %add_convert_fusion.1 = bf16[3,1536,2048]{2,1,0:T(8,128)(2,1)} fusion(f32[3,1536,2048]{2,1,0:T(8,128)} %fusion.27, bf16[2048,2048]{1,0:T(8,128)(2,1)} %param.24, bf16[3,1536,2048]{2,1,0:T(8,128)(2,1)} %convolution_convert_fusion.1, f32[3,1536,2048]{2,1,0:T(8,128)} %get-tuple-element.37), kind=kOutput, calls=%fused_computation.13 | convolution fusion | flops 38777389056 | bytes 121634816 | tf_op jit(solution)/shard_map/blf,df->bld/dot_general | solution.py:107
  741.4 46.4 %convolution_convert_fusion.2 = bf16[3,1536,2048]{2,1,0:T(8,128)(2,1)} fusion(bf16[3,1536,2048]{2,1,0:T(8,128)(2,1)} %get-tuple-element.22, bf16[2048,2048]{1,0:T(8,128)(2,1)} %param.25), kind=kOutput, calls=%fused_computation.38 | convolution fusion | flops 38664142848 | bytes 46137344 | tf_op jit(solution)/shard_map/blf,fd->bld/dot_general | solution.py:94
  787.9 73.4 %reduce-scatter.9.cloned.1.call-done = bf16[3,192,2048]{2,1,0:T(8,128)(2,1)} async-done(((bf16[3,1536,2048]{2,1,0:T(8,128)(2,1)}), bf16[3,192,2048]{2,1,0:T(8,128)(2,1)}) %reduce-scatter.9.cloned.1.call-update) | async-done | bytes 2359312 | tf_op jit(solution)/shard_map/reduce_scatter | solution.py:52
  865.7 118.9 %reduce-scatter.7.cloned.1.call-done = bf16[3,192,2048]{2,1,0:T(8,128)(2,1)} async-done(((bf16[3,1536,2048]{2,1,0:T(8,128)(2,1)}), bf16[3,192,2048]{2,1,0:T(8,128)(2,1)}) %reduce-scatter.7.cloned.1.call-update) | async-done | bytes 2359312 | tf_op jit(solution)/shard_map/reduce_scatter | solution.py:52
  990.7 94.8 %all-gather.11.cloned.1.call-done = bf16[3,1536,2048]{2,1,0:T(8,128)(2,1)} async-done(((bf16[3,192,2048]{2,1,0:T(8,128)(2,1)}), bf16[3,1536,2048]{2,1,0:T(8,128)(2,1)}) %all-gather.11.cloned.1.call-update) | async-done | bytes 18874384 | tf_op jit(solution)/shard_map/all_gather | solution.py:48
  1112.7 22.0 %fusion.16 = (f32[3,1536]{1,0:T(4,128)S(1)}, bf16[3,1536,1536]{1,2,0:T(8,128)(2,1)}) fusion(f32[3,1536]{1,0:T(4,128)S(1)} %multiply_divide_fusion, f32[3,1536]{1,0:T(4,128)S(1)} %copy-done.43, f32[3,1536,1536]{2,1,0:T(8,128)} %get-tuple-element.36, pred[1536,1536]{0,1:T(8,128)(4,1)S(1)} %copy-done.10, pred[3,1536]{1,0:T(4,128)(4,1)S(1)} %copy-done.45, ...), kind=kOutput, calls=%fused_computation.26 | convolution fusion | flops 3694652928 | bytes 49609728 | tf_op jit(solution)/shard_map/transpose(jvp(cirl,cle->crie))/dot_general | solution.py:40
  1134.7 23.1 %fusion.57 = f32[3,1536,256]{1,2,0:T(8,128)} fusion(bf16[3,1536,1536]{1,2,0:T(8,128)(2,1)} %get-tuple-element.39, f32[3,1536]{1,0:T(4,128)S(1)} %neg.13, f32[3,1536]{1,0:T(4,128)S(1)} %copy-done.32, pred[1536,1536]{0,1:T(8,128)(4,1)S(1)} %copy-done.10, pred[3,1536]{1,0:T(4,128)(4,1)S(1)} %copy-done.45, pred[3,1536]{1,0:T(4,128)(4,1)S(1)} %copy-done.47, ...), kind=kOutput, calls=%fused_computation.96 | convolution fusion | flops 3708813312 | bytes 51969024 | tf_op jit(solution)/shard_map/transpose(jvp(crie,cle->cirl))/dot_general | solution.py:33
  1157.8 21.0 %fusion.72 = f32[3,1536,1,256]{1,3,0,2:T(8,128)S(1)} fusion(bf16[3,1536,1536]{1,2,0:T(8,128)(2,1)} %get-tuple-element.39, f32[3,1536]{1,0:T(4,128)S(1)} %neg.13, f32[3,1536]{1,0:T(4,128)S(1)} %copy-done.32, pred[1536,1536]{0,1:T(8,128)(4,1)S(1)} %copy-done.10, pred[3,1536]{1,0:T(4,128)(4,1)S(1)} %copy-done.45, pred[3,1536]{1,0:T(4,128)(4,1)S(1)} %copy-done.47, ...), kind=kOutput, calls=%fused_computation.101 | convolution fusion | flops 3708813312 | bytes 51969024 | tf_op jit(solution)/shard_map/transpose(jvp(crie,cle->cirl))/dot_general | solution.py:33
  1183.7 17.2 %fusion.85 = f32[3,1536,2048]{2,1,0:T(8,128)} fusion(bf16[2048,256]{1,0:T(8,128)(2,1)} %param.19, f32[3,1536,128]{1,2,0:T(8,128)} %get-tuple-element.24, f32[3,1536,128]{1,2,0:T(8,128)S(1)} %get-tuple-element.23), kind=kOutput, calls=%fused_computation.128 | convolution fusion | flops 4834197504 | bytes 43515904 | tf_op jit(solution)/shard_map/ble,de->bld/dot_general | solution.py:123
  1217.2 31.7 %add_convert_fusion = bf16[3,1536,2048]{2,1,0:T(8,128)(2,1)} fusion(f32[3,1536,2048]{2,1,0:T(8,128)} %fusion.82, f32[3,1536,2048]{2,1,0:T(8,128)} %fusion.85, bf16[3,1536,256]{2,1,0:T(8,128)(2,1)S(1)} %copy-done.18, bf16[2048,256]{1,0:T(8,128)(2,1)} %param.20), kind=kOutput, calls=%fused_computation.12 | convolution fusion | flops 4860149760 | bytes 97779712 | tf_op jit(solution)/shard_map/ble,de->bld/dot_general | solution.py:124
  1249.0 49.0 %convolution_bitcast_fusion = f32[2048,2048]{1,0:T(8,128)} fusion(bf16[3,1536,2048]{2,1,0:T(8,128)(2,1)} %get-tuple-element.22, bf16[3,1536,2048]{2,1,0:T(8,128)(2,1)} %all-gather.9.cloned.1.call-done), kind=kOutput, calls=%fused_computation.51 | convolution fusion | flops 38654705664 | bytes 54525952 | tf_op jit(solution)/shard_map/blf,bld->fd/dot_general | solution.py:99
  1298.0 48.7 %convolution_bitcast_fusion.2 = f32[2048,2048]{1,0:T(8,128)} fusion(bf16[3,1536,2048]{2,1,0:T(8,128)(2,1)} %all-gather.7.cloned.1.call-done, bf16[3,1536,2048]{2,1,0:T(8,128)(2,1)} %get-tuple-element.21), kind=kOutput, calls=%fused_computation.53 | convolution fusion | flops 38654705664 | bytes 54525952 | tf_op jit(solution)/shard_map/bld,blf->df/dot_general | solution.py:104
  1346.8 56.9 %convolution_bitcast_fusion.1 = f32[2048,2048]{1,0:T(8,128)} fusion(bf16[3,1536,2048]{2,1,0:T(8,128)(2,1)} %all-gather.7.cloned.1.call-done, bf16[3,1536,2048]{2,1,0:T(8,128)(2,1)} %convolution_convert_fusion.1, f32[3,1536,2048]{2,1,0:T(8,128)} %get-tuple-element.37), kind=kOutput, calls=%fused_computation.52 | convolution fusion | flops 38758514688 | bytes 92274688 | tf_op jit(solution)/shard_map/bld,blf->df/dot_general | solution.py:105
  1451.0 24.4 %all-reduce.4 = (f32[2048]{0:T(1024)}, f32[2048]{0:T(1024)}) all-reduce(f32[2048]{0:T(1024)S(1)} %get-tuple-element.13, f32[2048]{0:T(1024)S(1)} %copy-done.41), channel_id=1, replica_groups=mesh['dp'=2,'tp'=8] {'tp'}, use_global_device_ids=true, to_apply=%region_12.13 | all-reduce | flops 4096 | bytes 32768 | tf_op jit(solution)/shard_map/psum | solution.py:127
  1480.7 18.2 %all-reduce.8.cloned.1.call-done = (f32[2048,256]{1,0:T(8,128)}, f32[2048,256]{1,0:T(8,128)}) async-done(((f32[2048,256]{1,0:T(8,128)}, f32[2048,256]{1,0:T(8,128)}), (f32[2048,256]{1,0:T(8,128)}, f32[2048,256]{1,0:T(8,128)})) %all-reduce.8.cloned.1.call-update) | async-done | bytes 4194320 | tf_op jit(solution)/shard_map/psum | solution.py:120
  (165 shorter events, 209.4 us)
Async XLA Ops:
  7.2 185.0 %copy-start = (bf16[256,2048]{1,0:T(8,128)(2,1)S(1)}, bf16[256,2048]{1,0:T(8,128)(2,1)}, u32[]{:S(2)}) copy-start(bf16[256,2048]{1,0:T(8,128)(2,1)} %param.21) | copy-start | bytes 3145732
  7.2 105.7 %all-gather.5.cloned.1.call-start = ((), (), s32[]{:S(2)}) async-start(), calls=%async_computation.4 | async-start | bytes 21233664 | tf_op jit(solution)/shard_map/all_gather | solution.py:48
  15.1 306.2 %reduce-scatter.5.cloned.1.call-start = ((), (), s32[]{:S(2)}) async-start(), calls=%async_computation.5 | async-start | bytes 21233664 | tf_op jit(solution)/shard_map/reduce_scatter | solution.py:52
  15.3 159.0 %copy-start.44 = (pred[3,1536]{1,0:T(4,128)(4,1)}, pred[3,1536]{1,0:T(4,128)(4,1)S(1)}, u32[]{:S(2)}) copy-start(pred[3,1536]{1,0:T(4,128)(4,1)S(1)} %get-tuple-element.40) | copy-start | bytes 13828
  15.3 159.0 %copy-start.46 = (pred[3,1536]{1,0:T(4,128)(4,1)}, pred[3,1536]{1,0:T(4,128)(4,1)S(1)}, u32[]{:S(2)}) copy-start(pred[3,1536]{1,0:T(4,128)(4,1)S(1)} %get-tuple-element.41) | copy-start | bytes 13828
  18.1 116.2 %copy-start.5 = (f32[1536,128]{0,1:T(8,128)}, f32[1536,128]{0,1:T(8,128)S(1)}, u32[]{:S(2)}) copy-start(f32[1536,128]{0,1:T(8,128)S(1)} %get-tuple-element.33) | copy-start | bytes 2359300
  18.1 116.2 %copy-start.7 = (f32[1536,128]{0,1:T(8,128)}, f32[1536,128]{0,1:T(8,128)S(1)}, u32[]{:S(2)}) copy-start(f32[1536,128]{0,1:T(8,128)S(1)} %get-tuple-element.34) | copy-start | bytes 2359300
  201.4 119.9 %copy-start.1 = (bf16[3,192,2048]{2,1,0:T(8,128)(2,1)S(1)}, bf16[3,192,2048]{2,1,0:T(8,128)(2,1)}, u32[]{:S(2)}) copy-start(bf16[3,192,2048]{2,1,0:T(8,128)(2,1)} %param.13) | copy-start | bytes 7077892
  201.5 216.6 %all-gather.9.cloned.1.call-start = ((), (), s32[]{:S(2)}) async-start(), calls=%async_computation.8 | async-start | bytes 21233664 | tf_op jit(solution)/shard_map/all_gather | solution.py:48
  202.2 312.9 %all-gather.7.cloned.1.call-start = ((), (), s32[]{:S(2)}) async-start(), calls=%async_computation.6 | async-start | bytes 21233664 | tf_op jit(solution)/shard_map/all_gather | solution.py:48
  202.3 125.1 %copy-start.29 = (f32[2048]{0:T(1024)}, f32[2048]{0:T(1024)S(1)}, u32[]{:S(2)}) copy-start(f32[2048]{0:T(1024)S(1)} %convert_add_fusion.2) | copy-start | bytes 24580
  327.4 533.8 %reduce-scatter.9.cloned.1.call-start = ((), (), s32[]{:S(2)}) async-start(), calls=%async_computation.9 | async-start | bytes 21233664 | tf_op jit(solution)/shard_map/reduce_scatter | solution.py:52
  741.4 243.2 %reduce-scatter.7.cloned.1.call-start = ((), (), s32[]{:S(2)}) async-start(), calls=%async_computation.7 | async-start | bytes 21233664 | tf_op jit(solution)/shard_map/reduce_scatter | solution.py:52
  787.8 73.5 %copy-start.30 = (f32[2048]{0:T(1024)S(1)}, f32[2048]{0:T(1024)}, u32[]{:S(2)}) copy-start(f32[2048]{0:T(1024)} %copy-done.29) | copy-start | bytes 24580
  787.8 73.5 %copy-start.36 = (f32[3,192]{1,0:T(4,128)S(1)}, f32[3,192]{1,0:T(4,128)}, u32[]{:S(2)}) copy-start(f32[3,192]{1,0:T(4,128)} %copy-done.35) | copy-start | bytes 6916
  787.8 77.8 %copy-start.40 = (f32[3,192]{1,0:T(4,128)S(1)}, f32[3,192]{1,0:T(4,128)}, u32[]{:S(2)}) copy-start(f32[3,192]{1,0:T(4,128)} %copy-done.39) | copy-start | bytes 6916
  787.9 297.7 %all-gather.11.cloned.1.call-start = ((), (), s32[]{:S(2)}) async-start(), calls=%async_computation.10 | async-start | bytes 21233664 | tf_op jit(solution)/shard_map/all_gather | solution.py:48
  865.6 125.0 %copy-start.32 = (f32[3,1536]{1,0:T(4,128)S(1)}, f32[3,1536]{1,0:T(4,128)}, u32[]{:S(2)}) copy-start(f32[3,1536]{1,0:T(4,128)} %copy-done.31) | copy-start | bytes 55300
  990.6 456.6 %reduce-scatter.11.cloned.1.call-start = ((), (), s32[]{:S(2)}) async-start(), calls=%async_computation.11 | async-start | bytes 21233664 | tf_op jit(solution)/shard_map/reduce_scatter | solution.py:52
  990.7 105.7 %copy-start.10 = (pred[1536,1536]{0,1:T(8,128)(4,1)S(1)}, pred[1536,1536]{0,1:T(8,128)(4,1)}, u32[]{:S(2)}) copy-start(pred[1536,1536]{0,1:T(8,128)(4,1)} %iota_compare_fusion) | copy-start | bytes 7077892
  990.7 105.7 %copy-start.43 = (f32[3,1536]{1,0:T(4,128)S(1)}, f32[3,1536]{1,0:T(4,128)}, u32[]{:S(2)}) copy-start(f32[3,1536]{1,0:T(4,128)} %copy-done.42) | copy-start | bytes 55300
  990.7 105.7 %copy-start.45 = (pred[3,1536]{1,0:T(4,128)(4,1)S(1)}, pred[3,1536]{1,0:T(4,128)(4,1)}, u32[]{:S(2)}) copy-start(pred[3,1536]{1,0:T(4,128)(4,1)} %copy-done.44) | copy-start | bytes 13828
  990.7 105.7 %copy-start.47 = (pred[3,1536]{1,0:T(4,128)(4,1)S(1)}, pred[3,1536]{1,0:T(4,128)(4,1)}, u32[]{:S(2)}) copy-start(pred[3,1536]{1,0:T(4,128)(4,1)} %copy-done.46) | copy-start | bytes 13828
  1248.9 249.9 %all-reduce.8.cloned.1.call-start = ((), (), s32[]{:S(2)}) async-start(), calls=%async_computation.12 | async-start | bytes 8388608 | tf_op jit(solution)/shard_map/psum | solution.py:120
  (38 other events, 548.9 us)
Sparse Core Ops, SparseCore 0:
  15.3 97.5 all-gather.4
  201.6 119.7 reduce-scatter.4
  323.3 94.7 all-gather.8
  420.3 94.7 all-gather.6
  741.5 119.7 reduce-scatter.8
  864.7 119.7 reduce-scatter.6
  990.7 94.7 all-gather.10
  1249.1 119.7 reduce-scatter.10
  1425.5 73.2 all-reduce.7
where the time goes:
time: 1520 us; the launch traced here: 1510 us
  matrix products  741 us (49%)
  waiting for transfers between devices  659 us (43%)
  other arithmetic  56.8 us (4%)
  blocking collectives  24.4 us (2%)
  local copies, waits for them, and re-layouts  15.5 us (1%)
    all_gather x4, waiting for transfers between devices, gather_seq(): return lax.all_gather(x_loc, 'tp', axis=1, tiled=True)  329 us
    reduce_scatter x4, waiting for transfers between devices, scatter_seq(): return lax.psum_scatter(x_part, 'tp', scatter_dimension=1, tiled=True)  311 us
    dot_general x1, matrix products, local_layer(): jnp.einsum('bld,df->blf', gated_all, w_gate, preferred_element_type=jnp.f...  77.4 us
    dot_general x1, matrix products, local_layer(): jnp.einsum('bld,blf->df', gated_all, d_upper, preferred_element_type=jnp....  56.9 us
    dot_general x3, matrix products, attend(): jnp.einsum('crie,cle->cirl', query, keys, preferred_element_type=jnp.floa...  56.8 us
    dot_general x3, matrix products, attend(): jnp.einsum('cirl,cle->crie', probs, values, preferred_element_type=jnp.fl...  54.6 us
    dot_general x1, matrix products, local_layer(): jnp.einsum('blf,df->bld', d_upper, w_up, preferred_element_type=jnp.float32)  54.3 us
    dot_general x1, matrix products, local_layer(): jnp.einsum('blf,bld->fd', act, grad_all, preferred_element_type=jnp.float32)  49 us
  transfers between devices with their start and end apart: 9, of which 8 were waited for; matrix products, arithmetic and copies ran while one was open for 21% of the time, Pallas kernels for 0%

commit v1 on v0

v1 whole, which is shorter than its diff:
```python
import functools
import math
import jax
import jax.numpy as jnp
from jax import lax
from jax.experimental import pallas as pl
from jax.experimental.pallas import tpu as pltpu
from jax.sharding import PartitionSpec as P

NORM_EPS = 1e-6
BF16 = jnp.bfloat16
F32 = jnp.float32
GELU_C = math.sqrt(2.0 / math.pi)
GELU_K = 0.044715
MASKED = -1e30
NT = (((1,), (1,)), ((), ()))
TN = (((0,), (0,)), ((), ()))


def rms_norm(x_in, gain):
    x_f = x_in.astype(F32)
    inv_rms = lax.rsqrt(jnp.mean(x_f * x_f, axis=-1, keepdims=True) + NORM_EPS)
    return (x_f * inv_rms * (1.0 + gain)).astype(BF16)


def rope_tables(positions, head_dim):
    half_dim = head_dim // 2
    exponent = jnp.arange(half_dim, dtype=F32) * (2.0 / head_dim)
    inv_freq = jnp.exp(exponent * (-math.log(10000.0)))
    angles = positions.astype(F32)[:, None] * inv_freq[None, :]
    return jnp.cos(angles), jnp.sin(angles)


def apply_rope(x_f, cos_t, sin_t):
    half_dim = x_f.shape[-1] // 2
    first = x_f[..., :half_dim]
    second = x_f[..., half_dim:]
    return jnp.concatenate([first * cos_t - second * sin_t, second * cos_t + first * sin_t], axis=-1)


def dot_nn(a, b):
    return jnp.dot(a, b, preferred_element_type=F32)


def dot_nt(a, b):
    return lax.dot_general(a, b, NT, preferred_element_type=F32)


def dot_tn(a, b):
    return lax.dot_general(a, b, TN, preferred_element_type=F32)


def swap(x, bit):
    return lax.ppermute(x, "tp", [(t, t ^ bit) for t in range(8)])


def gather_relative(own):
    half = own.shape[0] // 2
    part = swap(own, 1)
    side = swap(own, 2)
    back = swap(own, 4)
    diag = jnp.concatenate([swap(side[:half], 4), swap(back[half:], 2)], axis=0)
    return [own, part, side, swap(side, 1), back, swap(back, 1), diag, swap(diag, 1)]


def scatter_relative(parts):
    def join(kept, came):
        return kept.astype(F32) + came.astype(F32)

    near = [join(parts[s], swap(parts[s + 1], 1)) for s in (0, 2, 4, 6)]
    own, side, back, diag = near
    half = diag.shape[0] // 2
    diag = diag.astype(parts[0].dtype)
    came_side = swap(diag[:half], 2)
    came_back = swap(diag[half:], 4)
    back = jnp.concatenate([join(back[:half], came_side), back[half:]], axis=0).astype(parts[0].dtype)
    side = jnp.concatenate([side[:half], join(side[half:], came_back)], axis=0).astype(parts[0].dtype)
    return own + swap(side, 2).astype(F32) + swap(back, 4).astype(F32)


def all_sum_small(x):
    for bit in (1, 2, 4):
        x = x + swap(x, bit)
    return x


def attn_fwd_kernel(lens_ref, kpos_ref, q_ref, k_ref, v_ref, o_ref, p_ref):
    heads, shard, head_dim = q_ref.shape
    tp = k_ref.shape[0]
    total = tp * shard
    s_id = pl.program_id(0)
    prefix = lens_ref[0, s_id]
    valid = lens_ref[1, s_id]
    first = lens_ref[2, 0] * shard
    keys = k_ref[...].reshape(total, head_dim)
    values = v_ref[...].reshape(total, head_dim)
    q_pos = first + lax.broadcasted_iota(jnp.int32, (shard, 1), 0)
    visible = kpos_ref[...] < jnp.minimum(valid, jnp.maximum(prefix, q_pos + 1))
    scale = head_dim ** -0.5
    query = q_ref[...].reshape(heads * shard, head_dim)
    scores = dot_nt(query, keys)
    for h in range(heads):
        rows = slice(h * shard, (h + 1) * shard)
        s = jnp.where(visible, scores[rows] * scale, MASKED)
        e = jnp.exp(s - jnp.max(s, axis=-1, keepdims=True))
        p_ref[rows, :] = (e / jnp.sum(e, axis=-1, keepdims=True)).astype(BF16)
    mixed = dot_nn(p_ref[...], values).astype(BF16)
    for h in range(heads):
        o_ref[:, h * head_dim:(h + 1) * head_dim] = mixed[h * shard:(h + 1) * shard]


def attn_bwd_kernel(lens_ref, q_ref, k_ref, v_ref, do_ref, dq_ref, dk_ref, dv_ref, dkv_acc):
    heads, shard, head_dim = q_ref.shape
    tp = k_ref.shape[0]
    total = tp * shard
    rows = heads * shard
    s_id = pl.program_id(0)
    g_id = pl.program_id(1)
    prefix = lens_ref[0, s_id]
    valid = lens_ref[1, s_id]
    first = lens_ref[2, 0] * shard
    keys = k_ref[...].reshape(total, head_dim)
    values = v_ref[...].reshape(total, head_dim)
    query = q_ref[...].reshape(rows, head_dim)
    d_out = jnp.concatenate([do_ref[:, h * head_dim:(h + 1) * head_dim] for h in range(heads)], axis=0)
    scale = head_dim ** -0.5
    step = lax.broadcasted_iota(jnp.int32, (shard, 1), 0)
    k_pos = jnp.concatenate([step + lens_ref[3 + r, 0] for r in range(tp)], axis=0)
    q_pos = first + lax.rem(lax.broadcasted_iota(jnp.int32, (1, rows), 1), shard)
    limit = jnp.minimum(valid, jnp.maximum(prefix, q_pos + 1))
    s = jnp.where(k_pos < limit, dot_nt(keys, query) * scale, MASKED)
    e = jnp.exp(s - jnp.max(s, axis=0, keepdims=True))
    p = e * (1.0 / jnp.sum(e, axis=0, keepdims=True))
    d_p = dot_nt(values, d_out)
    delta = jnp.sum(p * d_p, axis=0, keepdims=True)
    d_s = (p * (d_p - delta) * scale).astype(BF16)
    d_v = dot_nn(p.astype(BF16), d_out)
    d_k = dot_nn(d_s, query)
    dq_ref[...] = dot_tn(d_s, keys).astype(BF16).reshape(heads, shard, head_dim)

    @pl.when(g_id == 0)
    def _():
        dkv_acc[0] = d_k
        dkv_acc[1] = d_v

    @pl.when(g_id > 0)
    def _():
        dkv_acc[0] += d_k
        dkv_acc[1] += d_v

    @pl.when(g_id == pl.num_programs(1) - 1)
    def _():
        dk_ref[...] = dkv_acc[0].astype(BF16).reshape(tp, shard, head_dim)
        dv_ref[...] = dkv_acc[1].astype(BF16).reshape(tp, shard, head_dim)


def attention_forward(lens, k_pos, query, kv_all, batch, group=4):
    heads, rows, head_dim = query.shape
    tp = kv_all.shape[0]
    shard = rows // batch
    total = tp * shard
    q_spec = pl.BlockSpec((group, shard, head_dim), lambda s, g, *_: (g, s, 0))
    return pl.pallas_call(
        attn_fwd_kernel,
        out_shape=jax.ShapeDtypeStruct((rows, heads * head_dim), BF16),
        grid_spec=pltpu.PrefetchScalarGridSpec(
            num_scalar_prefetch=1, grid=(batch, heads // group),
            in_specs=[pl.BlockSpec((1, total), lambda s, g, *_: (0, 0)), q_spec,
                      pl.BlockSpec((tp, shard, head_dim), lambda s, g, *_: (0, s, 0)),
                      pl.BlockSpec((tp, shard, head_dim), lambda s, g, *_: (0, s, 1))],
            out_specs=pl.BlockSpec((shard, group * head_dim), lambda s, g, *_: (s, g)),
            scratch_shapes=[pltpu.VMEM((group * shard, total), BF16)]),
        compiler_params=pltpu.CompilerParams(dimension_semantics=("arbitrary", "arbitrary"), vmem_limit_bytes=48 << 20),
        cost_estimate=pl.CostEstimate(flops=4 * heads * rows * total * head_dim, bytes_accessed=12 << 20, transcendentals=heads * rows * total),
        name="attn_fwd",
    )(lens, k_pos, query, kv_all, kv_all)


def attention_backward(lens, query, kv_all, d_mixed, batch, group=4):
    heads, rows, head_dim = query.shape
    tp = kv_all.shape[0]
    shard = rows // batch
    total = tp * shard
    q_spec = pl.BlockSpec((group, shard, head_dim), lambda s, g, *_: (g, s, 0))
    kv_specs = [pl.BlockSpec((tp, shard, head_dim), lambda s, g, *_: (0, s, 0)),
                pl.BlockSpec((tp, shard, head_dim), lambda s, g, *_: (0, s, 1))]
    kv_out = pl.BlockSpec((tp, shard, head_dim), lambda s, g, *_: (0, s, 0))
    return pl.pallas_call(
        attn_bwd_kernel,
        out_shape=(jax.ShapeDtypeStruct((heads, rows, head_dim), BF16),
                   jax.ShapeDtypeStruct((tp, rows, head_dim), BF16),
                   jax.ShapeDtypeStruct((tp, rows, head_dim), BF16)),
        grid_spec=pltpu.PrefetchScalarGridSpec(
            num_scalar_prefetch=1, grid=(batch, heads // group),
            in_specs=[q_spec] + kv_specs + [pl.BlockSpec((shard, group * head_dim), lambda s, g, *_: (s, g))],
            out_specs=(q_spec, kv_out, kv_out),
            scratch_shapes=[pltpu.VMEM((2, total, head_dim), F32)]),
        compiler_params=pltpu.CompilerParams(dimension_semantics=("arbitrary", "arbitrary"), vmem_limit_bytes=56 << 20),
        cost_estimate=pl.CostEstimate(flops=10 * heads * rows * total * head_dim, bytes_accessed=20 << 20, transcendentals=heads * rows * total),
        name="attn_bwd",
    )(lens, query, kv_all, kv_all, d_mixed)


def gated_kernel(z_ref, g_ref, wg_ref, wu_ref, wd_ref, act_ref, dg_ref, du_ref, *, sub):
    for lo in range(0, z_ref.shape[0], sub):
        rows = slice(lo, lo + sub)
        gate = dot_nn(z_ref[rows], wg_ref[...])
        upper = dot_nn(z_ref[rows], wu_ref[...])
        d_act = dot_nt(g_ref[rows], wd_ref[...]).astype(BF16).astype(F32)
        sq = gate * gate
        th = jnp.tanh(gate * (GELU_C + (GELU_C * GELU_K) * sq))
        half = 0.5 + 0.5 * th
        gelu = gate * half
        slope = half + gate * (0.5 - 0.5 * (th * th)) * (GELU_C + (3.0 * GELU_C * GELU_K) * sq)
        act_ref[rows, :] = (gelu * upper).astype(BF16)
        du_ref[rows, :] = (d_act * gelu).astype(BF16)
        dg_ref[rows, :] = (d_act * upper * slope).astype(BF16)


def gated_layer(z_all, grad_all, w_gate, w_up, w_down, bm=1152, bn=512, sub=576):
    rows, dim = z_all.shape
    width = w_gate.shape[1]
    lhs = pl.BlockSpec((bm, dim), lambda i, j: (i, 0))
    col = pl.BlockSpec((dim, bn), lambda i, j: (0, j))
    out = pl.BlockSpec((bm, bn), lambda i, j: (i, j))
    shape = jax.ShapeDtypeStruct((rows, width), BF16)
    return pl.pallas_call(
        functools.partial(gated_kernel, sub=sub),
        out_shape=(shape, shape, shape),
        grid=(rows // bm, width // bn),
        in_specs=[lhs, lhs, col, col, pl.BlockSpec((bn, dim), lambda i, j: (j, 0))],
        out_specs=(out, out, out),
        compiler_params=pltpu.CompilerParams(dimension_semantics=("arbitrary", "arbitrary"), vmem_limit_bytes=58 << 20),
        cost_estimate=pl.CostEstimate(flops=6 * rows * dim * width, bytes_accessed=200 << 20, transcendentals=rows * width),
        name="gated",
    )(z_all, grad_all, w_gate, w_up, w_down)


def pair_kernel(a_ref, b_ref, wa_ref, wb_ref, o_ref):
    o_ref[...] = (dot_nt(a_ref[...], wa_ref[...]) + dot_nt(b_ref[...], wb_ref[...])).astype(BF16)


def pair_back(a, b, w_a, w_b, bm=1152, bn=512):
    rows, width = a.shape
    dim = w_a.shape[0]
    lhs = pl.BlockSpec((bm, width), lambda i, j: (i, 0))
    row = pl.BlockSpec((bn, width), lambda i, j: (j, 0))
    return pl.pallas_call(
        pair_kernel,
        out_shape=jax.ShapeDtypeStruct((rows, dim), BF16),
        grid=(rows // bm, dim // bn),
        in_specs=[lhs, lhs, row, row],
        out_specs=pl.BlockSpec((bm, bn), lambda i, j: (i, j)),
        compiler_params=pltpu.CompilerParams(dimension_semantics=("arbitrary", "arbitrary"), vmem_limit_bytes=56 << 20),
        cost_estimate=pl.CostEstimate(flops=4 * rows * dim * width, bytes_accessed=140 << 20, transcendentals=0),
        name="pair_back",
    )(a, b, w_a, w_b)


def solution(mesh):
    tp_size = mesh.shape["tp"]
    act_spec = P("dp", "tp", None)
    in_specs = (act_spec, act_spec, P("dp"), P("dp"), P(None), P(None, "tp"), P(None, None), P(None, None), P("tp", None), P(None), P(None, "tp"), P(None, "tp"), P("tp", None))
    out_specs = (act_spec, act_spec, P("dp"), P("dp", "tp"), P("dp", None), P("dp", None), P(("dp", "tp"), None), P("dp"), P("dp", "tp"), P("dp", "tp"), P(("dp", "tp"), None))

    def local_layer(hidden, grad_out, prefix_len, valid_len, attn_norm, w_query, w_key, w_value, w_out, mlp_norm, w_gate, w_up, w_down):
        batch, shard, dim = hidden.shape
        head_dim = w_key.shape[1]
        rows = batch * shard
        me = lax.axis_index("tp")
        starts = (me ^ jnp.arange(tp_size, dtype=jnp.int32)) * shard
        k_pos = (starts[:, None] + jnp.arange(shard, dtype=jnp.int32)).reshape(1, tp_size * shard)
        lens = jnp.concatenate([jnp.stack([prefix_len, valid_len, jnp.full((batch,), me, jnp.int32)]),
                                jnp.broadcast_to(starts[:, None], (tp_size, batch))])
        cos_t, sin_t = rope_tables(me * shard + jnp.arange(shard), head_dim)
        cos_t, sin_t = jnp.tile(cos_t, (batch, 1)), jnp.tile(sin_t, (batch, 1))

        def rope(raw_proj):
            return apply_rope(raw_proj, cos_t, sin_t).astype(BF16)

        wq_all = lax.all_gather(w_query, "tp", axis=0)
        hidden = hidden.reshape(rows, dim)
        grad_out = grad_out.reshape(rows, dim)
        normed, norm1_pull = jax.vjp(rms_norm, hidden, attn_norm.astype(F32))
        keys, key_pull = jax.vjp(rope, dot_nn(normed, w_key))
        values = dot_nn(normed, w_value).astype(BF16)
        kv_all = jnp.stack(gather_relative(jnp.concatenate([keys, values], axis=1)))
        wo_all = lax.all_gather(w_out, "tp", axis=0, tiled=True)
        grad_all = lax.all_gather(grad_out, "tp", axis=0, tiled=True)

        q_raw = jnp.einsum("td,hde->hte", normed, wq_all, preferred_element_type=F32)
        query, query_pull = jax.vjp(rope, q_raw)
        mixed = attention_forward(lens, k_pos, query, kv_all, batch)
        attn_out = dot_nn(mixed, wo_all)
        resid = (hidden.astype(F32) + attn_out).astype(BF16)
        gated_in, norm2_pull = jax.vjp(rms_norm, resid, mlp_norm.astype(F32))
        gated_all = lax.all_gather(gated_in, "tp", axis=0, tiled=True)

        act, d_gate, d_upper = gated_layer(gated_all, grad_all, w_gate, w_up, w_down)
        d_gated_part = pair_back(d_gate, d_upper, w_gate, w_up)
        d_gated = lax.psum_scatter(d_gated_part, "tp", scatter_dimension=0, tiled=True)
        mlp_part = dot_nn(act, w_down).astype(BF16)
        mlp_sum = lax.psum_scatter(mlp_part, "tp", scatter_dimension=0, tiled=True)
        hidden_out = (resid.astype(F32) + mlp_sum.astype(F32)).astype(BF16)
        g_down = dot_tn(act, grad_all)
        g_gate = dot_tn(gated_all, d_gate)
        g_up = dot_tn(gated_all, d_upper)

        d_resid_norm, g_mlp_norm_part = norm2_pull(d_gated)
        d_resid = (grad_out.astype(F32) + d_resid_norm.astype(F32)).astype(BF16)
        g_out = lax.psum_scatter(dot_tn(mixed, d_resid), "tp", scatter_dimension=0, tiled=True)
        d_mixed = dot_nt(d_resid, wo_all).astype(BF16)
        d_query, d_keys_part, d_values_part = attention_backward(lens, query, kv_all, d_mixed, batch)
        d_keys = scatter_relative(d_keys_part).astype(BF16)
        d_values = scatter_relative(d_values_part).astype(BF16)
        d_q_raw = query_pull(d_query)[0].astype(BF16)
        d_k_raw = key_pull(d_keys)[0].astype(BF16)
        g_query = lax.psum_scatter(jnp.einsum("td,hte->hde", normed, d_q_raw, preferred_element_type=F32), "tp", scatter_dimension=0, tiled=False)
        g_key = lax.psum(dot_tn(normed, d_k_raw), "tp")
        g_value = lax.psum(dot_tn(normed, d_values), "tp")
        d_normed = (jnp.einsum("hte,hde->td", d_q_raw, wq_all, preferred_element_type=F32)
                    + dot_nt(d_k_raw, w_key) + dot_nt(d_values, w_value)).astype(BF16)
        d_hidden_norm, g_attn_norm_part = norm1_pull(d_normed)
        grad_hidden = (d_resid.astype(F32) + d_hidden_norm.astype(F32)).astype(BF16)
        g_norms = all_sum_small(jnp.stack([g_attn_norm_part, g_mlp_norm_part]))
        full = (batch, shard, dim)
        return (hidden_out.reshape(full), grad_hidden.reshape(full), g_norms[0], g_query, g_key, g_value, g_out, g_norms[1], g_gate, g_up, g_down)

    return jax.shard_map(local_layer, mesh=mesh, in_specs=in_specs, out_specs=out_specs, check_vma=False)
```

time: 1520 us -> 1170 us (0.77)
  matrix products: 741 us -> 261 us
  Pallas kernels: 0 us -> 280 us
  waiting for transfers between devices: 659 us -> 535 us
  other arithmetic: 56.8 us -> 25.6 us
  blocking collectives: 24.4 us -> 0 us
  starting transfers between devices: 0.37 us -> 21.6 us
    dot_general x27 -> x16, matrix products: 741 us -> 261 us  [the longest x6 163 us: dot_tn(): return lax.dot_general(a, b, TN, preferred_element_type=F32)]
    pallas_call x0 -> x4, Pallas kernels: none -> 280 us  [the longest x1 133 us: gated_layer(): pl.pallas_call(functools.partial(gated_kernel, sub=sub), out_shape=(shape...]
    all_gather x4, waiting for transfers between devices: 329 us -> 215 us  [the longest x1 97.1 us: local_layer(): gated_all = lax.all_gather(gated_in, 'tp', axis=0, tiled=True)]
    ppermute x0 -> x27, waiting for transfers between devices: none -> 48.1 us  [swap(): return lax.ppermute(x, 'tp', [(t, t ^ bit) for t in range(8)])]
    reduce_scatter x4, waiting for transfers between devices: 311 us -> 270 us  [the longest x1 119 us: local_layer(): mlp_sum = lax.psum_scatter(mlp_part, 'tp', scatter_dimension=0, tiled=True)]
    psum x1 -> x0, blocking collectives: 24.4 us -> none  [local_layer(): g_attn_norm = lax.psum(g_attn_norm_part, 'tp')]
    ppermute x0 -> x27, starting transfers between devices: none -> 21.2 us  [swap(): return lax.ppermute(x, 'tp', [(t, t ^ bit) for t in range(8)])]
    reduce_sum x3 -> x1, other arithmetic: 22.8 us -> 4.17 us  [rms_norm(): return (x_f * inv_rms * (1.0 + gain)).astype(BF16)]
  transfers between devices with their start and end apart: 9 -> 36, of which waited for: 8 -> 17; matrix products, arithmetic and copies ran while one was open for 21% -> 23% of each run, Pallas kernels for 0% -> 2%
where the time goes in v1:
time: 1170 us
  waiting for transfers between devices  535 us (46%)
  Pallas kernels  280 us (24%)
  matrix products  261 us (22%)
  local copies, waits for them, and re-layouts  30.6 us (3%)
  other arithmetic  25.6 us (2%)
  starting transfers between devices  21.6 us (2%)
  between operations  15.2 us (1%)
    dot_general x6, matrix products, dot_tn(): return lax.dot_general(a, b, TN, preferred_element_type=F32)  163 us
    pallas_call x1, Pallas kernels, gated_layer(): pl.pallas_call(functools.partial(gated_kernel, sub=sub), out_shape=(shape...  133 us
    reduce_scatter x1, waiting for transfers between devices, local_layer(): mlp_sum = lax.psum_scatter(mlp_part, 'tp', scatter_dimension=0, tiled=True)  119 us
    all_gather x1, waiting for transfers between devices, local_layer(): gated_all = lax.all_gather(gated_in, 'tp', axis=0, tiled=True)  97.1 us
    pallas_call x1, Pallas kernels, pair_back(): pl.pallas_call(pair_kernel, out_shape=jax.ShapeDtypeStruct((rows, dim), B...  88.8 us
    all_gather x1, waiting for transfers between devices, local_layer(): grad_all = lax.all_gather(grad_out, 'tp', axis=0, tiled=True)  85.1 us
    reduce_scatter x1, waiting for transfers between devices, local_layer(): lax.psum_scatter(dot_tn(mixed, d_resid), 'tp', scatter_dimension=0, tiled...  77.6 us
    reduce_scatter x1, waiting for transfers between devices, local_layer(): lax.psum_scatter(d_gated_part, 'tp', scatter_dimension=0, tiled=True)  73.7 us
  transfers between devices with their start and end apart: 36, of which 17 were waited for; matrix products, arithmetic and copies ran while one was open for 23% of the time, Pallas kernels for 2%

profile of v1, /device:TPU:0, one launch (start us, length us, event | category | flops | bytes accessed | tf_op | source)
XLA Modules:
  0.0 1169.0 jit_solution(8513122089964284813)
XLA Ops:
  20.5 21.1 %collective-permute-done.1 = bf16[576,512]{1,0:T(8,128)(2,1)S(1)} collective-permute-done((bf16[576,512]{1,0:T(8,128)(2,1)}, bf16[576,512]{1,0:T(8,128)(2,1)S(1)}, u32[]{:S(2)}, u32[]{:S(2)}) %collective-permute-start.1) | collective-permute-done | bytes 589856 | tf_op jit(solution)/shard_map/ppermute | solution.py:54
  53.0 6.7 collective-permute-done.6
  64.0 14.0 %all-gather.12.cloned.1.call-done = bf16[16384,256]{1,0:T(8,128)(2,1)} async-done(((bf16[2048,256]{1,0:T(8,128)(2,1)}), bf16[16384,256]{1,0:T(8,128)(2,1)}) %all-gather.12.cloned.1.call-update) | async-done | bytes 8388624 | tf_op jit(solution)/shard_map/all_gather | solution.py:281
  78.1 7.7 fusion.18
  86.8 23.5 %attn_fwd.1 = bf16[576,2048]{1,0:T(8,128)(2,1)S(1)} custom-call(s32[11,3]{1,0:T(8,128)S(1)} %add_add_fusion.2.lens_ref, s32[1,1536]{1,0:T(1,128)S(1)} %add.166.kpos_ref, bf16[8,576,256]{2,1,0:T(8,128)(2,1)S(1)} %pad_maximum_fusion.q_ref, bf16[8,576,512]{2,1,0:T(8,128)(2,1)} %bitcast_dynamic-update-slice_fusion.k_ref.v_ref, ...), custom_call_target="tpu_custom_call" | custom-call | flops 7247757312 | bytes 12582912 | tf_op jit(solution)/shard_map/attn_fwd/pallas_call | solution.py:163
  111.8 18.6 %all-gather.6.cloned.1.call-done = bf16[2048,2048]{1,0:T(8,128)(2,1)} async-done(((bf16[256,2048]{1,0:T(8,128)(2,1)}), bf16[2048,2048]{1,0:T(8,128)(2,1)}) %all-gather.6.cloned.1.call-update) | async-done | bytes 8388624 | tf_op jit(solution)/shard_map/all_gather | solution.py:288
  130.4 8.0 fusion.10
  142.0 85.1 %all-gather.10.cloned.1.call-done.g_ref = bf16[4608,2048]{1,0:T(8,128)(2,1)} async-done(((bf16[576,2048]{1,0:T(8,128)(2,1)}), bf16[4608,2048]{1,0:T(8,128)(2,1)}) %all-gather.10.cloned.1.call-update) | async-done | bytes 18874384 | tf_op jit(solution)/shard_map/all_gather | solution.py:289
  227.0 97.1 %all-gather.8.cloned.1.call-done.z_ref = bf16[4608,2048]{1,0:T(8,128)(2,1)} async-done(((bf16[576,2048]{1,0:T(8,128)(2,1)}), bf16[4608,2048]{1,0:T(8,128)(2,1)}) %all-gather.8.cloned.1.call-update) | async-done | bytes 18874384 | tf_op jit(solution)/shard_map/all_gather | solution.py:297
  324.1 133.0 %gated.1 = (bf16[4608,2048]{1,0:T(8,128)(2,1)}, bf16[4608,2048]{1,0:T(8,128)(2,1)}, bf16[4608,2048]{1,0:T(8,128)(2,1)}) custom-call(bf16[4608,2048]{1,0:T(8,128)(2,1)} %all-gather.8.cloned.1.call-done.z_ref, bf16[4608,2048]{1,0:T(8,128)(2,1)} %all-gather.10.cloned.1.call-done.g_ref, bf16[2048,2048]{1,0:T(8,128)(2,1)} %wa_ref.1, bf16[2048,2048]{1,0:T(8,128)(2,1)} %wb_ref.1, ...), custom_call_target="tpu_custom_call" | custom-call | flops 115964116992 | bytes 209715200 | tf_op jit(solution)/shard_map/gated/pallas_call | solution.py:227
  457.1 88.8 %pair_back.1 = bf16[4608,2048]{1,0:T(8,128)(2,1)} custom-call(bf16[4608,2048]{1,0:T(8,128)(2,1)} %get-tuple-element.18.a_ref, bf16[4608,2048]{1,0:T(8,128)(2,1)} %get-tuple-element.19.b_ref, bf16[2048,2048]{1,0:T(8,128)(2,1)} %wa_ref.1, bf16[2048,2048]{1,0:T(8,128)(2,1)} %wb_ref.1), custom_call_target="tpu_custom_call" | custom-call | flops 77309411328 | bytes 146800640 | tf_op jit(solution)/shard_map/pair_back/pallas_call | solution.py:248
  546.0 46.1 %convolution_convert_fusion = bf16[4608,2048]{1,0:T(8,128)(2,1)} fusion(bf16[4608,2048]{1,0:T(8,128)(2,1)} %get-tuple-element.17, bf16[2048,2048]{1,0:T(8,128)(2,1)} %wd_ref.1), kind=kOutput, calls=%fused_computation | convolution fusion | flops 38664142848 | bytes 46137344 | tf_op jit(solution)/shard_map/dot_general | solution.py:42
  592.2 73.7 %reduce-scatter.7.cloned.1.call-done = bf16[576,2048]{1,0:T(8,128)(2,1)} async-done(((bf16[4608,2048]{1,0:T(8,128)(2,1)}), bf16[576,2048]{1,0:T(8,128)(2,1)}) %reduce-scatter.7.cloned.1.call-update) | async-done | bytes 2359312 | tf_op jit(solution)/shard_map/reduce_scatter | solution.py:301
  670.1 119.0 %reduce-scatter.5.cloned.1.call-done = bf16[576,2048]{1,0:T(8,128)(2,1)} async-done(((bf16[4608,2048]{1,0:T(8,128)(2,1)}), bf16[576,2048]{1,0:T(8,128)(2,1)}) %reduce-scatter.5.cloned.1.call-update) | async-done | bytes 2359312 | tf_op jit(solution)/shard_map/reduce_scatter | solution.py:303
  789.2 5.8 add_convert_fusion.2
  796.4 9.7 convolution_convert_fusion.1.do_ref
  806.1 34.5 %attn_bwd.1 = (bf16[8,576,256]{2,1,0:T(8,128)(2,1)}, bf16[8,576,256]{2,1,0:T(8,128)(2,1)}, bf16[8,576,256]{2,1,0:T(8,128)(2,1)}) custom-call(s32[11,3]{1,0:T(8,128)} %copy-done.2, bf16[8,576,256]{2,1,0:T(8,128)(2,1)} %copy-done.1, bf16[8,576,512]{2,1,0:T(8,128)(2,1)} %bitcast_dynamic-update-slice_fusion.k_ref.v_ref, ...), custom_call_target="tpu_custom_call" | custom-call | flops 18119393280 | bytes 20971520 | tf_op jit(solution)/shard_map/attn_bwd/pallas_call | solution.py:188
  845.6 10.7 convolution_bitcast_fusion
  892.9 11.9 %fusion.56 = f32[2048,2048]{1,0:T(8,128)} fusion(bf16[576,2048]{1,0:T(8,128)(2,1)S(1)} %copy-done.4, bf16[576,2048]{1,0:T(8,128)(2,1)} %copy-done.9), kind=kOutput, calls=%fused_computation.141 | convolution fusion | flops 4831838208 | bytes 21495808 | tf_op jit(solution)/shard_map/dot_general | solution.py:50
  904.8 48.8 %fusion.59 = f32[2048,2048]{1,0:T(8,128)} fusion(bf16[4608,2048]{1,0:T(8,128)(2,1)} %get-tuple-element.17, bf16[4608,2048]{1,0:T(8,128)(2,1)} %all-gather.10.cloned.1.call-done.g_ref), kind=kOutput, calls=%fused_computation.144 | convolution fusion | flops 38654705664 | bytes 54525952 | tf_op jit(solution)/shard_map/dot_general | solution.py:50
  953.6 48.9 %fusion.57 = f32[2048,2048]{1,0:T(8,128)} fusion(bf16[4608,2048]{1,0:T(8,128)(2,1)} %all-gather.8.cloned.1.call-done.z_ref, bf16[4608,2048]{1,0:T(8,128)(2,1)} %get-tuple-element.18.a_ref), kind=kOutput, calls=%fused_computation.142 | convolution fusion | flops 38654705664 | bytes 54525952 | tf_op jit(solution)/shard_map/dot_general | solution.py:50
  1002.5 8.4 fusion.29
  1017.5 48.6 %fusion.58 = f32[2048,2048]{1,0:T(8,128)} fusion(bf16[4608,2048]{1,0:T(8,128)(2,1)} %all-gather.8.cloned.1.call-done.z_ref, bf16[4608,2048]{1,0:T(8,128)(2,1)} %get-tuple-element.19.b_ref), kind=kOutput, calls=%fused_computation.143 | convolution fusion | flops 38654705664 | bytes 54525952 | tf_op jit(solution)/shard_map/dot_general | solution.py:50
  1080.0 77.6 %reduce-scatter.11.cloned.1.call-done = f32[256,2048]{1,0:T(8,128)} async-done(((f32[2048,2048]{1,0:T(8,128)}), f32[256,2048]{1,0:T(8,128)}) %reduce-scatter.11.cloned.1.call-update) | async-done | bytes 2097168 | tf_op jit(solution)/shard_map/reduce_scatter | solution.py:311
  (270 shorter events, 106.4 us)
Async XLA Ops:
  7.2 70.8 %all-gather.12.cloned.1.call-start = ((), (), s32[]{:S(2)}) async-start(), calls=%async_computation.11 | async-start | bytes 9437184 | tf_op jit(solution)/shard_map/all_gather | solution.py:281
  7.9 122.4 %all-gather.6.cloned.1.call-start = ((), (), s32[]{:S(2)}) async-start(), calls=%async_computation.4 | async-start | bytes 9437184 | tf_op jit(solution)/shard_map/all_gather | solution.py:288
  8.7 218.3 %all-gather.10.cloned.1.call-start = ((), (), s32[]{:S(2)}) async-start(), calls=%async_computation.6 | async-start | bytes 21233664 | tf_op jit(solution)/shard_map/all_gather | solution.py:289
  9.4 314.7 %all-gather.8.cloned.1.call-start = ((), (), s32[]{:S(2)}) async-start(), calls=%async_computation.5 | async-start | bytes 21233664 | tf_op jit(solution)/shard_map/all_gather | solution.py:297
  14.5 27.1 %collective-permute-start.1 = (bf16[576,512]{1,0:T(8,128)(2,1)}, bf16[576,512]{1,0:T(8,128)(2,1)S(1)}, u32[]{:S(2)}, u32[]{:S(2)}) collective-permute-start(bf16[576,512]{1,0:T(8,128)(2,1)} %pad_maximum_fusion.1), channel_id=1, source_target_pairs={{0,2},{1,3},{2,0},{3,1},{4,6},{5,7},{6,4},{7,5},{8,10},{9,11},{10,... | collective-permute-start | bytes 1769480 | tf_op jit(solution)/shard_map/ppermute | solution.py:54
  17.7 29.3 %collective-permute-start = (bf16[576,512]{1,0:T(8,128)(2,1)}, bf16[576,512]{1,0:T(8,128)(2,1)}, u32[]{:S(2)}, u32[]{:S(2)}) collective-permute-start(bf16[576,512]{1,0:T(8,128)(2,1)} %pad_maximum_fusion.1), channel_id=1, source_target_pairs={{0,1},{1,0},{2,3},{3,2},{4,5},{5,4},{6,7},{7,6},{8,9},{9,8},{10,11... | collective-permute-start | bytes 1769480 | tf_op jit(solution)/shard_map/ppermute | solution.py:54
  17.7 27.4 %collective-permute-start.3 = (bf16[576,512]{1,0:T(8,128)(2,1)}, bf16[576,512]{1,0:T(8,128)(2,1)S(1)}, u32[]{:S(2)}, u32[]{:S(2)}) collective-permute-start(bf16[576,512]{1,0:T(8,128)(2,1)} %pad_maximum_fusion.1), channel_id=1, source_target_pairs={{0,4},{1,5},{2,6},{3,7},{4,0},{5,1},{6,2},{7,3},{8,12},{9,13},{10,... | collective-permute-start | bytes 1769480 | tf_op jit(solution)/shard_map/ppermute | solution.py:54
  41.6 11.4 collective-permute-start.5
  46.0 13.7 %collective-permute-start.6 = (bf16[288,512]{1,0:T(8,128)(2,1)S(1)}, bf16[288,512]{1,0:T(8,128)(2,1)S(1)}, u32[]{:S(2)}, u32[]{:S(2)}) collective-permute-start(bf16[288,512]{1,0:T(8,128)(2,1)S(1)} %slice.153), channel_id=1, source_target_pairs={{0,2},{1,3},{2,0},{3,1},{4,6},{5,7},{6,4},{7,5},{8,10},{9,11},{10,... | collective-permute-start | bytes 884744 | tf_op jit(solution)/shard_map/ppermute | solution.py:54
  46.5 13.3 %collective-permute-start.2 = (bf16[576,512]{1,0:T(8,128)(2,1)}, bf16[576,512]{1,0:T(8,128)(2,1)S(1)}, u32[]{:S(2)}, u32[]{:S(2)}) collective-permute-start(bf16[576,512]{1,0:T(8,128)(2,1)} %copy-done.31), channel_id=1, source_target_pairs={{0,1},{1,0},{2,3},{3,2},{4,5},{5,4},{6,7},{7,6},{8,9},{9,8},{10,11... | collective-permute-start | bytes 1769480 | tf_op jit(solution)/shard_map/ppermute | solution.py:54
  46.5 15.0 %collective-permute-start.4 = (bf16[576,512]{1,0:T(8,128)(2,1)}, bf16[576,512]{1,0:T(8,128)(2,1)S(1)}, u32[]{:S(2)}, u32[]{:S(2)}) collective-permute-start(bf16[576,512]{1,0:T(8,128)(2,1)} %copy-done.29), channel_id=1, source_target_pairs={{0,1},{1,0},{2,3},{3,2},{4,5},{5,4},{6,7},{7,6},{8,9},{9,8},{10,11... | collective-permute-start | bytes 1769480 | tf_op jit(solution)/shard_map/ppermute | solution.py:54
  141.9 524.0 %reduce-scatter.7.cloned.1.call-start = ((), (), s32[]{:S(2)}) async-start(), calls=%async_computation.8 | async-start | bytes 21233664 | tf_op jit(solution)/shard_map/reduce_scatter | solution.py:301
  546.0 243.2 %reduce-scatter.5.cloned.1.call-start = ((), (), s32[]{:S(2)}) async-start(), calls=%async_computation.7 | async-start | bytes 21233664 | tf_op jit(solution)/shard_map/reduce_scatter | solution.py:303
  592.2 484.9 %reduce-scatter.9.cloned.1.call-start = ((), (), s32[]{:S(2)}) async-start(), calls=%async_computation.9 | async-start | bytes 18874368 | tf_op jit(solution)/shard_map/reduce_scatter | solution.py:318
  856.3 223.6 %all-reduce.7.cloned.1.call-start = ((), (), s32[]{:S(2)}) async-start(), calls=%async_computation.12 | async-start | bytes 8388608 | tf_op jit(solution)/shard_map/psum | solution.py:319
  858.7 19.1 %collective-permute-start.8 = (bf16[576,256]{1,0:T(8,128)(2,1)S(1)}, bf16[576,256]{1,0:T(8,128)(2,1)S(1)}, u32[]{:S(2)}, u32[]{:S(2)}) collective-permute-start(bf16[576,256]{1,0:T(8,128)(2,1)S(1)} %get-tuple-element.73), channel_id=1, source_target_pairs={{0,1},{1,0},{2,3},{3,2},{4,5},{5,4},{6,7},{7,6},{8,9},{9,8},{10,11... | collective-permute-start | bytes 884744 | tf_op jit(solution)/shard_map/ppermute | solution.py:54
  860.4 28.4 %collective-permute-start.16 = (bf16[576,256]{1,0:T(8,128)(2,1)S(1)}, bf16[576,256]{1,0:T(8,128)(2,1)S(1)}, u32[]{:S(2)}, u32[]{:S(2)}) collective-permute-start(bf16[576,256]{1,0:T(8,128)(2,1)S(1)} %get-tuple-element.66), channel_id=1, source_target_pairs={{0,1},{1,0},{2,3},{3,2},{4,5},{5,4},{6,7},{7,6},{8,9},{9,8},{10,11... | collective-permute-start | bytes 884744 | tf_op jit(solution)/shard_map/ppermute | solution.py:54
  865.9 10.8 collective-permute-start.19
  871.6 9.9 collective-permute-start.15
  875.5 9.9 collective-permute-start.12
  876.7 12.1 %collective-permute-start.23 = (bf16[576,256]{1,0:T(8,128)(2,1)S(1)}, bf16[576,256]{1,0:T(8,128)(2,1)S(1)}, u32[]{:S(2)}, u32[]{:S(2)}) collective-permute-start(bf16[576,256]{1,0:T(8,128)(2,1)S(1)} %pad_maximum_fusion.5), channel_id=1, source_target_pairs={{0,4},{1,5},{2,6},{3,7},{4,0},{5,1},{6,2},{7,3},{8,12},{9,13},{10,... | collective-permute-start | bytes 884744 | tf_op jit(solution)/shard_map/ppermute | solution.py:54
  877.7 11.1 collective-permute-start.20
  892.8 264.8 %reduce-scatter.11.cloned.1.call-start = ((), (), s32[]{:S(2)}) async-start(), calls=%async_computation.10 | async-start | bytes 18874368 | tf_op jit(solution)/shard_map/reduce_scatter | solution.py:311
  1017.4 48.6 %collective-permute-start.24 = (f32[2,2048]{1,0:T(2,128)S(1)}, f32[2,2048]{1,0:T(2,128)S(1)}, u32[]{:S(2)}, u32[]{:S(2)}) collective-permute-start(f32[2,2048]{1,0:T(2,128)S(1)} %pad_maximum_fusion.6), channel_id=1, source_target_pairs={{0,1},{1,0},{2,3},{3,2},{4,5},{5,4},{6,7},{7,6},{8,9},{9,8},{10,11... | collective-permute-start | bytes 49160 | tf_op jit(solution)/shard_map/ppermute | solution.py:54
  (73 other events, 1380.2 us)
Sparse Core Ops, SparseCore 0:
  9.9 68.1 all-gather.11
  79.9 50.4 all-gather.5
  132.2 94.7 all-gather.9
  229.3 94.7 all-gather.7
  546.1 119.7 reduce-scatter.6
  669.4 119.7 reduce-scatter.4
  856.5 110.3 reduce-scatter.8
  970.8 72.9 all-reduce.6
  1047.8 109.7 reduce-scatter.10

commit v2 on v1

--- a/solution.py
+++ b/solution.py
@@ -201,39 +201,223 @@
     )(lens, query, kv_all, kv_all, d_mixed)
 
 
-def gated_kernel(z_ref, g_ref, wg_ref, wu_ref, wd_ref, act_ref, dg_ref, du_ref, *, sub):
-    for lo in range(0, z_ref.shape[0], sub):
-        rows = slice(lo, lo + sub)
-        gate = dot_nn(z_ref[rows], wg_ref[...])
-        upper = dot_nn(z_ref[rows], wu_ref[...])
-        d_act = dot_nt(g_ref[rows], wd_ref[...]).astype(BF16).astype(F32)
-        sq = gate * gate
-        th = jnp.tanh(gate * (GELU_C + (GELU_C * GELU_K) * sq))
-        half = 0.5 + 0.5 * th
-        gelu = gate * half
-        slope = half + gate * (0.5 - 0.5 * (th * th)) * (GELU_C + (3.0 * GELU_C * GELU_K) * sq)
-        act_ref[rows, :] = (gelu * upper).astype(BF16)
-        du_ref[rows, :] = (d_act * gelu).astype(BF16)
-        dg_ref[rows, :] = (d_act * upper * slope).astype(BF16)
-
-
-def gated_layer(z_all, grad_all, w_gate, w_up, w_down, bm=1152, bn=512, sub=576):
-    rows, dim = z_all.shape
+def flip(index, bit):
+    return index + bit - 2 * bit * ((index // bit) % 2)
+
+
+def neighbours():
+    me = lax.axis_index("tp")
+    return me, flip(me, 1), flip(me, 2), flip(me, 4)
+
+
+def enter(peers):
+    barrier = pltpu.get_barrier_semaphore()
+    for peer in peers:
+        pl.semaphore_signal(barrier, inc=1, device_id={"tp": peer}, device_id_type=pl.DeviceIdType.MESH)
+    pl.semaphore_wait(barrier, len(peers))
+
+
+def gated_tile(z, g, w_g, w_u, w_d):
+    gate = dot_nn(z, w_g)
+    upper = dot_nn(z, w_u)
+    d_act = dot_nt(g, w_d).astype(BF16).astype(F32)
+    sq = gate * gate
+    th = jnp.tanh(gate * (GELU_C + (GELU_C * GELU_K) * sq))
+    half = 0.5 + 0.5 * th
+    gelu = gate * half
+    slope = half + gate * (0.5 - 0.5 * (th * th)) * (GELU_C + (3.0 * GELU_C * GELU_K) * sq)
+    return (gelu * upper).astype(BF16), (d_act * upper * slope).astype(BF16), (d_act * gelu).astype(BF16)
+
+
+def gated_kernel(z_own, g_own, wg_hbm, wu_hbm, wd_hbm, z_all, g_all, act, d_gate, d_up,
+                 wg, wu, wd, z_buf, g_buf, outs, w_sem, in_sem, own_sem, out_sem, send, recv, send0, recv0, *, bn):
+    rows, dim = z_own.shape
+    width = wg_hbm.shape[1]
+    steps = width // bn
+    piece = rows // 4
+    me, core, side, back = neighbours()
+    corner = flip(side, 4)
+    own = (z_own, g_own)
+    full = (z_all, g_all)
+
+    def remote(src, dst, sems, peer):
+        return pltpu.make_async_remote_copy(src_ref=src, dst_ref=dst, send_sem=sems[0], recv_sem=sems[1],
+                                            device_id={"tp": peer}, device_id_type=pl.DeviceIdType.MESH)
+
+    def part(slot, q):
+        return pl.ds(pl.multiple_of(slot * rows + q * piece, 16), piece)
+
+    def link_rows(u, path):
+        turn = u // 2
+        diag = turn % 2
+        if path == 0:
+            return side + (corner - side) * diag, (u % 2) + 2 * (turn // 2) + diag * 2
+        return back + (corner - back) * diag, (u % 2) + 2 - 2 * (turn // 2) - diag * 2
+
+    def link_copy(u, path, a):
+        turn = u // 2
+        peer = side if path == 0 else back
+        sems = (send.at[path, u, a], recv.at[path, u, a])
+        if turn == 1:
+            slot = back if path == 0 else side
+            q = (2 if path == 0 else 0) + u % 2
+            return remote(full[a].at[part(slot, q)], full[a].at[part(slot, q)], sems, peer)
+        q = u % 2 + (2 * (turn // 2) if path == 0 else 2 - 2 * (turn // 2))
+        return remote(own[a].at[pl.ds(q * piece, piece)], full[a].at[part(me, q)], sems, peer)
+
+    def core_copy(u, path, a):
+        slot, q = link_rows(u, path)
+        return remote(full[a].at[part(slot, q)], full[a].at[part(slot, q)], (send.at[2 + path, u, a], recv.at[2 + path, u, a]), core)
+
+    def own_copy(a):
+        return remote(own[a], full[a].at[pl.ds(pl.multiple_of(me * rows, 16), rows)], (send0.at[a], recv0.at[a]), core)
+
+    def weight_copies(n):
+        cols = pl.ds(pl.multiple_of(n * bn, 128), bn)
+        return [pltpu.make_async_copy(wg_hbm.at[:, cols], wg.at[:, cols], w_sem.at[0, n]),
+                pltpu.make_async_copy(wu_hbm.at[:, cols], wu.at[:, cols], w_sem.at[1, n]),
+                pltpu.make_async_copy(wd_hbm.at[cols], wd.at[cols], w_sem.at[2, n])]
+
+    bufs = (z_buf, g_buf)
+    own_in = [pltpu.make_async_copy(own[a], bufs[a], own_sem.at[a]) for a in range(2)]
+    own_out = [pltpu.make_async_copy(bufs[a], full[a].at[pl.ds(pl.multiple_of(me * rows, 16), rows)], own_sem.at[2 + a]) for a in range(2)]
+    for cp in own_in:
+        cp.start()
+    for n in range(steps):
+        for cp in weight_copies(n):
+            cp.start()
+    enter((core, side, back))
+    for u in range(2):
+        for path in range(2):
+            for a in range(2):
+                link_copy(u, path, a).start()
+        if u == 0:
+            for a in range(2):
+                own_copy(a).start()
+
+    def out_copies(slot, s_rows, n):
+        cols = pl.ds(pl.multiple_of(n * bn, 128), bn)
+        return [pltpu.make_async_copy(outs.at[slot, k, pl.ds(i * piece, piece)], ref.at[s_rows[i], cols], out_sem.at[slot, k, i])
+                for k, ref in enumerate((act, d_gate, d_up)) for i in range(4)]
+
+    def stage_rows(s):
+        late = (s + 6) // 8
+        u = (s - 2) * late
+        first = me + (core - me) * s * (1 - late)
+        (slot_x, q_x), (slot_y, q_y) = link_rows(u, 0), link_rows(u, 1)
+        base_x, base_y = slot_x * rows + q_x * piece, slot_y * rows + q_y * piece
+        pair_x, pair_y = flip(slot_x, 1) * rows + q_x * piece, flip(slot_y, 1) * rows + q_y * piece
+        starts = [(1 - late) * (first * rows + i * piece) + late * base for i, base in enumerate((base_x, base_y, pair_x, pair_y))]
+        return [pl.ds(pl.multiple_of(st, 16), piece) for st in starts]
+
+    def compute(s):
+        s_rows = stage_rows(s)
+
+        def block(n, carry):
+            step = s * steps + n
+            slot = step % 2
+
+            @pl.when(step >= 2)
+            def _():
+                for cp in out_copies(slot, s_rows, n):
+                    cp.wait()
+
+            @pl.when(s == 0)
+            def _():
+                for cp in weight_copies(n):
+                    cp.wait()
+
+            cols = pl.ds(pl.multiple_of(n * bn, 128), bn)
+            res = gated_tile(z_buf[...], g_buf[...], wg[:, cols], wu[:, cols], wd[cols, :])
+            for k in range(3):
+                outs[slot, k] = res[k]
+            for cp in out_copies(slot, s_rows, n):
+                cp.start()
+            return carry
+
+        lax.fori_loop(0, steps, block, 0)
+
+    def stage(s, carry):
+        @pl.when(s == 0)
+        def _():
+            for cp in own_in:
+                cp.wait()
+            for cp in own_out:
+                cp.start()
+
+        @pl.when(s == 1)
+        def _():
+            for cp in own_out:
+                cp.wait()
+            for a in range(2):
+                own_copy(a).wait_recv()
+
+        for u in range(6):
+            @pl.when(s == u + 2)
+            def _(u=u):
+                for path in range(2):
+                    for a in range(2):
+                        link_copy(u, path, a).wait_recv()
+                        core_copy(u, path, a).start()
+                if u < 2:
+                    for path in range(2):
+                        for a in range(2):
+                            link_copy(u + 2, path, a).start()
+                if u == 1:
+                    for later in (4, 5):
+                        for path in range(2):
+                            for a in range(2):
+                                link_copy(later, path, a).start()
+                for path in range(2):
+                    for a in range(2):
+                        core_copy(u, path, a).wait_recv()
+
+        @pl.when(s >= 1)
+        def _():
+            s_rows = stage_rows(s)
+            copies = [pltpu.make_async_copy(full[a].at[s_rows[i]], bufs[a].at[pl.ds(i * piece, piece)], in_sem.at[a, i])
+                      for a in range(2) for i in range(4)]
+            for cp in copies:
+                cp.start()
+            for cp in copies:
+                cp.wait()
+
+        compute(s)
+        return carry
+
+    lax.fori_loop(0, 8, stage, 0)
+    last = stage_rows(7)
+    for slot in range(2):
+        for cp in out_copies(slot, last, 0):
+            cp.wait()
+    for a in range(2):
+        own_copy(a).wait_send()
+        for path in range(2):
+            for u in range(6):
+                link_copy(u, path, a).wait_send()
+                core_copy(u, path, a).wait_send()
+
+
+def gated_layer(z_own, g_own, w_gate, w_up, w_down, tp, bn=512):
+    rows, dim = z_own.shape
     width = w_gate.shape[1]
-    lhs = pl.BlockSpec((bm, dim), lambda i, j: (i, 0))
-    col = pl.BlockSpec((dim, bn), lambda i, j: (0, j))
-    out = pl.BlockSpec((bm, bn), lambda i, j: (i, j))
-    shape = jax.ShapeDtypeStruct((rows, width), BF16)
+    total = rows * tp
+    anyspace = pl.BlockSpec(memory_space=pl.ANY)
+    gathered = jax.ShapeDtypeStruct((total, dim), BF16)
+    made = jax.ShapeDtypeStruct((total, width), BF16)
+    dma = pltpu.SemaphoreType.DMA
     return pl.pallas_call(
-        functools.partial(gated_kernel, sub=sub),
-        out_shape=(shape, shape, shape),
-        grid=(rows // bm, width // bn),
-        in_specs=[lhs, lhs, col, col, pl.BlockSpec((bn, dim), lambda i, j: (j, 0))],
-        out_specs=(out, out, out),
-        compiler_params=pltpu.CompilerParams(dimension_semantics=("arbitrary", "arbitrary"), vmem_limit_bytes=58 << 20),
-        cost_estimate=pl.CostEstimate(flops=6 * rows * dim * width, bytes_accessed=200 << 20, transcendentals=rows * width),
+        functools.partial(gated_kernel, bn=bn),
+        out_shape=(gathered, gathered, made, made, made),
+        in_specs=[anyspace] * 5,
+        out_specs=(anyspace,) * 5,
+        scratch_shapes=[pltpu.VMEM((dim, width), BF16), pltpu.VMEM((dim, width), BF16), pltpu.VMEM((width, dim), BF16),
+                        pltpu.VMEM((rows, dim), BF16), pltpu.VMEM((rows, dim), BF16), pltpu.VMEM((2, 3, rows, bn), BF16),
+                        dma((3, width // bn)), dma((2, 4)), dma((4,)), dma((2, 3, 4)), dma((4, 6, 2)), dma((4, 6, 2)), dma((2,)), dma((2,))],
+        compiler_params=pltpu.CompilerParams(vmem_limit_bytes=60 << 20, collective_id=0, has_side_effects=True),
+        cost_estimate=pl.CostEstimate(flops=6 * total * dim * width, bytes_accessed=200 << 20, transcendentals=total * width),
         name="gated",
-    )(z_all, grad_all, w_gate, w_up, w_down)
+    )(z_own, g_own, w_gate, w_up, w_down)
 
 
 def pair_kernel(a_ref, b_ref, wa_ref, wb_ref, o_ref):
@@ -286,26 +470,22 @@
         values = dot_nn(normed, w_value).astype(BF16)
         kv_all = jnp.stack(gather_relative(jnp.concatenate([keys, values], axis=1)))
         wo_all = lax.all_gather(w_out, "tp", axis=0, tiled=True)
-        grad_all = lax.all_gather(grad_out, "tp", axis=0, tiled=True)
-
         q_raw = jnp.einsum("td,hde->hte", normed, wq_all, preferred_element_type=F32)
         query, query_pull = jax.vjp(rope, q_raw)
         mixed = attention_forward(lens, k_pos, query, kv_all, batch)
         attn_out = dot_nn(mixed, wo_all)
         resid = (hidden.astype(F32) + attn_out).astype(BF16)
         gated_in, norm2_pull = jax.vjp(rms_norm, resid, mlp_norm.astype(F32))
-        gated_all = lax.all_gather(gated_in, "tp", axis=0, tiled=True)
-
-        act, d_gate, d_upper = gated_layer(gated_all, grad_all, w_gate, w_up, w_down)
+        gated_all, grad_all, act, d_gate, d_upper = gated_layer(gated_in, grad_out, w_gate, w_up, w_down, tp_size)
         d_gated_part = pair_back(d_gate, d_upper, w_gate, w_up)
         d_gated = lax.psum_scatter(d_gated_part, "tp", scatter_dimension=0, tiled=True)
         mlp_part = dot_nn(act, w_down).astype(BF16)
         mlp_sum = lax.psum_scatter(mlp_part, "tp", scatter_dimension=0, tiled=True)
-        hidden_out = (resid.astype(F32) + mlp_sum.astype(F32)).astype(BF16)
         g_down = dot_tn(act, grad_all)
         g_gate = dot_tn(gated_all, d_gate)
         g_up = dot_tn(gated_all, d_upper)
 
+        d_gated, g_down = lax.optimization_barrier((d_gated, g_down))
         d_resid_norm, g_mlp_norm_part = norm2_pull(d_gated)
         d_resid = (grad_out.astype(F32) + d_resid_norm.astype(F32)).astype(BF16)
         g_out = lax.psum_scatter(dot_tn(mixed, d_resid), "tp", scatter_dimension=0, tiled=True)
@@ -320,8 +500,10 @@
         g_value = lax.psum(dot_tn(normed, d_values), "tp")
         d_normed = (jnp.einsum("hte,hde->td", d_q_raw, wq_all, preferred_element_type=F32)
                     + dot_nt(d_k_raw, w_key) + dot_nt(d_values, w_value)).astype(BF16)
+        mlp_sum, d_normed = lax.optimization_barrier((mlp_sum, d_normed))
         d_hidden_norm, g_attn_norm_part = norm1_pull(d_normed)
         grad_hidden = (d_resid.astype(F32) + d_hidden_norm.astype(F32)).astype(BF16)
+        hidden_out = (resid.astype(F32) + mlp_sum.astype(F32)).astype(BF16)
         g_norms = all_sum_small(jnp.stack([g_attn_norm_part, g_mlp_norm_part]))
         full = (batch, shard, dim)
         return (hidden_out.reshape(full), grad_hidden.reshape(full), g_norms[0], g_query, g_key, g_value, g_out, g_norms[1], g_gate, g_up, g_down)

time: 1170 us -> 994 us (0.85)
  waiting for transfers between devices: 535 us -> 309 us
  Pallas kernels: 280 us -> 330 us
    all_gather x2 -> x0, waiting for transfers between devices: 182 us -> none  [the longest x1 97.1 us: local_layer(): gated_all = lax.all_gather(gated_in, 'tp', axis=0, tiled=True)]
    reduce_scatter x1, waiting for transfers between devices: 119 us -> 0.01 us  [local_layer(): mlp_sum = lax.psum_scatter(mlp_part, 'tp', scatter_dimension=0, tiled=True)]
    psum x1, waiting for transfers between devices: 0.01 us -> 73.8 us  [local_layer(): g_key = lax.psum(dot_tn(normed, d_k_raw), 'tp')]
    pallas_call x1, Pallas kernels: 133 us -> 182 us  [gated_layer(): pl.pallas_call(functools.partial(gated_kernel, bn=bn), out_shape=(gathere...]
    reduce_scatter x1, waiting for transfers between devices: 73.7 us -> 24.5 us  [local_layer(): lax.psum_scatter(d_gated_part, 'tp', scatter_dimension=0, tiled=True)]
    reduce_scatter x1, waiting for transfers between devices: 77.6 us -> 114 us  [local_layer(): lax.psum_scatter(dot_tn(mixed, d_resid), 'tp', scatter_dimension=0, tiled...]
    ppermute x27, waiting for transfers between devices: 48.1 us -> 61.6 us  [swap(): return lax.ppermute(x, 'tp', [(t, t ^ bit) for t in range(8)])]
    unnamed x132 -> x134, local copies, waits for them, and re-layouts: 27.2 us -> 26.4 us
  transfers between devices with their start and end apart: 36 -> 34, of which waited for: 17 -> 19; matrix products, arithmetic and copies ran while one was open for 23% -> 29% of each run, Pallas kernels for 2% -> 6%
where the time goes in v2:
time: 994 us; the launch traced here: 990 us
  Pallas kernels  330 us (33%)
  waiting for transfers between devices  309 us (31%)
  matrix products  257 us (26%)
  local copies, waits for them, and re-layouts  29.9 us (3%)
  other arithmetic  27.7 us (3%)
  starting transfers between devices  21 us (2%)
  between operations  15.3 us (2%)
    pallas_call x1, Pallas kernels, gated_layer(): pl.pallas_call(functools.partial(gated_kernel, bn=bn), out_shape=(gathere...  182 us
    dot_general x6, matrix products, dot_tn(): return lax.dot_general(a, b, TN, preferred_element_type=F32)  165 us
    reduce_scatter x1, waiting for transfers between devices, local_layer(): lax.psum_scatter(dot_tn(mixed, d_resid), 'tp', scatter_dimension=0, tiled...  114 us
    pallas_call x1, Pallas kernels, pair_back(): pl.pallas_call(pair_kernel, out_shape=jax.ShapeDtypeStruct((rows, dim), B...  88.8 us
    psum x1, waiting for transfers between devices, local_layer(): g_key = lax.psum(dot_tn(normed, d_k_raw), 'tp')  73.8 us
    ppermute x27, waiting for transfers between devices, swap(): return lax.ppermute(x, 'tp', [(t, t ^ bit) for t in range(8)])  61.6 us
    dot_general x4, matrix products, dot_nn(): return jnp.dot(a, b, preferred_element_type=F32)  55.6 us
    pallas_call x1, Pallas kernels, attention_backward(): pl.pallas_call(attn_bwd_kernel, out_shape=(jax.ShapeDtypeStruct((heads, r...  34.9 us
  transfers between devices with their start and end apart: 34, of which 19 were waited for; matrix products, arithmetic and copies ran while one was open for 29% of the time, Pallas kernels for 6%

profile of v2, /device:TPU:0, one launch (start us, length us, event | category | flops | bytes accessed | tf_op | source)
XLA Modules:
  0.0 989.7 jit_solution(11971758394958720533)
XLA Ops:
  22.1 21.8 %collective-permute-done.1 = bf16[576,512]{1,0:T(8,128)(2,1)S(1)} collective-permute-done((bf16[576,512]{1,0:T(8,128)(2,1)}, bf16[576,512]{1,0:T(8,128)(2,1)S(1)}, u32[]{:S(2)}, u32[]{:S(2)}) %collective-permute-start.1) | collective-permute-done | bytes 589856 | tf_op jit(solution)/shard_map/ppermute | solution.py:54
  55.8 5.8 collective-permute-done.6
  65.9 13.4 %all-gather.6.cloned.1.call-done = bf16[16384,256]{1,0:T(8,128)(2,1)} async-done(((bf16[2048,256]{1,0:T(8,128)(2,1)}), bf16[16384,256]{1,0:T(8,128)(2,1)}) %all-gather.6.cloned.1.call-update) | async-done | bytes 8388624 | tf_op jit(solution)/shard_map/all_gather | solution.py:465
  79.3 7.6 fusion.18
  87.9 23.5 %attn_fwd.1 = bf16[576,2048]{1,0:T(8,128)(2,1)S(1)} custom-call(s32[11,3]{1,0:T(8,128)S(1)} %add_add_fusion.2.lens_ref, s32[1,1536]{1,0:T(1,128)S(1)} %add.166.kpos_ref, bf16[8,576,256]{2,1,0:T(8,128)(2,1)S(1)} %pad_maximum_fusion.q_ref, bf16[8,576,512]{2,1,0:T(8,128)(2,1)} %bitcast_dynamic-update-slice_fusion.k_ref.v_ref, ...), custom_call_target="tpu_custom_call" | custom-call | flops 7247757312 | bytes 12582912 | tf_op jit(solution)/shard_map/attn_fwd/pallas_call | solution.py:163
  112.9 18.4 %all-gather.4.cloned.1.call-done = bf16[2048,2048]{1,0:T(8,128)(2,1)} async-done(((bf16[256,2048]{1,0:T(8,128)(2,1)}), bf16[2048,2048]{1,0:T(8,128)(2,1)}) %all-gather.4.cloned.1.call-update) | async-done | bytes 8388624 | tf_op jit(solution)/shard_map/all_gather | solution.py:472
  131.3 8.0 fusion.10
  142.8 182.3 %gated.1 = (bf16[4608,2048]{1,0:T(8,128)(2,1)}, bf16[4608,2048]{1,0:T(8,128)(2,1)}, bf16[4608,2048]{1,0:T(8,128)(2,1)}, bf16[4608,2048]{1,0:T(8,128)(2,1)}, bf16[4608,2048]{1,0:T(8,128)(2,1)}) custom-call(bf16[576,2048]{1,0:T(8,128)(2,1)} %fusion.4.z_own, bf16[576,2048]{1,0:T(8,128)(2,1)} %bitcast.155, bf16[2048,2048]{1,0:T(8,128)(2,1)} %wa_ref.1, ...), custom_call_target="tpu_custom_call" | custom-call | flops 115964116992 | bytes 209715200 | tf_op jit(solution)/shard_map/gated/pallas_call | solution.py:409
  325.2 88.8 %pair_back.1 = bf16[4608,2048]{1,0:T(8,128)(2,1)} custom-call(bf16[4608,2048]{1,0:T(8,128)(2,1)} %get-tuple-element.24.a_ref, bf16[4608,2048]{1,0:T(8,128)(2,1)} %get-tuple-element.25.b_ref, bf16[2048,2048]{1,0:T(8,128)(2,1)} %wa_ref.1, bf16[2048,2048]{1,0:T(8,128)(2,1)} %wb_ref.1), custom_call_target="tpu_custom_call" | custom-call | flops 77309411328 | bytes 146800640 | tf_op jit(solution)/shard_map/pair_back/pallas_call | solution.py:432
  414.0 45.9 %convolution_convert_fusion = bf16[4608,2048]{1,0:T(8,128)(2,1)} fusion(bf16[4608,2048]{1,0:T(8,128)(2,1)} %get-tuple-element.23, bf16[2048,2048]{1,0:T(8,128)(2,1)} %wd_hbm.1), kind=kOutput, calls=%fused_computation | convolution fusion | flops 38664142848 | bytes 46137344 | tf_op jit(solution)/shard_map/dot_general | solution.py:42
  460.1 49.4 %fusion.56 = f32[2048,2048]{1,0:T(8,128)} fusion(bf16[4608,2048]{1,0:T(8,128)(2,1)} %get-tuple-element.23, bf16[4608,2048]{1,0:T(8,128)(2,1)} %get-tuple-element.26), kind=kOutput, calls=%fused_computation.141 | convolution fusion | flops 38654705664 | bytes 54525952 | tf_op jit(solution)/shard_map/dot_general | solution.py:50
  509.5 24.5 %reduce-scatter.7.cloned.1.call-done = bf16[576,2048]{1,0:T(8,128)(2,1)} async-done(((bf16[4608,2048]{1,0:T(8,128)(2,1)}), bf16[576,2048]{1,0:T(8,128)(2,1)}) %reduce-scatter.7.cloned.1.call-update) | async-done | bytes 2359312 | tf_op jit(solution)/shard_map/reduce_scatter | solution.py:481
  542.0 6.4 convolution_convert_fusion.1.do_ref
  548.3 34.9 %attn_bwd.1 = (bf16[8,576,256]{2,1,0:T(8,128)(2,1)}, bf16[8,576,256]{2,1,0:T(8,128)(2,1)}, bf16[8,576,256]{2,1,0:T(8,128)(2,1)}) custom-call(s32[11,3]{1,0:T(8,128)} %copy-done.2, bf16[8,576,256]{2,1,0:T(8,128)(2,1)} %copy-done.1, bf16[8,576,512]{2,1,0:T(8,128)(2,1)} %bitcast_dynamic-update-slice_fusion.k_ref.v_ref, ...), custom_call_target="tpu_custom_call" | custom-call | flops 18119393280 | bytes 20971520 | tf_op jit(solution)/shard_map/attn_bwd/pallas_call | solution.py:188
  588.3 10.3 %convolution_bitcast_fusion = f32[8,2048,256]{1,2,0:T(8,128)} fusion(bf16[576,2048]{1,0:T(8,128)(2,1)S(1)} %copy-done.22, f32[8,576,128]{2,1,0:T(8,128)S(1)} %get-tuple-element.75, f32[8,576,128]{2,1,0:T(8,128)S(1)} %get-tuple-element.74), kind=kOutput, calls=%fused_computation.8 | convolution fusion | flops 4834197504 | bytes 23855104 | tf_op jit(solution)/shard_map/td,hte->hde/dot_general | solution.py:498
  607.7 7.1 collective-permute-done.14
  617.0 7.1 collective-permute-done.22
  647.3 12.0 %fusion.57 = f32[2048,2048]{1,0:T(8,128)} fusion(bf16[576,2048]{1,0:T(8,128)(2,1)S(1)} %copy-done.4, bf16[576,2048]{1,0:T(8,128)(2,1)} %copy-done.9), kind=kOutput, calls=%fused_computation.142 | convolution fusion | flops 4831838208 | bytes 21495808 | tf_op jit(solution)/shard_map/dot_general | solution.py:50
  659.3 48.9 %fusion.58 = f32[2048,2048]{1,0:T(8,128)} fusion(bf16[4608,2048]{1,0:T(8,128)(2,1)} %get-tuple-element.33, bf16[4608,2048]{1,0:T(8,128)(2,1)} %get-tuple-element.24.a_ref), kind=kOutput, calls=%fused_computation.143 | convolution fusion | flops 38654705664 | bytes 54525952 | tf_op jit(solution)/shard_map/dot_general | solution.py:50
  708.2 8.3 fusion.29
  725.1 48.8 %fusion.59 = f32[2048,2048]{1,0:T(8,128)} fusion(bf16[4608,2048]{1,0:T(8,128)(2,1)} %get-tuple-element.33, bf16[4608,2048]{1,0:T(8,128)(2,1)} %get-tuple-element.25.b_ref), kind=kOutput, calls=%fused_computation.144 | convolution fusion | flops 38654705664 | bytes 54525952 | tf_op jit(solution)/shard_map/dot_general | solution.py:50
  778.9 6.4 fusion.12
  790.5 73.8 %all-reduce.7.cloned.1.call-done = (f32[2048,256]{1,0:T(8,128)}, f32[2048,256]{1,0:T(8,128)}) async-done(((f32[2048,256]{1,0:T(8,128)}, f32[2048,256]{1,0:T(8,128)}), (f32[2048,256]{1,0:T(8,128)}, f32[2048,256]{1,0:T(8,128)})) %all-reduce.7.cloned.1.call-update) | async-done | bytes 4194320 | tf_op jit(solution)/shard_map/psum | solution.py:499
  864.3 113.9 %reduce-scatter.11.cloned.1.call-done = f32[256,2048]{1,0:T(8,128)} async-done(((f32[2048,2048]{1,0:T(8,128)}), f32[256,2048]{1,0:T(8,128)}) %reduce-scatter.11.cloned.1.call-update) | async-done | bytes 2097168 | tf_op jit(solution)/shard_map/reduce_scatter | solution.py:491
  (267 shorter events, 107.1 us)
Async XLA Ops:
  7.2 72.1 %all-gather.6.cloned.1.call-start = ((), (), s32[]{:S(2)}) async-start(), calls=%async_computation.9 | async-start | bytes 9437184 | tf_op jit(solution)/shard_map/all_gather | solution.py:465
  7.9 123.4 %all-gather.4.cloned.1.call-start = ((), (), s32[]{:S(2)}) async-start(), calls=%async_computation.4 | async-start | bytes 9437184 | tf_op jit(solution)/shard_map/all_gather | solution.py:472
  8.7 525.2 %reduce-scatter.7.cloned.1.call-start = ((), (), s32[]{:S(2)}) async-start(), calls=%async_computation.6 | async-start | bytes 21233664 | tf_op jit(solution)/shard_map/reduce_scatter | solution.py:481
  16.1 27.8 %collective-permute-start.1 = (bf16[576,512]{1,0:T(8,128)(2,1)}, bf16[576,512]{1,0:T(8,128)(2,1)S(1)}, u32[]{:S(2)}, u32[]{:S(2)}) collective-permute-start(bf16[576,512]{1,0:T(8,128)(2,1)} %pad_maximum_fusion.1), channel_id=1, source_target_pairs={{0,2},{1,3},{2,0},{3,1},{4,6},{5,7},{6,4},{7,5},{8,10},{9,11},{10,... | collective-permute-start | bytes 1769480 | tf_op jit(solution)/shard_map/ppermute | solution.py:54
  19.3 29.2 %collective-permute-start = (bf16[576,512]{1,0:T(8,128)(2,1)}, bf16[576,512]{1,0:T(8,128)(2,1)}, u32[]{:S(2)}, u32[]{:S(2)}) collective-permute-start(bf16[576,512]{1,0:T(8,128)(2,1)} %pad_maximum_fusion.1), channel_id=1, source_target_pairs={{0,1},{1,0},{2,3},{3,2},{4,5},{5,4},{6,7},{7,6},{8,9},{9,8},{10,11... | collective-permute-start | bytes 1769480 | tf_op jit(solution)/shard_map/ppermute | solution.py:54
  19.3 26.4 %collective-permute-start.3 = (bf16[576,512]{1,0:T(8,128)(2,1)}, bf16[576,512]{1,0:T(8,128)(2,1)S(1)}, u32[]{:S(2)}, u32[]{:S(2)}) collective-permute-start(bf16[576,512]{1,0:T(8,128)(2,1)} %pad_maximum_fusion.1), channel_id=1, source_target_pairs={{0,4},{1,5},{2,6},{3,7},{4,0},{5,1},{6,2},{7,3},{8,12},{9,13},{10,... | collective-permute-start | bytes 1769480 | tf_op jit(solution)/shard_map/ppermute | solution.py:54
  43.9 11.9 %collective-permute-start.5 = (bf16[288,512]{1,0:T(8,128)(2,1)S(1)}, bf16[288,512]{1,0:T(8,128)(2,1)S(1)}, u32[]{:S(2)}, u32[]{:S(2)}) collective-permute-start(bf16[288,512]{1,0:T(8,128)(2,1)S(1)} %slice.152), channel_id=1, source_target_pairs={{0,4},{1,5},{2,6},{3,7},{4,0},{5,1},{6,2},{7,3},{8,12},{9,13},{10,... | collective-permute-start | bytes 884744 | tf_op jit(solution)/shard_map/ppermute | solution.py:54
  46.6 15.0 %collective-permute-start.6 = (bf16[288,512]{1,0:T(8,128)(2,1)S(1)}, bf16[288,512]{1,0:T(8,128)(2,1)S(1)}, u32[]{:S(2)}, u32[]{:S(2)}) collective-permute-start(bf16[288,512]{1,0:T(8,128)(2,1)S(1)} %slice.153), channel_id=1, source_target_pairs={{0,2},{1,3},{2,0},{3,1},{4,6},{5,7},{6,4},{7,5},{8,10},{9,11},{10,... | collective-permute-start | bytes 884744 | tf_op jit(solution)/shard_map/ppermute | solution.py:54
  48.0 13.6 %collective-permute-start.2 = (bf16[576,512]{1,0:T(8,128)(2,1)}, bf16[576,512]{1,0:T(8,128)(2,1)S(1)}, u32[]{:S(2)}, u32[]{:S(2)}) collective-permute-start(bf16[576,512]{1,0:T(8,128)(2,1)} %copy-done.33), channel_id=1, source_target_pairs={{0,1},{1,0},{2,3},{3,2},{4,5},{5,4},{6,7},{7,6},{8,9},{9,8},{10,11... | collective-permute-start | bytes 1769480 | tf_op jit(solution)/shard_map/ppermute | solution.py:54
  48.0 15.3 %collective-permute-start.4 = (bf16[576,512]{1,0:T(8,128)(2,1)}, bf16[576,512]{1,0:T(8,128)(2,1)S(1)}, u32[]{:S(2)}, u32[]{:S(2)}) collective-permute-start(bf16[576,512]{1,0:T(8,128)(2,1)} %copy-done.31), channel_id=1, source_target_pairs={{0,1},{1,0},{2,3},{3,2},{4,5},{5,4},{6,7},{7,6},{8,9},{9,8},{10,11... | collective-permute-start | bytes 1769480 | tf_op jit(solution)/shard_map/ppermute | solution.py:54
  414.0 307.6 %reduce-scatter.5.cloned.1.call-start = ((), (), s32[]{:S(2)}) async-start(), calls=%async_computation.5 | async-start | bytes 21233664 | tf_op jit(solution)/shard_map/reduce_scatter | solution.py:483
  460.0 327.6 %reduce-scatter.9.cloned.1.call-start = ((), (), s32[]{:S(2)}) async-start(), calls=%async_computation.7 | async-start | bytes 18874368 | tf_op jit(solution)/shard_map/reduce_scatter | solution.py:498
  598.6 265.7 %all-reduce.7.cloned.1.call-start = ((), (), s32[]{:S(2)}) async-start(), calls=%async_computation.10 | async-start | bytes 8388608 | tf_op jit(solution)/shard_map/psum | solution.py:499
  600.7 25.6 %collective-permute-start.8 = (bf16[576,256]{1,0:T(8,128)(2,1)S(1)}, bf16[576,256]{1,0:T(8,128)(2,1)S(1)}, u32[]{:S(2)}, u32[]{:S(2)}) collective-permute-start(bf16[576,256]{1,0:T(8,128)(2,1)S(1)} %get-tuple-element.85), channel_id=1, source_target_pairs={{0,1},{1,0},{2,3},{3,2},{4,5},{5,4},{6,7},{7,6},{8,9},{9,8},{10,11... | collective-permute-start | bytes 884744 | tf_op jit(solution)/shard_map/ppermute | solution.py:54
  601.3 39.0 %collective-permute-start.16 = (bf16[576,256]{1,0:T(8,128)(2,1)S(1)}, bf16[576,256]{1,0:T(8,128)(2,1)S(1)}, u32[]{:S(2)}, u32[]{:S(2)}) collective-permute-start(bf16[576,256]{1,0:T(8,128)(2,1)S(1)} %get-tuple-element.78), channel_id=1, source_target_pairs={{0,1},{1,0},{2,3},{3,2},{4,5},{5,4},{6,7},{7,6},{8,9},{9,8},{10,11... | collective-permute-start | bytes 884744 | tf_op jit(solution)/shard_map/ppermute | solution.py:54
  603.9 11.6 %collective-permute-start.11 = (bf16[288,256]{1,0:T(8,128)(2,1)S(1)}, bf16[288,256]{1,0:T(8,128)(2,1)S(1)}, u32[]{:S(2)}, u32[]{:S(2)}) collective-permute-start(bf16[288,256]{1,0:T(8,128)(2,1)S(1)} %get-tuple-element.98), channel_id=1, source_target_pairs={{0,4},{1,5},{2,6},{3,7},{4,0},{5,1},{6,2},{7,3},{8,12},{9,13},{10,... | collective-permute-start | bytes 442376 | tf_op jit(solution)/shard_map/ppermute | solution.py:54
  605.3 9.5 collective-permute-start.14
  606.2 18.6 %collective-permute-start.19 = (bf16[288,256]{1,0:T(8,128)(2,1)S(1)}, bf16[288,256]{1,0:T(8,128)(2,1)S(1)}, u32[]{:S(2)}, u32[]{:S(2)}) collective-permute-start(bf16[288,256]{1,0:T(8,128)(2,1)S(1)} %get-tuple-element.96), channel_id=1, source_target_pairs={{0,4},{1,5},{2,6},{3,7},{4,0},{5,1},{6,2},{7,3},{8,12},{9,13},{10,... | collective-permute-start | bytes 442376 | tf_op jit(solution)/shard_map/ppermute | solution.py:54
  615.5 17.2 %collective-permute-start.15 = (bf16[576,256]{1,0:T(8,128)(2,1)S(1)}, bf16[576,256]{1,0:T(8,128)(2,1)S(1)}, u32[]{:S(2)}, u32[]{:S(2)}) collective-permute-start(bf16[576,256]{1,0:T(8,128)(2,1)S(1)} %pad_maximum_fusion.3), channel_id=1, source_target_pairs={{0,4},{1,5},{2,6},{3,7},{4,0},{5,1},{6,2},{7,3},{8,12},{9,13},{10,... | collective-permute-start | bytes 884744 | tf_op jit(solution)/shard_map/ppermute | solution.py:54
  624.1 12.8 %collective-permute-start.12 = (bf16[576,256]{1,0:T(8,128)(2,1)S(1)}, bf16[576,256]{1,0:T(8,128)(2,1)S(1)}, u32[]{:S(2)}, u32[]{:S(2)}) collective-permute-start(bf16[576,256]{1,0:T(8,128)(2,1)S(1)} %pad_maximum_fusion.2), channel_id=1, source_target_pairs={{0,2},{1,3},{2,0},{3,1},{4,6},{5,7},{6,4},{7,5},{8,10},{9,11},{10,... | collective-permute-start | bytes 884744 | tf_op jit(solution)/shard_map/ppermute | solution.py:54
  624.8 17.5 %collective-permute-start.23 = (bf16[576,256]{1,0:T(8,128)(2,1)S(1)}, bf16[576,256]{1,0:T(8,128)(2,1)S(1)}, u32[]{:S(2)}, u32[]{:S(2)}) collective-permute-start(bf16[576,256]{1,0:T(8,128)(2,1)S(1)} %pad_maximum_fusion.5), channel_id=1, source_target_pairs={{0,4},{1,5},{2,6},{3,7},{4,0},{5,1},{6,2},{7,3},{8,12},{9,13},{10,... | collective-permute-start | bytes 884744 | tf_op jit(solution)/shard_map/ppermute | solution.py:54
  626.3 16.1 %collective-permute-start.20 = (bf16[576,256]{1,0:T(8,128)(2,1)S(1)}, bf16[576,256]{1,0:T(8,128)(2,1)S(1)}, u32[]{:S(2)}, u32[]{:S(2)}) collective-permute-start(bf16[576,256]{1,0:T(8,128)(2,1)S(1)} %pad_maximum_fusion.4), channel_id=1, source_target_pairs={{0,2},{1,3},{2,0},{3,1},{4,6},{5,7},{6,4},{7,5},{8,10},{9,11},{10,... | collective-permute-start | bytes 884744 | tf_op jit(solution)/shard_map/ppermute | solution.py:54
  647.3 331.0 %reduce-scatter.11.cloned.1.call-start = ((), (), s32[]{:S(2)}) async-start(), calls=%async_computation.8 | async-start | bytes 18874368 | tf_op jit(solution)/shard_map/reduce_scatter | solution.py:491
  725.0 48.8 %collective-permute-start.24 = (f32[2,2048]{1,0:T(2,128)S(1)}, f32[2,2048]{1,0:T(2,128)S(1)}, u32[]{:S(2)}, u32[]{:S(2)}) collective-permute-start(f32[2,2048]{1,0:T(2,128)S(1)} %pad_maximum_fusion.6), channel_id=1, source_target_pairs={{0,1},{1,0},{2,3},{3,2},{4,5},{5,4},{6,7},{7,6},{8,9},{9,8},{10,11... | collective-permute-start | bytes 49160 | tf_op jit(solution)/shard_map/ppermute | solution.py:54
  (72 other events, 1259.4 us)
Sparse Core Ops, SparseCore 0:
  9.9 69.4 all-gather.5
  81.2 50.1 all-gather.3
  414.1 119.7 reduce-scatter.6
  537.4 136.8 reduce-scatter.4
  677.6 109.9 reduce-scatter.8
  791.4 72.9 all-reduce.6
  868.4 109.7 reduce-scatter.10

commit v3 on v2

--- a/solution.py
+++ b/solution.py
@@ -54,28 +54,13 @@
     return lax.ppermute(x, "tp", [(t, t ^ bit) for t in range(8)])
 
 
-def gather_relative(own):
+def gather_near(own):
     half = own.shape[0] // 2
-    part = swap(own, 1)
     side = swap(own, 2)
     back = swap(own, 4)
     diag = jnp.concatenate([swap(side[:half], 4), swap(back[half:], 2)], axis=0)
-    return [own, part, side, swap(side, 1), back, swap(back, 1), diag, swap(diag, 1)]
-
-
-def scatter_relative(parts):
-    def join(kept, came):
-        return kept.astype(F32) + came.astype(F32)
-
-    near = [join(parts[s], swap(parts[s + 1], 1)) for s in (0, 2, 4, 6)]
-    own, side, back, diag = near
-    half = diag.shape[0] // 2
-    diag = diag.astype(parts[0].dtype)
-    came_side = swap(diag[:half], 2)
-    came_back = swap(diag[half:], 4)
-    back = jnp.concatenate([join(back[:half], came_side), back[half:]], axis=0).astype(parts[0].dtype)
-    side = jnp.concatenate([side[:half], join(side[half:], came_back)], axis=0).astype(parts[0].dtype)
-    return own + swap(side, 2).astype(F32) + swap(back, 4).astype(F32)
+    mine = jnp.stack([own, side, back, diag])
+    return mine, swap(mine, 1)
 
 
 def all_sum_small(x):
@@ -84,16 +69,19 @@
     return x
 
 
-def attn_fwd_kernel(lens_ref, kpos_ref, q_ref, k_ref, v_ref, o_ref, p_ref):
+def keys_values(kv0_ref, kv1_ref, total, head_dim):
+    both = jnp.concatenate([kv0_ref[...].reshape(total // 2, 2 * head_dim), kv1_ref[...].reshape(total // 2, 2 * head_dim)], axis=0)
+    return both[:, :head_dim], both[:, head_dim:]
+
+
+def attn_fwd_kernel(lens_ref, kpos_ref, q_ref, kv0_ref, kv1_ref, o_ref, p_ref):
     heads, shard, head_dim = q_ref.shape
-    tp = k_ref.shape[0]
-    total = tp * shard
+    total = 2 * kv0_ref.shape[0] * shard
     s_id = pl.program_id(0)
     prefix = lens_ref[0, s_id]
     valid = lens_ref[1, s_id]
     first = lens_ref[2, 0] * shard
-    keys = k_ref[...].reshape(total, head_dim)
-    values = v_ref[...].reshape(total, head_dim)
+    keys, values = keys_values(kv0_ref, kv1_ref, total, head_dim)
     q_pos = first + lax.broadcasted_iota(jnp.int32, (shard, 1), 0)
     visible = kpos_ref[...] < jnp.minimum(valid, jnp.maximum(prefix, q_pos + 1))
     scale = head_dim ** -0.5
@@ -109,9 +97,9 @@
         o_ref[:, h * head_dim:(h + 1) * head_dim] = mixed[h * shard:(h + 1) * shard]
 
 
-def attn_bwd_kernel(lens_ref, q_ref, k_ref, v_ref, do_ref, dq_ref, dk_ref, dv_ref, dkv_acc):
+def attn_bwd_kernel(lens_ref, q_ref, kv0_ref, kv1_ref, do_ref, dq_ref, dkv0_ref, dkv1_ref, dkv_acc):
     heads, shard, head_dim = q_ref.shape
-    tp = k_ref.shape[0]
+    tp = 2 * kv0_ref.shape[0]
     total = tp * shard
     rows = heads * shard
     s_id = pl.program_id(0)
@@ -119,8 +107,7 @@
     prefix = lens_ref[0, s_id]
     valid = lens_ref[1, s_id]
     first = lens_ref[2, 0] * shard
-    keys = k_ref[...].reshape(total, head_dim)
-    values = v_ref[...].reshape(total, head_dim)
+    keys, values = keys_values(kv0_ref, kv1_ref, total, head_dim)
     query = q_ref[...].reshape(rows, head_dim)
     d_out = jnp.concatenate([do_ref[:, h * head_dim:(h + 1) * head_dim] for h in range(heads)], axis=0)
     scale = head_dim ** -0.5
@@ -138,27 +125,28 @@
     d_k = dot_nn(d_s, query)
     dq_ref[...] = dot_tn(d_s, keys).astype(BF16).reshape(heads, shard, head_dim)
 
+    d_kv = jnp.concatenate([d_k, d_v], axis=1)
+
     @pl.when(g_id == 0)
     def _():
-        dkv_acc[0] = d_k
-        dkv_acc[1] = d_v
+        dkv_acc[...] = d_kv
 
     @pl.when(g_id > 0)
     def _():
-        dkv_acc[0] += d_k
-        dkv_acc[1] += d_v
+        dkv_acc[...] += d_kv
 
     @pl.when(g_id == pl.num_programs(1) - 1)
     def _():
-        dk_ref[...] = dkv_acc[0].astype(BF16).reshape(tp, shard, head_dim)
-        dv_ref[...] = dkv_acc[1].astype(BF16).reshape(tp, shard, head_dim)
-
-
-def attention_forward(lens, k_pos, query, kv_all, batch, group=4):
+        near = (tp // 2, shard, 2 * head_dim)
+        dkv0_ref[...] = dkv_acc[:total // 2].astype(BF16).reshape(near)
+        dkv1_ref[...] = dkv_acc[total // 2:].astype(BF16).reshape(near)
+
+
+def attention_forward(lens, k_pos, query, kv0, kv1, batch, group=4):
     heads, rows, head_dim = query.shape
-    tp = kv_all.shape[0]
+    near = kv0.shape[0]
     shard = rows // batch
-    total = tp * shard
+    total = 2 * near * shard
     q_spec = pl.BlockSpec((group, shard, head_dim), lambda s, g, *_: (g, s, 0))
     return pl.pallas_call(
         attn_fwd_kernel,
@@ -166,39 +154,36 @@
         grid_spec=pltpu.PrefetchScalarGridSpec(
             num_scalar_prefetch=1, grid=(batch, heads // group),
             in_specs=[pl.BlockSpec((1, total), lambda s, g, *_: (0, 0)), q_spec,
-                      pl.BlockSpec((tp, shard, head_dim), lambda s, g, *_: (0, s, 0)),
-                      pl.BlockSpec((tp, shard, head_dim), lambda s, g, *_: (0, s, 1))],
+                      pl.BlockSpec((near, shard, 2 * head_dim), lambda s, g, *_: (0, s, 0)),
+                      pl.BlockSpec((near, shard, 2 * head_dim), lambda s, g, *_: (0, s, 0))],
             out_specs=pl.BlockSpec((shard, group * head_dim), lambda s, g, *_: (s, g)),
             scratch_shapes=[pltpu.VMEM((group * shard, total), BF16)]),
         compiler_params=pltpu.CompilerParams(dimension_semantics=("arbitrary", "arbitrary"), vmem_limit_bytes=48 << 20),
         cost_estimate=pl.CostEstimate(flops=4 * heads * rows * total * head_dim, bytes_accessed=12 << 20, transcendentals=heads * rows * total),
         name="attn_fwd",
-    )(lens, k_pos, query, kv_all, kv_all)
-
-
-def attention_backward(lens, query, kv_all, d_mixed, batch, group=4):
+    )(lens, k_pos, query, kv0, kv1)
+
+
+def attention_backward(lens, query, kv0, kv1, d_mixed, batch, group=4):
     heads, rows, head_dim = query.shape
-    tp = kv_all.shape[0]
+    near = kv0.shape[0]
     shard = rows // batch
-    total = tp * shard
+    total = 2 * near * shard
     q_spec = pl.BlockSpec((group, shard, head_dim), lambda s, g, *_: (g, s, 0))
-    kv_specs = [pl.BlockSpec((tp, shard, head_dim), lambda s, g, *_: (0, s, 0)),
-                pl.BlockSpec((tp, shard, head_dim), lambda s, g, *_: (0, s, 1))]
-    kv_out = pl.BlockSpec((tp, shard, head_dim), lambda s, g, *_: (0, s, 0))
+    kv_spec = pl.BlockSpec((near, shard, 2 * head_dim), lambda s, g, *_: (0, s, 0))
+    kv_shape = jax.ShapeDtypeStruct((near, rows, 2 * head_dim), BF16)
     return pl.pallas_call(
         attn_bwd_kernel,
-        out_shape=(jax.ShapeDtypeStruct((heads, rows, head_dim), BF16),
-                   jax.ShapeDtypeStruct((tp, rows, head_dim), BF16),
-                   jax.ShapeDtypeStruct((tp, rows, head_dim), BF16)),
+        out_shape=(jax.ShapeDtypeStruct((heads, rows, head_dim), BF16), kv_shape, kv_shape),
         grid_spec=pltpu.PrefetchScalarGridSpec(
             num_scalar_prefetch=1, grid=(batch, heads // group),
-            in_specs=[q_spec] + kv_specs + [pl.BlockSpec((shard, group * head_dim), lambda s, g, *_: (s, g))],
-            out_specs=(q_spec, kv_out, kv_out),
-            scratch_shapes=[pltpu.VMEM((2, total, head_dim), F32)]),
+            in_specs=[q_spec, kv_spec, kv_spec, pl.BlockSpec((shard, group * head_dim), lambda s, g, *_: (s, g))],
+            out_specs=(q_spec, kv_spec, kv_spec),
+            scratch_shapes=[pltpu.VMEM((total, 2 * head_dim), F32)]),
         compiler_params=pltpu.CompilerParams(dimension_semantics=("arbitrary", "arbitrary"), vmem_limit_bytes=56 << 20),
         cost_estimate=pl.CostEstimate(flops=10 * heads * rows * total * head_dim, bytes_accessed=20 << 20, transcendentals=heads * rows * total),
         name="attn_bwd",
-    )(lens, query, kv_all, kv_all, d_mixed)
+    )(lens, query, kv0, kv1, d_mixed)
 
 
 def flip(index, bit):
@@ -231,7 +216,7 @@
 
 def gated_kernel(z_own, g_own, wg_hbm, wu_hbm, wd_hbm, z_all, g_all, act, d_gate, d_up,
                  wg, wu, wd, z_buf, g_buf, outs, w_sem, in_sem, own_sem, out_sem, send, recv, send0, recv0, *, bn):
-    rows, dim = z_own.shape
+    rows, _ = z_own.shape
     width = wg_hbm.shape[1]
     steps = width // bn
     piece = rows // 4
@@ -420,25 +405,195 @@
     )(z_own, g_own, w_gate, w_up, w_down)
 
 
-def pair_kernel(a_ref, b_ref, wa_ref, wb_ref, o_ref):
-    o_ref[...] = (dot_nt(a_ref[...], wa_ref[...]) + dot_nt(b_ref[...], wb_ref[...])).astype(BF16)
-
-
-def pair_back(a, b, w_a, w_b, bm=1152, bn=512):
-    rows, width = a.shape
-    dim = w_a.shape[0]
-    lhs = pl.BlockSpec((bm, width), lambda i, j: (i, 0))
-    row = pl.BlockSpec((bn, width), lambda i, j: (j, 0))
+def back_kernel(act, d_gate, d_up, wg_hbm, wu_hbm, wd_hbm, own_out, x_in, y_in,
+                wa, wb, lhs, st, from_core, from_diag, own_st, w_sem, l_sem, o_sem, c_send, c_recv, d_send, d_recv, f_send, f_recv, *, rows, bn):
+    dim = wg_hbm.shape[0]
+    steps = dim // bn
+    half = rows // 2
+    me, core, side, back = neighbours()
+
+    def remote(src, dst, send, recv, peer):
+        return pltpu.make_async_remote_copy(src_ref=src, dst_ref=dst, send_sem=send, recv_sem=recv,
+                                            device_id={"tp": peer}, device_id_type=pl.DeviceIdType.MESH)
+
+    def cols(j):
+        return pl.ds(pl.multiple_of(j * bn, 128), bn)
+
+    def pair_of(t):
+        return ((t + 5) // 7) * ((t + 1) % 3 + 1)
+
+    def lhs_copies(phase, t):
+        pair = pair_of(t)
+        theirs = 1 - t // 5 - ((t + 6) // 7 - (t + 5) // 7)
+        dev = me + (1 - pair // 2) * (side - me) + (1 - pair % 2) * (back - me)
+        dev = dev + theirs * (flip(dev, 1) - dev)
+        src = pl.ds(pl.multiple_of(dev * rows, 16), rows)
+        refs = (act,) if phase == 0 else (d_gate, d_up)
+        return [pltpu.make_async_copy(ref.at[src], lhs.at[t % 2, k], l_sem.at[t % 2, k]) for k, ref in enumerate(refs)]
+
+    def weight_copy(k, j):
+        if k == 0:
+            return pltpu.make_async_copy(wd_hbm.at[:, cols(j)], wa.at[:, cols(j)], w_sem.at[0, j])
+        src, dst = (wg_hbm, wb) if k == 1 else (wu_hbm, wa)
+        return pltpu.make_async_copy(src.at[cols(j)], dst.at[cols(j)], w_sem.at[k, j])
+
+    def core_copy(pair, j):
+        return remote(st.at[0, j], from_core.at[pair, j], c_send.at[j], c_recv.at[pair, j], core)
+
+    def diag_copy(phase, k, j):
+        return remote(st.at[1, j, pl.ds(k * half, half)], from_diag.at[phase, k, j], d_send.at[k, j], d_recv.at[phase, k, j], (side, back)[k])
+
+    def final_copy(phase, k, j):
+        return remote(st.at[2 + k, j], (x_in, y_in)[k].at[phase, :, cols(j)], f_send.at[k, j], f_recv.at[phase, k, j], (side, back)[k])
+
+    def own_copy(phase, j):
+        return pltpu.make_async_copy(own_st.at[j % 2], own_out.at[phase, :, cols(j)], o_sem.at[j % 2])
+
+    def product(phase, slot, j):
+        if phase == 0:
+            return dot_nn(lhs[slot, 0], wa[:, cols(j)])
+        return dot_nt(lhs[slot, 0], wb[cols(j), :]) + dot_nt(lhs[slot, 1], wa[cols(j), :])
+
+    for cp in lhs_copies(0, 0):
+        cp.start()
+    for j in range(steps):
+        weight_copy(0, j).start()
+    enter((core, side, back))
+
+    def tiles(body):
+        def step(j, carry):
+            body(j)
+            return carry
+
+        lax.fori_loop(0, steps, step, 0)
+
+    for phase in (0, 1):
+        def step(t, carry, phase=phase):
+            for cp in lhs_copies(phase, t):
+                cp.wait()
+
+            @pl.when(t < 7)
+            def _():
+                for cp in lhs_copies(phase, t + 1):
+                    cp.start()
+
+            if phase == 0:
+                @pl.when(t == 1)
+                def _():
+                    for j in range(steps):
+                        weight_copy(1, j).start()
+
+                @pl.when(t == 7)
+                def _():
+                    for cp in lhs_copies(1, 0):
+                        cp.start()
+
+            @pl.when((t == 0) | ((t >= 2) & (t <= 4)))
+            def _():
+                pair = pair_of(t)
+
+                def body(j):
+                    @pl.when(t == 0)
+                    def _():
+                        for k in ((0,) if phase == 0 else (1, 2)):
+                            weight_copy(k, j).wait()
+
+                    if phase == 0:
+                        @pl.when(t > 0)
+                        def _():
+                            core_copy(0, j).wait_send()
+                    else:
+                        core_copy(0, j).wait_send()
+                    st[0, j] = product(phase, t % 2, j).astype(BF16)
+                    core_copy(pair, j).start()
+
+                tiles(body)
+
+            @pl.when(t == 1)
+            def _():
+                def body(j):
+                    core_copy(0, j).wait_recv()
+                    if phase == 1:
+                        for k in range(2):
+                            diag_copy(0, k, j).wait_send()
+                    st[1, j] = (product(phase, 1, j) + from_core[0, j].astype(F32)).astype(BF16)
+                    for k in range(2):
+                        diag_copy(phase, k, j).start()
+
+                tiles(body)
+
+            for k in range(2):
+                @pl.when(t == 5 + k)
+                def _(k=k):
+                    def body(j):
+                        core_copy(1 + k, j).wait_recv()
+                        diag_copy(phase, 1 - k, j).wait_recv()
+                        if phase == 1:
+                            final_copy(0, k, j).wait_send()
+                        total = product(phase, (5 + k) % 2, j) + from_core[1 + k, j].astype(F32)
+                        came = from_diag[phase, 1 - k, j].astype(F32)
+                        split = slice(half, rows) if k == 0 else slice(0, half)
+                        rest = slice(0, half) if k == 0 else slice(half, rows)
+                        st[2 + k, j, split, :] = (total[split] + came).astype(BF16)
+                        st[2 + k, j, rest, :] = total[rest].astype(BF16)
+                        final_copy(phase, k, j).start()
+
+                    tiles(body)
+
+            @pl.when(t == 7)
+            def _():
+                def body(j):
+                    core_copy(3, j).wait_recv()
+
+                    @pl.when(j >= 2)
+                    def _():
+                        own_copy(phase, j).wait()
+
+                    own_st[j % 2] = product(phase, 1, j) + from_core[3, j].astype(F32)
+                    own_copy(phase, j).start()
+
+                tiles(body)
+                for j in (0, 1):
+                    own_copy(phase, j).wait()
+                if phase == 0:
+                    for j in range(steps):
+                        weight_copy(2, j).start()
+
+            return carry
+
+        lax.fori_loop(0, 8, step, 0)
+
+    for j in range(steps):
+        core_copy(0, j).wait_send()
+        for k in range(2):
+            diag_copy(1, k, j).wait_send()
+            final_copy(1, k, j).wait_send()
+            for phase in (0, 1):
+                final_copy(phase, k, j).wait_recv()
+
+
+def back_layer(act, d_gate, d_up, w_gate, w_up, w_down, tp, bn=512):
+    total, width = act.shape
+    dim = w_gate.shape[0]
+    rows = total // tp
+    steps = dim // bn
+    anyspace = pl.BlockSpec(memory_space=pl.ANY)
+    dma = pltpu.SemaphoreType.DMA
+    came = jax.ShapeDtypeStruct((2, rows, dim), BF16)
     return pl.pallas_call(
-        pair_kernel,
-        out_shape=jax.ShapeDtypeStruct((rows, dim), BF16),
-        grid=(rows // bm, dim // bn),
-        in_specs=[lhs, lhs, row, row],
-        out_specs=pl.BlockSpec((bm, bn), lambda i, j: (i, j)),
-        compiler_params=pltpu.CompilerParams(dimension_semantics=("arbitrary", "arbitrary"), vmem_limit_bytes=56 << 20),
-        cost_estimate=pl.CostEstimate(flops=4 * rows * dim * width, bytes_accessed=140 << 20, transcendentals=0),
-        name="pair_back",
-    )(a, b, w_a, w_b)
+        functools.partial(back_kernel, rows=rows, bn=bn),
+        out_shape=(jax.ShapeDtypeStruct((2, rows, dim), F32), came, came),
+        in_specs=[anyspace] * 6,
+        out_specs=(anyspace,) * 3,
+        scratch_shapes=[pltpu.VMEM((width, dim), BF16), pltpu.VMEM((dim, width), BF16), pltpu.VMEM((2, 2, rows, width), BF16),
+                        pltpu.VMEM((4, steps, rows, bn), BF16), pltpu.VMEM((4, steps, rows, bn), BF16),
+                        pltpu.VMEM((2, 2, steps, rows // 2, bn), BF16), pltpu.VMEM((2, rows, bn), F32),
+                        dma((3, steps)), dma((2, 2)), dma((2,)), dma((steps,)), dma((4, steps)),
+                        dma((2, steps)), dma((2, 2, steps)), dma((2, steps)), dma((2, 2, steps))],
+        compiler_params=pltpu.CompilerParams(vmem_limit_bytes=67043328, collective_id=1, has_side_effects=True),
+        cost_estimate=pl.CostEstimate(flops=6 * total * dim * width, bytes_accessed=200 << 20, transcendentals=0),
+        name="back",
+    )(act, d_gate, d_up, w_gate, w_up, w_down)
 
 
 def solution(mesh):
@@ -447,12 +602,12 @@
     in_specs = (act_spec, act_spec, P("dp"), P("dp"), P(None), P(None, "tp"), P(None, None), P(None, None), P("tp", None), P(None), P(None, "tp"), P(None, "tp"), P("tp", None))
     out_specs = (act_spec, act_spec, P("dp"), P("dp", "tp"), P("dp", None), P("dp", None), P(("dp", "tp"), None), P("dp"), P("dp", "tp"), P("dp", "tp"), P(("dp", "tp"), None))
 
-    def local_layer(hidden, grad_out, prefix_len, valid_len, attn_norm, w_query, w_key, w_value, w_out, mlp_norm, w_gate, w_up, w_down):
+    def layer(hidden, grad_out, prefix_len, valid_len, attn_norm, w_query, w_key, w_value, w_out, mlp_norm, w_gate, w_up, w_down):
         batch, shard, dim = hidden.shape
         head_dim = w_key.shape[1]
         rows = batch * shard
         me = lax.axis_index("tp")
-        starts = (me ^ jnp.arange(tp_size, dtype=jnp.int32)) * shard
+        starts = (me ^ jnp.array([0, 2, 4, 6, 1, 3, 5, 7], jnp.int32)) * shard
         k_pos = (starts[:, None] + jnp.arange(shard, dtype=jnp.int32)).reshape(1, tp_size * shard)
         lens = jnp.concatenate([jnp.stack([prefix_len, valid_len, jnp.full((batch,), me, jnp.int32)]),
                                 jnp.broadcast_to(starts[:, None], (tp_size, batch))])
@@ -468,44 +623,59 @@
         normed, norm1_pull = jax.vjp(rms_norm, hidden, attn_norm.astype(F32))
         keys, key_pull = jax.vjp(rope, dot_nn(normed, w_key))
         values = dot_nn(normed, w_value).astype(BF16)
-        kv_all = jnp.stack(gather_relative(jnp.concatenate([keys, values], axis=1)))
+        kv0, kv1 = gather_near(jnp.concatenate([keys, values], axis=1))
         wo_all = lax.all_gather(w_out, "tp", axis=0, tiled=True)
         q_raw = jnp.einsum("td,hde->hte", normed, wq_all, preferred_element_type=F32)
         query, query_pull = jax.vjp(rope, q_raw)
-        mixed = attention_forward(lens, k_pos, query, kv_all, batch)
+        mixed = attention_forward(lens, k_pos, query, kv0, kv1, batch)
         attn_out = dot_nn(mixed, wo_all)
         resid = (hidden.astype(F32) + attn_out).astype(BF16)
         gated_in, norm2_pull = jax.vjp(rms_norm, resid, mlp_norm.astype(F32))
         gated_all, grad_all, act, d_gate, d_upper = gated_layer(gated_in, grad_out, w_gate, w_up, w_down, tp_size)
-        d_gated_part = pair_back(d_gate, d_upper, w_gate, w_up)
-        d_gated = lax.psum_scatter(d_gated_part, "tp", scatter_dimension=0, tiled=True)
-        mlp_part = dot_nn(act, w_down).astype(BF16)
-        mlp_sum = lax.psum_scatter(mlp_part, "tp", scatter_dimension=0, tiled=True)
+        own_part, x_part, y_part = back_layer(act, d_gate, d_upper, w_gate, w_up, w_down, tp_size)
+        mlp_sum, d_gated = [own_part[k] + x_part[k].astype(F32) + y_part[k].astype(F32) for k in range(2)]
+        d_gated = d_gated.astype(BF16)
+        hidden_out = (resid.astype(F32) + mlp_sum).astype(BF16)
         g_down = dot_tn(act, grad_all)
         g_gate = dot_tn(gated_all, d_gate)
         g_up = dot_tn(gated_all, d_upper)
 
-        d_gated, g_down = lax.optimization_barrier((d_gated, g_down))
         d_resid_norm, g_mlp_norm_part = norm2_pull(d_gated)
         d_resid = (grad_out.astype(F32) + d_resid_norm.astype(F32)).astype(BF16)
-        g_out = lax.psum_scatter(dot_tn(mixed, d_resid), "tp", scatter_dimension=0, tiled=True)
+        g_out_part = dot_tn(mixed, d_resid)
         d_mixed = dot_nt(d_resid, wo_all).astype(BF16)
-        d_query, d_keys_part, d_values_part = attention_backward(lens, query, kv_all, d_mixed, batch)
-        d_keys = scatter_relative(d_keys_part).astype(BF16)
-        d_values = scatter_relative(d_values_part).astype(BF16)
+        d_mixed, g_out_part = lax.optimization_barrier((d_mixed, g_out_part))
+        g_out = lax.psum_scatter(g_out_part, "tp", scatter_dimension=0, tiled=True)
+        d_query, dkv_near, dkv_far = attention_backward(lens, query, kv0, kv1, d_mixed, batch)
         d_q_raw = query_pull(d_query)[0].astype(BF16)
-        d_k_raw = key_pull(d_keys)[0].astype(BF16)
-        g_query = lax.psum_scatter(jnp.einsum("td,hte->hde", normed, d_q_raw, preferred_element_type=F32), "tp", scatter_dimension=0, tiled=False)
-        g_key = lax.psum(dot_tn(normed, d_k_raw), "tp")
-        g_value = lax.psum(dot_tn(normed, d_values), "tp")
-        d_normed = (jnp.einsum("hte,hde->td", d_q_raw, wq_all, preferred_element_type=F32)
-                    + dot_nt(d_k_raw, w_key) + dot_nt(d_values, w_value)).astype(BF16)
-        mlp_sum, d_normed = lax.optimization_barrier((mlp_sum, d_normed))
+
+        came = swap(dkv_far, 1)
+        g_query_part = jnp.einsum("td,hte->hde", normed, d_q_raw, preferred_element_type=F32)
+        came, g_query_part = lax.optimization_barrier((came, g_query_part))
+        g_query = lax.psum_scatter(g_query_part, "tp", scatter_dimension=0, tiled=False)
+        own, side, back, diag = [dkv_near[k].astype(F32) + came[k].astype(F32) for k in range(4)]
+        diag = diag.astype(BF16)
+        half = rows // 2
+        came_side, came_back = swap(diag[:half], 2), swap(diag[half:], 4)
+        d_normed_q = jnp.einsum("hte,hde->td", d_q_raw, wq_all, preferred_element_type=F32)
+        came_side, came_back, d_normed_q = lax.optimization_barrier((came_side, came_back, d_normed_q))
+        back = jnp.concatenate([back[:half] + came_side.astype(F32), back[half:]], axis=0).astype(BF16)
+        side = jnp.concatenate([side[:half], side[half:] + came_back.astype(F32)], axis=0).astype(BF16)
+        last_side, last_back = swap(side, 2), swap(back, 4)
+        last_side, last_back, g_gate = lax.optimization_barrier((last_side, last_back, g_gate))
+        d_kv = (own + last_side.astype(F32) + last_back.astype(F32)).astype(BF16)
+        d_k_raw = key_pull(d_kv[:, :head_dim])[0].astype(BF16)
+        d_values = d_kv[:, head_dim:]
+        g_kv_part = dot_tn(normed, jnp.concatenate([d_k_raw, d_values], axis=1))
+        g_kv = lax.psum_scatter(g_kv_part, "tp", scatter_dimension=0, tiled=True)
+        g_kv, g_down, g_up = lax.optimization_barrier((g_kv, g_down, g_up))
+        g_kv = lax.all_gather(g_kv, "tp", axis=0, tiled=True)
+        g_key, g_value = g_kv[:, :head_dim], g_kv[:, head_dim:]
+        d_normed = (d_normed_q + dot_nt(d_k_raw, w_key) + dot_nt(d_values, w_value)).astype(BF16)
         d_hidden_norm, g_attn_norm_part = norm1_pull(d_normed)
         grad_hidden = (d_resid.astype(F32) + d_hidden_norm.astype(F32)).astype(BF16)
-        hidden_out = (resid.astype(F32) + mlp_sum.astype(F32)).astype(BF16)
         g_norms = all_sum_small(jnp.stack([g_attn_norm_part, g_mlp_norm_part]))
         full = (batch, shard, dim)
         return (hidden_out.reshape(full), grad_hidden.reshape(full), g_norms[0], g_query, g_key, g_value, g_out, g_norms[1], g_gate, g_up, g_down)
 
-    return jax.shard_map(local_layer, mesh=mesh, in_specs=in_specs, out_specs=out_specs, check_vma=False)
+    return jax.shard_map(layer, mesh=mesh, in_specs=in_specs, out_specs=out_specs, check_vma=False)

time: 994 us -> 1040 us (1.046)
  Pallas kernels: 330 us -> 420 us
  matrix products: 257 us -> 215 us
  local copies, waits for them, and re-layouts: 29.9 us -> 17.3 us
  waiting for transfers between devices: 309 us -> 320 us
    pallas_call x1, Pallas kernels: 88.8 us -> 177 us  [back_layer(): pl.pallas_call(functools.partial(back_kernel, rows=rows, bn=bn), out_shap...]
    reduce_scatter x4 -> x3, waiting for transfers between devices: 140 us -> 221 us  [the longest x1 112 us: layer(): g_out = lax.psum_scatter(g_out_part, 'tp', scatter_dimension=0, tiled=True)]
    psum x1 -> x0, waiting for transfers between devices: 73.8 us -> none  [local_layer(): g_key = lax.psum(dot_tn(normed, d_k_raw), 'tp')]
    dot_general x4 -> x3, matrix products: 55.6 us -> 9.61 us  [dot_nn(): return jnp.dot(a, b, preferred_element_type=F32)]
    all_gather x2 -> x3, waiting for transfers between devices: 31.8 us -> 48.5 us  [the longest x1 18.2 us: layer(): wo_all = lax.all_gather(w_out, 'tp', axis=0, tiled=True)]
    unnamed x134 -> x99, local copies, waits for them, and re-layouts: 26.4 us -> 11.6 us
    ppermute x27 -> x13, waiting for transfers between devices: 61.6 us -> 47.8 us  [swap(): return lax.ppermute(x, 'tp', [(t, t ^ bit) for t in range(8)])]
    dot_general x6 -> x5, matrix products: 165 us -> 161 us  [dot_tn(): return lax.dot_general(a, b, TN, preferred_element_type=F32)]
  transfers between devices with their start and end apart: 34 -> 19, of which waited for: 19 -> 12; matrix products, arithmetic and copies ran while one was open for 29% -> 20% of each run, Pallas kernels for 6% -> 2%
where the time goes in v3:
time: 1040 us; the launch traced here: 1030 us
  Pallas kernels  420 us (40%)
  waiting for transfers between devices  320 us (31%)
  matrix products  215 us (21%)
  other arithmetic  30.6 us (3%)
  local copies, waits for them, and re-layouts  17.3 us (2%)
  between operations  15.1 us (1%)
  starting transfers between devices  14.6 us (1%)
    pallas_call x1, Pallas kernels, gated_layer(): pl.pallas_call(functools.partial(gated_kernel, bn=bn), out_shape=(gathere...  185 us
    pallas_call x1, Pallas kernels, back_layer(): pl.pallas_call(functools.partial(back_kernel, rows=rows, bn=bn), out_shap...  177 us
    dot_general x5, matrix products, dot_tn(): return lax.dot_general(a, b, TN, preferred_element_type=F32)  161 us
    reduce_scatter x1, waiting for transfers between devices, layer(): g_out = lax.psum_scatter(g_out_part, 'tp', scatter_dimension=0, tiled=True)  112 us
    reduce_scatter x1, waiting for transfers between devices, layer(): lax.psum_scatter(g_query_part, 'tp', scatter_dimension=0, tiled=False)  109 us
    ppermute x13, waiting for transfers between devices, swap(): return lax.ppermute(x, 'tp', [(t, t ^ bit) for t in range(8)])  47.8 us
    pallas_call x1, Pallas kernels, attention_backward(): pl.pallas_call(attn_bwd_kernel, out_shape=(jax.ShapeDtypeStruct((heads, r...  34.8 us
    pallas_call x1, Pallas kernels, attention_forward(): pl.pallas_call(attn_fwd_kernel, out_shape=jax.ShapeDtypeStruct((rows, hea...  23.5 us
  transfers between devices with their start and end apart: 19, of which 12 were waited for; matrix products, arithmetic and copies ran while one was open for 20% of the time, Pallas kernels for 2%

profile of v3, /device:TPU:0, one launch (start us, length us, event | category | flops | bytes accessed | tf_op | source)
XLA Modules:
  0.0 1032.2 jit_solution(641445879844622390)
XLA Ops:
  21.3 22.8 %collective-permute-done = bf16[576,512]{1,0:T(8,128)(2,1)S(1)} collective-permute-done((bf16[576,512]{1,0:T(8,128)(2,1)S(1)}, bf16[576,512]{1,0:T(8,128)(2,1)S(1)}, u32[]{:S(2)}, u32[]{:S(2)}) %collective-permute-start) | collective-permute-done | bytes 589856 | tf_op jit(solution)/shard_map/ppermute | solution.py:54
  47.5 9.7 collective-permute-done.2
  61.7 16.4 %all-gather.9.cloned.1.call-done = bf16[16384,256]{1,0:T(8,128)(2,1)} async-done(((bf16[2048,256]{1,0:T(8,128)(2,1)}), bf16[16384,256]{1,0:T(8,128)(2,1)}) %all-gather.9.cloned.1.call-update) | async-done | bytes 8388624 | tf_op jit(solution)/shard_map/all_gather | solution.py:620
  78.1 8.3 fusion.17
  87.6 23.5 %attn_fwd.1 = bf16[576,2048]{1,0:T(8,128)(2,1)S(1)} custom-call(s32[11,3]{1,0:T(8,128)S(1)} %add_add_fusion.2.lens_ref, s32[1,1536]{1,0:T(1,128)S(1)} %add.160.kpos_ref, bf16[8,576,256]{2,1,0:T(8,128)(2,1)S(1)} %pad_maximum_fusion.q_ref, bf16[4,576,512]{2,1,0:T(8,128)(2,1)} %copy-done.16, bf16[4,576,512]{2,1,0:T(8,128)(2,1)} %collective-permute-done.4.kv1_ref), custom_call_target="tpu_custom_call" | custom-call | flops 7247757312 | bytes 12582912 | tf_op jit(solution)/shard_map/attn_fwd/pallas_call | solution.py:151
  112.5 18.2 %all-gather.5.cloned.1.call-done = bf16[2048,2048]{1,0:T(8,128)(2,1)} async-done(((bf16[256,2048]{1,0:T(8,128)(2,1)}), bf16[2048,2048]{1,0:T(8,128)(2,1)}) %all-gather.5.cloned.1.call-update) | async-done | bytes 8388624 | tf_op jit(solution)/shard_map/all_gather | solution.py:627
  130.7 8.0 fusion.10
  141.0 184.7 %gated.1 = (bf16[4608,2048]{1,0:T(8,128)(2,1)}, bf16[4608,2048]{1,0:T(8,128)(2,1)}, bf16[4608,2048]{1,0:T(8,128)(2,1)}, bf16[4608,2048]{1,0:T(8,128)(2,1)}, bf16[4608,2048]{1,0:T(8,128)(2,1)}) custom-call(bf16[576,2048]{1,0:T(8,128)(2,1)} %fusion.4.z_own, bf16[576,2048]{1,0:T(8,128)(2,1)} %bitcast.127, bf16[2048,2048]{1,0:T(8,128)(2,1)} %wg_hbm.3, ...), custom_call_target="tpu_custom_call" | custom-call | flops 115964116992 | bytes 209715200 | tf_op jit(solution)/shard_map/gated/pallas_call | solution.py:394
  325.7 176.8 %back.1 = (f32[2,576,2048]{2,1,0:T(8,128)}, bf16[2,576,2048]{2,1,0:T(8,128)(2,1)}, bf16[2,576,2048]{2,1,0:T(8,128)(2,1)}) custom-call(bf16[4608,2048]{1,0:T(8,128)(2,1)} %get-tuple-element.35.act, bf16[4608,2048]{1,0:T(8,128)(2,1)} %get-tuple-element.36.d_gate, bf16[4608,2048]{1,0:T(8,128)(2,1)} %get-tuple-element.37.d_up, bf16[2048,2048]{1,0:T(8,128)(2,1)} %wg_hbm.3, ...), custom_call_target="tpu_custom_call" | custom-call | flops 115964116992 | bytes 209715200 | tf_op jit(solution)/shard_map/back/pallas_call | solution.py:583
  502.6 11.1 %fusion.7 = (f32[2048]{0:T(1024)}, f32[576]{0:T(1024)S(1)}, bf16[576,2048]{1,0:T(8,128)(2,1)S(1)}, bf16[576,2048]{1,0:T(8,128)(2,1)}) fusion(bf16[576,2048]{1,0:T(8,128)(2,1)} %copy-done.6, f32[576]{0:T(1024)} %copy-done.38, f32[2048]{0:T(1024)} %copy-done.33, bf16[2,576,2048]{2,1,0:T(8,128)(2,1)} %get-tuple-element.40, ...), kind=kLoop, calls=%fused_computation.19 | loop fusion | flops 22410688 | bytes 25973248 | tf_op jit(solution)/shard_map/transpose(jvp())/reduce_sum | solution.py:23
  515.4 10.4 %fusion.53 = f32[2048,2048]{1,0:T(8,128)} fusion(bf16[576,2048]{1,0:T(8,128)(2,1)S(1)} %copy-done.3, bf16[576,2048]{1,0:T(8,128)(2,1)S(1)} %add_convert_fusion.3), kind=kOutput, calls=%fused_computation.115 | convolution fusion | flops 4831838208 | bytes 21495808 | tf_op jit(solution)/shard_map/dot_general | solution.py:50
  525.8 9.7 convolution_convert_fusion.do_ref
  535.5 34.8 %attn_bwd.1 = (bf16[8,576,256]{2,1,0:T(8,128)(2,1)}, bf16[4,576,512]{2,1,0:T(8,128)(2,1)}, bf16[4,576,512]{2,1,0:T(8,128)(2,1)}) custom-call(s32[11,3]{1,0:T(8,128)} %copy-done.1, bf16[8,576,256]{2,1,0:T(8,128)(2,1)} %copy-done, bf16[4,576,512]{2,1,0:T(8,128)(2,1)} %copy-done.16, bf16[4,576,512]{2,1,0:T(8,128)(2,1)} %collective-permute-done.4.kv1_ref, ...), custom_call_target="tpu_custom_call" | custom-call | flops 18119393280 | bytes 20971520 | tf_op jit(solution)/shard_map/attn_bwd/pallas_call | solution.py:175
  574.5 10.3 convolution_bitcast_fusion
  584.8 10.0 convolution_bitcast_fusion.1
  599.3 6.9 collective-permute-done.7
  609.2 48.9 %fusion.54 = f32[2048,2048]{1,0:T(8,128)} fusion(bf16[4608,2048]{1,0:T(8,128)(2,1)} %get-tuple-element.49, bf16[4608,2048]{1,0:T(8,128)(2,1)} %get-tuple-element.36.d_gate), kind=kOutput, calls=%fused_computation.116 | convolution fusion | flops 38654705664 | bytes 54525952 | tf_op jit(solution)/shard_map/dot_general | solution.py:50
  665.4 49.4 %fusion.57 = f32[2048,2048]{1,0:T(8,128)} fusion(bf16[4608,2048]{1,0:T(8,128)(2,1)} %get-tuple-element.49, bf16[4608,2048]{1,0:T(8,128)(2,1)} %get-tuple-element.37.d_up), kind=kOutput, calls=%fused_computation.119 | convolution fusion | flops 38654705664 | bytes 54525952 | tf_op jit(solution)/shard_map/dot_general | solution.py:50
  714.8 48.7 %fusion.56 = f32[2048,2048]{1,0:T(8,128)} fusion(bf16[4608,2048]{1,0:T(8,128)(2,1)} %get-tuple-element.35.act, bf16[4608,2048]{1,0:T(8,128)(2,1)} %get-tuple-element.53), kind=kOutput, calls=%fused_computation.118 | convolution fusion | flops 38654705664 | bytes 54525952 | tf_op jit(solution)/shard_map/dot_general | solution.py:50
  767.3 4.7 fusion.6
  782.6 13.9 %all-gather.7.cloned.1.call-done = f32[2048,512]{1,0:T(8,128)} async-done(((f32[256,512]{1,0:T(8,128)}), f32[2048,512]{1,0:T(8,128)}) %all-gather.7.cloned.1.call-update) | async-done | bytes 4194320 | tf_op jit(solution)/shard_map/all_gather | solution.py:672
  796.5 4.5 fusion.49
  801.0 109.5 %reduce-scatter.4.cloned.1.call-done = f32[1,2048,256]{1,2,0:T(8,128)} async-done(((f32[8,2048,256]{1,2,0:T(8,128)}), f32[1,2048,256]{1,2,0:T(8,128)}) %reduce-scatter.4.cloned.1.call-update) | async-done | bytes 2097168 | tf_op jit(solution)/shard_map/reduce_scatter | solution.py:655
  913.4 111.7 %reduce-scatter.8.cloned.1.call-done = f32[256,2048]{1,0:T(8,128)} async-done(((f32[2048,2048]{1,0:T(8,128)}), f32[256,2048]{1,0:T(8,128)}) %reduce-scatter.8.cloned.1.call-update) | async-done | bytes 2097168 | tf_op jit(solution)/shard_map/reduce_scatter | solution.py:648
  (190 shorter events, 64.1 us)
Async XLA Ops:
  7.2 70.9 %all-gather.9.cloned.1.call-start = ((), (), s32[]{:S(2)}) async-start(), calls=%async_computation.8 | async-start | bytes 9437184 | tf_op jit(solution)/shard_map/all_gather | solution.py:620
  7.9 122.8 %all-gather.5.cloned.1.call-start = ((), (), s32[]{:S(2)}) async-start(), calls=%async_computation.3 | async-start | bytes 9437184 | tf_op jit(solution)/shard_map/all_gather | solution.py:627
  8.7 754.8 %reduce-scatter.6.cloned.1.call-start = ((), (), s32[]{:S(2)}) async-start(), calls=%async_computation.5 | async-start | bytes 4718592 | tf_op jit(solution)/shard_map/reduce_scatter | solution.py:670
  12.1 74.4 %copy-start.21 = (f32[192,128]{1,0:T(8,128)}, f32[192,128]{1,0:T(8,128)S(1)}, u32[]{:S(2)}) copy-start(f32[192,128]{1,0:T(8,128)S(1)} %get-tuple-element.119) | copy-start | bytes 294916
  12.1 74.4 %copy-start.23 = (f32[192,128]{1,0:T(8,128)}, f32[192,128]{1,0:T(8,128)S(1)}, u32[]{:S(2)}) copy-start(f32[192,128]{1,0:T(8,128)S(1)} %get-tuple-element.120) | copy-start | bytes 294916
  16.2 31.3 %copy-start.45 = (bf16[2048]{0:T(1024)(128)(2,1)S(1)}, bf16[2048]{0:T(1024)(128)(2,1)}, u32[]{:S(2)}) copy-start(bf16[2048]{0:T(1024)(128)(2,1)} %param.23) | copy-start | bytes 12292
  16.3 27.8 %collective-permute-start = (bf16[576,512]{1,0:T(8,128)(2,1)S(1)}, bf16[576,512]{1,0:T(8,128)(2,1)S(1)}, u32[]{:S(2)}, u32[]{:S(2)}) collective-permute-start(bf16[576,512]{1,0:T(8,128)(2,1)S(1)} %get-tuple-element.116), channel_id=1, source_target_pairs={{0,2},{1,3},{2,0},{3,1},{4,6},{5,7},{6,4},{7,5},{8,10},{9,11},{10,... | collective-permute-start | bytes 1769480 | tf_op jit(solution)/shard_map/ppermute | solution.py:54
  19.5 26.4 %collective-permute-start.1 = (bf16[576,512]{1,0:T(8,128)(2,1)S(1)}, bf16[576,512]{1,0:T(8,128)(2,1)S(1)}, u32[]{:S(2)}, u32[]{:S(2)}) collective-permute-start(bf16[576,512]{1,0:T(8,128)(2,1)S(1)} %get-tuple-element.116), channel_id=1, source_target_pairs={{0,4},{1,5},{2,6},{3,7},{4,0},{5,1},{6,2},{7,3},{8,12},{9,13},{10,... | collective-permute-start | bytes 1769480 | tf_op jit(solution)/shard_map/ppermute | solution.py:54
  21.3 66.4 %copy-start.1 = (s32[11,3]{1,0:T(8,128)}, s32[11,3]{1,0:T(8,128)S(1)}, u32[]{:S(2)}) copy-start(s32[11,3]{1,0:T(8,128)S(1)} %add_add_fusion.2.lens_ref) | copy-start | bytes 400
  44.1 13.1 %collective-permute-start.2 = (bf16[288,512]{1,0:T(8,128)(2,1)S(1)}, bf16[288,512]{1,0:T(8,128)(2,1)S(1)}, u32[]{:S(2)}, u32[]{:S(2)}) collective-permute-start(bf16[288,512]{1,0:T(8,128)(2,1)S(1)} %slice.158), channel_id=1, source_target_pairs={{0,4},{1,5},{2,6},{3,7},{4,0},{5,1},{6,2},{7,3},{8,12},{9,13},{10,... | collective-permute-start | bytes 884744 | tf_op jit(solution)/shard_map/ppermute | solution.py:54
  45.9 14.1 %collective-permute-start.3 = (bf16[288,512]{1,0:T(8,128)(2,1)S(1)}, bf16[288,512]{1,0:T(8,128)(2,1)S(1)}, u32[]{:S(2)}, u32[]{:S(2)}) collective-permute-start(bf16[288,512]{1,0:T(8,128)(2,1)S(1)} %slice.159), channel_id=1, source_target_pairs={{0,2},{1,3},{2,0},{3,1},{4,6},{5,7},{6,4},{7,5},{8,10},{9,11},{10,... | collective-permute-start | bytes 884744 | tf_op jit(solution)/shard_map/ppermute | solution.py:54
  47.5 91.4 %copy-start.33 = (f32[2048]{0:T(1024)}, f32[2048]{0:T(1024)S(1)}, u32[]{:S(2)}) copy-start(f32[2048]{0:T(1024)S(1)} %convert_add_fusion.3) | copy-start | bytes 24580
  61.7 25.9 %collective-permute-start.4 = (bf16[4,576,512]{2,1,0:T(8,128)(2,1)S(1)}, bf16[4,576,512]{2,1,0:T(8,128)(2,1)}, u32[]{:S(2)}, u32[]{:S(2)}) collective-permute-start(bf16[4,576,512]{2,1,0:T(8,128)(2,1)S(1)} %pad_maximum_fusion.1.kv0_ref), channel_id=1, source_target_pairs={{0,1},{1,0},{2,3},{3,2},{4,5},{5,4},{6,7},{7,6},{8,9},{9,8},{10,11... | collective-permute-start | bytes 7077896 | tf_op jit(solution)/shard_map/ppermute | solution.py:54
  570.3 24.5 %collective-permute-start.5 = (bf16[4,576,512]{2,1,0:T(8,128)(2,1)}, bf16[4,576,512]{2,1,0:T(8,128)(2,1)}, u32[]{:S(2)}, u32[]{:S(2)}) collective-permute-start(bf16[4,576,512]{2,1,0:T(8,128)(2,1)} %get-tuple-element.43), channel_id=1, source_target_pairs={{0,1},{1,0},{2,3},{3,2},{4,5},{5,4},{6,7},{7,6},{8,9},{9,8},{10,11... | collective-permute-start | bytes 7077896 | tf_op jit(solution)/shard_map/ppermute | solution.py:54
  596.8 9.4 collective-permute-start.7
  597.9 9.1 collective-permute-start.6
  607.3 50.9 %collective-permute-start.8 = (bf16[576,512]{1,0:T(8,128)(2,1)S(1)}, bf16[576,512]{1,0:T(8,128)(2,1)S(1)}, u32[]{:S(2)}, u32[]{:S(2)}) collective-permute-start(bf16[576,512]{1,0:T(8,128)(2,1)S(1)} %pad_maximum_fusion.3), channel_id=1, source_target_pairs={{0,2},{1,3},{2,0},{3,1},{4,6},{5,7},{6,4},{7,5},{8,10},{9,11},{10,... | collective-permute-start | bytes 1769480 | tf_op jit(solution)/shard_map/ppermute | solution.py:54
  608.7 49.5 %collective-permute-start.9 = (bf16[576,512]{1,0:T(8,128)(2,1)S(1)}, bf16[576,512]{1,0:T(8,128)(2,1)S(1)}, u32[]{:S(2)}, u32[]{:S(2)}) collective-permute-start(bf16[576,512]{1,0:T(8,128)(2,1)S(1)} %pad_maximum_fusion.4), channel_id=1, source_target_pairs={{0,4},{1,5},{2,6},{3,7},{4,0},{5,1},{6,2},{7,3},{8,12},{9,13},{10,... | collective-permute-start | bytes 1769480 | tf_op jit(solution)/shard_map/ppermute | solution.py:54
  665.4 131.2 %all-gather.7.cloned.1.call-start = ((), (), s32[]{:S(2)}) async-start(), calls=%async_computation.6 | async-start | bytes 4718592 | tf_op jit(solution)/shard_map/all_gather | solution.py:672
  763.5 147.0 %reduce-scatter.4.cloned.1.call-start = ((), (), s32[]{:S(2)}) async-start(), calls=%async_computation.4 | async-start | bytes 18874368 | tf_op jit(solution)/shard_map/reduce_scatter | solution.py:655
  764.1 261.0 %reduce-scatter.8.cloned.1.call-start = ((), (), s32[]{:S(2)}) async-start(), calls=%async_computation.7 | async-start | bytes 18874368 | tf_op jit(solution)/shard_map/reduce_scatter | solution.py:648
  772.1 1.2 collective-permute-start.10
  773.3 4.2 collective-permute-start.11
  777.6 4.4 collective-permute-start.12
  (44 other events, 247.8 us)
Sparse Core Ops, SparseCore 0:
  9.9 68.2 all-gather.8
  80.0 50.7 all-gather.4
  665.5 45.7 reduce-scatter.5
  763.6 32.8 all-gather.6
  799.9 110.5 reduce-scatter.3
  914.5 110.5 reduce-scatter.7

commit v4 on v3

--- a/solution.py
+++ b/solution.py
@@ -61,12 +61,6 @@
     diag = jnp.concatenate([swap(side[:half], 4), swap(back[half:], 2)], axis=0)
     mine = jnp.stack([own, side, back, diag])
     return mine, swap(mine, 1)
-
-
-def all_sum_small(x):
-    for bit in (1, 2, 4):
-        x = x + swap(x, bit)
-    return x
 
 
 def keys_values(kv0_ref, kv1_ref, total, head_dim):
@@ -84,20 +78,19 @@
     keys, values = keys_values(kv0_ref, kv1_ref, total, head_dim)
     q_pos = first + lax.broadcasted_iota(jnp.int32, (shard, 1), 0)
     visible = kpos_ref[...] < jnp.minimum(valid, jnp.maximum(prefix, q_pos + 1))
-    scale = head_dim ** -0.5
-    query = q_ref[...].reshape(heads * shard, head_dim)
+    query = q_ref[...].reshape(heads * shard, head_dim) * BF16(head_dim ** -0.5)
     scores = dot_nt(query, keys)
     for h in range(heads):
         rows = slice(h * shard, (h + 1) * shard)
-        s = jnp.where(visible, scores[rows] * scale, MASKED)
+        s = jnp.where(visible, scores[rows], MASKED)
         e = jnp.exp(s - jnp.max(s, axis=-1, keepdims=True))
-        p_ref[rows, :] = (e / jnp.sum(e, axis=-1, keepdims=True)).astype(BF16)
+        p_ref[rows, :] = (e * (1.0 / jnp.sum(e, axis=-1, keepdims=True))).astype(BF16)
     mixed = dot_nn(p_ref[...], values).astype(BF16)
     for h in range(heads):
         o_ref[:, h * head_dim:(h + 1) * head_dim] = mixed[h * shard:(h + 1) * shard]
 
 
-def attn_bwd_kernel(lens_ref, q_ref, kv0_ref, kv1_ref, do_ref, dq_ref, dkv0_ref, dkv1_ref, dkv_acc):
+def attn_bwd_kernel(lens_ref, cos_ref, sin_ref, q_ref, kv0_ref, kv1_ref, do_ref, dq_ref, dkv0_ref, dkv1_ref, dkv_acc):
     heads, shard, head_dim = q_ref.shape
     tp = 2 * kv0_ref.shape[0]
     total = tp * shard
@@ -108,22 +101,25 @@
     valid = lens_ref[1, s_id]
     first = lens_ref[2, 0] * shard
     keys, values = keys_values(kv0_ref, kv1_ref, total, head_dim)
-    query = q_ref[...].reshape(rows, head_dim)
+    query = q_ref[...].reshape(rows, head_dim) * BF16(head_dim ** -0.5)
     d_out = jnp.concatenate([do_ref[:, h * head_dim:(h + 1) * head_dim] for h in range(heads)], axis=0)
-    scale = head_dim ** -0.5
     step = lax.broadcasted_iota(jnp.int32, (shard, 1), 0)
     k_pos = jnp.concatenate([step + lens_ref[3 + r, 0] for r in range(tp)], axis=0)
     q_pos = first + lax.rem(lax.broadcasted_iota(jnp.int32, (1, rows), 1), shard)
     limit = jnp.minimum(valid, jnp.maximum(prefix, q_pos + 1))
-    s = jnp.where(k_pos < limit, dot_nt(keys, query) * scale, MASKED)
+    s = jnp.where(k_pos < limit, dot_nt(keys, query), MASKED)
     e = jnp.exp(s - jnp.max(s, axis=0, keepdims=True))
     p = e * (1.0 / jnp.sum(e, axis=0, keepdims=True))
     d_p = dot_nt(values, d_out)
     delta = jnp.sum(p * d_p, axis=0, keepdims=True)
-    d_s = (p * (d_p - delta) * scale).astype(BF16)
+    d_s = (p * (d_p - delta)).astype(BF16)
     d_v = dot_nn(p.astype(BF16), d_out)
     d_k = dot_nn(d_s, query)
-    dq_ref[...] = dot_tn(d_s, keys).astype(BF16).reshape(heads, shard, head_dim)
+    d_q = (dot_tn(d_s, keys) * (head_dim ** -0.5)).reshape(heads, shard, head_dim)
+    first, second = d_q[:, :, :head_dim // 2], d_q[:, :, head_dim // 2:]
+    cos_t, sin_t = cos_ref[...][None], sin_ref[...][None]
+    dq_ref[:, :, :head_dim // 2] = (first * cos_t + second * sin_t).astype(BF16)
+    dq_ref[:, :, head_dim // 2:] = (second * cos_t - first * sin_t).astype(BF16)
 
     d_kv = jnp.concatenate([d_k, d_v], axis=1)
 
@@ -164,26 +160,27 @@
     )(lens, k_pos, query, kv0, kv1)
 
 
-def attention_backward(lens, query, kv0, kv1, d_mixed, batch, group=4):
+def attention_backward(lens, cos_t, sin_t, query, kv0, kv1, d_mixed, batch, group=4):
     heads, rows, head_dim = query.shape
     near = kv0.shape[0]
     shard = rows // batch
     total = 2 * near * shard
     q_spec = pl.BlockSpec((group, shard, head_dim), lambda s, g, *_: (g, s, 0))
     kv_spec = pl.BlockSpec((near, shard, 2 * head_dim), lambda s, g, *_: (0, s, 0))
+    table = pl.BlockSpec((shard, head_dim // 2), lambda s, g, *_: (0, 0))
     kv_shape = jax.ShapeDtypeStruct((near, rows, 2 * head_dim), BF16)
     return pl.pallas_call(
         attn_bwd_kernel,
         out_shape=(jax.ShapeDtypeStruct((heads, rows, head_dim), BF16), kv_shape, kv_shape),
         grid_spec=pltpu.PrefetchScalarGridSpec(
             num_scalar_prefetch=1, grid=(batch, heads // group),
-            in_specs=[q_spec, kv_spec, kv_spec, pl.BlockSpec((shard, group * head_dim), lambda s, g, *_: (s, g))],
+            in_specs=[table, table, q_spec, kv_spec, kv_spec, pl.BlockSpec((shard, group * head_dim), lambda s, g, *_: (s, g))],
             out_specs=(q_spec, kv_spec, kv_spec),
             scratch_shapes=[pltpu.VMEM((total, 2 * head_dim), F32)]),
         compiler_params=pltpu.CompilerParams(dimension_semantics=("arbitrary", "arbitrary"), vmem_limit_bytes=56 << 20),
         cost_estimate=pl.CostEstimate(flops=10 * heads * rows * total * head_dim, bytes_accessed=20 << 20, transcendentals=heads * rows * total),
         name="attn_bwd",
-    )(lens, query, kv0, kv1, d_mixed)
+    )(lens, cos_t, sin_t, query, kv0, kv1, d_mixed)
 
 
 def flip(index, bit):
@@ -596,6 +593,42 @@
     )(act, d_gate, d_up, w_gate, w_up, w_down)
 
 
+def product_kernel(a_ref, b_ref, o_ref):
+    o_ref[...] = dot_tn(a_ref[...], b_ref[...])
+
+
+def weight_grad(a, b, bm=512, bn=1024):
+    rows, m = a.shape
+    n = b.shape[1]
+    return pl.pallas_call(
+        product_kernel,
+        out_shape=jax.ShapeDtypeStruct((m, n), F32),
+        grid=(m // bm, n // bn),
+        in_specs=[pl.BlockSpec((rows, bm), lambda i, j: (0, i)), pl.BlockSpec((rows, bn), lambda i, j: (0, j))],
+        out_specs=pl.BlockSpec((bm, bn), lambda i, j: (i, j)),
+        compiler_params=pltpu.CompilerParams(dimension_semantics=("arbitrary", "arbitrary"), vmem_limit_bytes=56 << 20),
+        cost_estimate=pl.CostEstimate(flops=2 * rows * m * n, bytes_accessed=110 << 20, transcendentals=0),
+        name="weight_grad",
+    )(a, b)
+
+
+def pick(x, index):
+    return lax.dynamic_index_in_dim(x, index, axis=0, keepdims=False)
+
+
+def hop_diagonal(diag):
+    half = diag.shape[0] // 2
+    return swap(diag[:half], 2), swap(diag[half:], 4)
+
+
+def hop_near(side, back, came_side, came_back):
+    half = side.shape[0] // 2
+    kind = came_side.dtype
+    side = jnp.concatenate([side[:half], side[half:] + came_back.astype(F32)], axis=0).astype(kind)
+    back = jnp.concatenate([back[:half] + came_side.astype(F32), back[half:]], axis=0).astype(kind)
+    return side, back
+
+
 def solution(mesh):
     tp_size = mesh.shape["tp"]
     act_spec = P("dp", "tp", None)
@@ -611,8 +644,8 @@
         k_pos = (starts[:, None] + jnp.arange(shard, dtype=jnp.int32)).reshape(1, tp_size * shard)
         lens = jnp.concatenate([jnp.stack([prefix_len, valid_len, jnp.full((batch,), me, jnp.int32)]),
                                 jnp.broadcast_to(starts[:, None], (tp_size, batch))])
-        cos_t, sin_t = rope_tables(me * shard + jnp.arange(shard), head_dim)
-        cos_t, sin_t = jnp.tile(cos_t, (batch, 1)), jnp.tile(sin_t, (batch, 1))
+        cos_own, sin_own = rope_tables(me * shard + jnp.arange(shard), head_dim)
+        cos_t, sin_t = jnp.tile(cos_own, (batch, 1)), jnp.tile(sin_own, (batch, 1))
 
         def rope(raw_proj):
             return apply_rope(raw_proj, cos_t, sin_t).astype(BF16)
@@ -626,7 +659,7 @@
         kv0, kv1 = gather_near(jnp.concatenate([keys, values], axis=1))
         wo_all = lax.all_gather(w_out, "tp", axis=0, tiled=True)
         q_raw = jnp.einsum("td,hde->hte", normed, wq_all, preferred_element_type=F32)
-        query, query_pull = jax.vjp(rope, q_raw)
+        query = rope(q_raw)
         mixed = attention_forward(lens, k_pos, query, kv0, kv1, batch)
         attn_out = dot_nn(mixed, wo_all)
         resid = (hidden.astype(F32) + attn_out).astype(BF16)
@@ -636,45 +669,50 @@
         mlp_sum, d_gated = [own_part[k] + x_part[k].astype(F32) + y_part[k].astype(F32) for k in range(2)]
         d_gated = d_gated.astype(BF16)
         hidden_out = (resid.astype(F32) + mlp_sum).astype(BF16)
-        g_down = dot_tn(act, grad_all)
-        g_gate = dot_tn(gated_all, d_gate)
-        g_up = dot_tn(gated_all, d_upper)
-
         d_resid_norm, g_mlp_norm_part = norm2_pull(d_gated)
         d_resid = (grad_out.astype(F32) + d_resid_norm.astype(F32)).astype(BF16)
         g_out_part = dot_tn(mixed, d_resid)
         d_mixed = dot_nt(d_resid, wo_all).astype(BF16)
         d_mixed, g_out_part = lax.optimization_barrier((d_mixed, g_out_part))
         g_out = lax.psum_scatter(g_out_part, "tp", scatter_dimension=0, tiled=True)
-        d_query, dkv_near, dkv_far = attention_backward(lens, query, kv0, kv1, d_mixed, batch)
-        d_q_raw = query_pull(d_query)[0].astype(BF16)
-
-        came = swap(dkv_far, 1)
-        g_query_part = jnp.einsum("td,hte->hde", normed, d_q_raw, preferred_element_type=F32)
-        came, g_query_part = lax.optimization_barrier((came, g_query_part))
-        g_query = lax.psum_scatter(g_query_part, "tp", scatter_dimension=0, tiled=False)
-        own, side, back, diag = [dkv_near[k].astype(F32) + came[k].astype(F32) for k in range(4)]
-        diag = diag.astype(BF16)
-        half = rows // 2
-        came_side, came_back = swap(diag[:half], 2), swap(diag[half:], 4)
+        d_q_raw, dkv_near, dkv_far = attention_backward(lens, cos_own, sin_own, query, kv0, kv1, d_mixed, batch)
+        came_kv = swap(dkv_far, 1)
+        plane = me // 2
+        by_core = d_q_raw.reshape(tp_size // 2, 2, rows, head_dim)
+        theirs = lax.dynamic_index_in_dim(by_core, 1 - me % 2, axis=1, keepdims=False)
+        mine = lax.dynamic_index_in_dim(by_core, me % 2, axis=1, keepdims=False)
+        came_q = swap(jnp.einsum("td,kte->kde", normed, theirs, preferred_element_type=F32), 1)
         d_normed_q = jnp.einsum("hte,hde->td", d_q_raw, wq_all, preferred_element_type=F32)
-        came_side, came_back, d_normed_q = lax.optimization_barrier((came_side, came_back, d_normed_q))
-        back = jnp.concatenate([back[:half] + came_side.astype(F32), back[half:]], axis=0).astype(BF16)
-        side = jnp.concatenate([side[:half], side[half:] + came_back.astype(F32)], axis=0).astype(BF16)
-        last_side, last_back = swap(side, 2), swap(back, 4)
-        last_side, last_back, g_gate = lax.optimization_barrier((last_side, last_back, g_gate))
-        d_kv = (own + last_side.astype(F32) + last_back.astype(F32)).astype(BF16)
+        came_kv, d_normed_q = lax.optimization_barrier((came_kv, d_normed_q))
+        kv_own, kv_side, kv_back, kv_diag = [dkv_near[k].astype(F32) + came_kv[k].astype(F32) for k in range(4)]
+        kv_came = hop_diagonal(kv_diag.astype(BF16))
+        g_query_sum = jnp.einsum("td,kte->kde", normed, mine, preferred_element_type=F32) + came_q
+        kv_came, g_query_sum, d_gate = lax.optimization_barrier((kv_came, g_query_sum, d_gate))
+        kv_next = hop_near(kv_side, kv_back, *kv_came)
+        kv_last = (swap(kv_next[0], 2), swap(kv_next[1], 4))
+        q_came = hop_diagonal(pick(g_query_sum, plane ^ 3))
+        g_gate = weight_grad(gated_all, d_gate)
+        kv_last, q_came, g_gate = lax.optimization_barrier((kv_last, q_came, g_gate))
+        d_kv = (kv_own + kv_last[0].astype(F32) + kv_last[1].astype(F32)).astype(BF16)
         d_k_raw = key_pull(d_kv[:, :head_dim])[0].astype(BF16)
         d_values = d_kv[:, head_dim:]
-        g_kv_part = dot_tn(normed, jnp.concatenate([d_k_raw, d_values], axis=1))
-        g_kv = lax.psum_scatter(g_kv_part, "tp", scatter_dimension=0, tiled=True)
-        g_kv, g_down, g_up = lax.optimization_barrier((g_kv, g_down, g_up))
-        g_kv = lax.all_gather(g_kv, "tp", axis=0, tiled=True)
-        g_key, g_value = g_kv[:, :head_dim], g_kv[:, head_dim:]
+        q_next = hop_near(pick(g_query_sum, plane ^ 1), pick(g_query_sum, plane ^ 2), *q_came)
+        g_key_part, g_value_part = dot_tn(normed, d_k_raw), dot_tn(normed, d_values)
+        q_next, g_key_part, g_value_part, d_upper = lax.optimization_barrier((q_next, g_key_part, g_value_part, d_upper))
+        g_key, g_value = lax.psum((g_key_part, g_value_part), "tp")
+        q_last = (swap(q_next[0], 2), swap(q_next[1], 4))
+        g_up = weight_grad(gated_all, d_upper)
         d_normed = (d_normed_q + dot_nt(d_k_raw, w_key) + dot_nt(d_values, w_value)).astype(BF16)
+        q_last, g_up, d_normed, act = lax.optimization_barrier((q_last, g_up, d_normed, act))
+        g_query = pick(g_query_sum, plane) + q_last[0] + q_last[1]
         d_hidden_norm, g_attn_norm_part = norm1_pull(d_normed)
+        norms = jnp.stack([g_attn_norm_part, g_mlp_norm_part])
+        norms_near = [swap(norms, bit) for bit in (2, 4, 6)]
+        g_down = weight_grad(act, grad_all)
+        norms_near, g_down, d_hidden_norm = lax.optimization_barrier((norms_near, g_down, d_hidden_norm))
+        norms = norms + norms_near[0] + norms_near[1] + norms_near[2]
+        g_norms = norms + swap(norms, 1)
         grad_hidden = (d_resid.astype(F32) + d_hidden_norm.astype(F32)).astype(BF16)
-        g_norms = all_sum_small(jnp.stack([g_attn_norm_part, g_mlp_norm_part]))
         full = (batch, shard, dim)
         return (hidden_out.reshape(full), grad_hidden.reshape(full), g_norms[0], g_query, g_key, g_value, g_out, g_norms[1], g_gate, g_up, g_down)
 

time: 1040 us -> 910 us (0.88)
  waiting for transfers between devices: 320 us -> 157 us
  Pallas kernels: 420 us -> 575 us
  matrix products: 215 us -> 71.5 us
  other arithmetic: 30.6 us -> 48.9 us
    pallas_call x0 -> x3, Pallas kernels: none -> 156 us  [weight_grad(): pl.pallas_call(product_kernel, out_shape=jax.ShapeDtypeStruct((m, n), F32...]
    dot_general x5 -> x3, matrix products: 161 us -> 15 us  [dot_tn(): return lax.dot_general(a, b, TN, preferred_element_type=F32)]
    reduce_scatter x2 -> x0, waiting for transfers between devices: 109 us -> none  [the longest x1 109 us: layer(): lax.psum_scatter(g_query_part, 'tp', scatter_dimension=0, tiled=False)]
    reduce_scatter x1, waiting for transfers between devices: 112 us -> 64.7 us  [layer(): g_out = lax.psum_scatter(g_out_part, 'tp', scatter_dimension=0, tiled=True)]
    all_gather x1 -> x0, waiting for transfers between devices: 13.9 us -> none  [layer(): g_kv = lax.all_gather(g_kv, 'tp', axis=0, tiled=True)]
    ppermute x13 -> x19, waiting for transfers between devices: 47.8 us -> 57.8 us  [swap(): return lax.ppermute(x, 'tp', [(t, t ^ bit) for t in range(8)])]
    ppermute x13 -> x19, starting transfers between devices: 14.4 us -> 20.9 us  [swap(): return lax.ppermute(x, 'tp', [(t, t ^ bit) for t in range(8)])]
  transfers between devices with their start and end apart: 19 -> 23, of which waited for: 12 -> 11; matrix products, arithmetic and copies ran while one was open for 20% -> 7% of each run, Pallas kernels for 2% -> 20%
where the time goes in v4:
time: 910 us; the launch traced here: 905 us
  Pallas kernels  575 us (63%)
  waiting for transfers between devices  157 us (17%)
  matrix products  71.5 us (8%)
  other arithmetic  48.9 us (5%)
  starting transfers between devices  21.1 us (2%)
  local copies, waits for them, and re-layouts  16.4 us (2%)
  between operations  14.7 us (2%)
    pallas_call x1, Pallas kernels, gated_layer(): pl.pallas_call(functools.partial(gated_kernel, bn=bn), out_shape=(gathere...  185 us
    pallas_call x1, Pallas kernels, back_layer(): pl.pallas_call(functools.partial(back_kernel, rows=rows, bn=bn), out_shap...  177 us
    pallas_call x3, Pallas kernels, weight_grad(): pl.pallas_call(product_kernel, out_shape=jax.ShapeDtypeStruct((m, n), F32...  156 us
    reduce_scatter x1, waiting for transfers between devices, layer(): g_out = lax.psum_scatter(g_out_part, 'tp', scatter_dimension=0, tiled=True)  64.7 us
    ppermute x19, waiting for transfers between devices, swap(): return lax.ppermute(x, 'tp', [(t, t ^ bit) for t in range(8)])  57.8 us
    pallas_call x1, Pallas kernels, attention_backward(): pl.pallas_call(attn_bwd_kernel, out_shape=(jax.ShapeDtypeStruct((heads, r...  34.7 us
    pallas_call x1, Pallas kernels, attention_forward(): pl.pallas_call(attn_fwd_kernel, out_shape=jax.ShapeDtypeStruct((rows, hea...  23.5 us
    ppermute x19, starting transfers between devices, swap(): return lax.ppermute(x, 'tp', [(t, t ^ bit) for t in range(8)])  20.9 us
  transfers between devices with their start and end apart: 23, of which 11 were waited for; matrix products, arithmetic and copies ran while one was open for 7% of the time, Pallas kernels for 20%

profile of v4, /device:TPU:0, one launch (start us, length us, event | category | flops | bytes accessed | tf_op | source)
XLA Modules:
  0.0 905.2 jit_solution(6041206766286413905)
XLA Ops:
  22.7 20.8 %collective-permute-done = bf16[576,512]{1,0:T(8,128)(2,1)S(1)} collective-permute-done((bf16[576,512]{1,0:T(8,128)(2,1)S(1)}, bf16[576,512]{1,0:T(8,128)(2,1)S(1)}, u32[]{:S(2)}, u32[]{:S(2)}) %collective-permute-start) | collective-permute-done | bytes 589856 | tf_op jit(solution)/shard_map/ppermute | solution.py:54
  48.7 8.1 collective-permute-done.2
  56.8 4.9 collective-permute-done.3
  64.6 14.5 %all-gather.6.cloned.1.call-done = bf16[16384,256]{1,0:T(8,128)(2,1)} async-done(((bf16[2048,256]{1,0:T(8,128)(2,1)}), bf16[16384,256]{1,0:T(8,128)(2,1)}) %all-gather.6.cloned.1.call-update) | async-done | bytes 8388624 | tf_op jit(solution)/shard_map/all_gather | solution.py:653
  79.1 8.6 fusion.16
  88.8 23.5 %attn_fwd.1 = bf16[576,2048]{1,0:T(8,128)(2,1)S(1)} custom-call(s32[11,3]{1,0:T(8,128)S(1)} %add_add_fusion.3.lens_ref, s32[1,1536]{1,0:T(1,128)S(1)} %add.202.kpos_ref, bf16[8,576,256]{2,1,0:T(8,128)(2,1)S(1)} %pad_maximum_fusion.q_ref, bf16[4,576,512]{2,1,0:T(8,128)(2,1)} %pad_maximum_fusion.1.kv0_ref, bf16[4,576,512]{2,1,0:T(8,128)(2,1)} %collective-permute-done.4.kv1_ref), custom_call_target="tpu_custom_call" | custom-call | flops 7247757312 | bytes 12582912 | tf_op jit(solution)/shard_map/attn_fwd/pallas_call | solution.py:147
  113.7 18.2 %all-gather.4.cloned.1.call-done = bf16[2048,2048]{1,0:T(8,128)(2,1)} async-done(((bf16[256,2048]{1,0:T(8,128)(2,1)}), bf16[2048,2048]{1,0:T(8,128)(2,1)}) %all-gather.4.cloned.1.call-update) | async-done | bytes 8388624 | tf_op jit(solution)/shard_map/all_gather | solution.py:660
  131.9 8.1 fusion.10
  143.4 184.7 %gated.1 = (bf16[4608,2048]{1,0:T(8,128)(2,1)}, bf16[4608,2048]{1,0:T(8,128)(2,1)}, bf16[4608,2048]{1,0:T(8,128)(2,1)}, bf16[4608,2048]{1,0:T(8,128)(2,1)}, bf16[4608,2048]{1,0:T(8,128)(2,1)}) custom-call(bf16[576,2048]{1,0:T(8,128)(2,1)} %fusion.4.z_own, bf16[576,2048]{1,0:T(8,128)(2,1)} %bitcast.152, bf16[2048,2048]{1,0:T(8,128)(2,1)} %wg_hbm.3, ...), custom_call_target="tpu_custom_call" | custom-call | flops 115964116992 | bytes 209715200 | tf_op jit(solution)/shard_map/gated/pallas_call | solution.py:391
  328.1 176.9 %back.1 = (f32[2,576,2048]{2,1,0:T(8,128)}, bf16[2,576,2048]{2,1,0:T(8,128)(2,1)}, bf16[2,576,2048]{2,1,0:T(8,128)(2,1)}) custom-call(bf16[4608,2048]{1,0:T(8,128)(2,1)} %get-tuple-element.75.act.a_ref, bf16[4608,2048]{1,0:T(8,128)(2,1)} %get-tuple-element.65.d_gate.b_ref, bf16[4608,2048]{1,0:T(8,128)(2,1)} %get-tuple-element.72.d_up.b_ref, ...), custom_call_target="tpu_custom_call" | custom-call | flops 115964116992 | bytes 209715200 | tf_op jit(solution)/shard_map/back/pallas_call | solution.py:580
  505.0 10.9 %fusion.12 = (f32[576]{0:T(1024)S(1)}, f32[2048]{0:T(1024)}, bf16[576,2048]{1,0:T(8,128)(2,1)S(1)}, bf16[576,2048]{1,0:T(8,128)(2,1)}) fusion(bf16[576,2048]{1,0:T(8,128)(2,1)} %copy-done.7, f32[2048]{0:T(1024)} %copy-done.34, f32[576]{0:T(1024)} %copy-done.39, bf16[2,576,2048]{2,1,0:T(8,128)(2,1)} %get-tuple-element.55, ...), kind=kLoop, calls=%fused_computation.24 | loop fusion | flops 22410688 | bytes 25973248 | tf_op jit(solution)/shard_map/transpose(jvp())/reduce_sum | solution.py:23
  517.7 10.2 %fusion.58 = f32[2048,2048]{1,0:T(8,128)} fusion(bf16[576,2048]{1,0:T(8,128)(2,1)S(1)} %copy-done.3, bf16[576,2048]{1,0:T(8,128)(2,1)S(1)} %add_convert_fusion.2), kind=kOutput, calls=%fused_computation.129 | convolution fusion | flops 4831838208 | bytes 21495808 | tf_op jit(solution)/shard_map/dot_general | solution.py:50
  527.9 9.7 %convolution_convert_fusion.do_ref = bf16[576,2048]{1,0:T(8,128)(2,1)} fusion(bf16[576,2048]{1,0:T(8,128)(2,1)S(1)} %add_convert_fusion.2, bf16[2048,2048]{1,0:T(8,128)(2,1)} %all-gather.4.cloned.1.call-done), kind=kOutput, calls=%fused_computation.35 | convolution fusion | flops 4833017856 | bytes 13107200 | tf_op jit(solution)/shard_map/dot_general | solution.py:46
  537.5 34.7 %attn_bwd.1 = (bf16[8,576,256]{2,1,0:T(8,128)(2,1)}, bf16[4,576,512]{2,1,0:T(8,128)(2,1)}, bf16[4,576,512]{2,1,0:T(8,128)(2,1)}) custom-call(s32[11,3]{1,0:T(8,128)} %copy-done.1, f32[192,128]{1,0:T(8,128)} %copy-done.20, f32[192,128]{1,0:T(8,128)} %copy-done.22, bf16[8,576,256]{2,1,0:T(8,128)(2,1)} %copy-done, ...), custom_call_target="tpu_custom_call" | custom-call | flops 18119393280 | bytes 20971520 | tf_op jit(solution)/shard_map/attn_bwd/pallas_call | solution.py:172
  572.3 7.0 convolution_bitcast_fusion
  579.8 9.8 %convolution_bitcast_fusion.1 = f32[576,2048]{1,0:T(8,128)} fusion(bf16[8,576,256]{2,1,0:T(8,128)(2,1)} %get-tuple-element.59, bf16[8,2048,256]{2,1,0:T(8,128)(2,1)} %bitcast.169), kind=kOutput, calls=%fused_computation.34 | convolution fusion | flops 4831838208 | bytes 15466496 | tf_op jit(solution)/shard_map/hte,hde->td/dot_general | solution.py:685
  589.6 6.6 collective-permute-done.5
  600.8 6.1 bitcast_add_fusion
  615.6 49.5 %weight_grad.3 = f32[2048,2048]{1,0:T(8,128)} custom-call(bf16[4608,2048]{1,0:T(8,128)(2,1)} %get-tuple-element.64.a_ref, bf16[4608,2048]{1,0:T(8,128)(2,1)} %get-tuple-element.65.d_gate.b_ref), custom_call_target="tpu_custom_call" | custom-call | flops 38654705664 | bytes 115343360 | tf_op jit(solution)/shard_map/weight_grad/pallas_call | solution.py:603
  688.2 51.0 %weight_grad.4 = f32[2048,2048]{1,0:T(8,128)} custom-call(bf16[4608,2048]{1,0:T(8,128)(2,1)} %get-tuple-element.64.a_ref, bf16[4608,2048]{1,0:T(8,128)(2,1)} %get-tuple-element.72.d_up.b_ref), custom_call_target="tpu_custom_call" | custom-call | flops 38654705664 | bytes 115343360 | tf_op jit(solution)/shard_map/weight_grad/pallas_call | solution.py:603
  739.2 14.7 %collective-permute-done.13 = f32[2048,256]{0,1:T(8,128)S(1)} collective-permute-done((f32[2048,256]{0,1:T(8,128)}, f32[2048,256]{0,1:T(8,128)S(1)}, u32[]{:S(2)}, u32[]{:S(2)}) %collective-permute-start.13) | collective-permute-done | bytes 2097184 | tf_op jit(solution)/shard_map/ppermute | solution.py:54
  762.2 55.1 %weight_grad.5 = f32[2048,2048]{1,0:T(8,128)} custom-call(bf16[4608,2048]{1,0:T(8,128)(2,1)} %get-tuple-element.75.act.a_ref, bf16[4608,2048]{1,0:T(8,128)(2,1)} %get-tuple-element.76.b_ref), custom_call_target="tpu_custom_call" | custom-call | flops 38654705664 | bytes 115343360 | tf_op jit(solution)/shard_map/weight_grad/pallas_call | solution.py:603
  824.5 4.2 add_convert_fusion
  829.3 64.7 %reduce-scatter.2.cloned.1.call-done = f32[256,2048]{1,0:T(8,128)} async-done(((f32[2048,2048]{1,0:T(8,128)}), f32[256,2048]{1,0:T(8,128)}) %reduce-scatter.2.cloned.1.call-update) | async-done | bytes 2097168 | tf_op jit(solution)/shard_map/reduce_scatter | solution.py:677
  (204 shorter events, 88.1 us)
Async XLA Ops:
  7.2 71.9 %all-gather.6.cloned.1.call-start = ((), (), s32[]{:S(2)}) async-start(), calls=%async_computation.3 | async-start | bytes 9437184 | tf_op jit(solution)/shard_map/all_gather | solution.py:653
  7.9 124.0 %all-gather.4.cloned.1.call-start = ((), (), s32[]{:S(2)}) async-start(), calls=%async_computation.1 | async-start | bytes 9437184 | tf_op jit(solution)/shard_map/all_gather | solution.py:660
  8.7 820.7 %all-reduce.5.cloned.1.call-start = ((), (), s32[]{:S(2)}) async-start(), calls=%async_computation.4 | async-start | bytes 8388608 | tf_op jit(solution)/shard_map/psum | solution.py:702
  15.7 27.8 %collective-permute-start = (bf16[576,512]{1,0:T(8,128)(2,1)S(1)}, bf16[576,512]{1,0:T(8,128)(2,1)S(1)}, u32[]{:S(2)}, u32[]{:S(2)}) collective-permute-start(bf16[576,512]{1,0:T(8,128)(2,1)S(1)} %get-tuple-element.148), channel_id=1, source_target_pairs={{0,2},{1,3},{2,0},{3,1},{4,6},{5,7},{6,4},{7,5},{8,10},{9,11},{10,... | collective-permute-start | bytes 1769480 | tf_op jit(solution)/shard_map/ppermute | solution.py:54
  18.9 27.2 %collective-permute-start.1 = (bf16[576,512]{1,0:T(8,128)(2,1)S(1)}, bf16[576,512]{1,0:T(8,128)(2,1)S(1)}, u32[]{:S(2)}, u32[]{:S(2)}) collective-permute-start(bf16[576,512]{1,0:T(8,128)(2,1)S(1)} %get-tuple-element.148), channel_id=1, source_target_pairs={{0,4},{1,5},{2,6},{3,7},{4,0},{5,1},{6,2},{7,3},{8,12},{9,13},{10,... | collective-permute-start | bytes 1769480 | tf_op jit(solution)/shard_map/ppermute | solution.py:54
  44.3 12.5 %collective-permute-start.2 = (bf16[288,512]{1,0:T(8,128)(2,1)S(1)}, bf16[288,512]{1,0:T(8,128)(2,1)S(1)}, u32[]{:S(2)}, u32[]{:S(2)}) collective-permute-start(bf16[288,512]{1,0:T(8,128)(2,1)S(1)} %slice.198), channel_id=1, source_target_pairs={{0,4},{1,5},{2,6},{3,7},{4,0},{5,1},{6,2},{7,3},{8,12},{9,13},{10,... | collective-permute-start | bytes 884744 | tf_op jit(solution)/shard_map/ppermute | solution.py:54
  47.0 14.7 %collective-permute-start.3 = (bf16[288,512]{1,0:T(8,128)(2,1)S(1)}, bf16[288,512]{1,0:T(8,128)(2,1)S(1)}, u32[]{:S(2)}, u32[]{:S(2)}) collective-permute-start(bf16[288,512]{1,0:T(8,128)(2,1)S(1)} %slice.199), channel_id=1, source_target_pairs={{0,2},{1,3},{2,0},{3,1},{4,6},{5,7},{6,4},{7,5},{8,10},{9,11},{10,... | collective-permute-start | bytes 884744 | tf_op jit(solution)/shard_map/ppermute | solution.py:54
  48.7 91.3 %copy-start.34 = (f32[2048]{0:T(1024)}, f32[2048]{0:T(1024)S(1)}, u32[]{:S(2)}) copy-start(f32[2048]{0:T(1024)S(1)} %convert_add_fusion.3) | copy-start | bytes 24580
  64.6 24.1 %collective-permute-start.4 = (bf16[4,576,512]{2,1,0:T(8,128)(2,1)}, bf16[4,576,512]{2,1,0:T(8,128)(2,1)}, u32[]{:S(2)}, u32[]{:S(2)}) collective-permute-start(bf16[4,576,512]{2,1,0:T(8,128)(2,1)} %pad_maximum_fusion.1.kv0_ref), channel_id=1, source_target_pairs={{0,1},{1,0},{2,3},{3,2},{4,5},{5,4},{6,7},{7,6},{8,9},{9,8},{10,11... | collective-permute-start | bytes 7077896 | tf_op jit(solution)/shard_map/ppermute | solution.py:54
  579.3 21.5 %collective-permute-start.8 = (f32[4,2048,256]{1,2,0:T(8,128)}, f32[4,2048,256]{1,2,0:T(8,128)}, u32[]{:S(2)}, u32[]{:S(2)}) collective-permute-start(f32[4,2048,256]{1,2,0:T(8,128)} %convolution_bitcast_fusion), channel_id=1, source_target_pairs={{0,1},{1,0},{2,3},{3,2},{4,5},{5,4},{6,7},{7,6},{8,9},{9,8},{10,11... | collective-permute-start | bytes 25165832 | tf_op jit(solution)/shard_map/ppermute | solution.py:54
  579.3 16.9 %collective-permute-start.5 = (bf16[4,576,512]{2,1,0:T(8,128)(2,1)}, bf16[4,576,512]{2,1,0:T(8,128)(2,1)}, u32[]{:S(2)}, u32[]{:S(2)}) collective-permute-start(bf16[4,576,512]{2,1,0:T(8,128)(2,1)} %get-tuple-element.58), channel_id=1, source_target_pairs={{0,1},{1,0},{2,3},{3,2},{4,5},{5,4},{6,7},{7,6},{8,9},{9,8},{10,11... | collective-permute-start | bytes 7077896 | tf_op jit(solution)/shard_map/ppermute | solution.py:54
  598.2 9.1 %collective-permute-start.7 = (bf16[288,512]{1,0:T(8,128)(2,1)S(1)}, bf16[288,512]{1,0:T(8,128)(2,1)S(1)}, u32[]{:S(2)}, u32[]{:S(2)}) collective-permute-start(bf16[288,512]{1,0:T(8,128)(2,1)S(1)} %get-tuple-element.145), channel_id=1, source_target_pairs={{0,4},{1,5},{2,6},{3,7},{4,0},{5,1},{6,2},{7,3},{8,12},{9,13},{10,... | collective-permute-start | bytes 884744 | tf_op jit(solution)/shard_map/ppermute | solution.py:54
  599.1 8.8 collective-permute-start.6
  609.4 55.8 %collective-permute-start.10 = (bf16[576,512]{1,0:T(8,128)(2,1)}, bf16[576,512]{1,0:T(8,128)(2,1)}, u32[]{:S(2)}, u32[]{:S(2)}) collective-permute-start(bf16[576,512]{1,0:T(8,128)(2,1)} %pad_maximum_fusion.6), channel_id=1, source_target_pairs={{0,4},{1,5},{2,6},{3,7},{4,0},{5,1},{6,2},{7,3},{8,12},{9,13},{10,... | collective-permute-start | bytes 1769480 | tf_op jit(solution)/shard_map/ppermute | solution.py:54
  611.5 53.7 %collective-permute-start.9 = (bf16[576,512]{1,0:T(8,128)(2,1)}, bf16[576,512]{1,0:T(8,128)(2,1)}, u32[]{:S(2)}, u32[]{:S(2)}) collective-permute-start(bf16[576,512]{1,0:T(8,128)(2,1)} %pad_maximum_fusion.5), channel_id=1, source_target_pairs={{0,2},{1,3},{2,0},{3,1},{4,6},{5,7},{6,4},{7,5},{8,10},{9,11},{10,... | collective-permute-start | bytes 1769480 | tf_op jit(solution)/shard_map/ppermute | solution.py:54
  613.8 51.4 %collective-permute-start.11 = (f32[1024,256]{0,1:T(8,128)}, f32[1024,256]{0,1:T(8,128)}, u32[]{:S(2)}, u32[]{:S(2)}) collective-permute-start(f32[1024,256]{0,1:T(8,128)} %get-tuple-element.133), channel_id=1, source_target_pairs={{0,2},{1,3},{2,0},{3,1},{4,6},{5,7},{6,4},{7,5},{8,10},{9,11},{10,... | collective-permute-start | bytes 3145736 | tf_op jit(solution)/shard_map/ppermute | solution.py:54
  614.8 50.4 %collective-permute-start.12 = (f32[1024,256]{0,1:T(8,128)S(1)}, f32[1024,256]{0,1:T(8,128)}, u32[]{:S(2)}, u32[]{:S(2)}) collective-permute-start(f32[1024,256]{0,1:T(8,128)S(1)} %get-tuple-element.135), channel_id=1, source_target_pairs={{0,4},{1,5},{2,6},{3,7},{4,0},{5,1},{6,2},{7,3},{8,12},{9,13},{10,... | collective-permute-start | bytes 3145736 | tf_op jit(solution)/shard_map/ppermute | solution.py:54
  679.6 214.5 %reduce-scatter.2.cloned.1.call-start = ((), (), s32[]{:S(2)}) async-start(), calls=%async_computation.2 | async-start | bytes 18874368 | tf_op jit(solution)/shard_map/reduce_scatter | solution.py:677
  680.2 73.7 %collective-permute-start.13 = (f32[2048,256]{0,1:T(8,128)}, f32[2048,256]{0,1:T(8,128)S(1)}, u32[]{:S(2)}, u32[]{:S(2)}) collective-permute-start(f32[2048,256]{0,1:T(8,128)} %get-tuple-element.70), channel_id=1, source_target_pairs={{0,2},{1,3},{2,0},{3,1},{4,6},{5,7},{6,4},{7,5},{8,10},{9,11},{10,... | collective-permute-start | bytes 6291464 | tf_op jit(solution)/shard_map/ppermute | solution.py:54
  681.7 74.0 %collective-permute-start.14 = (f32[2048,256]{0,1:T(8,128)}, f32[2048,256]{0,1:T(8,128)}, u32[]{:S(2)}, u32[]{:S(2)}) collective-permute-start(f32[2048,256]{0,1:T(8,128)} %get-tuple-element.71), channel_id=1, source_target_pairs={{0,4},{1,5},{2,6},{3,7},{4,0},{5,1},{6,2},{7,3},{8,12},{9,13},{10,... | collective-permute-start | bytes 6291464 | tf_op jit(solution)/shard_map/ppermute | solution.py:54
  757.5 66.9 %collective-permute-start.17 = (f32[2,2048]{1,0:T(2,128)S(1)}, f32[2,2048]{1,0:T(2,128)S(1)}, u32[]{:S(2)}, u32[]{:S(2)}) collective-permute-start(f32[2,2048]{1,0:T(2,128)S(1)} %pad_maximum_fusion.7), channel_id=1, source_target_pairs={{0,6},{1,7},{2,4},{3,5},{4,2},{5,3},{6,0},{7,1},{8,14},{9,15},{10,... | collective-permute-start | bytes 49160 | tf_op jit(solution)/shard_map/ppermute | solution.py:54
  758.6 65.8 %collective-permute-start.16 = (f32[2,2048]{1,0:T(2,128)S(1)}, f32[2,2048]{1,0:T(2,128)S(1)}, u32[]{:S(2)}, u32[]{:S(2)}) collective-permute-start(f32[2,2048]{1,0:T(2,128)S(1)} %pad_maximum_fusion.7), channel_id=1, source_target_pairs={{0,4},{1,5},{2,6},{3,7},{4,0},{5,1},{6,2},{7,3},{8,12},{9,13},{10,... | collective-permute-start | bytes 49160 | tf_op jit(solution)/shard_map/ppermute | solution.py:54
  759.3 65.1 %collective-permute-start.15 = (f32[2,2048]{1,0:T(2,128)S(1)}, f32[2,2048]{1,0:T(2,128)S(1)}, u32[]{:S(2)}, u32[]{:S(2)}) collective-permute-start(f32[2,2048]{1,0:T(2,128)S(1)} %pad_maximum_fusion.7), channel_id=1, source_target_pairs={{0,2},{1,3},{2,0},{3,1},{4,6},{5,7},{6,4},{7,5},{8,10},{9,11},{10,... | collective-permute-start | bytes 49160 | tf_op jit(solution)/shard_map/ppermute | solution.py:54
  824.5 4.2 collective-permute-start.18
  (49 other events, 848.7 us)
Sparse Core Ops, SparseCore 0:
  9.9 69.2 all-gather.5
  81.0 50.8 all-gather.3
  679.7 99.8 all-reduce.4
  783.6 110.4 reduce-scatter.1

commit v5 on v4

--- a/solution.py
+++ b/solution.py
@@ -54,45 +54,25 @@
     return lax.ppermute(x, "tp", [(t, t ^ bit) for t in range(8)])
 
 
-def gather_near(own):
-    half = own.shape[0] // 2
-    side = swap(own, 2)
-    back = swap(own, 4)
-    diag = jnp.concatenate([swap(side[:half], 4), swap(back[half:], 2)], axis=0)
-    mine = jnp.stack([own, side, back, diag])
-    return mine, swap(mine, 1)
-
-
-def keys_values(kv0_ref, kv1_ref, total, head_dim):
-    both = jnp.concatenate([kv0_ref[...].reshape(total // 2, 2 * head_dim), kv1_ref[...].reshape(total // 2, 2 * head_dim)], axis=0)
-    return both[:, :head_dim], both[:, head_dim:]
-
-
-def attn_fwd_kernel(lens_ref, kpos_ref, q_ref, kv0_ref, kv1_ref, o_ref, p_ref):
+def flip(index, bit):
+    return index + bit - 2 * bit * ((index // bit) % 2)
+
+
+def neighbours():
+    me = lax.axis_index("tp")
+    return me, flip(me, 1), flip(me, 2), flip(me, 4)
+
+
+def enter(peers):
+    barrier = pltpu.get_barrier_semaphore()
+    for peer in peers:
+        pl.semaphore_signal(barrier, inc=1, device_id={"tp": peer}, device_id_type=pl.DeviceIdType.MESH)
+    pl.semaphore_wait(barrier, len(peers))
+
+
+def attn_bwd_kernel(lens_ref, cos_ref, sin_ref, q_ref, kv_ref, do_ref, dq_ref, dkv0_ref, dkv1_ref, dkv_acc):
     heads, shard, head_dim = q_ref.shape
-    total = 2 * kv0_ref.shape[0] * shard
-    s_id = pl.program_id(0)
-    prefix = lens_ref[0, s_id]
-    valid = lens_ref[1, s_id]
-    first = lens_ref[2, 0] * shard
-    keys, values = keys_values(kv0_ref, kv1_ref, total, head_dim)
-    q_pos = first + lax.broadcasted_iota(jnp.int32, (shard, 1), 0)
-    visible = kpos_ref[...] < jnp.minimum(valid, jnp.maximum(prefix, q_pos + 1))
-    query = q_ref[...].reshape(heads * shard, head_dim) * BF16(head_dim ** -0.5)
-    scores = dot_nt(query, keys)
-    for h in range(heads):
-        rows = slice(h * shard, (h + 1) * shard)
-        s = jnp.where(visible, scores[rows], MASKED)
-        e = jnp.exp(s - jnp.max(s, axis=-1, keepdims=True))
-        p_ref[rows, :] = (e * (1.0 / jnp.sum(e, axis=-1, keepdims=True))).astype(BF16)
-    mixed = dot_nn(p_ref[...], values).astype(BF16)
-    for h in range(heads):
-        o_ref[:, h * head_dim:(h + 1) * head_dim] = mixed[h * shard:(h + 1) * shard]
-
-
-def attn_bwd_kernel(lens_ref, cos_ref, sin_ref, q_ref, kv0_ref, kv1_ref, do_ref, dq_ref, dkv0_ref, dkv1_ref, dkv_acc):
-    heads, shard, head_dim = q_ref.shape
-    tp = 2 * kv0_ref.shape[0]
+    tp = kv_ref.shape[0]
     total = tp * shard
     rows = heads * shard
     s_id = pl.program_id(0)
@@ -100,7 +80,8 @@
     prefix = lens_ref[0, s_id]
     valid = lens_ref[1, s_id]
     first = lens_ref[2, 0] * shard
-    keys, values = keys_values(kv0_ref, kv1_ref, total, head_dim)
+    keys = kv_ref[:, :, :head_dim].reshape(total, head_dim)
+    values = kv_ref[:, :, head_dim:].reshape(total, head_dim)
     query = q_ref[...].reshape(rows, head_dim) * BF16(head_dim ** -0.5)
     d_out = jnp.concatenate([do_ref[:, h * head_dim:(h + 1) * head_dim] for h in range(heads)], axis=0)
     step = lax.broadcasted_iota(jnp.int32, (shard, 1), 0)
@@ -138,31 +119,233 @@
         dkv1_ref[...] = dkv_acc[total // 2:].astype(BF16).reshape(near)
 
 
-def attention_forward(lens, k_pos, query, kv0, kv1, batch, group=4):
+def remote(src, dst, send, recv, peer):
+    return pltpu.make_async_remote_copy(src_ref=src, dst_ref=dst, send_sem=send, recv_sem=recv,
+                                        device_id={"tp": peer}, device_id_type=pl.DeviceIdType.MESH)
+
+
+def front_kernel(lens_ref, kpos_ref, cos_ref, sin_ref, gain1_ref, gain2_ref, hidden, w_query, w_key, w_value, w_out,
+                 normed_out, wq_all, wo_all, kv_all, query_out, mixed_out, resid_out, gated_out,
+                 x_buf, n_buf, wkv, wq, wo, kv, q, probs, mix, acc, load, store, send, recv, *, batch):
+    rows, dim = x_buf.shape
+    shard = rows // batch
+    head_dim = w_key.shape[1]
+    tp = wq.shape[0]
+    near = tp // 2
+    total = tp * shard
+    half_dim = head_dim // 2
+    me, core, side, back = neighbours()
+    bufs = (wq, kv, wo)
+
+    def to_side(a):
+        return remote(bufs[a].at[0], bufs[a].at[1], send.at[a, 0], recv.at[a, 0], side)
+
+    def to_back(a):
+        return remote(bufs[a].at[0], bufs[a].at[2], send.at[a, 1], recv.at[a, 1], back)
+
+    def onward(a, k):
+        half = bufs[a].shape[1] // 2
+        part = pl.ds(k * half, half)
+        return remote(bufs[a].at[1 + k, part], bufs[a].at[3, part], send.at[a, 2 + k], recv.at[a, 2 + k], (back, side)[k])
+
+    def to_core(a, k):
+        return remote(bufs[a].at[k], bufs[a].at[near + k], send.at[a, 4 + k], recv.at[a, 4 + k], core)
+
+    loads = [pltpu.make_async_copy(src, dst, load.at[i]) for i, (src, dst) in enumerate((
+        (w_query, wq.at[0]), (hidden, x_buf), (w_key, wkv.at[:, :head_dim]), (w_value, wkv.at[:, head_dim:]), (w_out, wo.at[0])))]
+    mixed_at = [me, side, back, flip(side, 4)]
+    mixed_at = mixed_at + [flip(dev, 1) for dev in mixed_at]
+    stores = {name: pltpu.make_async_copy(src, dst, store.at[i]) for i, (name, src, dst) in enumerate((
+        ("normed", n_buf, normed_out), ("wq", wq, wq_all), ("wo", wo, wo_all), ("kv", kv, kv_all), ("query", q, query_out),
+        ("resid", x_buf, resid_out), ("gated", n_buf, gated_out)))}
+    mixed_stores = [pltpu.make_async_copy(mix.at[:, pl.ds(k * head_dim, head_dim)],
+                                          mixed_out.at[:, pl.ds(pl.multiple_of(dev * head_dim, 128), head_dim)], store.at[7 + k])
+                    for k, dev in enumerate(mixed_at)]
+
+    for cp in loads:
+        cp.start()
+    enter((core, side, back))
+    loads[0].wait()
+    to_side(0).start()
+    to_back(0).start()
+    to_core(0, 0).start()
+
+    def norm_rows(src, gain_ref):
+        x_f = src.astype(F32)
+        inv_rms = lax.rsqrt(jnp.mean(x_f * x_f, axis=-1, keepdims=True) + NORM_EPS)
+        return (x_f * inv_rms * (1.0 + gain_ref[...].astype(F32))).astype(BF16)
+
+    def seq_rows(i):
+        return pl.ds(pl.multiple_of(i * shard, 16), shard)
+
+    def rotate(x_f):
+        first, second = x_f[:, :half_dim], x_f[:, half_dim:]
+        cos_t, sin_t = cos_ref[...], sin_ref[...]
+        return first * cos_t - second * sin_t, second * cos_t + first * sin_t
+
+    def norm1(i, carry):
+        n_buf[seq_rows(i), :] = norm_rows(x_buf[seq_rows(i), :], gain1_ref)
+        return carry
+
+    loads[1].wait()
+    lax.fori_loop(0, batch, norm1, 0)
+    stores["normed"].start()
+    loads[2].wait()
+    loads[3].wait()
+
+    def own_kv(i, carry):
+        raw = dot_nn(n_buf[seq_rows(i), :], wkv[...])
+        first, second = rotate(raw[:, :head_dim])
+        kv[0, seq_rows(i), :half_dim] = first.astype(BF16)
+        kv[0, seq_rows(i), half_dim:head_dim] = second.astype(BF16)
+        kv[0, seq_rows(i), head_dim:] = raw[:, head_dim:].astype(BF16)
+        return carry
+
+    lax.fori_loop(0, batch, own_kv, 0)
+    to_side(1).start()
+    to_back(1).start()
+    to_core(1, 0).start()
+
+    def own_query(k):
+        def step(i, carry):
+            for h in (k, near + k):
+                first, second = rotate(dot_nn(n_buf[seq_rows(i), :], wq[h]))
+                q[h, seq_rows(i), :half_dim] = first.astype(BF16)
+                q[h, seq_rows(i), half_dim:] = second.astype(BF16)
+            return carry
+
+        to_core(0, k).wait_recv()
+        lax.fori_loop(0, batch, step, 0)
+
+    def pass_on(a):
+        to_side(a).wait_recv()
+        onward(a, 0).start()
+        to_core(a, 1).start()
+        to_back(a).wait_recv()
+        onward(a, 1).start()
+        to_core(a, 2).start()
+
+    def pass_last(a):
+        onward(a, 0).wait_recv()
+        onward(a, 1).wait_recv()
+        to_core(a, 3).start()
+
+    own_query(0)
+    pass_on(0)
+    own_query(1)
+    own_query(2)
+    pass_on(1)
+    loads[4].wait()
+    to_side(2).start()
+    to_back(2).start()
+    to_core(2, 0).start()
+    pass_last(0)
+    own_query(3)
+    stores["query"].start()
+    stores["wq"].start()
+    pass_last(1)
+    for k in range(near):
+        to_core(1, k).wait_recv()
+    stores["kv"].start()
+
+    q_pos = me * shard + lax.broadcasted_iota(jnp.int32, (shard, 1), 0)
+
+    def attend(step, carry):
+        i, g = step // 2, step % 2
+        keys = kv[:, seq_rows(i), :head_dim].reshape(total, head_dim)
+        values = kv[:, seq_rows(i), head_dim:].reshape(total, head_dim)
+        query = q[pl.ds(g * near, near), seq_rows(i), :].reshape(near * shard, head_dim) * BF16(head_dim ** -0.5)
+        visible = kpos_ref[...] < jnp.minimum(lens_ref[1, i], jnp.maximum(lens_ref[0, i], q_pos + 1))
+        scores = dot_nt(query, keys)
+        for h in range(near):
+            part = slice(h * shard, (h + 1) * shard)
+            s = jnp.where(visible, scores[part], MASKED)
+            e = jnp.exp(s - jnp.max(s, axis=-1, keepdims=True))
+            probs[part, :] = (e * (1.0 / jnp.sum(e, axis=-1, keepdims=True))).astype(BF16)
+        mixed = dot_nn(probs[...], values).astype(BF16)
+        for h in range(near):
+            cols = pl.ds(pl.multiple_of((g * near + h) * head_dim, 128), head_dim)
+            mix[seq_rows(i), cols] = mixed[h * shard:(h + 1) * shard]
+        return carry
+
+    lax.fori_loop(0, 2 * batch, attend, 0)
+    for cp in mixed_stores:
+        cp.start()
+    pass_on(2)
+
+    def project(k, first):
+        def step(n, carry):
+            cols = pl.ds(pl.multiple_of(n * 512, 128), 512)
+            part = (dot_nn(mix[:, k * head_dim:(k + 1) * head_dim], wo[k, :, cols])
+                    + dot_nn(mix[:, (near + k) * head_dim:(near + k + 1) * head_dim], wo[near + k, :, cols]))
+            acc[:, cols] = part if first else acc[:, cols] + part
+            return carry
+
+        to_core(2, k).wait_recv()
+        lax.fori_loop(0, dim // 512, step, 0)
+
+    project(0, True)
+    project(1, False)
+    project(2, False)
+    pass_last(2)
+    project(3, False)
+    stores["wo"].start()
+    stores["normed"].wait()
+
+    def norm2(i, carry):
+        resid = (x_buf[seq_rows(i), :].astype(F32) + acc[seq_rows(i), :]).astype(BF16)
+        x_buf[seq_rows(i), :] = resid
+        n_buf[seq_rows(i), :] = norm_rows(resid, gain2_ref)
+        return carry
+
+    lax.fori_loop(0, batch, norm2, 0)
+    stores["resid"].start()
+    stores["gated"].start()
+    for cp in mixed_stores:
+        cp.wait()
+    for name in ("wq", "wo", "kv", "query", "resid", "gated"):
+        stores[name].wait()
+    for a in range(3):
+        to_side(a).wait_send()
+        to_back(a).wait_send()
+        for k in range(2):
+            onward(a, k).wait_send()
+        for k in range(near):
+            to_core(a, k).wait_send()
+
+
+def front_layer(lens, k_pos, cos_t, sin_t, attn_norm, mlp_norm, hidden, w_query, w_key, w_value, w_out, batch, tp):
+    rows, dim = hidden.shape
+    head_dim = w_key.shape[1]
+    shard = rows // batch
+    total = tp * shard
+    anyspace = pl.BlockSpec(memory_space=pl.ANY)
+    vmem = pl.BlockSpec(memory_space=pltpu.VMEM)
+    dma = pltpu.SemaphoreType.DMA
+
+    def shape(*dims):
+        return jax.ShapeDtypeStruct(dims, BF16)
+
+    return pl.pallas_call(
+        functools.partial(front_kernel, batch=batch),
+        out_shape=(shape(rows, dim), shape(tp, dim, head_dim), shape(tp, head_dim, dim), shape(tp, rows, 2 * head_dim),
+                   shape(tp, rows, head_dim), shape(rows, tp * head_dim), shape(rows, dim), shape(rows, dim)),
+        in_specs=[pl.BlockSpec(memory_space=pltpu.SMEM)] + [vmem] * 5 + [anyspace] * 5,
+        out_specs=(anyspace,) * 8,
+        scratch_shapes=[pltpu.VMEM((rows, dim), BF16), pltpu.VMEM((rows, dim), BF16), pltpu.VMEM((dim, 2 * head_dim), BF16),
+                        pltpu.VMEM((tp, dim, head_dim), BF16), pltpu.VMEM((tp, head_dim, dim), BF16),
+                        pltpu.VMEM((tp, rows, 2 * head_dim), BF16), pltpu.VMEM((tp, rows, head_dim), BF16),
+                        pltpu.VMEM((tp // 2 * shard, total), BF16), pltpu.VMEM((rows, tp * head_dim), BF16), pltpu.VMEM((rows, dim), F32),
+                        dma((5,)), dma((15,)), dma((3, 8)), dma((3, 8))],
+        compiler_params=pltpu.CompilerParams(vmem_limit_bytes=62 << 20, collective_id=2, has_side_effects=True),
+        cost_estimate=pl.CostEstimate(flops=8 * rows * dim * tp * head_dim, bytes_accessed=60 << 20, transcendentals=tp * rows * total),
+        name="front",
+    )(lens, k_pos, cos_t, sin_t, attn_norm.reshape(1, dim), mlp_norm.reshape(1, dim), hidden, w_query, w_key, w_value, w_out)
+
+
+def attention_backward(lens, cos_t, sin_t, query, kv_all, d_mixed, batch, group=4):
     heads, rows, head_dim = query.shape
-    near = kv0.shape[0]
-    shard = rows // batch
-    total = 2 * near * shard
-    q_spec = pl.BlockSpec((group, shard, head_dim), lambda s, g, *_: (g, s, 0))
-    return pl.pallas_call(
-        attn_fwd_kernel,
-        out_shape=jax.ShapeDtypeStruct((rows, heads * head_dim), BF16),
-        grid_spec=pltpu.PrefetchScalarGridSpec(
-            num_scalar_prefetch=1, grid=(batch, heads // group),
-            in_specs=[pl.BlockSpec((1, total), lambda s, g, *_: (0, 0)), q_spec,
-                      pl.BlockSpec((near, shard, 2 * head_dim), lambda s, g, *_: (0, s, 0)),
-                      pl.BlockSpec((near, shard, 2 * head_dim), lambda s, g, *_: (0, s, 0))],
-            out_specs=pl.BlockSpec((shard, group * head_dim), lambda s, g, *_: (s, g)),
-            scratch_shapes=[pltpu.VMEM((group * shard, total), BF16)]),
-        compiler_params=pltpu.CompilerParams(dimension_semantics=("arbitrary", "arbitrary"), vmem_limit_bytes=48 << 20),
-        cost_estimate=pl.CostEstimate(flops=4 * heads * rows * total * head_dim, bytes_accessed=12 << 20, transcendentals=heads * rows * total),
-        name="attn_fwd",
-    )(lens, k_pos, query, kv0, kv1)
-
-
-def attention_backward(lens, cos_t, sin_t, query, kv0, kv1, d_mixed, batch, group=4):
-    heads, rows, head_dim = query.shape
-    near = kv0.shape[0]
+    near = kv_all.shape[0] // 2
     shard = rows // batch
     total = 2 * near * shard
     q_spec = pl.BlockSpec((group, shard, head_dim), lambda s, g, *_: (g, s, 0))
@@ -174,29 +357,13 @@
         out_shape=(jax.ShapeDtypeStruct((heads, rows, head_dim), BF16), kv_shape, kv_shape),
         grid_spec=pltpu.PrefetchScalarGridSpec(
             num_scalar_prefetch=1, grid=(batch, heads // group),
-            in_specs=[table, table, q_spec, kv_spec, kv_spec, pl.BlockSpec((shard, group * head_dim), lambda s, g, *_: (s, g))],
+            in_specs=[table, table, q_spec, pl.BlockSpec((2 * near, shard, 2 * head_dim), lambda s, g, *_: (0, s, 0)), pl.BlockSpec((shard, group * head_dim), lambda s, g, *_: (s, g))],
             out_specs=(q_spec, kv_spec, kv_spec),
             scratch_shapes=[pltpu.VMEM((total, 2 * head_dim), F32)]),
         compiler_params=pltpu.CompilerParams(dimension_semantics=("arbitrary", "arbitrary"), vmem_limit_bytes=56 << 20),
         cost_estimate=pl.CostEstimate(flops=10 * heads * rows * total * head_dim, bytes_accessed=20 << 20, transcendentals=heads * rows * total),
         name="attn_bwd",
-    )(lens, cos_t, sin_t, query, kv0, kv1, d_mixed)
-
-
-def flip(index, bit):
-    return index + bit - 2 * bit * ((index // bit) % 2)
-
-
-def neighbours():
-    me = lax.axis_index("tp")
-    return me, flip(me, 1), flip(me, 2), flip(me, 4)
-
-
-def enter(peers):
-    barrier = pltpu.get_barrier_semaphore()
-    for peer in peers:
-        pl.semaphore_signal(barrier, inc=1, device_id={"tp": peer}, device_id_type=pl.DeviceIdType.MESH)
-    pl.semaphore_wait(barrier, len(peers))
+    )(lens, cos_t, sin_t, query, kv_all, d_mixed)
 
 
 def gated_tile(z, g, w_g, w_u, w_d):
@@ -222,10 +389,6 @@
     own = (z_own, g_own)
     full = (z_all, g_all)
 
-    def remote(src, dst, sems, peer):
-        return pltpu.make_async_remote_copy(src_ref=src, dst_ref=dst, send_sem=sems[0], recv_sem=sems[1],
-                                            device_id={"tp": peer}, device_id_type=pl.DeviceIdType.MESH)
-
     def part(slot, q):
         return pl.ds(pl.multiple_of(slot * rows + q * piece, 16), piece)
 
@@ -243,16 +406,16 @@
         if turn == 1:
             slot = back if path == 0 else side
             q = (2 if path == 0 else 0) + u % 2
-            return remote(full[a].at[part(slot, q)], full[a].at[part(slot, q)], sems, peer)
+            return remote(full[a].at[part(slot, q)], full[a].at[part(slot, q)], *sems, peer)
         q = u % 2 + (2 * (turn // 2) if path == 0 else 2 - 2 * (turn // 2))
-        return remote(own[a].at[pl.ds(q * piece, piece)], full[a].at[part(me, q)], sems, peer)
+        return remote(own[a].at[pl.ds(q * piece, piece)], full[a].at[part(me, q)], *sems, peer)
 
     def core_copy(u, path, a):
         slot, q = link_rows(u, path)
-        return remote(full[a].at[part(slot, q)], full[a].at[part(slot, q)], (send.at[2 + path, u, a], recv.at[2 + path, u, a]), core)
+        return remote(full[a].at[part(slot, q)], full[a].at[part(slot, q)], send.at[2 + path, u, a], recv.at[2 + path, u, a], core)
 
     def own_copy(a):
-        return remote(own[a], full[a].at[pl.ds(pl.multiple_of(me * rows, 16), rows)], (send0.at[a], recv0.at[a]), core)
+        return remote(own[a], full[a].at[pl.ds(pl.multiple_of(me * rows, 16), rows)], send0.at[a], recv0.at[a], core)
 
     def weight_copies(n):
         cols = pl.ds(pl.multiple_of(n * bn, 128), bn)
@@ -408,10 +571,6 @@
     steps = dim // bn
     half = rows // 2
     me, core, side, back = neighbours()
-
-    def remote(src, dst, send, recv, peer):
-        return pltpu.make_async_remote_copy(src_ref=src, dst_ref=dst, send_sem=send, recv_sem=recv,
-                                            device_id={"tp": peer}, device_id_type=pl.DeviceIdType.MESH)
 
     def cols(j):
         return pl.ds(pl.multiple_of(j * bn, 128), bn)
@@ -612,10 +771,6 @@
     )(a, b)
 
 
-def pick(x, index):
-    return lax.dynamic_index_in_dim(x, index, axis=0, keepdims=False)
-
-
 def hop_diagonal(diag):
     half = diag.shape[0] // 2
     return swap(diag[:half], 2), swap(diag[half:], 4)
@@ -642,30 +797,23 @@
         me = lax.axis_index("tp")
         starts = (me ^ jnp.array([0, 2, 4, 6, 1, 3, 5, 7], jnp.int32)) * shard
         k_pos = (starts[:, None] + jnp.arange(shard, dtype=jnp.int32)).reshape(1, tp_size * shard)
-        lens = jnp.concatenate([jnp.stack([prefix_len, valid_len, jnp.full((batch,), me, jnp.int32)]),
-                                jnp.broadcast_to(starts[:, None], (tp_size, batch))])
+        lens = jnp.stack([prefix_len, valid_len])
         cos_own, sin_own = rope_tables(me * shard + jnp.arange(shard), head_dim)
-        cos_t, sin_t = jnp.tile(cos_own, (batch, 1)), jnp.tile(sin_own, (batch, 1))
-
-        def rope(raw_proj):
-            return apply_rope(raw_proj, cos_t, sin_t).astype(BF16)
-
-        wq_all = lax.all_gather(w_query, "tp", axis=0)
         hidden = hidden.reshape(rows, dim)
         grad_out = grad_out.reshape(rows, dim)
-        normed, norm1_pull = jax.vjp(rms_norm, hidden, attn_norm.astype(F32))
-        keys, key_pull = jax.vjp(rope, dot_nn(normed, w_key))
-        values = dot_nn(normed, w_value).astype(BF16)
-        kv0, kv1 = gather_near(jnp.concatenate([keys, values], axis=1))
-        wo_all = lax.all_gather(w_out, "tp", axis=0, tiled=True)
-        q_raw = jnp.einsum("td,hde->hte", normed, wq_all, preferred_element_type=F32)
-        query = rope(q_raw)
-        mixed = attention_forward(lens, k_pos, query, kv0, kv1, batch)
-        attn_out = dot_nn(mixed, wo_all)
-        resid = (hidden.astype(F32) + attn_out).astype(BF16)
-        gated_in, norm2_pull = jax.vjp(rms_norm, resid, mlp_norm.astype(F32))
+        normed, wq_all, wo_all, kv_all, query, mixed, resid, gated_in = front_layer(
+            lens, k_pos, cos_own, sin_own, attn_norm, mlp_norm, hidden, w_query, w_key, w_value, w_out, batch, tp_size)
+        wo_all = wo_all.reshape(tp_size * head_dim, dim)
+
+        def rope(raw_proj):
+            return apply_rope(raw_proj, jnp.tile(cos_own, (batch, 1)), jnp.tile(sin_own, (batch, 1)))
+
         gated_all, grad_all, act, d_gate, d_upper = gated_layer(gated_in, grad_out, w_gate, w_up, w_down, tp_size)
         own_part, x_part, y_part = back_layer(act, d_gate, d_upper, w_gate, w_up, w_down, tp_size)
+        hidden, resid, own_part = lax.optimization_barrier((hidden, resid, own_part))
+        norm1_pull = jax.vjp(rms_norm, hidden, attn_norm.astype(F32))[1]
+        norm2_pull = jax.vjp(rms_norm, resid, mlp_norm.astype(F32))[1]
+        key_pull = jax.linear_transpose(rope, jax.ShapeDtypeStruct((rows, head_dim), F32))
         mlp_sum, d_gated = [own_part[k] + x_part[k].astype(F32) + y_part[k].astype(F32) for k in range(2)]
         d_gated = d_gated.astype(BF16)
         hidden_out = (resid.astype(F32) + mlp_sum).astype(BF16)
@@ -673,30 +821,28 @@
         d_resid = (grad_out.astype(F32) + d_resid_norm.astype(F32)).astype(BF16)
         g_out_part = dot_tn(mixed, d_resid)
         d_mixed = dot_nt(d_resid, wo_all).astype(BF16)
+        lens_back = jnp.concatenate([lens, jnp.full((1, batch), me, jnp.int32), jnp.broadcast_to(starts[:, None], (tp_size, batch))])
         d_mixed, g_out_part = lax.optimization_barrier((d_mixed, g_out_part))
         g_out = lax.psum_scatter(g_out_part, "tp", scatter_dimension=0, tiled=True)
-        d_q_raw, dkv_near, dkv_far = attention_backward(lens, cos_own, sin_own, query, kv0, kv1, d_mixed, batch)
+        d_q_raw, dkv_near, dkv_far = attention_backward(lens_back, cos_own, sin_own, query, kv_all, d_mixed, batch)
         came_kv = swap(dkv_far, 1)
-        plane = me // 2
-        by_core = d_q_raw.reshape(tp_size // 2, 2, rows, head_dim)
-        theirs = lax.dynamic_index_in_dim(by_core, 1 - me % 2, axis=1, keepdims=False)
-        mine = lax.dynamic_index_in_dim(by_core, me % 2, axis=1, keepdims=False)
-        came_q = swap(jnp.einsum("td,kte->kde", normed, theirs, preferred_element_type=F32), 1)
+        near = tp_size // 2
+        came_q = swap(jnp.einsum("td,kte->kde", normed, d_q_raw[near:], preferred_element_type=F32), 1)
         d_normed_q = jnp.einsum("hte,hde->td", d_q_raw, wq_all, preferred_element_type=F32)
         came_kv, d_normed_q = lax.optimization_barrier((came_kv, d_normed_q))
         kv_own, kv_side, kv_back, kv_diag = [dkv_near[k].astype(F32) + came_kv[k].astype(F32) for k in range(4)]
         kv_came = hop_diagonal(kv_diag.astype(BF16))
-        g_query_sum = jnp.einsum("td,kte->kde", normed, mine, preferred_element_type=F32) + came_q
+        g_query_sum = jnp.einsum("td,kte->kde", normed, d_q_raw[:near], preferred_element_type=F32) + came_q
         kv_came, g_query_sum, d_gate = lax.optimization_barrier((kv_came, g_query_sum, d_gate))
         kv_next = hop_near(kv_side, kv_back, *kv_came)
         kv_last = (swap(kv_next[0], 2), swap(kv_next[1], 4))
-        q_came = hop_diagonal(pick(g_query_sum, plane ^ 3))
+        q_came = hop_diagonal(g_query_sum[3])
         g_gate = weight_grad(gated_all, d_gate)
         kv_last, q_came, g_gate = lax.optimization_barrier((kv_last, q_came, g_gate))
         d_kv = (kv_own + kv_last[0].astype(F32) + kv_last[1].astype(F32)).astype(BF16)
-        d_k_raw = key_pull(d_kv[:, :head_dim])[0].astype(BF16)
+        d_k_raw = key_pull(d_kv[:, :head_dim].astype(F32))[0].astype(BF16)
         d_values = d_kv[:, head_dim:]
-        q_next = hop_near(pick(g_query_sum, plane ^ 1), pick(g_query_sum, plane ^ 2), *q_came)
+        q_next = hop_near(g_query_sum[1], g_query_sum[2], *q_came)
         g_key_part, g_value_part = dot_tn(normed, d_k_raw), dot_tn(normed, d_values)
         q_next, g_key_part, g_value_part, d_upper = lax.optimization_barrier((q_next, g_key_part, g_value_part, d_upper))
         g_key, g_value = lax.psum((g_key_part, g_value_part), "tp")
@@ -704,7 +850,7 @@
         g_up = weight_grad(gated_all, d_upper)
         d_normed = (d_normed_q + dot_nt(d_k_raw, w_key) + dot_nt(d_values, w_value)).astype(BF16)
         q_last, g_up, d_normed, act = lax.optimization_barrier((q_last, g_up, d_normed, act))
-        g_query = pick(g_query_sum, plane) + q_last[0] + q_last[1]
+        g_query = g_query_sum[0] + q_last[0] + q_last[1]
         d_hidden_norm, g_attn_norm_part = norm1_pull(d_normed)
         norms = jnp.stack([g_attn_norm_part, g_mlp_norm_part])
         norms_near = [swap(norms, bit) for bit in (2, 4, 6)]

time: 910 us -> 892 us (0.980)
  Pallas kernels: 575 us -> 654 us
  waiting for transfers between devices: 157 us -> 91.3 us
  matrix products: 71.5 us -> 46.7 us
    pallas_call x1, Pallas kernels: 23.5 us -> 104 us  [front_layer(): pl.pallas_call(functools.partial(front_kernel, batch=batch), out_shape=(s...]
    all_gather x2 -> x0, waiting for transfers between devices: 32.7 us -> none  [the longest x1 18.2 us: layer(): wo_all = lax.all_gather(w_out, 'tp', axis=0, tiled=True)]
    ppermute x19 -> x14, waiting for transfers between devices: 57.8 us -> 27.9 us  [swap(): return lax.ppermute(x, 'tp', [(t, t ^ bit) for t in range(8)])]
    dot_general x6 -> x2, matrix products: 31.3 us -> 10.7 us  [the longest x1 7.13 us: layer(): jnp.einsum('td,kte->kde', normed, d_q_raw[near:], preferred_element_type=...]
    ppermute x19 -> x14, starting transfers between devices: 20.9 us -> 12.5 us  [swap(): return lax.ppermute(x, 'tp', [(t, t ^ bit) for t in range(8)])]
  transfers between devices with their start and end apart: 23 -> 16, of which waited for: 11 -> 6; matrix products, arithmetic and copies ran while one was open for 7% -> 4% of each run, Pallas kernels for 20% -> 18%
where the time goes in v5:
time: 892 us; the launch traced here: 883 us
  Pallas kernels  654 us (73%)
  waiting for transfers between devices  91.3 us (10%)
  matrix products  46.7 us (5%)
  other arithmetic  44.3 us (5%)
  local copies, waits for them, and re-layouts  19.8 us (2%)
  between operations  14.9 us (2%)
  starting transfers between devices  12.6 us (1%)
    pallas_call x1, Pallas kernels, gated_layer(): pl.pallas_call(functools.partial(gated_kernel, bn=bn), out_shape=(gathere...  185 us
    pallas_call x1, Pallas kernels, back_layer(): pl.pallas_call(functools.partial(back_kernel, rows=rows, bn=bn), out_shap...  174 us
    pallas_call x3, Pallas kernels, weight_grad(): pl.pallas_call(product_kernel, out_shape=jax.ShapeDtypeStruct((m, n), F32...  156 us
    pallas_call x1, Pallas kernels, front_layer(): pl.pallas_call(functools.partial(front_kernel, batch=batch), out_shape=(s...  104 us
    reduce_scatter x1, waiting for transfers between devices, layer(): g_out = lax.psum_scatter(g_out_part, 'tp', scatter_dimension=0, tiled=True)  62.7 us
    pallas_call x1, Pallas kernels, attention_backward(): pl.pallas_call(attn_bwd_kernel, out_shape=(jax.ShapeDtypeStruct((heads, r...  34.4 us
    ppermute x14, waiting for transfers between devices, swap(): return lax.ppermute(x, 'tp', [(t, t ^ bit) for t in range(8)])  27.9 us
  transfers between devices with their start and end apart: 16, of which 6 were waited for; matrix products, arithmetic and copies ran while one was open for 4% of the time, Pallas kernels for 18%

profile of v5, /device:TPU:0, one launch (start us, length us, event | category | flops | bytes accessed | tf_op | source)
XLA Modules:
  0.0 883.1 jit_solution(9398877896771702343)
XLA Ops:
  16.0 104.2 %front.1 = (bf16[576,2048]{1,0:T(8,128)(2,1)}, bf16[8,2048,256]{2,1,0:T(8,128)(2,1)}, bf16[8,256,2048]{2,1,0:T(8,128)(2,1)}, bf16[8,576,512]{2,1,0:T(8,128)(2,1)...) custom-call(s32[2,3]{1,0:T(2,128)} %pad_add_fusion.lens_ref, ...), custom_call_target="tpu_custom_call" | custom-call | flops 19327352832 | bytes 62914560 | tf_op jit(solution)/shard_map/front/pallas_call | solution.py:329
  120.3 184.8 %gated.1 = (bf16[4608,2048]{1,0:T(8,128)(2,1)}, bf16[4608,2048]{1,0:T(8,128)(2,1)}, bf16[4608,2048]{1,0:T(8,128)(2,1)}, bf16[4608,2048]{1,0:T(8,128)(2,1)}, bf16[4608,2048]{1,0:T(8,128)(2,1)}) custom-call(bf16[576,2048]{1,0:T(8,128)(2,1)} %get-tuple-element.62.z_own, bf16[576,2048]{1,0:T(8,128)(2,1)} %bitcast.103, bf16[2048,2048]{1,0:T(8,128)(2,1)} %wg_hbm.3, ...), custom_call_target="tpu_custom_call" | custom-call | flops 115964116992 | bytes 209715200 | tf_op jit(solution)/shard_map/gated/pallas_call | solution.py:554
  305.1 174.3 %back.1 = (f32[2,576,2048]{2,1,0:T(8,128)}, bf16[2,576,2048]{2,1,0:T(8,128)(2,1)}, bf16[2,576,2048]{2,1,0:T(8,128)(2,1)}) custom-call(bf16[4608,2048]{1,0:T(8,128)(2,1)} %get-tuple-element.97.act.a_ref, bf16[4608,2048]{1,0:T(8,128)(2,1)} %get-tuple-element.87.d_gate.b_ref, bf16[4608,2048]{1,0:T(8,128)(2,1)} %get-tuple-element.94.d_up.b_ref, ...), custom_call_target="tpu_custom_call" | custom-call | flops 115964116992 | bytes 209715200 | tf_op jit(solution)/shard_map/back/pallas_call | solution.py:739
  481.8 10.4 %fusion.10 = (f32[576]{0:T(1024)S(1)}, f32[2048]{0:T(1024)}, bf16[576,2048]{1,0:T(8,128)(2,1)S(1)}, bf16[576,2048]{1,0:T(8,128)(2,1)}) fusion(bf16[576,2048]{1,0:T(8,128)(2,1)S(1)} %copy-done.2, f32[2048]{0:T(1024)S(1)} %copy-done.21, f32[576]{0:T(1024)S(1)} %fusion.33, bf16[2,576,2048]{2,1,0:T(8,128)(2,1)} %get-tuple-element.70, ...), kind=kLoop, calls=%fused_computation.26 | loop fusion | flops 22410688 | bytes 25973248 | tf_op jit(solution)/shard_map/transpose(jvp())/reduce_sum | solution.py:23
  496.4 6.3 convolution_convert_fusion.do_ref
  502.8 10.4 %fusion.39 = f32[2048,2048]{1,0:T(8,128)} fusion(bf16[576,2048]{1,0:T(8,128)(2,1)S(1)} %copy-done.30, bf16[576,2048]{1,0:T(8,128)(2,1)S(1)} %add_convert_fusion.2), kind=kOutput, calls=%fused_computation.102 | convolution fusion | flops 4831838208 | bytes 21495808 | tf_op jit(solution)/shard_map/dot_general | solution.py:50
  513.8 34.4 %attn_bwd.1 = (bf16[8,576,256]{2,1,0:T(8,128)(2,1)}, bf16[4,576,512]{2,1,0:T(8,128)(2,1)}, bf16[4,576,512]{2,1,0:T(8,128)(2,1)}) custom-call(s32[11,3]{1,0:T(8,128)} %add_add_fusion.3.lens_ref, f32[192,128]{1,0:T(8,128)} %get-tuple-element.168.cos_ref, f32[192,128]{1,0:T(8,128)} %get-tuple-element.167.sin_ref, bf16[8,576,256]{2,1,0:T(8,128)(2,1)} %get-tuple-element.72.q_ref, ...), custom_call_target="tpu_custom_call" | custom-call | flops 18119393280 | bytes 20971520 | tf_op jit(solution)/shard_map/attn_bwd/pallas_call | solution.py:355
  548.3 7.1 convolution_bitcast_fusion
  555.9 10.4 %convolution_bitcast_fusion.1 = f32[576,2048]{1,0:T(8,128)} fusion(bf16[8,576,256]{2,1,0:T(8,128)(2,1)S(1)} %copy-done.17, bf16[8,2048,256]{2,1,0:T(8,128)(2,1)} %get-tuple-element.80), kind=kOutput, calls=%fused_computation.32 | convolution fusion | flops 4831838208 | bytes 15466496 | tf_op jit(solution)/shard_map/hte,hde->td/dot_general | solution.py:831
  566.3 5.8 collective-permute-done
  576.1 3.5 bitcast_add_fusion
  579.7 3.6 collective-permute-done.2
  592.5 49.4 %weight_grad.3 = f32[2048,2048]{1,0:T(8,128)} custom-call(bf16[4608,2048]{1,0:T(8,128)(2,1)} %get-tuple-element.86.a_ref, bf16[4608,2048]{1,0:T(8,128)(2,1)} %get-tuple-element.87.d_gate.b_ref), custom_call_target="tpu_custom_call" | custom-call | flops 38654705664 | bytes 115343360 | tf_op jit(solution)/shard_map/weight_grad/pallas_call | solution.py:762
  647.3 2.7 bitcast_add_fusion.3
  652.4 3.6 pad_maximum_fusion
  661.2 3.4 add_convert_fusion.1
  664.6 50.9 %weight_grad.4 = f32[2048,2048]{1,0:T(8,128)} custom-call(bf16[4608,2048]{1,0:T(8,128)(2,1)} %get-tuple-element.86.a_ref, bf16[4608,2048]{1,0:T(8,128)(2,1)} %get-tuple-element.94.d_up.b_ref), custom_call_target="tpu_custom_call" | custom-call | flops 38654705664 | bytes 115343360 | tf_op jit(solution)/shard_map/weight_grad/pallas_call | solution.py:762
  715.5 16.6 %collective-permute-done.8 = f32[2048,256]{0,1:T(8,128)} collective-permute-done((f32[2048,256]{0,1:T(8,128)}, f32[2048,256]{0,1:T(8,128)}, u32[]{:S(2)}, u32[]{:S(2)}) %collective-permute-start.8) | collective-permute-done | bytes 2097184 | tf_op jit(solution)/shard_map/ppermute | solution.py:54
  737.8 5.1 fusion.14
  742.9 55.5 %weight_grad.5 = f32[2048,2048]{1,0:T(8,128)} custom-call(bf16[4608,2048]{1,0:T(8,128)(2,1)} %get-tuple-element.97.act.a_ref, bf16[4608,2048]{1,0:T(8,128)(2,1)} %get-tuple-element.98.b_ref), custom_call_target="tpu_custom_call" | custom-call | flops 38654705664 | bytes 115343360 | tf_op jit(solution)/shard_map/weight_grad/pallas_call | solution.py:762
  801.0 3.0 copy.30
  804.1 4.0 add_convert_fusion
  808.7 62.7 %reduce-scatter.2.cloned.1.call-done = f32[256,2048]{1,0:T(8,128)} async-done(((f32[2048,2048]{1,0:T(8,128)}), f32[256,2048]{1,0:T(8,128)}) %reduce-scatter.2.cloned.1.call-update) | async-done | bytes 2097168 | tf_op jit(solution)/shard_map/reduce_scatter | solution.py:826
  871.4 3.0 copy.33
  (135 shorter events, 52.9 us)
Async XLA Ops:
  7.2 801.5 %all-reduce.5.cloned.1.call-start = ((), (), s32[]{:S(2)}) async-start(), calls=%async_computation.2 | async-start | bytes 8388608 | tf_op jit(solution)/shard_map/psum | solution.py:848
  481.7 10.4 %copy-start.10 = (bf16[3,192,2048]{2,1,0:T(8,128)(2,1)S(1)}, bf16[3,192,2048]{2,1,0:T(8,128)(2,1)}, u32[]{:S(2)}) copy-start(bf16[3,192,2048]{2,1,0:T(8,128)(2,1)} %param.15) | copy-start | bytes 7077892
  502.7 10.4 %copy-start.24 = (s32[3]{0:T(128)S(1)}, s32[3]{0:T(128)}, u32[]{:S(2)}) copy-start(s32[3]{0:T(128)} %param.17) | copy-start | bytes 40
  502.7 10.4 %copy-start.25 = (s32[3]{0:T(128)S(1)}, s32[3]{0:T(128)}, u32[]{:S(2)}) copy-start(s32[3]{0:T(128)} %param.16) | copy-start | bytes 40
  513.8 34.4 %copy-start.5 = (bf16[576,2048]{1,0:T(8,128)(2,1)S(1)}, bf16[576,2048]{1,0:T(8,128)(2,1)}, u32[]{:S(2)}) copy-start(bf16[576,2048]{1,0:T(8,128)(2,1)} %get-tuple-element.82) | copy-start | bytes 7077892
  555.4 20.7 %collective-permute-start.3 = (f32[4,2048,256]{1,2,0:T(8,128)}, f32[4,2048,256]{1,2,0:T(8,128)S(1)}, u32[]{:S(2)}, u32[]{:S(2)}) collective-permute-start(f32[4,2048,256]{1,2,0:T(8,128)} %convolution_bitcast_fusion), channel_id=1, source_target_pairs={{0,1},{1,0},{2,3},{3,2},{4,5},{5,4},{6,7},{7,6},{8,9},{9,8},{10,11... | collective-permute-start | bytes 25165832 | tf_op jit(solution)/shard_map/ppermute | solution.py:54
  555.4 16.7 %collective-permute-start = (bf16[4,576,512]{2,1,0:T(8,128)(2,1)S(1)}, bf16[4,576,512]{2,1,0:T(8,128)(2,1)S(1)}, u32[]{:S(2)}, u32[]{:S(2)}) collective-permute-start(bf16[4,576,512]{2,1,0:T(8,128)(2,1)S(1)} %copy-done.28), channel_id=1, source_target_pairs={{0,1},{1,0},{2,3},{3,2},{4,5},{5,4},{6,7},{7,6},{8,9},{9,8},{10,11... | collective-permute-start | bytes 7077896 | tf_op jit(solution)/shard_map/ppermute | solution.py:54
  555.9 16.2 %copy-start.8 = (bf16[4,576,512]{2,1,0:T(8,128)(2,1)S(1)}, bf16[4,576,512]{2,1,0:T(8,128)(2,1)}, u32[]{:S(2)}) copy-start(bf16[4,576,512]{2,1,0:T(8,128)(2,1)} %get-tuple-element.77) | copy-start | bytes 7077892
  573.6 9.7 %collective-permute-start.2 = (bf16[288,512]{1,0:T(8,128)(2,1)S(1)}, bf16[288,512]{1,0:T(8,128)(2,1)S(1)}, u32[]{:S(2)}, u32[]{:S(2)}) collective-permute-start(bf16[288,512]{1,0:T(8,128)(2,1)S(1)} %get-tuple-element.163), channel_id=1, source_target_pairs={{0,4},{1,5},{2,6},{3,7},{4,0},{5,1},{6,2},{7,3},{8,12},{9,13},{10,... | collective-permute-start | bytes 884744 | tf_op jit(solution)/shard_map/ppermute | solution.py:54
  576.0 8.8 collective-permute-start.1
  579.7 10.7 %copy-start = (f32[4,2048,256]{1,2,0:T(8,128)}, f32[4,2048,256]{1,2,0:T(8,128)S(1)}, u32[]{:S(2)}) copy-start(f32[4,2048,256]{1,2,0:T(8,128)S(1)} %bitcast_add_fusion) | copy-start | bytes 25165828
  585.8 56.0 %collective-permute-start.5 = (bf16[576,512]{1,0:T(8,128)(2,1)}, bf16[576,512]{1,0:T(8,128)(2,1)}, u32[]{:S(2)}, u32[]{:S(2)}) collective-permute-start(bf16[576,512]{1,0:T(8,128)(2,1)} %pad_maximum_fusion.3), channel_id=1, source_target_pairs={{0,4},{1,5},{2,6},{3,7},{4,0},{5,1},{6,2},{7,3},{8,12},{9,13},{10,... | collective-permute-start | bytes 1769480 | tf_op jit(solution)/shard_map/ppermute | solution.py:54
  587.0 54.8 %collective-permute-start.4 = (bf16[576,512]{1,0:T(8,128)(2,1)}, bf16[576,512]{1,0:T(8,128)(2,1)S(1)}, u32[]{:S(2)}, u32[]{:S(2)}) collective-permute-start(bf16[576,512]{1,0:T(8,128)(2,1)} %pad_maximum_fusion.2), channel_id=1, source_target_pairs={{0,2},{1,3},{2,0},{3,1},{4,6},{5,7},{6,4},{7,5},{8,10},{9,11},{10,... | collective-permute-start | bytes 1769480 | tf_op jit(solution)/shard_map/ppermute | solution.py:54
  590.4 51.5 %collective-permute-start.7 = (f32[1024,256]{0,1:T(8,128)}, f32[1024,256]{0,1:T(8,128)S(1)}, u32[]{:S(2)}, u32[]{:S(2)}) collective-permute-start(f32[1024,256]{0,1:T(8,128)} %get-tuple-element.155), channel_id=1, source_target_pairs={{0,4},{1,5},{2,6},{3,7},{4,0},{5,1},{6,2},{7,3},{8,12},{9,13},{10,... | collective-permute-start | bytes 3145736 | tf_op jit(solution)/shard_map/ppermute | solution.py:54
  590.7 52.0 %collective-permute-start.6 = (f32[1024,256]{0,1:T(8,128)}, f32[1024,256]{0,1:T(8,128)}, u32[]{:S(2)}, u32[]{:S(2)}) collective-permute-start(f32[1024,256]{0,1:T(8,128)} %get-tuple-element.156), channel_id=1, source_target_pairs={{0,2},{1,3},{2,0},{3,1},{4,6},{5,7},{6,4},{7,5},{8,10},{9,11},{10,... | collective-permute-start | bytes 3145736 | tf_op jit(solution)/shard_map/ppermute | solution.py:54
  656.0 215.4 %reduce-scatter.2.cloned.1.call-start = ((), (), s32[]{:S(2)}) async-start(), calls=%async_computation.1 | async-start | bytes 18874368 | tf_op jit(solution)/shard_map/reduce_scatter | solution.py:826
  658.3 73.8 %collective-permute-start.8 = (f32[2048,256]{0,1:T(8,128)}, f32[2048,256]{0,1:T(8,128)}, u32[]{:S(2)}, u32[]{:S(2)}) collective-permute-start(f32[2048,256]{0,1:T(8,128)} %get-tuple-element.92), channel_id=1, source_target_pairs={{0,2},{1,3},{2,0},{3,1},{4,6},{5,7},{6,4},{7,5},{8,10},{9,11},{10,... | collective-permute-start | bytes 6291464 | tf_op jit(solution)/shard_map/ppermute | solution.py:54
  658.6 73.8 %collective-permute-start.9 = (f32[2048,256]{0,1:T(8,128)}, f32[2048,256]{0,1:T(8,128)}, u32[]{:S(2)}, u32[]{:S(2)}) collective-permute-start(f32[2048,256]{0,1:T(8,128)} %get-tuple-element.93), channel_id=1, source_target_pairs={{0,4},{1,5},{2,6},{3,7},{4,0},{5,1},{6,2},{7,3},{8,12},{9,13},{10,... | collective-permute-start | bytes 6291464 | tf_op jit(solution)/shard_map/ppermute | solution.py:54
  715.5 18.7 %copy-start.22 = (f32[2048]{0:T(1024)S(1)}, f32[2048]{0:T(1024)}, u32[]{:S(2)}) copy-start(f32[2048]{0:T(1024)} %get-tuple-element.147) | copy-start | bytes 24580
  734.2 69.8 %collective-permute-start.12 = (f32[2,2048]{1,0:T(2,128)S(1)}, f32[2,2048]{1,0:T(2,128)S(1)}, u32[]{:S(2)}, u32[]{:S(2)}) collective-permute-start(f32[2,2048]{1,0:T(2,128)S(1)} %pad_maximum_fusion.4), channel_id=1, source_target_pairs={{0,6},{1,7},{2,4},{3,5},{4,2},{5,3},{6,0},{7,1},{8,14},{9,15},{10,... | collective-permute-start | bytes 49160 | tf_op jit(solution)/shard_map/ppermute | solution.py:54
  735.9 68.1 %collective-permute-start.11 = (f32[2,2048]{1,0:T(2,128)S(1)}, f32[2,2048]{1,0:T(2,128)S(1)}, u32[]{:S(2)}, u32[]{:S(2)}) collective-permute-start(f32[2,2048]{1,0:T(2,128)S(1)} %pad_maximum_fusion.4), channel_id=1, source_target_pairs={{0,4},{1,5},{2,6},{3,7},{4,0},{5,1},{6,2},{7,3},{8,12},{9,13},{10,... | collective-permute-start | bytes 49160 | tf_op jit(solution)/shard_map/ppermute | solution.py:54
  737.2 66.8 %collective-permute-start.10 = (f32[2,2048]{1,0:T(2,128)S(1)}, f32[2,2048]{1,0:T(2,128)S(1)}, u32[]{:S(2)}, u32[]{:S(2)}) collective-permute-start(f32[2,2048]{1,0:T(2,128)S(1)} %pad_maximum_fusion.4), channel_id=1, source_target_pairs={{0,2},{1,3},{2,0},{3,1},{4,6},{5,7},{6,4},{7,5},{8,10},{9,11},{10,... | collective-permute-start | bytes 49160 | tf_op jit(solution)/shard_map/ppermute | solution.py:54
  804.0 4.0 collective-permute-start.13
  808.7 65.8 %copy-start.11 = (f32[2048,256]{1,0:T(8,128)S(1)}, f32[2048,256]{1,0:T(8,128)}, u32[]{:S(2)}) copy-start(f32[2048,256]{1,0:T(8,128)} %get-tuple-element.176) | copy-start | bytes 6291460
  (23 other events, 93.0 us)
Sparse Core Ops, SparseCore 0:
  656.1 100.3 all-reduce.4
  760.6 110.7 reduce-scatter.1

commit v6 on v5

--- a/solution.py
+++ b/solution.py
@@ -88,20 +88,27 @@
     k_pos = jnp.concatenate([step + lens_ref[3 + r, 0] for r in range(tp)], axis=0)
     q_pos = first + lax.rem(lax.broadcasted_iota(jnp.int32, (1, rows), 1), shard)
     limit = jnp.minimum(valid, jnp.maximum(prefix, q_pos + 1))
-    s = jnp.where(k_pos < limit, dot_nt(keys, query), MASKED)
-    e = jnp.exp(s - jnp.max(s, axis=0, keepdims=True))
-    p = e * (1.0 / jnp.sum(e, axis=0, keepdims=True))
-    d_p = dot_nt(values, d_out)
-    delta = jnp.sum(p * d_p, axis=0, keepdims=True)
-    d_s = (p * (d_p - delta)).astype(BF16)
-    d_v = dot_nn(p.astype(BF16), d_out)
-    d_k = dot_nn(d_s, query)
-    d_q = (dot_tn(d_s, keys) * (head_dim ** -0.5)).reshape(heads, shard, head_dim)
-    first, second = d_q[:, :, :head_dim // 2], d_q[:, :, head_dim // 2:]
     cos_t, sin_t = cos_ref[...][None], sin_ref[...][None]
-    dq_ref[:, :, :head_dim // 2] = (first * cos_t + second * sin_t).astype(BF16)
-    dq_ref[:, :, head_dim // 2:] = (second * cos_t - first * sin_t).astype(BF16)
-
+    d_k = d_v = None
+    count = heads // 2
+    width = count * shard
+    for c in range(2):
+        cols = slice(c * width, (c + 1) * width)
+        q_c, do_c = query[cols], d_out[cols]
+        s = jnp.where(k_pos < limit[:, cols], dot_nt(keys, q_c), MASKED)
+        e = jnp.exp(s - jnp.max(s, axis=0, keepdims=True))
+        p = e * (1.0 / jnp.sum(e, axis=0, keepdims=True))
+        d_p = dot_nt(values, do_c)
+        delta = jnp.sum(p * d_p, axis=0, keepdims=True)
+        d_s = (p * (d_p - delta)).astype(BF16)
+        d_v_c = dot_nn(p.astype(BF16), do_c)
+        d_k_c = dot_nn(d_s, q_c)
+        d_k, d_v = (d_k_c, d_v_c) if d_k is None else (d_k + d_k_c, d_v + d_v_c)
+        d_q = (dot_tn(d_s, keys) * (head_dim ** -0.5)).reshape(count, shard, head_dim)
+        first, second = d_q[:, :, :head_dim // 2], d_q[:, :, head_dim // 2:]
+        some = slice(c * count, (c + 1) * count)
+        dq_ref[some, :, :head_dim // 2] = (first * cos_t + second * sin_t).astype(BF16)
+        dq_ref[some, :, head_dim // 2:] = (second * cos_t - first * sin_t).astype(BF16)
     d_kv = jnp.concatenate([d_k, d_v], axis=1)
 
     @pl.when(g_id == 0)
@@ -250,25 +257,25 @@
 
     q_pos = me * shard + lax.broadcasted_iota(jnp.int32, (shard, 1), 0)
 
-    def attend(step, carry):
-        i, g = step // 2, step % 2
+    def attend(i, carry):
         keys = kv[:, seq_rows(i), :head_dim].reshape(total, head_dim)
         values = kv[:, seq_rows(i), head_dim:].reshape(total, head_dim)
-        query = q[pl.ds(g * near, near), seq_rows(i), :].reshape(near * shard, head_dim) * BF16(head_dim ** -0.5)
         visible = kpos_ref[...] < jnp.minimum(lens_ref[1, i], jnp.maximum(lens_ref[0, i], q_pos + 1))
-        scores = dot_nt(query, keys)
-        for h in range(near):
-            part = slice(h * shard, (h + 1) * shard)
-            s = jnp.where(visible, scores[part], MASKED)
-            e = jnp.exp(s - jnp.max(s, axis=-1, keepdims=True))
-            probs[part, :] = (e * (1.0 / jnp.sum(e, axis=-1, keepdims=True))).astype(BF16)
-        mixed = dot_nn(probs[...], values).astype(BF16)
-        for h in range(near):
-            cols = pl.ds(pl.multiple_of((g * near + h) * head_dim, 128), head_dim)
-            mix[seq_rows(i), cols] = mixed[h * shard:(h + 1) * shard]
+        for g in range(2):
+            query = q[g * near:(g + 1) * near, seq_rows(i), :].reshape(near * shard, head_dim) * BF16(head_dim ** -0.5)
+            scores = dot_nt(query, keys)
+            for h in range(near):
+                part = slice(h * shard, (h + 1) * shard)
+                s = jnp.where(visible, scores[part], MASKED)
+                e = jnp.exp(s - jnp.max(s, axis=-1, keepdims=True))
+                probs[g, part, :] = (e * (1.0 / jnp.sum(e, axis=-1, keepdims=True))).astype(BF16)
+            mixed = dot_nn(probs[g], values).astype(BF16)
+            for h in range(near):
+                head = g * near + h
+                mix[seq_rows(i), head * head_dim:(head + 1) * head_dim] = mixed[h * shard:(h + 1) * shard]
         return carry
 
-    lax.fori_loop(0, 2 * batch, attend, 0)
+    lax.fori_loop(0, batch, attend, 0)
     for cp in mixed_stores:
         cp.start()
     pass_on(2)
@@ -335,7 +342,7 @@
         scratch_shapes=[pltpu.VMEM((rows, dim), BF16), pltpu.VMEM((rows, dim), BF16), pltpu.VMEM((dim, 2 * head_dim), BF16),
                         pltpu.VMEM((tp, dim, head_dim), BF16), pltpu.VMEM((tp, head_dim, dim), BF16),
                         pltpu.VMEM((tp, rows, 2 * head_dim), BF16), pltpu.VMEM((tp, rows, head_dim), BF16),
-                        pltpu.VMEM((tp // 2 * shard, total), BF16), pltpu.VMEM((rows, tp * head_dim), BF16), pltpu.VMEM((rows, dim), F32),
+                        pltpu.VMEM((2, tp // 2 * shard, total), BF16), pltpu.VMEM((rows, tp * head_dim), BF16), pltpu.VMEM((rows, dim), F32),
                         dma((5,)), dma((15,)), dma((3, 8)), dma((3, 8))],
         compiler_params=pltpu.CompilerParams(vmem_limit_bytes=62 << 20, collective_id=2, has_side_effects=True),
         cost_estimate=pl.CostEstimate(flops=8 * rows * dim * tp * head_dim, bytes_accessed=60 << 20, transcendentals=tp * rows * total),
@@ -343,7 +350,7 @@
     )(lens, k_pos, cos_t, sin_t, attn_norm.reshape(1, dim), mlp_norm.reshape(1, dim), hidden, w_query, w_key, w_value, w_out)
 
 
-def attention_backward(lens, cos_t, sin_t, query, kv_all, d_mixed, batch, group=4):
+def attention_backward(lens, cos_t, sin_t, query, kv_all, d_mixed, batch, group=8):
     heads, rows, head_dim = query.shape
     near = kv_all.shape[0] // 2
     shard = rows // batch
@@ -378,9 +385,9 @@
     return (gelu * upper).astype(BF16), (d_act * upper * slope).astype(BF16), (d_act * gelu).astype(BF16)
 
 
-def gated_kernel(z_own, g_own, wg_hbm, wu_hbm, wd_hbm, z_all, g_all, act, d_gate, d_up,
-                 wg, wu, wd, z_buf, g_buf, outs, w_sem, in_sem, own_sem, out_sem, send, recv, send0, recv0, *, bn):
-    rows, _ = z_own.shape
+def gated_kernel(z_own, g_own, wg_hbm, wu_hbm, wd_hbm, z_all, g_all, act, d_gate, d_up, g_down,
+                 wg, wu, wd, z_buf, g_buf, outs, acc, acc_sem, w_sem, in_sem, own_sem, out_sem, send, recv, send0, recv0, *, bn):
+    rows, dim = z_own.shape
     width = wg_hbm.shape[1]
     steps = width // bn
     piece = rows // 4
@@ -445,6 +452,10 @@
         return [pltpu.make_async_copy(outs.at[slot, k, pl.ds(i * piece, piece)], ref.at[s_rows[i], cols], out_sem.at[slot, k, i])
                 for k, ref in enumerate((act, d_gate, d_up)) for i in range(4)]
 
+    def acc_copy(n):
+        part = pl.ds(pl.multiple_of(n * bn, 128), bn)
+        return pltpu.make_async_copy(acc.at[part], g_down.at[part], acc_sem.at[n])
+
     def stage_rows(s):
         late = (s + 6) // 8
         u = (s - 2) * late
@@ -478,6 +489,17 @@
                 outs[slot, k] = res[k]
             for cp in out_copies(slot, s_rows, n):
                 cp.start()
+
+            @pl.when(s >= 2)
+            def _():
+                for c in range(2):
+                    part = slice(c * (dim // 2), (c + 1) * (dim // 2))
+                    acc[cols, part] += dot_tn(outs[slot, 0], g_buf[:, part])
+
+                @pl.when(s == 7)
+                def _():
+                    acc_copy(n).start()
+
             return carry
 
         lax.fori_loop(0, steps, block, 0)
@@ -492,6 +514,7 @@
 
         @pl.when(s == 1)
         def _():
+            acc[...] = jnp.zeros_like(acc)
             for cp in own_out:
                 cp.wait()
             for a in range(2):
@@ -535,6 +558,8 @@
     for slot in range(2):
         for cp in out_copies(slot, last, 0):
             cp.wait()
+    for n in range(steps):
+        acc_copy(n).wait()
     for a in range(2):
         own_copy(a).wait_send()
         for path in range(2):
@@ -553,21 +578,21 @@
     dma = pltpu.SemaphoreType.DMA
     return pl.pallas_call(
         functools.partial(gated_kernel, bn=bn),
-        out_shape=(gathered, gathered, made, made, made),
+        out_shape=(gathered, gathered, made, made, made, jax.ShapeDtypeStruct((width, dim), F32)),
         in_specs=[anyspace] * 5,
-        out_specs=(anyspace,) * 5,
+        out_specs=(anyspace,) * 6,
         scratch_shapes=[pltpu.VMEM((dim, width), BF16), pltpu.VMEM((dim, width), BF16), pltpu.VMEM((width, dim), BF16),
                         pltpu.VMEM((rows, dim), BF16), pltpu.VMEM((rows, dim), BF16), pltpu.VMEM((2, 3, rows, bn), BF16),
-                        dma((3, width // bn)), dma((2, 4)), dma((4,)), dma((2, 3, 4)), dma((4, 6, 2)), dma((4, 6, 2)), dma((2,)), dma((2,))],
-        compiler_params=pltpu.CompilerParams(vmem_limit_bytes=60 << 20, collective_id=0, has_side_effects=True),
+                        pltpu.VMEM((width, dim), F32), dma((width // bn,)), dma((3, width // bn)), dma((2, 4)), dma((4,)), dma((2, 3, 4)), dma((4, 6, 2)), dma((4, 6, 2)), dma((2,)), dma((2,))],
+        compiler_params=pltpu.CompilerParams(vmem_limit_bytes=67043328, collective_id=0, has_side_effects=True),
         cost_estimate=pl.CostEstimate(flops=6 * total * dim * width, bytes_accessed=200 << 20, transcendentals=total * width),
         name="gated",
     )(z_own, g_own, w_gate, w_up, w_down)
 
 
-def back_kernel(act, d_gate, d_up, wg_hbm, wu_hbm, wd_hbm, own_out, x_in, y_in,
-                wa, wb, lhs, st, from_core, from_diag, own_st, w_sem, l_sem, o_sem, c_send, c_recv, d_send, d_recv, f_send, f_recv, *, rows, bn):
-    dim = wg_hbm.shape[0]
+def back_kernel(act, d_gate, d_up, z_all, wg_hbm, wu_hbm, wd_hbm, own_out, x_in, y_in, g_gate,
+                wa, wb, lhs, st, from_core, from_diag, own_st, z_sem, w_sem, l_sem, o_sem, c_send, c_recv, d_send, d_recv, f_send, f_recv, *, rows, bn):
+    dim, width = wg_hbm.shape
     steps = dim // bn
     half = rows // 2
     me, core, side, back = neighbours()
@@ -589,7 +614,7 @@
 
     def weight_copy(k, j):
         if k == 0:
-            return pltpu.make_async_copy(wd_hbm.at[:, cols(j)], wa.at[:, cols(j)], w_sem.at[0, j])
+            return pltpu.make_async_copy(wd_hbm.at[:, cols(j)], wa.at[pl.ds(0, width), cols(j)], w_sem.at[0, j])
         src, dst = (wg_hbm, wb) if k == 1 else (wu_hbm, wa)
         return pltpu.make_async_copy(src.at[cols(j)], dst.at[cols(j)], w_sem.at[k, j])
 
@@ -607,7 +632,7 @@
 
     def product(phase, slot, j):
         if phase == 0:
-            return dot_nn(lhs[slot, 0], wa[:, cols(j)])
+            return dot_nn(lhs[slot, 0], wa[:width, cols(j)])
         return dot_nt(lhs[slot, 0], wb[cols(j), :]) + dot_nt(lhs[slot, 1], wa[cols(j), :])
 
     for cp in lhs_copies(0, 0):
@@ -719,6 +744,44 @@
 
         lax.fori_loop(0, 8, step, 0)
 
+    def z_copy(j, c):
+        return pltpu.make_async_copy(z_all.at[pl.ds(c * rows, rows), cols(j)], lhs.at[c // 2, c % 2, :, cols(j)], z_sem.at[j, c])
+
+    def gate_copy(j):
+        return pltpu.make_async_copy(d_gate.at[pl.ds(0, 4 * rows), cols(j)], wa.at[:, cols(j)], w_sem.at[0, j])
+
+    def grad_copy(i, j):
+        slot = j % 2
+        return pltpu.make_async_copy(own_st.at[slot, pl.ds(0, bn)], g_gate.at[cols(i), cols(j)], o_sem.at[slot])
+
+    for j in range(steps):
+        for c in range(4):
+            z_copy(j, c).start()
+        gate_copy(j).start()
+
+    def grad_tile(step, carry):
+        i, j = step // steps, step % steps
+
+        @pl.when(i == 0)
+        def _():
+            gate_copy(j).wait()
+
+        @pl.when(j == 0)
+        def _():
+            for c in range(4):
+                z_copy(i, c).wait()
+
+        @pl.when(step >= 2)
+        def _():
+            grad_copy(i, j).wait()
+
+        own_st[j % 2, :bn] = dot_tn(lhs[:, :, :, cols(i)].reshape(4 * rows, bn), wa[:, cols(j)])
+        grad_copy(i, j).start()
+        return carry
+
+    lax.fori_loop(0, steps * steps, grad_tile, 0)
+    for j in range(2):
+        grad_copy(0, j).wait()
     for j in range(steps):
         core_copy(0, j).wait_send()
         for k in range(2):
@@ -728,7 +791,7 @@
                 final_copy(phase, k, j).wait_recv()
 
 
-def back_layer(act, d_gate, d_up, w_gate, w_up, w_down, tp, bn=512):
+def back_layer(act, d_gate, d_up, z_all, w_gate, w_up, w_down, tp, bn=512):
     total, width = act.shape
     dim = w_gate.shape[0]
     rows = total // tp
@@ -738,18 +801,18 @@
     came = jax.ShapeDtypeStruct((2, rows, dim), BF16)
     return pl.pallas_call(
         functools.partial(back_kernel, rows=rows, bn=bn),
-        out_shape=(jax.ShapeDtypeStruct((2, rows, dim), F32), came, came),
-        in_specs=[anyspace] * 6,
-        out_specs=(anyspace,) * 3,
-        scratch_shapes=[pltpu.VMEM((width, dim), BF16), pltpu.VMEM((dim, width), BF16), pltpu.VMEM((2, 2, rows, width), BF16),
+        out_shape=(jax.ShapeDtypeStruct((2, rows, dim), F32), came, came, jax.ShapeDtypeStruct((dim, width), F32)),
+        in_specs=[anyspace] * 7,
+        out_specs=(anyspace,) * 4,
+        scratch_shapes=[pltpu.VMEM((4 * rows, dim), BF16), pltpu.VMEM((dim, width), BF16), pltpu.VMEM((2, 2, rows, width), BF16),
                         pltpu.VMEM((4, steps, rows, bn), BF16), pltpu.VMEM((4, steps, rows, bn), BF16),
                         pltpu.VMEM((2, 2, steps, rows // 2, bn), BF16), pltpu.VMEM((2, rows, bn), F32),
-                        dma((3, steps)), dma((2, 2)), dma((2,)), dma((steps,)), dma((4, steps)),
+                        dma((steps, 4)), dma((3, steps)), dma((2, 2)), dma((2,)), dma((steps,)), dma((4, steps)),
                         dma((2, steps)), dma((2, 2, steps)), dma((2, steps)), dma((2, 2, steps))],
         compiler_params=pltpu.CompilerParams(vmem_limit_bytes=67043328, collective_id=1, has_side_effects=True),
         cost_estimate=pl.CostEstimate(flops=6 * total * dim * width, bytes_accessed=200 << 20, transcendentals=0),
         name="back",
-    )(act, d_gate, d_up, w_gate, w_up, w_down)
+    )(act, d_gate, d_up, z_all, w_gate, w_up, w_down)
 
 
 def product_kernel(a_ref, b_ref, o_ref):
@@ -769,6 +832,26 @@
         cost_estimate=pl.CostEstimate(flops=2 * rows * m * n, bytes_accessed=110 << 20, transcendentals=0),
         name="weight_grad",
     )(a, b)
+
+
+def rest_kernel(at_ref, a_ref, b_ref, part_ref, o_ref):
+    o_ref[...] = part_ref[...] + dot_tn(a_ref[...], b_ref[...])
+
+
+def weight_grad_rest(a, b, part, block, count, bm=512, bn=1024):
+    m, n = part.shape
+    out = pl.BlockSpec((bm, bn), lambda i, j, at: (i, j))
+    return pl.pallas_call(
+        rest_kernel,
+        out_shape=jax.ShapeDtypeStruct((m, n), F32),
+        grid_spec=pltpu.PrefetchScalarGridSpec(
+            num_scalar_prefetch=1, grid=(m // bm, n // bn),
+            in_specs=[pl.BlockSpec((count, bm), lambda i, j, at: (at[0], i)), pl.BlockSpec((count, bn), lambda i, j, at: (at[0], j)), out],
+            out_specs=out),
+        compiler_params=pltpu.CompilerParams(dimension_semantics=("arbitrary", "arbitrary"), vmem_limit_bytes=56 << 20),
+        cost_estimate=pl.CostEstimate(flops=2 * count * m * n, bytes_accessed=80 << 20, transcendentals=0),
+        name="weight_grad_rest",
+    )(jnp.asarray(block, jnp.int32).reshape(1), a, b, part)
 
 
 def hop_diagonal(diag):
@@ -808,8 +891,8 @@
         def rope(raw_proj):
             return apply_rope(raw_proj, jnp.tile(cos_own, (batch, 1)), jnp.tile(sin_own, (batch, 1)))
 
-        gated_all, grad_all, act, d_gate, d_upper = gated_layer(gated_in, grad_out, w_gate, w_up, w_down, tp_size)
-        own_part, x_part, y_part = back_layer(act, d_gate, d_upper, w_gate, w_up, w_down, tp_size)
+        gated_all, grad_all, act, d_gate, d_upper, g_down_part = gated_layer(gated_in, grad_out, w_gate, w_up, w_down, tp_size)
+        own_part, x_part, y_part, g_gate_part = back_layer(act, d_gate, d_upper, gated_all, w_gate, w_up, w_down, tp_size)
         hidden, resid, own_part = lax.optimization_barrier((hidden, resid, own_part))
         norm1_pull = jax.vjp(rms_norm, hidden, attn_norm.astype(F32))[1]
         norm2_pull = jax.vjp(rms_norm, resid, mlp_norm.astype(F32))[1]
@@ -833,31 +916,32 @@
         kv_own, kv_side, kv_back, kv_diag = [dkv_near[k].astype(F32) + came_kv[k].astype(F32) for k in range(4)]
         kv_came = hop_diagonal(kv_diag.astype(BF16))
         g_query_sum = jnp.einsum("td,kte->kde", normed, d_q_raw[:near], preferred_element_type=F32) + came_q
-        kv_came, g_query_sum, d_gate = lax.optimization_barrier((kv_came, g_query_sum, d_gate))
+        kv_came, g_query_sum, act = lax.optimization_barrier((kv_came, g_query_sum, act))
         kv_next = hop_near(kv_side, kv_back, *kv_came)
         kv_last = (swap(kv_next[0], 2), swap(kv_next[1], 4))
         q_came = hop_diagonal(g_query_sum[3])
-        g_gate = weight_grad(gated_all, d_gate)
-        kv_last, q_came, g_gate = lax.optimization_barrier((kv_last, q_came, g_gate))
+        g_down = weight_grad_rest(act, grad_all, g_down_part, me // 2, 2 * rows)
+        kv_last, g_down = lax.optimization_barrier((kv_last, g_down))
         d_kv = (kv_own + kv_last[0].astype(F32) + kv_last[1].astype(F32)).astype(BF16)
         d_k_raw = key_pull(d_kv[:, :head_dim].astype(F32))[0].astype(BF16)
         d_values = d_kv[:, head_dim:]
+        g_key_part, g_value_part = dot_tn(normed, d_k_raw), dot_tn(normed, d_values)
+        g_key_part, g_value_part, d_gate = lax.optimization_barrier((g_key_part, g_value_part, d_gate))
+        g_key, g_value = lax.psum((g_key_part, g_value_part), "tp")
+        g_gate = weight_grad_rest(gated_all, d_gate, g_gate_part, 1, 4 * rows)
+        q_came, g_gate = lax.optimization_barrier((q_came, g_gate))
         q_next = hop_near(g_query_sum[1], g_query_sum[2], *q_came)
-        g_key_part, g_value_part = dot_tn(normed, d_k_raw), dot_tn(normed, d_values)
-        q_next, g_key_part, g_value_part, d_upper = lax.optimization_barrier((q_next, g_key_part, g_value_part, d_upper))
-        g_key, g_value = lax.psum((g_key_part, g_value_part), "tp")
-        q_last = (swap(q_next[0], 2), swap(q_next[1], 4))
-        g_up = weight_grad(gated_all, d_upper)
         d_normed = (d_normed_q + dot_nt(d_k_raw, w_key) + dot_nt(d_values, w_value)).astype(BF16)
-        q_last, g_up, d_normed, act = lax.optimization_barrier((q_last, g_up, d_normed, act))
-        g_query = g_query_sum[0] + q_last[0] + q_last[1]
         d_hidden_norm, g_attn_norm_part = norm1_pull(d_normed)
         norms = jnp.stack([g_attn_norm_part, g_mlp_norm_part])
+        q_next, norms, d_upper = lax.optimization_barrier((q_next, norms, d_upper))
+        q_last = (swap(q_next[0], 2), swap(q_next[1], 4))
         norms_near = [swap(norms, bit) for bit in (2, 4, 6)]
-        g_down = weight_grad(act, grad_all)
-        norms_near, g_down, d_hidden_norm = lax.optimization_barrier((norms_near, g_down, d_hidden_norm))
+        g_up = weight_grad(gated_all, d_upper)
+        norms_near, q_last, g_up, d_hidden_norm = lax.optimization_barrier((norms_near, q_last, g_up, d_hidden_norm))
         norms = norms + norms_near[0] + norms_near[1] + norms_near[2]
         g_norms = norms + swap(norms, 1)
+        g_query = g_query_sum[0] + q_last[0] + q_last[1]
         grad_hidden = (d_resid.astype(F32) + d_hidden_norm.astype(F32)).astype(BF16)
         full = (batch, shard, dim)
         return (hidden_out.reshape(full), grad_hidden.reshape(full), g_norms[0], g_query, g_key, g_value, g_out, g_norms[1], g_gate, g_up, g_down)

time: 892 us -> 908 us (1.018)
  waiting for transfers between devices: 91.3 us -> 116 us
    pallas_call x3 -> x1, Pallas kernels: 156 us -> 49.8 us  [weight_grad(): pl.pallas_call(product_kernel, out_shape=jax.ShapeDtypeStruct((m, n), F32...]
    pallas_call x0 -> x2, Pallas kernels: none -> 58.7 us  [weight_grad_rest(): pl.pallas_call(rest_kernel, out_shape=jax.ShapeDtypeStruct((m, n), F32),...]
    pallas_call x1, Pallas kernels: 185 us -> 230 us  [gated_layer(): pl.pallas_call(functools.partial(gated_kernel, bn=bn), out_shape=(gathere...]
    reduce_scatter x1, waiting for transfers between devices: 62.7 us -> 91.1 us  [layer(): g_out = lax.psum_scatter(g_out_part, 'tp', scatter_dimension=0, tiled=True)]
  transfers between devices with their start and end apart: 16 -> 16, of which waited for: 6 -> 6; matrix products, arithmetic and copies ran while one was open for 4% -> 5% of each run, Pallas kernels for 18% -> 12%
where the time goes in v6:
time: 908 us; the launch traced here: 900 us
  Pallas kernels  649 us (71%)
  waiting for transfers between devices  116 us (13%)
  matrix products  48.8 us (5%)
  other arithmetic  35.8 us (4%)
  local copies, waits for them, and re-layouts  22.9 us (3%)
  between operations  14.7 us (2%)
  starting transfers between devices  12.2 us (1%)
    pallas_call x1, Pallas kernels, gated_layer(): pl.pallas_call(functools.partial(gated_kernel, bn=bn), out_shape=(gathere...  230 us
    pallas_call x1, Pallas kernels, back_layer(): pl.pallas_call(functools.partial(back_kernel, rows=rows, bn=bn), out_shap...  176 us
    pallas_call x1, Pallas kernels, front_layer(): pl.pallas_call(functools.partial(front_kernel, batch=batch), out_shape=(s...  102 us
    reduce_scatter x1, waiting for transfers between devices, layer(): g_out = lax.psum_scatter(g_out_part, 'tp', scatter_dimension=0, tiled=True)  91.1 us
    pallas_call x2, Pallas kernels, weight_grad_rest(): pl.pallas_call(rest_kernel, out_shape=jax.ShapeDtypeStruct((m, n), F32),...  58.7 us
    pallas_call x1, Pallas kernels, weight_grad(): pl.pallas_call(product_kernel, out_shape=jax.ShapeDtypeStruct((m, n), F32...  49.8 us
    pallas_call x1, Pallas kernels, attention_backward(): pl.pallas_call(attn_bwd_kernel, out_shape=(jax.ShapeDtypeStruct((heads, r...  32.7 us
    ppermute x14, waiting for transfers between devices, swap(): return lax.ppermute(x, 'tp', [(t, t ^ bit) for t in range(8)])  24.2 us
  transfers between devices with their start and end apart: 16, of which 6 were waited for; matrix products, arithmetic and copies ran while one was open for 5% of the time, Pallas kernels for 12%

profile of v6, /device:TPU:0, one launch (start us, length us, event | category | flops | bytes accessed | tf_op | source)
XLA Modules:
  0.0 899.7 jit_solution(17501724850182726010)
XLA Ops:
  16.0 101.8 %front.1 = (bf16[576,2048]{1,0:T(8,128)(2,1)}, bf16[8,2048,256]{2,1,0:T(8,128)(2,1)}, bf16[8,256,2048]{2,1,0:T(8,128)(2,1)}, bf16[8,576,512]{2,1,0:T(8,128)(2,1)...) custom-call(s32[2,3]{1,0:T(2,128)} %pad_add_fusion.lens_ref, ...), custom_call_target="tpu_custom_call" | custom-call | flops 19327352832 | bytes 62914560 | tf_op jit(solution)/shard_map/front/pallas_call | solution.py:336
  117.8 230.1 %gated.1 = (bf16[4608,2048]{1,0:T(8,128)(2,1)}, bf16[4608,2048]{1,0:T(8,128)(2,1)}, bf16[4608,2048]{1,0:T(8,128)(2,1)}, bf16[4608,2048]{1,0:T(8,128)(2,1)}, bf16...) custom-call(bf16[576,2048]{1,0:T(8,128)(2,1)} %get-tuple-element.64.z_own, bf16[576,2048]{1,0:T(8,128)(2,1)} %bitcast.106, ...), custom_call_target="tpu_custom_call" | custom-call | flops 115964116992 | bytes 209715200 | tf_op jit(solution)/shard_map/gated/pallas_call | solution.py:579
  347.9 176.3 %back.1 = (f32[2,576,2048]{2,1,0:T(8,128)}, bf16[2,576,2048]{2,1,0:T(8,128)(2,1)}, bf16[2,576,2048]{2,1,0:T(8,128)(2,1)}, f32[2048,2048]{1,0:T(8,128)}) custom-call(bf16[4608,2048]{1,0:T(8,128)(2,1)} %get-tuple-element.88.act.a_ref, bf16[4608,2048]{1,0:T(8,128)(2,1)} %get-tuple-element.93.d_gate.b_ref, bf16[4608,2048]{1,0:T(8,128)(2,1)} %get-tuple-element.102.d_up.b_ref, ...), custom_call_target="tpu_custom_call" | custom-call | flops 115964116992 | bytes 209715200 | tf_op jit(solution)/shard_map/back/pallas_call | solution.py:802
  526.7 9.6 %fusion.3 = (f32[2048]{0:T(1024)S(1)}, f32[576]{0:T(1024)S(1)}, bf16[576,2048]{1,0:T(8,128)(2,1)S(1)}, bf16[576,2048]{1,0:T(8,128)(2,1)}) fusion(bf16[576,2048]{1,0:T(8,128)(2,1)S(1)} %copy-done.1, f32[576]{0:T(1024)S(1)} %fusion.33, f32[2048]{0:T(1024)S(1)} %copy-done.21, bf16[2,576,2048]{2,1,0:T(8,128)(2,1)} %get-tuple-element.73, ...), kind=kLoop, calls=%fused_computation.19 | loop fusion | flops 22410688 | bytes 25973248 | tf_op jit(solution)/shard_map/transpose(jvp())/reduce_sum | solution.py:23
  537.9 2.6 copy-done.27
  540.5 6.3 convolution_convert_fusion.do_ref
  546.9 10.2 %fusion.39 = f32[2048,2048]{1,0:T(8,128)} fusion(bf16[576,2048]{1,0:T(8,128)(2,1)S(1)} %copy-done.28, bf16[576,2048]{1,0:T(8,128)(2,1)S(1)} %add_convert_fusion.2), kind=kOutput, calls=%fused_computation.102 | convolution fusion | flops 4831838208 | bytes 21495808 | tf_op jit(solution)/shard_map/dot_general | solution.py:50
  557.8 32.7 %attn_bwd.1 = (bf16[8,576,256]{2,1,0:T(8,128)(2,1)}, bf16[4,576,512]{2,1,0:T(8,128)(2,1)}, bf16[4,576,512]{2,1,0:T(8,128)(2,1)}) custom-call(s32[11,3]{1,0:T(8,128)} %add_add_fusion.3.lens_ref, f32[192,128]{1,0:T(8,128)} %get-tuple-element.172.cos_ref, f32[192,128]{1,0:T(8,128)} %get-tuple-element.171.sin_ref, bf16[8,576,256]{2,1,0:T(8,128)(2,1)} %get-tuple-element.74.q_ref, ...), custom_call_target="tpu_custom_call" | custom-call | flops 18119393280 | bytes 20971520 | tf_op jit(solution)/shard_map/attn_bwd/pallas_call | solution.py:362
  590.5 7.0 convolution_bitcast_fusion
  598.0 9.9 %convolution_bitcast_fusion.1 = f32[576,2048]{1,0:T(8,128)} fusion(bf16[8,576,256]{2,1,0:T(8,128)(2,1)} %get-tuple-element.81, bf16[8,2048,256]{2,1,0:T(8,128)(2,1)} %get-tuple-element.82), kind=kOutput, calls=%fused_computation.32 | convolution fusion | flops 4831838208 | bytes 15466496 | tf_op jit(solution)/shard_map/hte,hde->td/dot_general | solution.py:914
  607.9 6.5 collective-permute-done
  616.3 2.6 collective-permute-start.2
  619.0 7.8 bitcast_add_fusion
  630.0 24.4 %weight_grad_rest.2 = f32[2048,2048]{1,0:T(8,128)} custom-call(s32[1]{0:T(128)} %bitcast.23.at_ref, bf16[4608,2048]{1,0:T(8,128)(2,1)} %get-tuple-element.88.act.a_ref, bf16[4608,2048]{1,0:T(8,128)(2,1)} %get-tuple-element.89.b_ref, f32[2048,2048]{1,0:T(8,128)} %get-tuple-element.90.part_ref), custom_call_target="tpu_custom_call" | custom-call | flops 9663676416 | bytes 83886080 | tf_op jit(solution)/shard_map/weight_grad_rest/pallas_call | solution.py:844
  655.8 2.4 fusion.27
  663.9 4.9 slice_bitcast_fusion
  673.4 34.4 %weight_grad_rest.3 = f32[2048,2048]{1,0:T(8,128)} custom-call(s32[1]{0:T(128)} %constant.39.clone.1.at_ref, bf16[4608,2048]{1,0:T(8,128)(2,1)} %get-tuple-element.68.z_all.a_ref, bf16[4608,2048]{1,0:T(8,128)(2,1)} %get-tuple-element.93.d_gate.b_ref, f32[2048,2048]{1,0:T(8,128)} %get-tuple-element.94.part_ref), custom_call_target="tpu_custom_call" | custom-call | flops 19327352832 | bytes 83886080 | tf_op jit(solution)/shard_map/weight_grad_rest/pallas_call | solution.py:844
  709.2 2.7 bitcast_add_fusion.3
  719.4 49.8 %weight_grad.1 = f32[2048,2048]{1,0:T(8,128)} custom-call(bf16[4608,2048]{1,0:T(8,128)(2,1)} %get-tuple-element.68.z_all.a_ref, bf16[4608,2048]{1,0:T(8,128)(2,1)} %get-tuple-element.102.d_up.b_ref), custom_call_target="tpu_custom_call" | custom-call | flops 38654705664 | bytes 115343360 | tf_op jit(solution)/shard_map/weight_grad/pallas_call | solution.py:825
  769.1 16.0 %collective-permute-done.11 = f32[2048,256]{0,1:T(8,128)} collective-permute-done((f32[2048,256]{0,1:T(8,128)}, f32[2048,256]{0,1:T(8,128)}, u32[]{:S(2)}, u32[]{:S(2)}) %collective-permute-start.11) | collective-permute-done | bytes 2097184 | tf_op jit(solution)/shard_map/ppermute | solution.py:54
  787.1 4.7 fusion.14
  792.2 2.5 add_convert_fusion
  797.1 91.1 %reduce-scatter.2.cloned.1.call-done = f32[256,2048]{1,0:T(8,128)} async-done(((f32[2048,2048]{1,0:T(8,128)}), f32[256,2048]{1,0:T(8,128)}) %reduce-scatter.2.cloned.1.call-update) | async-done | bytes 2097168 | tf_op jit(solution)/shard_map/reduce_scatter | solution.py:909
  888.2 3.0 copy.33
  (135 shorter events, 45.8 us)
Async XLA Ops:
  7.2 790.0 %all-reduce.5.cloned.1.call-start = ((), (), s32[]{:S(2)}) async-start(), calls=%async_computation.2 | async-start | bytes 8388608 | tf_op jit(solution)/shard_map/psum | solution.py:930
  526.6 9.6 %copy-start.7 = (bf16[3,192,2048]{2,1,0:T(8,128)(2,1)S(1)}, bf16[3,192,2048]{2,1,0:T(8,128)(2,1)}, u32[]{:S(2)}) copy-start(bf16[3,192,2048]{2,1,0:T(8,128)(2,1)} %param.15) | copy-start | bytes 7077892
  546.8 10.2 %copy-start.23 = (s32[3]{0:T(128)S(1)}, s32[3]{0:T(128)}, u32[]{:S(2)}) copy-start(s32[3]{0:T(128)} %param.17) | copy-start | bytes 40
  546.8 10.2 %copy-start.24 = (s32[3]{0:T(128)S(1)}, s32[3]{0:T(128)}, u32[]{:S(2)}) copy-start(s32[3]{0:T(128)} %param.16) | copy-start | bytes 40
  546.9 10.2 %copy-start.25 = (s32[11]{0:T(128)S(1)}, s32[11]{0:T(128)}, u32[]{:S(2)}) copy-start(s32[11]{0:T(128)} %pad.21.clone) | copy-start | bytes 136
  546.9 10.2 %copy-start.26 = (s32[11]{0:T(128)S(1)}, s32[11]{0:T(128)}, u32[]{:S(2)}) copy-start(s32[11]{0:T(128)} %pad.20.clone) | copy-start | bytes 136
  557.8 32.7 %copy-start.5 = (bf16[576,2048]{1,0:T(8,128)(2,1)S(1)}, bf16[576,2048]{1,0:T(8,128)(2,1)}, u32[]{:S(2)}) copy-start(bf16[576,2048]{1,0:T(8,128)(2,1)} %get-tuple-element.84) | copy-start | bytes 7077892
  597.4 21.6 %collective-permute-start.3 = (f32[4,2048,256]{1,2,0:T(8,128)}, f32[4,2048,256]{1,2,0:T(8,128)}, u32[]{:S(2)}, u32[]{:S(2)}) collective-permute-start(f32[4,2048,256]{1,2,0:T(8,128)} %convolution_bitcast_fusion), channel_id=1, source_target_pairs={{0,1},{1,0},{2,3},{3,2},{4,5},{5,4},{6,7},{7,6},{8,9},{9,8},{10,11... | collective-permute-start | bytes 25165832 | tf_op jit(solution)/shard_map/ppermute | solution.py:54
  597.8 16.5 %collective-permute-start = (bf16[4,576,512]{2,1,0:T(8,128)(2,1)}, bf16[4,576,512]{2,1,0:T(8,128)(2,1)}, u32[]{:S(2)}, u32[]{:S(2)}) collective-permute-start(bf16[4,576,512]{2,1,0:T(8,128)(2,1)} %get-tuple-element.80), channel_id=1, source_target_pairs={{0,1},{1,0},{2,3},{3,2},{4,5},{5,4},{6,7},{7,6},{8,9},{9,8},{10,11... | collective-permute-start | bytes 7077896 | tf_op jit(solution)/shard_map/ppermute | solution.py:54
  598.0 16.4 %copy-start.6 = (bf16[4,576,512]{2,1,0:T(8,128)(2,1)S(1)}, bf16[4,576,512]{2,1,0:T(8,128)(2,1)}, u32[]{:S(2)}) copy-start(bf16[4,576,512]{2,1,0:T(8,128)(2,1)} %get-tuple-element.79) | copy-start | bytes 7077892
  616.3 10.6 %collective-permute-start.2 = (bf16[288,512]{1,0:T(8,128)(2,1)S(1)}, bf16[288,512]{1,0:T(8,128)(2,1)S(1)}, u32[]{:S(2)}, u32[]{:S(2)}) collective-permute-start(bf16[288,512]{1,0:T(8,128)(2,1)S(1)} %get-tuple-element.167), channel_id=1, source_target_pairs={{0,4},{1,5},{2,6},{3,7},{4,0},{5,1},{6,2},{7,3},{8,12},{9,13},{10,... | collective-permute-start | bytes 884744 | tf_op jit(solution)/shard_map/ppermute | solution.py:54
  618.9 8.8 collective-permute-start.1
  628.0 26.4 %collective-permute-start.6 = (bf16[576,512]{1,0:T(8,128)(2,1)S(1)}, bf16[576,512]{1,0:T(8,128)(2,1)S(1)}, u32[]{:S(2)}, u32[]{:S(2)}) collective-permute-start(bf16[576,512]{1,0:T(8,128)(2,1)S(1)} %pad_maximum_fusion.2), channel_id=1, source_target_pairs={{0,2},{1,3},{2,0},{3,1},{4,6},{5,7},{6,4},{7,5},{8,10},{9,11},{10,... | collective-permute-start | bytes 1769480 | tf_op jit(solution)/shard_map/ppermute | solution.py:54
  629.2 25.1 %collective-permute-start.7 = (bf16[576,512]{1,0:T(8,128)(2,1)S(1)}, bf16[576,512]{1,0:T(8,128)(2,1)S(1)}, u32[]{:S(2)}, u32[]{:S(2)}) collective-permute-start(bf16[576,512]{1,0:T(8,128)(2,1)S(1)} %pad_maximum_fusion.3), channel_id=1, source_target_pairs={{0,4},{1,5},{2,6},{3,7},{4,0},{5,1},{6,2},{7,3},{8,12},{9,13},{10,... | collective-permute-start | bytes 1769480 | tf_op jit(solution)/shard_map/ppermute | solution.py:54
  661.5 226.7 %reduce-scatter.2.cloned.1.call-start = ((), (), s32[]{:S(2)}) async-start(), calls=%async_computation.1 | async-start | bytes 18874368 | tf_op jit(solution)/shard_map/reduce_scatter | solution.py:909
  668.8 40.4 %collective-permute-start.5 = (f32[1024,256]{0,1:T(8,128)}, f32[1024,256]{0,1:T(8,128)}, u32[]{:S(2)}, u32[]{:S(2)}) collective-permute-start(f32[1024,256]{0,1:T(8,128)} %get-tuple-element.159), channel_id=1, source_target_pairs={{0,4},{1,5},{2,6},{3,7},{4,0},{5,1},{6,2},{7,3},{8,12},{9,13},{10,... | collective-permute-start | bytes 3145736 | tf_op jit(solution)/shard_map/ppermute | solution.py:54
  669.7 39.5 %collective-permute-start.4 = (f32[1024,256]{0,1:T(8,128)}, f32[1024,256]{0,1:T(8,128)}, u32[]{:S(2)}, u32[]{:S(2)}) collective-permute-start(f32[1024,256]{0,1:T(8,128)} %get-tuple-element.160), channel_id=1, source_target_pairs={{0,2},{1,3},{2,0},{3,1},{4,6},{5,7},{6,4},{7,5},{8,10},{9,11},{10,... | collective-permute-start | bytes 3145736 | tf_op jit(solution)/shard_map/ppermute | solution.py:54
  713.7 55.4 %collective-permute-start.10 = (f32[2,2048]{1,0:T(2,128)S(1)}, f32[2,2048]{1,0:T(2,128)S(1)}, u32[]{:S(2)}, u32[]{:S(2)}) collective-permute-start(f32[2,2048]{1,0:T(2,128)S(1)} %pad_maximum_fusion.4), channel_id=1, source_target_pairs={{0,6},{1,7},{2,4},{3,5},{4,2},{5,3},{6,0},{7,1},{8,14},{9,15},{10,... | collective-permute-start | bytes 49160 | tf_op jit(solution)/shard_map/ppermute | solution.py:54
  715.3 53.8 %collective-permute-start.9 = (f32[2,2048]{1,0:T(2,128)S(1)}, f32[2,2048]{1,0:T(2,128)S(1)}, u32[]{:S(2)}, u32[]{:S(2)}) collective-permute-start(f32[2,2048]{1,0:T(2,128)S(1)} %pad_maximum_fusion.4), channel_id=1, source_target_pairs={{0,4},{1,5},{2,6},{3,7},{4,0},{5,1},{6,2},{7,3},{8,12},{9,13},{10,... | collective-permute-start | bytes 49160 | tf_op jit(solution)/shard_map/ppermute | solution.py:54
  716.3 52.8 %collective-permute-start.8 = (f32[2,2048]{1,0:T(2,128)S(1)}, f32[2,2048]{1,0:T(2,128)S(1)}, u32[]{:S(2)}, u32[]{:S(2)}) collective-permute-start(f32[2,2048]{1,0:T(2,128)S(1)} %pad_maximum_fusion.4), channel_id=1, source_target_pairs={{0,2},{1,3},{2,0},{3,1},{4,6},{5,7},{6,4},{7,5},{8,10},{9,11},{10,... | collective-permute-start | bytes 49160 | tf_op jit(solution)/shard_map/ppermute | solution.py:54
  717.2 68.0 %collective-permute-start.11 = (f32[2048,256]{0,1:T(8,128)}, f32[2048,256]{0,1:T(8,128)}, u32[]{:S(2)}, u32[]{:S(2)}) collective-permute-start(f32[2048,256]{0,1:T(8,128)} %get-tuple-element.100), channel_id=1, source_target_pairs={{0,2},{1,3},{2,0},{3,1},{4,6},{5,7},{6,4},{7,5},{8,10},{9,11},{10,... | collective-permute-start | bytes 6291464 | tf_op jit(solution)/shard_map/ppermute | solution.py:54
  718.3 67.4 %collective-permute-start.12 = (f32[2048,256]{0,1:T(8,128)S(1)}, f32[2048,256]{0,1:T(8,128)S(1)}, u32[]{:S(2)}, u32[]{:S(2)}) collective-permute-start(f32[2048,256]{0,1:T(8,128)S(1)} %get-tuple-element.101), channel_id=1, source_target_pairs={{0,4},{1,5},{2,6},{3,7},{4,0},{5,1},{6,2},{7,3},{8,12},{9,13},{10,... | collective-permute-start | bytes 6291464 | tf_op jit(solution)/shard_map/ppermute | solution.py:54
  787.1 9.4 %collective-permute-start.13 = (f32[2,2048]{1,0:T(2,128)S(1)}, f32[2,2048]{1,0:T(2,128)S(1)}, u32[]{:S(2)}, u32[]{:S(2)}) collective-permute-start(f32[2,2048]{1,0:T(2,128)S(1)} %add_add_fusion.2), channel_id=1, source_target_pairs={{0,1},{1,0},{2,3},{3,2},{4,5},{5,4},{6,7},{7,6},{8,9},{9,8},{10,11... | collective-permute-start | bytes 49160 | tf_op jit(solution)/shard_map/ppermute | solution.py:54
  797.1 94.1 %copy-start.10 = (f32[2048,256]{1,0:T(8,128)S(1)}, f32[2048,256]{1,0:T(8,128)}, u32[]{:S(2)}) copy-start(f32[2048,256]{1,0:T(8,128)} %get-tuple-element.181) | copy-start | bytes 6291460
  (23 other events, 77.7 us)
Sparse Core Ops, SparseCore 0:
  661.6 111.8 all-reduce.4
  777.6 110.5 reduce-scatter.1

commit v7 on v6

--- a/solution.py
+++ b/solution.py
@@ -385,9 +385,9 @@
     return (gelu * upper).astype(BF16), (d_act * upper * slope).astype(BF16), (d_act * gelu).astype(BF16)
 
 
-def gated_kernel(z_own, g_own, wg_hbm, wu_hbm, wd_hbm, z_all, g_all, act, d_gate, d_up, g_down,
-                 wg, wu, wd, z_buf, g_buf, outs, acc, acc_sem, w_sem, in_sem, own_sem, out_sem, send, recv, send0, recv0, *, bn):
-    rows, dim = z_own.shape
+def gated_kernel(z_own, g_own, wg_hbm, wu_hbm, wd_hbm, z_all, g_all, act, d_gate, d_up,
+                 wg, wu, wd, z_buf, g_buf, outs, w_sem, in_sem, own_sem, out_sem, send, recv, send0, recv0, *, bn):
+    rows, _ = z_own.shape
     width = wg_hbm.shape[1]
     steps = width // bn
     piece = rows // 4
@@ -452,10 +452,6 @@
         return [pltpu.make_async_copy(outs.at[slot, k, pl.ds(i * piece, piece)], ref.at[s_rows[i], cols], out_sem.at[slot, k, i])
                 for k, ref in enumerate((act, d_gate, d_up)) for i in range(4)]
 
-    def acc_copy(n):
-        part = pl.ds(pl.multiple_of(n * bn, 128), bn)
-        return pltpu.make_async_copy(acc.at[part], g_down.at[part], acc_sem.at[n])
-
     def stage_rows(s):
         late = (s + 6) // 8
         u = (s - 2) * late
@@ -489,17 +485,6 @@
                 outs[slot, k] = res[k]
             for cp in out_copies(slot, s_rows, n):
                 cp.start()
-
-            @pl.when(s >= 2)
-            def _():
-                for c in range(2):
-                    part = slice(c * (dim // 2), (c + 1) * (dim // 2))
-                    acc[cols, part] += dot_tn(outs[slot, 0], g_buf[:, part])
-
-                @pl.when(s == 7)
-                def _():
-                    acc_copy(n).start()
-
             return carry
 
         lax.fori_loop(0, steps, block, 0)
@@ -514,7 +499,6 @@
 
         @pl.when(s == 1)
         def _():
-            acc[...] = jnp.zeros_like(acc)
             for cp in own_out:
                 cp.wait()
             for a in range(2):
@@ -558,8 +542,6 @@
     for slot in range(2):
         for cp in out_copies(slot, last, 0):
             cp.wait()
-    for n in range(steps):
-        acc_copy(n).wait()
     for a in range(2):
         own_copy(a).wait_send()
         for path in range(2):
@@ -578,12 +560,12 @@
     dma = pltpu.SemaphoreType.DMA
     return pl.pallas_call(
         functools.partial(gated_kernel, bn=bn),
-        out_shape=(gathered, gathered, made, made, made, jax.ShapeDtypeStruct((width, dim), F32)),
+        out_shape=(gathered, gathered, made, made, made),
         in_specs=[anyspace] * 5,
-        out_specs=(anyspace,) * 6,
+        out_specs=(anyspace,) * 5,
         scratch_shapes=[pltpu.VMEM((dim, width), BF16), pltpu.VMEM((dim, width), BF16), pltpu.VMEM((width, dim), BF16),
                         pltpu.VMEM((rows, dim), BF16), pltpu.VMEM((rows, dim), BF16), pltpu.VMEM((2, 3, rows, bn), BF16),
-                        pltpu.VMEM((width, dim), F32), dma((width // bn,)), dma((3, width // bn)), dma((2, 4)), dma((4,)), dma((2, 3, 4)), dma((4, 6, 2)), dma((4, 6, 2)), dma((2,)), dma((2,))],
+                        dma((3, width // bn)), dma((2, 4)), dma((4,)), dma((2, 3, 4)), dma((4, 6, 2)), dma((4, 6, 2)), dma((2,)), dma((2,))],
         compiler_params=pltpu.CompilerParams(vmem_limit_bytes=67043328, collective_id=0, has_side_effects=True),
         cost_estimate=pl.CostEstimate(flops=6 * total * dim * width, bytes_accessed=200 << 20, transcendentals=total * width),
         name="gated",
@@ -815,6 +797,41 @@
     )(act, d_gate, d_up, z_all, w_gate, w_up, w_down)
 
 
+def join_kernel(own_ref, x_ref, y_ref, resid_ref, grad_ref, gain_ref, out_ref, d_resid_ref, g_gain_ref):
+    mlp_sum, d_gated = [own_ref[k] + x_ref[k].astype(F32) + y_ref[k].astype(F32) for k in range(2)]
+    resid = resid_ref[...].astype(F32)
+    out_ref[...] = (resid + mlp_sum).astype(BF16)
+    d_gated = d_gated.astype(BF16).astype(F32)
+    inv_rms = lax.rsqrt(jnp.mean(resid * resid, axis=-1, keepdims=True) + NORM_EPS)
+    unit = resid * inv_rms
+    scaled = d_gated * (1.0 + gain_ref[...].astype(F32))
+    d_norm = inv_rms * (scaled - unit * jnp.mean(unit * scaled, axis=-1, keepdims=True))
+    d_resid_ref[...] = (grad_ref[...].astype(F32) + d_norm).astype(BF16)
+
+    @pl.when(pl.program_id(0) == 0)
+    def _():
+        g_gain_ref[...] = jnp.zeros_like(g_gain_ref)
+
+    g_gain_ref[...] += jnp.sum(d_gated * unit, axis=0, keepdims=True)
+
+
+def join_layer(own_part, x_part, y_part, resid, grad_out, gain, bm=96):
+    rows, dim = resid.shape
+    pair = pl.BlockSpec((2, bm, dim), lambda i: (0, i, 0))
+    row = pl.BlockSpec((bm, dim), lambda i: (i, 0))
+    one = pl.BlockSpec((1, dim), lambda i: (0, 0))
+    return pl.pallas_call(
+        join_kernel,
+        out_shape=(jax.ShapeDtypeStruct((rows, dim), BF16), jax.ShapeDtypeStruct((rows, dim), BF16), jax.ShapeDtypeStruct((1, dim), F32)),
+        grid=(rows // bm,),
+        in_specs=[pair, pair, pair, row, row, one],
+        out_specs=(row, row, one),
+        compiler_params=pltpu.CompilerParams(dimension_semantics=("arbitrary",), vmem_limit_bytes=32 << 20),
+        cost_estimate=pl.CostEstimate(flops=40 * rows * dim, bytes_accessed=28 << 20, transcendentals=rows),
+        name="join",
+    )(own_part, x_part, y_part, resid, grad_out, gain.reshape(1, dim))
+
+
 def product_kernel(a_ref, b_ref, o_ref):
     o_ref[...] = dot_tn(a_ref[...], b_ref[...])
 
@@ -891,57 +908,56 @@
         def rope(raw_proj):
             return apply_rope(raw_proj, jnp.tile(cos_own, (batch, 1)), jnp.tile(sin_own, (batch, 1)))
 
-        gated_all, grad_all, act, d_gate, d_upper, g_down_part = gated_layer(gated_in, grad_out, w_gate, w_up, w_down, tp_size)
+        gated_all, grad_all, act, d_gate, d_upper = gated_layer(gated_in, grad_out, w_gate, w_up, w_down, tp_size)
         own_part, x_part, y_part, g_gate_part = back_layer(act, d_gate, d_upper, gated_all, w_gate, w_up, w_down, tp_size)
-        hidden, resid, own_part = lax.optimization_barrier((hidden, resid, own_part))
+        hidden, own_part = lax.optimization_barrier((hidden, own_part))
         norm1_pull = jax.vjp(rms_norm, hidden, attn_norm.astype(F32))[1]
-        norm2_pull = jax.vjp(rms_norm, resid, mlp_norm.astype(F32))[1]
         key_pull = jax.linear_transpose(rope, jax.ShapeDtypeStruct((rows, head_dim), F32))
-        mlp_sum, d_gated = [own_part[k] + x_part[k].astype(F32) + y_part[k].astype(F32) for k in range(2)]
-        d_gated = d_gated.astype(BF16)
-        hidden_out = (resid.astype(F32) + mlp_sum).astype(BF16)
-        d_resid_norm, g_mlp_norm_part = norm2_pull(d_gated)
-        d_resid = (grad_out.astype(F32) + d_resid_norm.astype(F32)).astype(BF16)
+        hidden_out, d_resid, g_mlp_norm_part = join_layer(own_part, x_part, y_part, resid, grad_out, mlp_norm)
         g_out_part = dot_tn(mixed, d_resid)
+        g_out_part, d_resid = lax.optimization_barrier((g_out_part, d_resid))
+        g_out = lax.psum_scatter(g_out_part, "tp", scatter_dimension=0, tiled=True)
         d_mixed = dot_nt(d_resid, wo_all).astype(BF16)
         lens_back = jnp.concatenate([lens, jnp.full((1, batch), me, jnp.int32), jnp.broadcast_to(starts[:, None], (tp_size, batch))])
-        d_mixed, g_out_part = lax.optimization_barrier((d_mixed, g_out_part))
-        g_out = lax.psum_scatter(g_out_part, "tp", scatter_dimension=0, tiled=True)
         d_q_raw, dkv_near, dkv_far = attention_backward(lens_back, cos_own, sin_own, query, kv_all, d_mixed, batch)
+        near = tp_size // 2
         came_kv = swap(dkv_far, 1)
-        near = tp_size // 2
-        came_q = swap(jnp.einsum("td,kte->kde", normed, d_q_raw[near:], preferred_element_type=F32), 1)
-        d_normed_q = jnp.einsum("hte,hde->td", d_q_raw, wq_all, preferred_element_type=F32)
-        came_kv, d_normed_q = lax.optimization_barrier((came_kv, d_normed_q))
+        g_far = jnp.einsum("kte,td->ked", d_q_raw[near:], normed, preferred_element_type=F32)
+        came_kv, g_far = lax.optimization_barrier((came_kv, g_far))
+        came_q = swap(g_far, 1)
         kv_own, kv_side, kv_back, kv_diag = [dkv_near[k].astype(F32) + came_kv[k].astype(F32) for k in range(4)]
         kv_came = hop_diagonal(kv_diag.astype(BF16))
-        g_query_sum = jnp.einsum("td,kte->kde", normed, d_q_raw[:near], preferred_element_type=F32) + came_q
-        kv_came, g_query_sum, act = lax.optimization_barrier((kv_came, g_query_sum, act))
+        d_normed_q = jnp.einsum("hte,hde->td", d_q_raw, wq_all, preferred_element_type=F32)
+        kv_came, d_normed_q = lax.optimization_barrier((kv_came, d_normed_q))
         kv_next = hop_near(kv_side, kv_back, *kv_came)
         kv_last = (swap(kv_next[0], 2), swap(kv_next[1], 4))
+        came_q, dq_near = lax.optimization_barrier((came_q, d_q_raw[:near]))
+        g_query_sum = jnp.einsum("kte,td->ked", dq_near, normed, preferred_element_type=F32) + came_q
+        g_query_sum, act = lax.optimization_barrier((g_query_sum, act))
         q_came = hop_diagonal(g_query_sum[3])
-        g_down = weight_grad_rest(act, grad_all, g_down_part, me // 2, 2 * rows)
-        kv_last, g_down = lax.optimization_barrier((kv_last, g_down))
+        g_down = weight_grad(act, grad_all)
+        kv_last, q_came, g_down = lax.optimization_barrier((kv_last, q_came, g_down))
         d_kv = (kv_own + kv_last[0].astype(F32) + kv_last[1].astype(F32)).astype(BF16)
         d_k_raw = key_pull(d_kv[:, :head_dim].astype(F32))[0].astype(BF16)
         d_values = d_kv[:, head_dim:]
+        q_next = hop_near(g_query_sum[1], g_query_sum[2], *q_came)
         g_key_part, g_value_part = dot_tn(normed, d_k_raw), dot_tn(normed, d_values)
-        g_key_part, g_value_part, d_gate = lax.optimization_barrier((g_key_part, g_value_part, d_gate))
+        q_next, g_key_part, g_value_part, d_gate = lax.optimization_barrier((q_next, g_key_part, g_value_part, d_gate))
+        last_side = swap(q_next[0], 2)
+        q_last = (last_side, swap(q_next[1], 4))
         g_key, g_value = lax.psum((g_key_part, g_value_part), "tp")
         g_gate = weight_grad_rest(gated_all, d_gate, g_gate_part, 1, 4 * rows)
-        q_came, g_gate = lax.optimization_barrier((q_came, g_gate))
-        q_next = hop_near(g_query_sum[1], g_query_sum[2], *q_came)
         d_normed = (d_normed_q + dot_nt(d_k_raw, w_key) + dot_nt(d_values, w_value)).astype(BF16)
+        d_normed, g_gate = lax.optimization_barrier((d_normed, g_gate))
         d_hidden_norm, g_attn_norm_part = norm1_pull(d_normed)
-        norms = jnp.stack([g_attn_norm_part, g_mlp_norm_part])
-        q_next, norms, d_upper = lax.optimization_barrier((q_next, norms, d_upper))
-        q_last = (swap(q_next[0], 2), swap(q_next[1], 4))
+        norms = jnp.concatenate([g_attn_norm_part.reshape(1, dim), g_mlp_norm_part])
+        norms, d_upper = lax.optimization_barrier((norms, d_upper))
         norms_near = [swap(norms, bit) for bit in (2, 4, 6)]
         g_up = weight_grad(gated_all, d_upper)
         norms_near, q_last, g_up, d_hidden_norm = lax.optimization_barrier((norms_near, q_last, g_up, d_hidden_norm))
         norms = norms + norms_near[0] + norms_near[1] + norms_near[2]
         g_norms = norms + swap(norms, 1)
-        g_query = g_query_sum[0] + q_last[0] + q_last[1]
+        g_query = (g_query_sum[0] + q_last[0] + q_last[1]).T
         grad_hidden = (d_resid.astype(F32) + d_hidden_norm.astype(F32)).astype(BF16)
         full = (batch, shard, dim)
         return (hidden_out.reshape(full), grad_hidden.reshape(full), g_norms[0], g_query, g_key, g_value, g_out, g_norms[1], g_gate, g_up, g_down)

time: 908 us -> 878 us (0.967)
  other arithmetic: 35.8 us -> 23.7 us
  Pallas kernels: 649 us -> 639 us
  waiting for transfers between devices: 116 us -> 106 us
    pallas_call x1 -> x2, Pallas kernels: 49.8 us -> 99.2 us  [weight_grad(): pl.pallas_call(product_kernel, out_shape=jax.ShapeDtypeStruct((m, n), F32...]
    pallas_call x1, Pallas kernels: 230 us -> 185 us  [gated_layer(): pl.pallas_call(functools.partial(gated_kernel, bn=bn), out_shape=(gathere...]
    pallas_call x2 -> x1, Pallas kernels: 58.7 us -> 34.9 us  [weight_grad_rest(): pl.pallas_call(rest_kernel, out_shape=jax.ShapeDtypeStruct((m, n), F32),...]
    pallas_call x0 -> x1, Pallas kernels: none -> 9.86 us  [join_layer(): pl.pallas_call(join_kernel, out_shape=(jax.ShapeDtypeStruct((rows, dim),...]
    unnamed x65 -> x57, local copies, waits for them, and re-layouts: 12.8 us -> 21.8 us
  transfers between devices with their start and end apart: 16 -> 16, of which waited for: 6 -> 4; matrix products, arithmetic and copies ran while one was open for 5% -> 4% of each run, Pallas kernels for 12% -> 15%
where the time goes in v7:
time: 878 us; the launch traced here: 870 us
  Pallas kernels  639 us (73%)
  waiting for transfers between devices  106 us (12%)
  matrix products  46.7 us (5%)
  local copies, waits for them, and re-layouts  27.3 us (3%)
  other arithmetic  23.7 us (3%)
  between operations  14.7 us (2%)
  starting transfers between devices  12.9 us (1%)
    pallas_call x1, Pallas kernels, gated_layer(): pl.pallas_call(functools.partial(gated_kernel, bn=bn), out_shape=(gathere...  185 us
    pallas_call x1, Pallas kernels, back_layer(): pl.pallas_call(functools.partial(back_kernel, rows=rows, bn=bn), out_shap...  176 us
    pallas_call x1, Pallas kernels, front_layer(): pl.pallas_call(functools.partial(front_kernel, batch=batch), out_shape=(s...  102 us
    pallas_call x2, Pallas kernels, weight_grad(): pl.pallas_call(product_kernel, out_shape=jax.ShapeDtypeStruct((m, n), F32...  99.2 us
    reduce_scatter x1, waiting for transfers between devices, layer(): g_out = lax.psum_scatter(g_out_part, 'tp', scatter_dimension=0, tiled=True)  85.9 us
    pallas_call x1, Pallas kernels, weight_grad_rest(): pl.pallas_call(rest_kernel, out_shape=jax.ShapeDtypeStruct((m, n), F32),...  34.9 us
    pallas_call x1, Pallas kernels, attention_backward(): pl.pallas_call(attn_bwd_kernel, out_shape=(jax.ShapeDtypeStruct((heads, r...  32.3 us
    unnamed x57, local copies, waits for them, and re-layouts  21.8 us
  transfers between devices with their start and end apart: 16, of which 4 were waited for; matrix products, arithmetic and copies ran while one was open for 4% of the time, Pallas kernels for 15%

profile of v7, /device:TPU:0, one launch (start us, length us, event | category | flops | bytes accessed | tf_op | source)
XLA Modules:
  0.0 869.9 jit_solution(13557387039866084547)
XLA Ops:
  14.7 101.9 %front.1 = (bf16[576,2048]{1,0:T(8,128)(2,1)}, bf16[8,2048,256]{2,1,0:T(8,128)(2,1)}, bf16[8,256,2048]{2,1,0:T(8,128)(2,1)}, bf16[8,576,512]{2,1,0:T(8,128)(2,1)...) custom-call(s32[2,3]{1,0:T(2,128)} %pad_add_fusion.lens_ref, ...), custom_call_target="tpu_custom_call" | custom-call | flops 19327352832 | bytes 62914560 | tf_op jit(solution)/shard_map/front/pallas_call | solution.py:336
  116.6 184.7 %gated.1 = (bf16[4608,2048]{1,0:T(8,128)(2,1)}, bf16[4608,2048]{1,0:T(8,128)(2,1)}, bf16[4608,2048]{1,0:T(8,128)(2,1)}, bf16[4608,2048]{1,0:T(8,128)(2,1)}, bf16[4608,2048]{1,0:T(8,128)(2,1)}) custom-call(bf16[576,2048]{1,0:T(8,128)(2,1)} %get-tuple-element.68.z_own, bf16[576,2048]{1,0:T(8,128)(2,1)} %bitcast.90, bf16[2048,2048]{1,0:T(8,128)(2,1)} %wg_hbm.3, ...), custom_call_target="tpu_custom_call" | custom-call | flops 115964116992 | bytes 209715200 | tf_op jit(solution)/shard_map/gated/pallas_call | solution.py:561
  301.3 176.2 %back.1 = (f32[2,576,2048]{2,1,0:T(8,128)}, bf16[2,576,2048]{2,1,0:T(8,128)(2,1)}, bf16[2,576,2048]{2,1,0:T(8,128)(2,1)}, f32[2048,2048]{1,0:T(8,128)}) custom-call(bf16[4608,2048]{1,0:T(8,128)(2,1)} %get-tuple-element.99.act.a_ref, bf16[4608,2048]{1,0:T(8,128)(2,1)} %get-tuple-element.105.d_gate.b_ref, bf16[4608,2048]{1,0:T(8,128)(2,1)} %get-tuple-element.112.d_up.b_ref, ...), custom_call_target="tpu_custom_call" | custom-call | flops 115964116992 | bytes 209715200 | tf_op jit(solution)/shard_map/back/pallas_call | solution.py:784
  486.2 9.9 %join.1 = (bf16[576,2048]{1,0:T(8,128)(2,1)}, bf16[576,2048]{1,0:T(8,128)(2,1)S(1)}, f32[1,2048]{1,0:T(1,128)S(1)}) custom-call(f32[2,576,2048]{2,1,0:T(8,128)} %get-tuple-element.74.own_ref, bf16[2,576,2048]{2,1,0:T(8,128)(2,1)S(1)} %copy-done, bf16[2,576,2048]{2,1,0:T(8,128)(2,1)S(1)} %copy-done.1, bf16[576,2048]{1,0:T(8,128)(2,1)S(1)} %copy-done.5, ...), custom_call_target="tpu_custom_call" | custom-call | flops 47185920 | bytes 29360128 | tf_op jit(solution)/shard_map/join/pallas_call | solution.py:823
  496.2 10.5 %fusion.32 = f32[2048,2048]{1,0:T(8,128)} fusion(bf16[576,2048]{1,0:T(8,128)(2,1)S(1)} %copy-done.24, bf16[576,2048]{1,0:T(8,128)(2,1)S(1)} %get-tuple-element.81), kind=kOutput, calls=%fused_computation.82 | convolution fusion | flops 4831838208 | bytes 21495808 | tf_op jit(solution)/shard_map/dot_general | solution.py:50
  507.3 9.7 %convolution_convert_fusion.do_ref = bf16[576,2048]{1,0:T(8,128)(2,1)} fusion(bf16[576,2048]{1,0:T(8,128)(2,1)S(1)} %get-tuple-element.81, bf16[2048,2048]{1,0:T(8,128)(2,1)} %bitcast.105), kind=kOutput, calls=%fused_computation.16 | convolution fusion | flops 4833017856 | bytes 13107200 | tf_op jit(solution)/shard_map/dot_general | solution.py:46
  517.1 32.3 %attn_bwd.1 = (bf16[8,576,256]{2,1,0:T(8,128)(2,1)}, bf16[4,576,512]{2,1,0:T(8,128)(2,1)}, bf16[4,576,512]{2,1,0:T(8,128)(2,1)}) custom-call(s32[11,3]{1,0:T(8,128)} %add_add_fusion.2.lens_ref, f32[192,128]{1,0:T(8,128)} %get-tuple-element.178.cos_ref, f32[192,128]{1,0:T(8,128)} %get-tuple-element.177.sin_ref, bf16[8,576,256]{2,1,0:T(8,128)(2,1)} %get-tuple-element.83.q_ref, ...), custom_call_target="tpu_custom_call" | custom-call | flops 18119393280 | bytes 20971520 | tf_op jit(solution)/shard_map/attn_bwd/pallas_call | solution.py:362
  549.7 7.1 fusion.6
  557.1 6.9 convolution_bitcast_fusion
  564.6 2.6 collective-permute-start.2
  567.3 7.2 collective-permute-done.2
  579.8 3.5 convolution_add_fusion
  583.3 3.2 copy-done.7
  589.1 49.4 %weight_grad.2 = f32[2048,2048]{1,0:T(8,128)} custom-call(bf16[4608,2048]{1,0:T(8,128)(2,1)} %get-tuple-element.99.act.a_ref, bf16[4608,2048]{1,0:T(8,128)(2,1)} %get-tuple-element.100.b_ref), custom_call_target="tpu_custom_call" | custom-call | flops 38654705664 | bytes 115343360 | tf_op jit(solution)/shard_map/weight_grad/pallas_call | solution.py:842
  643.9 2.4 fusion.26
  646.3 2.5 bitcast_add_fusion.2
  655.7 3.4 add_convert_fusion.1
  659.1 34.9 %weight_grad_rest.1 = f32[2048,2048]{1,0:T(8,128)} custom-call(s32[1]{0:T(128)} %constant.8.clone.1.at_ref, bf16[4608,2048]{1,0:T(8,128)(2,1)} %get-tuple-element.72.z_all.a_ref, bf16[4608,2048]{1,0:T(8,128)(2,1)} %get-tuple-element.105.d_gate.b_ref, f32[2048,2048]{1,0:T(8,128)} %get-tuple-element.106.part_ref), custom_call_target="tpu_custom_call" | custom-call | flops 19327352832 | bytes 83886080 | tf_op jit(solution)/shard_map/weight_grad_rest/pallas_call | solution.py:861
  701.2 49.8 %weight_grad.3 = f32[2048,2048]{1,0:T(8,128)} custom-call(bf16[4608,2048]{1,0:T(8,128)(2,1)} %get-tuple-element.72.z_all.a_ref, bf16[4608,2048]{1,0:T(8,128)(2,1)} %get-tuple-element.112.d_up.b_ref), custom_call_target="tpu_custom_call" | custom-call | flops 38654705664 | bytes 115343360 | tf_op jit(solution)/shard_map/weight_grad/pallas_call | solution.py:842
  752.3 10.3 %collective-permute-done.11 = f32[256,2048]{1,0:T(8,128)} collective-permute-done((f32[256,2048]{1,0:T(8,128)}, f32[256,2048]{1,0:T(8,128)}, u32[]{:S(2)}, u32[]{:S(2)}) %collective-permute-start.11) | collective-permute-done | bytes 2097184 | tf_op jit(solution)/shard_map/ppermute | solution.py:54
  762.7 4.7 fusion.9
  767.7 2.5 add_convert_fusion
  772.6 85.9 %reduce-scatter.2.cloned.1.call-done = f32[256,2048]{1,0:T(8,128)} async-done(((f32[2048,2048]{1,0:T(8,128)}), f32[256,2048]{1,0:T(8,128)}) %reduce-scatter.2.cloned.1.call-update) | async-done | bytes 2097168 | tf_op jit(solution)/shard_map/reduce_scatter | solution.py:919
  858.5 3.0 copy.33
  (124 shorter events, 50.8 us)
Async XLA Ops:
  7.2 765.4 %all-reduce.5.cloned.1.call-start = ((), (), s32[]{:S(2)}) async-start(), calls=%async_computation.2 | async-start | bytes 8388608 | tf_op jit(solution)/shard_map/psum | solution.py:948
  486.2 9.9 %copy-start.24 = (bf16[576,2048]{1,0:T(8,128)(2,1)S(1)}, bf16[576,2048]{1,0:T(8,128)(2,1)}, u32[]{:S(2)}) copy-start(bf16[576,2048]{1,0:T(8,128)(2,1)} %get-tuple-element.79) | copy-start | bytes 7077892
  496.1 11.2 %copy-start.2 = (bf16[576,2048]{1,0:T(8,128)(2,1)}, bf16[576,2048]{1,0:T(8,128)(2,1)S(1)}, u32[]{:S(2)}) copy-start(bf16[576,2048]{1,0:T(8,128)(2,1)S(1)} %get-tuple-element.81) | copy-start | bytes 7077892
  496.1 10.5 %copy-start.20 = (s32[3]{0:T(128)S(1)}, s32[3]{0:T(128)}, u32[]{:S(2)}) copy-start(s32[3]{0:T(128)} %param.17) | copy-start | bytes 40
  496.1 10.5 %copy-start.21 = (s32[3]{0:T(128)S(1)}, s32[3]{0:T(128)}, u32[]{:S(2)}) copy-start(s32[3]{0:T(128)} %param.16) | copy-start | bytes 40
  496.1 10.5 %copy-start.22 = (s32[11]{0:T(128)S(1)}, s32[11]{0:T(128)}, u32[]{:S(2)}) copy-start(s32[11]{0:T(128)} %pad.21.clone) | copy-start | bytes 136
  496.2 10.5 %copy-start.23 = (s32[11]{0:T(128)S(1)}, s32[11]{0:T(128)}, u32[]{:S(2)}) copy-start(s32[11]{0:T(128)} %pad.20.clone) | copy-start | bytes 136
  517.1 32.6 %copy-start.9 = (bf16[576,2048]{1,0:T(8,128)(2,1)S(1)}, bf16[576,2048]{1,0:T(8,128)(2,1)}, u32[]{:S(2)}) copy-start(bf16[576,2048]{1,0:T(8,128)(2,1)} %get-tuple-element.89) | copy-start | bytes 7077892
  549.3 7.5 collective-permute-start
  556.8 22.9 %collective-permute-start.5 = (f32[4,256,2048]{2,1,0:T(8,128)}, f32[4,256,2048]{2,1,0:T(8,128)S(1)}, u32[]{:S(2)}, u32[]{:S(2)}) collective-permute-start(f32[4,256,2048]{2,1,0:T(8,128)} %fusion.6), channel_id=1, source_target_pairs={{0,1},{1,0},{2,3},{3,2},{4,5},{5,4},{6,7},{7,6},{8,9},{9,8},{10,11... | collective-permute-start | bytes 25165832 | tf_op jit(solution)/shard_map/ppermute | solution.py:54
  564.6 9.9 %collective-permute-start.2 = (bf16[288,512]{1,0:T(8,128)(2,1)S(1)}, bf16[288,512]{1,0:T(8,128)(2,1)S(1)}, u32[]{:S(2)}, u32[]{:S(2)}) collective-permute-start(bf16[288,512]{1,0:T(8,128)(2,1)S(1)} %get-tuple-element.173), channel_id=1, source_target_pairs={{0,4},{1,5},{2,6},{3,7},{4,0},{5,1},{6,2},{7,3},{8,12},{9,13},{10,... | collective-permute-start | bytes 884744 | tf_op jit(solution)/shard_map/ppermute | solution.py:54
  567.2 8.7 %collective-permute-start.1 = (bf16[288,512]{1,0:T(8,128)(2,1)S(1)}, bf16[288,512]{1,0:T(8,128)(2,1)S(1)}, u32[]{:S(2)}, u32[]{:S(2)}) collective-permute-start(bf16[288,512]{1,0:T(8,128)(2,1)S(1)} %get-tuple-element.174), channel_id=1, source_target_pairs={{0,2},{1,3},{2,0},{3,1},{4,6},{5,7},{6,4},{7,5},{8,10},{9,11},{10,... | collective-permute-start | bytes 884744 | tf_op jit(solution)/shard_map/ppermute | solution.py:54
  576.9 61.5 %collective-permute-start.3 = (bf16[576,512]{1,0:T(8,128)(2,1)}, bf16[576,512]{1,0:T(8,128)(2,1)}, u32[]{:S(2)}, u32[]{:S(2)}) collective-permute-start(bf16[576,512]{1,0:T(8,128)(2,1)} %pad_maximum_fusion.2), channel_id=1, source_target_pairs={{0,2},{1,3},{2,0},{3,1},{4,6},{5,7},{6,4},{7,5},{8,10},{9,11},{10,... | collective-permute-start | bytes 1769480 | tf_op jit(solution)/shard_map/ppermute | solution.py:54
  578.2 60.3 %collective-permute-start.4 = (bf16[576,512]{1,0:T(8,128)(2,1)}, bf16[576,512]{1,0:T(8,128)(2,1)}, u32[]{:S(2)}, u32[]{:S(2)}) collective-permute-start(bf16[576,512]{1,0:T(8,128)(2,1)} %pad_maximum_fusion.3), channel_id=1, source_target_pairs={{0,4},{1,5},{2,6},{3,7},{4,0},{5,1},{6,2},{7,3},{8,12},{9,13},{10,... | collective-permute-start | bytes 1769480 | tf_op jit(solution)/shard_map/ppermute | solution.py:54
  586.9 51.6 %collective-permute-start.7 = (f32[128,2048]{1,0:T(8,128)S(1)}, f32[128,2048]{1,0:T(8,128)}, u32[]{:S(2)}, u32[]{:S(2)}) collective-permute-start(f32[128,2048]{1,0:T(8,128)S(1)} %get-tuple-element.166), channel_id=1, source_target_pairs={{0,4},{1,5},{2,6},{3,7},{4,0},{5,1},{6,2},{7,3},{8,12},{9,13},{10,... | collective-permute-start | bytes 3145736 | tf_op jit(solution)/shard_map/ppermute | solution.py:54
  587.3 51.1 %collective-permute-start.6 = (f32[128,2048]{1,0:T(8,128)S(1)}, f32[128,2048]{1,0:T(8,128)S(1)}, u32[]{:S(2)}, u32[]{:S(2)}) collective-permute-start(f32[128,2048]{1,0:T(8,128)S(1)} %get-tuple-element.167), channel_id=1, source_target_pairs={{0,2},{1,3},{2,0},{3,1},{4,6},{5,7},{6,4},{7,5},{8,10},{9,11},{10,... | collective-permute-start | bytes 3145736 | tf_op jit(solution)/shard_map/ppermute | solution.py:54
  651.2 207.3 %reduce-scatter.2.cloned.1.call-start = ((), (), s32[]{:S(2)}) async-start(), calls=%async_computation.1 | async-start | bytes 18874368 | tf_op jit(solution)/shard_map/reduce_scatter | solution.py:919
  695.7 56.5 %collective-permute-start.10 = (f32[2,2048]{1,0:T(2,128)S(1)}, f32[2,2048]{1,0:T(2,128)S(1)}, u32[]{:S(2)}, u32[]{:S(2)}) collective-permute-start(f32[2,2048]{1,0:T(2,128)S(1)} %pad_maximum_fusion.4), channel_id=1, source_target_pairs={{0,6},{1,7},{2,4},{3,5},{4,2},{5,3},{6,0},{7,1},{8,14},{9,15},{10,... | collective-permute-start | bytes 49160 | tf_op jit(solution)/shard_map/ppermute | solution.py:54
  697.2 55.1 %collective-permute-start.9 = (f32[2,2048]{1,0:T(2,128)S(1)}, f32[2,2048]{1,0:T(2,128)S(1)}, u32[]{:S(2)}, u32[]{:S(2)}) collective-permute-start(f32[2,2048]{1,0:T(2,128)S(1)} %pad_maximum_fusion.4), channel_id=1, source_target_pairs={{0,4},{1,5},{2,6},{3,7},{4,0},{5,1},{6,2},{7,3},{8,12},{9,13},{10,... | collective-permute-start | bytes 49160 | tf_op jit(solution)/shard_map/ppermute | solution.py:54
  697.7 54.6 %collective-permute-start.8 = (f32[2,2048]{1,0:T(2,128)S(1)}, f32[2,2048]{1,0:T(2,128)S(1)}, u32[]{:S(2)}, u32[]{:S(2)}) collective-permute-start(f32[2,2048]{1,0:T(2,128)S(1)} %pad_maximum_fusion.4), channel_id=1, source_target_pairs={{0,2},{1,3},{2,0},{3,1},{4,6},{5,7},{6,4},{7,5},{8,10},{9,11},{10,... | collective-permute-start | bytes 49160 | tf_op jit(solution)/shard_map/ppermute | solution.py:54
  699.2 63.4 %collective-permute-start.11 = (f32[256,2048]{1,0:T(8,128)}, f32[256,2048]{1,0:T(8,128)}, u32[]{:S(2)}, u32[]{:S(2)}) collective-permute-start(f32[256,2048]{1,0:T(8,128)} %get-tuple-element.110), channel_id=1, source_target_pairs={{0,2},{1,3},{2,0},{3,1},{4,6},{5,7},{6,4},{7,5},{8,10},{9,11},{10,... | collective-permute-start | bytes 6291464 | tf_op jit(solution)/shard_map/ppermute | solution.py:54
  699.7 62.9 %collective-permute-start.12 = (f32[256,2048]{1,0:T(8,128)}, f32[256,2048]{1,0:T(8,128)}, u32[]{:S(2)}, u32[]{:S(2)}) collective-permute-start(f32[256,2048]{1,0:T(8,128)} %get-tuple-element.111), channel_id=1, source_target_pairs={{0,4},{1,5},{2,6},{3,7},{4,0},{5,1},{6,2},{7,3},{8,12},{9,13},{10,... | collective-permute-start | bytes 6291464 | tf_op jit(solution)/shard_map/ppermute | solution.py:54
  762.6 9.3 %collective-permute-start.13 = (f32[2,2048]{1,0:T(2,128)S(1)}, f32[2,2048]{1,0:T(2,128)S(1)}, u32[]{:S(2)}, u32[]{:S(2)}) collective-permute-start(f32[2,2048]{1,0:T(2,128)S(1)} %add_add_fusion.1), channel_id=1, source_target_pairs={{0,1},{1,0},{2,3},{3,2},{4,5},{5,4},{6,7},{7,6},{8,9},{9,8},{10,11... | collective-permute-start | bytes 49160 | tf_op jit(solution)/shard_map/ppermute | solution.py:54
  772.6 88.9 %copy-start.12 = (f32[2048,256]{1,0:T(8,128)S(1)}, f32[2048,256]{1,0:T(8,128)}, u32[]{:S(2)}) copy-start(f32[2048,256]{1,0:T(8,128)} %get-tuple-element.186) | copy-start | bytes 6291460
  (19 other events, 64.1 us)
Sparse Core Ops, SparseCore 0:
  651.3 92.4 all-reduce.4
  747.9 110.5 reduce-scatter.1

commit v8 on v7

--- a/solution.py
+++ b/solution.py
@@ -17,25 +17,12 @@
 TN = (((0,), (0,)), ((), ()))
 
 
-def rms_norm(x_in, gain):
-    x_f = x_in.astype(F32)
-    inv_rms = lax.rsqrt(jnp.mean(x_f * x_f, axis=-1, keepdims=True) + NORM_EPS)
-    return (x_f * inv_rms * (1.0 + gain)).astype(BF16)
-
-
 def rope_tables(positions, head_dim):
     half_dim = head_dim // 2
     exponent = jnp.arange(half_dim, dtype=F32) * (2.0 / head_dim)
     inv_freq = jnp.exp(exponent * (-math.log(10000.0)))
     angles = positions.astype(F32)[:, None] * inv_freq[None, :]
     return jnp.cos(angles), jnp.sin(angles)
-
-
-def apply_rope(x_f, cos_t, sin_t):
-    half_dim = x_f.shape[-1] // 2
-    first = x_f[..., :half_dim]
-    second = x_f[..., half_dim:]
-    return jnp.concatenate([first * cos_t - second * sin_t, second * cos_t + first * sin_t], axis=-1)
 
 
 def dot_nn(a, b):
@@ -131,7 +118,7 @@
                                         device_id={"tp": peer}, device_id_type=pl.DeviceIdType.MESH)
 
 
-def front_kernel(lens_ref, kpos_ref, cos_ref, sin_ref, gain1_ref, gain2_ref, hidden, w_query, w_key, w_value, w_out,
+def front_kernel(prefix_ref, valid_ref, kpos_ref, cos_ref, sin_ref, gain1_ref, gain2_ref, hidden, w_query, w_key, w_value, w_out,
                  normed_out, wq_all, wo_all, kv_all, query_out, mixed_out, resid_out, gated_out,
                  x_buf, n_buf, wkv, wq, wo, kv, q, probs, mix, acc, load, store, send, recv, *, batch):
     rows, dim = x_buf.shape
@@ -260,7 +247,7 @@
     def attend(i, carry):
         keys = kv[:, seq_rows(i), :head_dim].reshape(total, head_dim)
         values = kv[:, seq_rows(i), head_dim:].reshape(total, head_dim)
-        visible = kpos_ref[...] < jnp.minimum(lens_ref[1, i], jnp.maximum(lens_ref[0, i], q_pos + 1))
+        visible = kpos_ref[...] < jnp.minimum(valid_ref[i], jnp.maximum(prefix_ref[i], q_pos + 1))
         for g in range(2):
             query = q[g * near:(g + 1) * near, seq_rows(i), :].reshape(near * shard, head_dim) * BF16(head_dim ** -0.5)
             scores = dot_nt(query, keys)
@@ -321,7 +308,7 @@
             to_core(a, k).wait_send()
 
 
-def front_layer(lens, k_pos, cos_t, sin_t, attn_norm, mlp_norm, hidden, w_query, w_key, w_value, w_out, batch, tp):
+def front_layer(prefix_len, valid_len, k_pos, cos_t, sin_t, attn_norm, mlp_norm, hidden, w_query, w_key, w_value, w_out, batch, tp):
     rows, dim = hidden.shape
     head_dim = w_key.shape[1]
     shard = rows // batch
@@ -337,7 +324,7 @@
         functools.partial(front_kernel, batch=batch),
         out_shape=(shape(rows, dim), shape(tp, dim, head_dim), shape(tp, head_dim, dim), shape(tp, rows, 2 * head_dim),
                    shape(tp, rows, head_dim), shape(rows, tp * head_dim), shape(rows, dim), shape(rows, dim)),
-        in_specs=[pl.BlockSpec(memory_space=pltpu.SMEM)] + [vmem] * 5 + [anyspace] * 5,
+        in_specs=[pl.BlockSpec(memory_space=pltpu.SMEM)] * 2 + [vmem] * 5 + [anyspace] * 5,
         out_specs=(anyspace,) * 8,
         scratch_shapes=[pltpu.VMEM((rows, dim), BF16), pltpu.VMEM((rows, dim), BF16), pltpu.VMEM((dim, 2 * head_dim), BF16),
                         pltpu.VMEM((tp, dim, head_dim), BF16), pltpu.VMEM((tp, head_dim, dim), BF16),
@@ -347,7 +334,7 @@
         compiler_params=pltpu.CompilerParams(vmem_limit_bytes=62 << 20, collective_id=2, has_side_effects=True),
         cost_estimate=pl.CostEstimate(flops=8 * rows * dim * tp * head_dim, bytes_accessed=60 << 20, transcendentals=tp * rows * total),
         name="front",
-    )(lens, k_pos, cos_t, sin_t, attn_norm.reshape(1, dim), mlp_norm.reshape(1, dim), hidden, w_query, w_key, w_value, w_out)
+    )(prefix_len, valid_len, k_pos, cos_t, sin_t, attn_norm.reshape(1, dim), mlp_norm.reshape(1, dim), hidden, w_query, w_key, w_value, w_out)
 
 
 def attention_backward(lens, cos_t, sin_t, query, kv_all, d_mixed, batch, group=8):
@@ -367,7 +354,7 @@
             in_specs=[table, table, q_spec, pl.BlockSpec((2 * near, shard, 2 * head_dim), lambda s, g, *_: (0, s, 0)), pl.BlockSpec((shard, group * head_dim), lambda s, g, *_: (s, g))],
             out_specs=(q_spec, kv_spec, kv_spec),
             scratch_shapes=[pltpu.VMEM((total, 2 * head_dim), F32)]),
-        compiler_params=pltpu.CompilerParams(dimension_semantics=("arbitrary", "arbitrary"), vmem_limit_bytes=56 << 20),
+        compiler_params=pltpu.CompilerParams(dimension_semantics=("arbitrary", "arbitrary"), vmem_limit_bytes=62 << 20),
         cost_estimate=pl.CostEstimate(flops=10 * heads * rows * total * head_dim, bytes_accessed=20 << 20, transcendentals=heads * rows * total),
         name="attn_bwd",
     )(lens, cos_t, sin_t, query, kv_all, d_mixed)
@@ -797,46 +784,122 @@
     )(act, d_gate, d_up, z_all, w_gate, w_up, w_down)
 
 
-def join_kernel(own_ref, x_ref, y_ref, resid_ref, grad_ref, gain_ref, out_ref, d_resid_ref, g_gain_ref):
-    mlp_sum, d_gated = [own_ref[k] + x_ref[k].astype(F32) + y_ref[k].astype(F32) for k in range(2)]
-    resid = resid_ref[...].astype(F32)
-    out_ref[...] = (resid + mlp_sum).astype(BF16)
-    d_gated = d_gated.astype(BF16).astype(F32)
-    inv_rms = lax.rsqrt(jnp.mean(resid * resid, axis=-1, keepdims=True) + NORM_EPS)
-    unit = resid * inv_rms
-    scaled = d_gated * (1.0 + gain_ref[...].astype(F32))
-    d_norm = inv_rms * (scaled - unit * jnp.mean(unit * scaled, axis=-1, keepdims=True))
-    d_resid_ref[...] = (grad_ref[...].astype(F32) + d_norm).astype(BF16)
+def norm_back(x, gain, d_out):
+    inv_rms = lax.rsqrt(jnp.mean(x * x, axis=-1, keepdims=True) + NORM_EPS)
+    unit = x * inv_rms
+    scaled = d_out * (1.0 + gain.astype(F32))
+    return inv_rms * (scaled - unit * jnp.mean(unit * scaled, axis=-1, keepdims=True)), d_out * unit
+
+
+def join_kernel(own_ref, x_ref, y_ref, resid_ref, grad_ref, gain_ref, wo_ref, mixed_ref,
+                out_ref, d_resid_ref, g_gain_ref, d_mixed_ref, g_out_ref, keep, *, joins):
+    step = pl.program_id(0)
+    bm = resid_ref.shape[0]
+
+    @pl.when(step == 0)
+    def _():
+        g_gain_ref[...] = jnp.zeros_like(g_gain_ref)
+
+    @pl.when(step < joins)
+    def _():
+        mlp_sum, d_gated = [own_ref[k] + x_ref[k].astype(F32) + y_ref[k].astype(F32) for k in range(2)]
+        resid = resid_ref[...].astype(F32)
+        out_ref[...] = (resid + mlp_sum).astype(BF16)
+        d_norm, terms = norm_back(resid, gain_ref[...], d_gated.astype(BF16).astype(F32))
+        d_resid = (grad_ref[...].astype(F32) + d_norm).astype(BF16)
+        d_resid_ref[...] = d_resid
+        keep[pl.ds(pl.multiple_of(step * bm, 16), bm), :] = d_resid
+        g_gain_ref[...] += jnp.sum(terms, axis=0, keepdims=True)
+
+    @pl.when(step >= joins)
+    def _():
+        d_mixed_ref[...] = dot_nt(keep[...], wo_ref[...]).astype(BF16)
+        g_out_ref[...] = dot_tn(mixed_ref[...], keep[...])
+
+
+def join_layer(own_part, x_part, y_part, resid, grad_out, gain, wo_all, mixed, bm=96, bn=512):
+    rows, dim = resid.shape
+    width = mixed.shape[1]
+    joins = rows // bm
+    pair = pl.BlockSpec((2, bm, dim), lambda i: (0, jnp.minimum(i, joins - 1), 0))
+    row = pl.BlockSpec((bm, dim), lambda i: (jnp.minimum(i, joins - 1), 0))
+    one = pl.BlockSpec((1, dim), lambda i: (0, 0))
+    col = pl.BlockSpec((rows, bn), lambda i: (0, jnp.maximum(i - joins, 0)))
+    block = pl.BlockSpec((bn, dim), lambda i: (jnp.maximum(i - joins, 0), 0))
+    act = jax.ShapeDtypeStruct((rows, dim), BF16)
+    return pl.pallas_call(
+        functools.partial(join_kernel, joins=joins),
+        out_shape=(act, act, jax.ShapeDtypeStruct((1, dim), F32), jax.ShapeDtypeStruct((rows, width), BF16),
+                   jax.ShapeDtypeStruct((width, dim), F32)),
+        grid=(joins + width // bn,),
+        in_specs=[pair, pair, pair, row, row, one, block, col],
+        out_specs=(row, row, one, col, block),
+        scratch_shapes=[pltpu.VMEM((rows, dim), BF16)],
+        compiler_params=pltpu.CompilerParams(dimension_semantics=("arbitrary",), vmem_limit_bytes=62 << 20),
+        cost_estimate=pl.CostEstimate(flops=4 * rows * dim * width, bytes_accessed=60 << 20, transcendentals=rows),
+        name="join",
+    )(own_part, x_part, y_part, resid, grad_out, gain.reshape(1, dim), wo_all, mixed)
+
+
+def finish_kernel(kv_ref, side_ref, back_ref, cos_ref, sin_ref, normed_ref, wk_ref, wv_ref, part_ref, hidden_ref, d_resid_ref, gain_ref,
+                  g_key_ref, g_value_ref, out_ref, g_gain_ref):
+    head_dim = wk_ref.shape[1]
+    half_dim = head_dim // 2
+    d_kv = (kv_ref[...] + side_ref[...].astype(F32) + back_ref[...].astype(F32)).astype(BF16)
+    first, second = d_kv[:, :half_dim].astype(F32), d_kv[:, half_dim:head_dim].astype(F32)
+    cos_t, sin_t = cos_ref[...], sin_ref[...]
+    d_key = jnp.concatenate([first * cos_t + second * sin_t, second * cos_t - first * sin_t], axis=1).astype(BF16)
+    d_value = d_kv[:, head_dim:]
+    d_normed = (part_ref[...] + dot_nt(d_key, wk_ref[...]) + dot_nt(d_value, wv_ref[...])).astype(BF16).astype(F32)
+    d_norm, terms = norm_back(hidden_ref[...].astype(F32), gain_ref[...], d_normed)
+    out_ref[...] = (d_resid_ref[...].astype(F32) + d_norm).astype(BF16)
+    g_key = dot_tn(normed_ref[...], d_key)
+    g_value = dot_tn(normed_ref[...], d_value)
+    g_gain = jnp.sum(terms, axis=0, keepdims=True)
 
     @pl.when(pl.program_id(0) == 0)
     def _():
-        g_gain_ref[...] = jnp.zeros_like(g_gain_ref)
-
-    g_gain_ref[...] += jnp.sum(d_gated * unit, axis=0, keepdims=True)
-
-
-def join_layer(own_part, x_part, y_part, resid, grad_out, gain, bm=96):
-    rows, dim = resid.shape
-    pair = pl.BlockSpec((2, bm, dim), lambda i: (0, i, 0))
-    row = pl.BlockSpec((bm, dim), lambda i: (i, 0))
-    one = pl.BlockSpec((1, dim), lambda i: (0, 0))
+        g_key_ref[...] = g_key
+        g_value_ref[...] = g_value
+        g_gain_ref[...] = g_gain
+
+    @pl.when(pl.program_id(0) > 0)
+    def _():
+        g_key_ref[...] += g_key
+        g_value_ref[...] += g_value
+        g_gain_ref[...] += g_gain
+
+
+def finish_layer(kv_own, kv_side, kv_back, cos_t, sin_t, normed, w_key, w_value, part, hidden, d_resid, gain):
+    rows, dim = hidden.shape
+    shard, half_dim = cos_t.shape
+    head_dim = w_key.shape[1]
+
+    def row(width):
+        return pl.BlockSpec((shard, width), lambda i: (i, 0))
+
+    def whole(*shape):
+        return pl.BlockSpec(shape, lambda i: (0, 0))
+
+    kv, act, table, weight, one = row(2 * head_dim), row(dim), whole(shard, half_dim), whole(dim, head_dim), whole(1, dim)
+    grad = jax.ShapeDtypeStruct((dim, head_dim), F32)
     return pl.pallas_call(
-        join_kernel,
-        out_shape=(jax.ShapeDtypeStruct((rows, dim), BF16), jax.ShapeDtypeStruct((rows, dim), BF16), jax.ShapeDtypeStruct((1, dim), F32)),
-        grid=(rows // bm,),
-        in_specs=[pair, pair, pair, row, row, one],
-        out_specs=(row, row, one),
-        compiler_params=pltpu.CompilerParams(dimension_semantics=("arbitrary",), vmem_limit_bytes=32 << 20),
-        cost_estimate=pl.CostEstimate(flops=40 * rows * dim, bytes_accessed=28 << 20, transcendentals=rows),
-        name="join",
-    )(own_part, x_part, y_part, resid, grad_out, gain.reshape(1, dim))
+        finish_kernel,
+        out_shape=(grad, grad, jax.ShapeDtypeStruct((rows, dim), BF16), jax.ShapeDtypeStruct((1, dim), F32)),
+        grid=(rows // shard,),
+        in_specs=[kv, kv, kv, table, table, act, weight, weight, act, act, act, one],
+        out_specs=(weight, weight, act, one),
+        compiler_params=pltpu.CompilerParams(dimension_semantics=("arbitrary",), vmem_limit_bytes=62 << 20),
+        cost_estimate=pl.CostEstimate(flops=8 * rows * dim * head_dim, bytes_accessed=24 << 20, transcendentals=rows),
+        name="finish",
+    )(kv_own, kv_side, kv_back, cos_t, sin_t, normed, w_key, w_value, part, hidden, d_resid, gain.reshape(1, dim))
 
 
 def product_kernel(a_ref, b_ref, o_ref):
     o_ref[...] = dot_tn(a_ref[...], b_ref[...])
 
 
-def weight_grad(a, b, bm=512, bn=1024):
+def weight_grad(a, b, bm=1024, bn=512):
     rows, m = a.shape
     n = b.shape[1]
     return pl.pallas_call(
@@ -845,7 +908,7 @@
         grid=(m // bm, n // bn),
         in_specs=[pl.BlockSpec((rows, bm), lambda i, j: (0, i)), pl.BlockSpec((rows, bn), lambda i, j: (0, j))],
         out_specs=pl.BlockSpec((bm, bn), lambda i, j: (i, j)),
-        compiler_params=pltpu.CompilerParams(dimension_semantics=("arbitrary", "arbitrary"), vmem_limit_bytes=56 << 20),
+        compiler_params=pltpu.CompilerParams(dimension_semantics=("arbitrary", "arbitrary"), vmem_limit_bytes=62 << 20),
         cost_estimate=pl.CostEstimate(flops=2 * rows * m * n, bytes_accessed=110 << 20, transcendentals=0),
         name="weight_grad",
     )(a, b)
@@ -855,7 +918,7 @@
     o_ref[...] = part_ref[...] + dot_tn(a_ref[...], b_ref[...])
 
 
-def weight_grad_rest(a, b, part, block, count, bm=512, bn=1024):
+def weight_grad_rest(a, b, part, block, count, bm=1024, bn=512):
     m, n = part.shape
     out = pl.BlockSpec((bm, bn), lambda i, j, at: (i, j))
     return pl.pallas_call(
@@ -865,7 +928,7 @@
             num_scalar_prefetch=1, grid=(m // bm, n // bn),
             in_specs=[pl.BlockSpec((count, bm), lambda i, j, at: (at[0], i)), pl.BlockSpec((count, bn), lambda i, j, at: (at[0], j)), out],
             out_specs=out),
-        compiler_params=pltpu.CompilerParams(dimension_semantics=("arbitrary", "arbitrary"), vmem_limit_bytes=56 << 20),
+        compiler_params=pltpu.CompilerParams(dimension_semantics=("arbitrary", "arbitrary"), vmem_limit_bytes=62 << 20),
         cost_estimate=pl.CostEstimate(flops=2 * count * m * n, bytes_accessed=80 << 20, transcendentals=0),
         name="weight_grad_rest",
     )(jnp.asarray(block, jnp.int32).reshape(1), a, b, part)
@@ -897,28 +960,20 @@
         me = lax.axis_index("tp")
         starts = (me ^ jnp.array([0, 2, 4, 6, 1, 3, 5, 7], jnp.int32)) * shard
         k_pos = (starts[:, None] + jnp.arange(shard, dtype=jnp.int32)).reshape(1, tp_size * shard)
-        lens = jnp.stack([prefix_len, valid_len])
         cos_own, sin_own = rope_tables(me * shard + jnp.arange(shard), head_dim)
         hidden = hidden.reshape(rows, dim)
         grad_out = grad_out.reshape(rows, dim)
         normed, wq_all, wo_all, kv_all, query, mixed, resid, gated_in = front_layer(
-            lens, k_pos, cos_own, sin_own, attn_norm, mlp_norm, hidden, w_query, w_key, w_value, w_out, batch, tp_size)
+            prefix_len, valid_len, k_pos, cos_own, sin_own, attn_norm, mlp_norm, hidden, w_query, w_key, w_value, w_out, batch, tp_size)
         wo_all = wo_all.reshape(tp_size * head_dim, dim)
-
-        def rope(raw_proj):
-            return apply_rope(raw_proj, jnp.tile(cos_own, (batch, 1)), jnp.tile(sin_own, (batch, 1)))
 
         gated_all, grad_all, act, d_gate, d_upper = gated_layer(gated_in, grad_out, w_gate, w_up, w_down, tp_size)
         own_part, x_part, y_part, g_gate_part = back_layer(act, d_gate, d_upper, gated_all, w_gate, w_up, w_down, tp_size)
-        hidden, own_part = lax.optimization_barrier((hidden, own_part))
-        norm1_pull = jax.vjp(rms_norm, hidden, attn_norm.astype(F32))[1]
-        key_pull = jax.linear_transpose(rope, jax.ShapeDtypeStruct((rows, head_dim), F32))
-        hidden_out, d_resid, g_mlp_norm_part = join_layer(own_part, x_part, y_part, resid, grad_out, mlp_norm)
-        g_out_part = dot_tn(mixed, d_resid)
-        g_out_part, d_resid = lax.optimization_barrier((g_out_part, d_resid))
+        hidden_out, d_resid, g_mlp_norm_part, d_mixed, g_out_part = join_layer(
+            own_part, x_part, y_part, resid, grad_out, mlp_norm, wo_all, mixed)
         g_out = lax.psum_scatter(g_out_part, "tp", scatter_dimension=0, tiled=True)
-        d_mixed = dot_nt(d_resid, wo_all).astype(BF16)
-        lens_back = jnp.concatenate([lens, jnp.full((1, batch), me, jnp.int32), jnp.broadcast_to(starts[:, None], (tp_size, batch))])
+        lens_back = jnp.concatenate([jnp.stack([prefix_len, valid_len, jnp.full((batch,), me, jnp.int32)]),
+                                     jnp.broadcast_to(starts[:, None], (tp_size, batch))])
         d_q_raw, dkv_near, dkv_far = attention_backward(lens_back, cos_own, sin_own, query, kv_all, d_mixed, batch)
         near = tp_size // 2
         came_kv = swap(dkv_far, 1)
@@ -937,28 +992,24 @@
         q_came = hop_diagonal(g_query_sum[3])
         g_down = weight_grad(act, grad_all)
         kv_last, q_came, g_down = lax.optimization_barrier((kv_last, q_came, g_down))
-        d_kv = (kv_own + kv_last[0].astype(F32) + kv_last[1].astype(F32)).astype(BF16)
-        d_k_raw = key_pull(d_kv[:, :head_dim].astype(F32))[0].astype(BF16)
-        d_values = d_kv[:, head_dim:]
         q_next = hop_near(g_query_sum[1], g_query_sum[2], *q_came)
-        g_key_part, g_value_part = dot_tn(normed, d_k_raw), dot_tn(normed, d_values)
-        q_next, g_key_part, g_value_part, d_gate = lax.optimization_barrier((q_next, g_key_part, g_value_part, d_gate))
+        g_key_part, g_value_part, grad_hidden, g_attn_norm_part = finish_layer(
+            kv_own, kv_last[0], kv_last[1], cos_own, sin_own, normed, w_key, w_value, d_normed_q, hidden, d_resid, attn_norm)
+        norms = jnp.concatenate([g_attn_norm_part, g_mlp_norm_part])
+        q_next, g_key_part, g_value_part, norms, d_gate = lax.optimization_barrier((q_next, g_key_part, g_value_part, norms, d_gate))
+        g_key, g_value = lax.psum((g_key_part, g_value_part), "tp")
         last_side = swap(q_next[0], 2)
         q_last = (last_side, swap(q_next[1], 4))
-        g_key, g_value = lax.psum((g_key_part, g_value_part), "tp")
+        norms_near = [swap(norms, bit) for bit in (2, 4, 6)]
         g_gate = weight_grad_rest(gated_all, d_gate, g_gate_part, 1, 4 * rows)
-        d_normed = (d_normed_q + dot_nt(d_k_raw, w_key) + dot_nt(d_values, w_value)).astype(BF16)
-        d_normed, g_gate = lax.optimization_barrier((d_normed, g_gate))
-        d_hidden_norm, g_attn_norm_part = norm1_pull(d_normed)
-        norms = jnp.concatenate([g_attn_norm_part.reshape(1, dim), g_mlp_norm_part])
+        norms_near, g_gate, d_upper = lax.optimization_barrier((norms_near, g_gate, d_upper))
+        norms = norms + norms_near[0] + norms_near[1] + norms_near[2]
         norms, d_upper = lax.optimization_barrier((norms, d_upper))
-        norms_near = [swap(norms, bit) for bit in (2, 4, 6)]
+        norms_core = swap(norms, 1)
         g_up = weight_grad(gated_all, d_upper)
-        norms_near, q_last, g_up, d_hidden_norm = lax.optimization_barrier((norms_near, q_last, g_up, d_hidden_norm))
-        norms = norms + norms_near[0] + norms_near[1] + norms_near[2]
-        g_norms = norms + swap(norms, 1)
+        norms_core, q_last, g_up = lax.optimization_barrier((norms_core, q_last, g_up))
+        g_norms = norms + norms_core
         g_query = (g_query_sum[0] + q_last[0] + q_last[1]).T
-        grad_hidden = (d_resid.astype(F32) + d_hidden_norm.astype(F32)).astype(BF16)
         full = (batch, shard, dim)
         return (hidden_out.reshape(full), grad_hidden.reshape(full), g_norms[0], g_query, g_key, g_value, g_out, g_norms[1], g_gate, g_up, g_down)
 

time: 878 us -> 884 us (level)
  waiting for transfers between devices: 106 us -> 135 us
  matrix products: 46.7 us -> 19.5 us
  Pallas kernels: 639 us -> 662 us
  local copies, waits for them, and re-layouts: 27.3 us -> 16.5 us
    pallas_call x1 -> x2, Pallas kernels: 9.86 us -> 40.9 us  [the longest x1 28.2 us: join_layer(): pl.pallas_call(functools.partial(join_kernel, joins=joins), out_shape=(ac...]
    dot_general x6 -> x0, matrix products: 29.2 us -> none  [the longest x3 15.3 us: dot_tn(): return lax.dot_general(a, b, TN, preferred_element_type=F32)]
    reduce_scatter x1, waiting for transfers between devices: 85.9 us -> 115 us  [layer(): g_out = lax.psum_scatter(g_out_part, 'tp', scatter_dimension=0, tiled=True)]
    unnamed x57 -> x19, local copies, waits for them, and re-layouts: 21.8 us -> 9.33 us
    psum x1, waiting for transfers between devices: 0.01 us -> 10.8 us  [layer(): g_key, g_value = lax.psum((g_key_part, g_value_part), 'tp')]
    ppermute x14, waiting for transfers between devices: 19 us -> 8.49 us  [swap(): return lax.ppermute(x, 'tp', [(t, t ^ bit) for t in range(8)])]
  transfers between devices with their start and end apart: 16 -> 16, of which waited for: 4 -> 4; matrix products, arithmetic and copies ran while one was open for 4% -> 4% of each run, Pallas kernels for 15% -> 14%
where the time goes in v8:
time: 884 us; the launch traced here: 877 us
  Pallas kernels  662 us (75%)
  waiting for transfers between devices  135 us (15%)
  matrix products  19.5 us (2%)
  local copies, waits for them, and re-layouts  16.5 us (2%)
  other arithmetic  16.2 us (2%)
  between operations  14.5 us (2%)
  starting transfers between devices  13.1 us (1%)
    pallas_call x1, Pallas kernels, gated_layer(): pl.pallas_call(functools.partial(gated_kernel, bn=bn), out_shape=(gathere...  185 us
    pallas_call x1, Pallas kernels, back_layer(): pl.pallas_call(functools.partial(back_kernel, rows=rows, bn=bn), out_shap...  176 us
    reduce_scatter x1, waiting for transfers between devices, layer(): g_out = lax.psum_scatter(g_out_part, 'tp', scatter_dimension=0, tiled=True)  115 us
    pallas_call x1, Pallas kernels, front_layer(): pl.pallas_call(functools.partial(front_kernel, batch=batch), out_shape=(s...  102 us
    pallas_call x2, Pallas kernels, weight_grad(): pl.pallas_call(product_kernel, out_shape=jax.ShapeDtypeStruct((m, n), F32...  96 us
    pallas_call x1, Pallas kernels, attention_backward(): pl.pallas_call(attn_bwd_kernel, out_shape=(jax.ShapeDtypeStruct((heads, r...  32.3 us
    pallas_call x1, Pallas kernels, weight_grad_rest(): pl.pallas_call(rest_kernel, out_shape=jax.ShapeDtypeStruct((m, n), F32),...  30.1 us
    pallas_call x1, Pallas kernels, join_layer(): pl.pallas_call(functools.partial(join_kernel, joins=joins), out_shape=(ac...  28.2 us
  transfers between devices with their start and end apart: 16, of which 4 were waited for; matrix products, arithmetic and copies ran while one was open for 4% of the time, Pallas kernels for 14%

profile of v8, /device:TPU:0, one launch (start us, length us, event | category | flops | bytes accessed | tf_op | source)
XLA Modules:
  0.0 876.6 jit_solution(5757012783043877491)
XLA Ops:
  13.5 101.8 %front.1 = (bf16[576,2048]{1,0:T(8,128)(2,1)}, bf16[8,2048,256]{2,1,0:T(8,128)(2,1)}, bf16[8,256,2048]{2,1,0:T(8,128)(2,1)}, bf16[8,576,512]{2,1,0:T(8,128)(2,1)...) custom-call(s32[3]{0:T(128)} %prefix_ref.1, ...), custom_call_target="tpu_custom_call" | custom-call | flops 19327352832 | bytes 62914560 | tf_op jit(solution)/shard_map/front/pallas_call | solution.py:323
  115.3 184.8 %gated.1 = (bf16[4608,2048]{1,0:T(8,128)(2,1)}, bf16[4608,2048]{1,0:T(8,128)(2,1)}, bf16[4608,2048]{1,0:T(8,128)(2,1)}, bf16[4608,2048]{1,0:T(8,128)(2,1)}, bf16[4608,2048]{1,0:T(8,128)(2,1)}) custom-call(bf16[576,2048]{1,0:T(8,128)(2,1)} %get-tuple-element.71.z_own, bf16[576,2048]{1,0:T(8,128)(2,1)} %bitcast.69, bf16[2048,2048]{1,0:T(8,128)(2,1)} %wg_hbm.3, ...), custom_call_target="tpu_custom_call" | custom-call | flops 115964116992 | bytes 209715200 | tf_op jit(solution)/shard_map/gated/pallas_call | solution.py:548
  300.1 176.3 %back.1 = (f32[2,576,2048]{2,1,0:T(8,128)}, bf16[2,576,2048]{2,1,0:T(8,128)(2,1)}, bf16[2,576,2048]{2,1,0:T(8,128)(2,1)}, f32[2048,2048]{1,0:T(8,128)}) custom-call(bf16[4608,2048]{1,0:T(8,128)(2,1)} %get-tuple-element.98.act.a_ref, bf16[4608,2048]{1,0:T(8,128)(2,1)} %get-tuple-element.112.d_gate.b_ref, bf16[4608,2048]{1,0:T(8,128)(2,1)} %get-tuple-element.121.d_up.b_ref, ...), custom_call_target="tpu_custom_call" | custom-call | flops 115964116992 | bytes 209715200 | tf_op jit(solution)/shard_map/back/pallas_call | solution.py:771
  477.7 28.2 %join.1 = (bf16[576,2048]{1,0:T(8,128)(2,1)}, bf16[576,2048]{1,0:T(8,128)(2,1)}, f32[1,2048]{1,0:T(1,128)}, bf16[576,2048]{1,0:T(8,128)(2,1)}, f32[2048,2048]{1,0:T(8,128)}) custom-call(f32[2,576,2048]{2,1,0:T(8,128)} %get-tuple-element.76.own_ref, bf16[2,576,2048]{2,1,0:T(8,128)(2,1)} %get-tuple-element.77.x_ref, ...), custom_call_target="tpu_custom_call" | custom-call | flops 9663676416 | bytes 62914560 | tf_op jit(solution)/shard_map/join/pallas_call | solution.py:830
  505.9 32.3 %attn_bwd.1 = (bf16[8,576,256]{2,1,0:T(8,128)(2,1)}, bf16[4,576,512]{2,1,0:T(8,128)(2,1)}, bf16[4,576,512]{2,1,0:T(8,128)(2,1)}) custom-call(s32[11,3]{1,0:T(8,128)} %add_add_fusion.1.lens_ref, f32[192,128]{1,0:T(8,128)} %get-tuple-element.181.cos_ref, f32[192,128]{1,0:T(8,128)} %get-tuple-element.180.sin_ref, bf16[8,576,256]{2,1,0:T(8,128)(2,1)} %get-tuple-element.83.q_ref, ...), custom_call_target="tpu_custom_call" | custom-call | flops 18119393280 | bytes 20971520 | tf_op jit(solution)/shard_map/attn_bwd/pallas_call | solution.py:349
  538.6 5.7 fusion.1
  544.7 10.2 %convolution_bitcast_fusion.part_ref = f32[576,2048]{1,0:T(8,128)} fusion(bf16[8,576,256]{2,1,0:T(8,128)(2,1)S(1)} %copy-done.6, bf16[8,2048,256]{2,1,0:T(8,128)(2,1)} %get-tuple-element.91), kind=kOutput, calls=%fused_computation.1 | convolution fusion | flops 4831838208 | bytes 15466496 | tf_op jit(solution)/shard_map/hte,hde->td/dot_general | solution.py:985
  556.7 2.5 collective-permute-start.1
  559.4 7.0 collective-permute-done.1
  572.0 3.5 convolution_add_fusion
  575.6 1.9 slice_bitcast_fusion
  577.5 2.3 copy-done
  581.7 48.1 %weight_grad.2 = f32[2048,2048]{1,0:T(8,128)} custom-call(bf16[4608,2048]{1,0:T(8,128)(2,1)} %get-tuple-element.98.act.a_ref, bf16[4608,2048]{1,0:T(8,128)(2,1)} %get-tuple-element.99.b_ref), custom_call_target="tpu_custom_call" | custom-call | flops 38654705664 | bytes 115343360 | tf_op jit(solution)/shard_map/weight_grad/pallas_call | solution.py:905
  630.6 12.7 %finish.1 = (f32[2048,256]{1,0:T(8,128)}, f32[2048,256]{1,0:T(8,128)}, bf16[576,2048]{1,0:T(8,128)(2,1)}, f32[1,2048]{1,0:T(1,128)}) custom-call(f32[576,512]{1,0:T(8,128)} %get-tuple-element.175.kv_ref, bf16[576,512]{1,0:T(8,128)(2,1)} %collective-permute-done.3.side_ref, bf16[576,512]{1,0:T(8,128)(2,1)} %copy-done.5, ...), custom_call_target="tpu_custom_call" | custom-call | flops 2415919104 | bytes 25165824 | tf_op jit(solution)/shard_map/finish/pallas_call | solution.py:886
  644.0 2.6 bitcast_add_fusion.1
  646.6 2.5 pad_maximum_fusion
  653.9 1.7 collective-permute-start.13
  655.6 30.1 %weight_grad_rest.1 = f32[2048,2048]{1,0:T(8,128)} custom-call(s32[1]{0:T(128)} %constant.3.clone.1.at_ref, bf16[4608,2048]{1,0:T(8,128)(2,1)} %get-tuple-element.75.z_all.a_ref, bf16[4608,2048]{1,0:T(8,128)(2,1)} %get-tuple-element.112.d_gate.b_ref, f32[2048,2048]{1,0:T(8,128)} %get-tuple-element.113.part_ref), custom_call_target="tpu_custom_call" | custom-call | flops 19327352832 | bytes 83886080 | tf_op jit(solution)/shard_map/weight_grad_rest/pallas_call | solution.py:924
  685.8 48.0 %weight_grad.3 = f32[2048,2048]{1,0:T(8,128)} custom-call(bf16[4608,2048]{1,0:T(8,128)(2,1)} %get-tuple-element.75.z_all.a_ref, bf16[4608,2048]{1,0:T(8,128)(2,1)} %get-tuple-element.121.d_up.b_ref), custom_call_target="tpu_custom_call" | custom-call | flops 38654705664 | bytes 115343360 | tf_op jit(solution)/shard_map/weight_grad/pallas_call | solution.py:905
  733.8 3.4 fusion.4
  737.2 1.8 copy.30
  739.7 10.8 %all-reduce.3.cloned.1.call-done = (f32[2048,256]{1,0:T(8,128)}, f32[2048,256]{1,0:T(8,128)}) async-done(((f32[2048,256]{1,0:T(8,128)}, f32[2048,256]{1,0:T(8,128)}), (f32[2048,256]{1,0:T(8,128)}, f32[2048,256]{1,0:T(8,128)})) %all-reduce.3.cloned.1.call-update) | async-done | bytes 4194320 | tf_op jit(solution)/shard_map/psum | solution.py:1000
  750.4 114.8 %reduce-scatter.2.cloned.1.call-done = f32[256,2048]{1,0:T(8,128)} async-done(((f32[2048,2048]{1,0:T(8,128)}), f32[256,2048]{1,0:T(8,128)}) %reduce-scatter.2.cloned.1.call-update) | async-done | bytes 2097168 | tf_op jit(solution)/shard_map/reduce_scatter | solution.py:974
  865.2 3.0 copy.33
  (69 shorter events, 26.1 us)
Async XLA Ops:
  7.2 743.3 %all-reduce.3.cloned.1.call-start = ((), (), s32[]{:S(2)}) async-start(), calls=%async_computation.2 | async-start | bytes 8388608 | tf_op jit(solution)/shard_map/psum | solution.py:1000
  538.3 6.0 collective-permute-start
  538.6 5.9 copy-start.6
  544.3 27.7 %collective-permute-start.5 = (f32[4,256,2048]{2,1,0:T(8,128)S(1)}, f32[4,256,2048]{2,1,0:T(8,128)S(1)}, u32[]{:S(2)}, u32[]{:S(2)}) collective-permute-start(f32[4,256,2048]{2,1,0:T(8,128)S(1)} %fusion.1), channel_id=1, source_target_pairs={{0,1},{1,0},{2,3},{3,2},{4,5},{5,4},{6,7},{7,6},{8,9},{9,8},{10,11... | collective-permute-start | bytes 25165832 | tf_op jit(solution)/shard_map/ppermute | solution.py:41
  544.6 10.3 %copy-start.3 = (bf16[4,576,512]{2,1,0:T(8,128)(2,1)S(1)}, bf16[4,576,512]{2,1,0:T(8,128)(2,1)}, u32[]{:S(2)}) copy-start(bf16[4,576,512]{2,1,0:T(8,128)(2,1)} %get-tuple-element.86) | copy-start | bytes 7077892
  556.7 9.8 %collective-permute-start.1 = (bf16[288,512]{1,0:T(8,128)(2,1)S(1)}, bf16[288,512]{1,0:T(8,128)(2,1)S(1)}, u32[]{:S(2)}, u32[]{:S(2)}) collective-permute-start(bf16[288,512]{1,0:T(8,128)(2,1)S(1)} %get-tuple-element.177), channel_id=1, source_target_pairs={{0,2},{1,3},{2,0},{3,1},{4,6},{5,7},{6,4},{7,5},{8,10},{9,11},{10,... | collective-permute-start | bytes 884744 | tf_op jit(solution)/shard_map/ppermute | solution.py:41
  559.1 8.8 collective-permute-start.2
  559.4 12.6 %copy-start.1 = (bf16[576,2048]{1,0:T(8,128)(2,1)S(1)}, bf16[576,2048]{1,0:T(8,128)(2,1)}, u32[]{:S(2)}) copy-start(bf16[576,2048]{1,0:T(8,128)(2,1)} %get-tuple-element.89.normed_ref) | copy-start | bytes 7077892
  568.9 60.9 %collective-permute-start.4 = (bf16[576,512]{1,0:T(8,128)(2,1)}, bf16[576,512]{1,0:T(8,128)(2,1)S(1)}, u32[]{:S(2)}, u32[]{:S(2)}) collective-permute-start(bf16[576,512]{1,0:T(8,128)(2,1)} %pad_maximum_fusion.3), channel_id=1, source_target_pairs={{0,4},{1,5},{2,6},{3,7},{4,0},{5,1},{6,2},{7,3},{8,12},{9,13},{10,... | collective-permute-start | bytes 1769480 | tf_op jit(solution)/shard_map/ppermute | solution.py:41
  570.3 59.4 %collective-permute-start.3 = (bf16[576,512]{1,0:T(8,128)(2,1)}, bf16[576,512]{1,0:T(8,128)(2,1)}, u32[]{:S(2)}, u32[]{:S(2)}) collective-permute-start(bf16[576,512]{1,0:T(8,128)(2,1)} %pad_maximum_fusion.2), channel_id=1, source_target_pairs={{0,2},{1,3},{2,0},{3,1},{4,6},{5,7},{6,4},{7,5},{8,10},{9,11},{10,... | collective-permute-start | bytes 1769480 | tf_op jit(solution)/shard_map/ppermute | solution.py:41
  575.5 4.2 copy-start
  579.8 50.0 %collective-permute-start.6 = (f32[128,2048]{1,0:T(8,128)}, f32[128,2048]{1,0:T(8,128)}, u32[]{:S(2)}, u32[]{:S(2)}) collective-permute-start(f32[128,2048]{1,0:T(8,128)} %get-tuple-element.171), channel_id=1, source_target_pairs={{0,2},{1,3},{2,0},{3,1},{4,6},{5,7},{6,4},{7,5},{8,10},{9,11},{10,... | collective-permute-start | bytes 3145736 | tf_op jit(solution)/shard_map/ppermute | solution.py:41
  580.1 49.6 %collective-permute-start.7 = (f32[128,2048]{1,0:T(8,128)}, f32[128,2048]{1,0:T(8,128)}, u32[]{:S(2)}, u32[]{:S(2)}) collective-permute-start(f32[128,2048]{1,0:T(8,128)} %get-tuple-element.170), channel_id=1, source_target_pairs={{0,4},{1,5},{2,6},{3,7},{4,0},{5,1},{6,2},{7,3},{8,12},{9,13},{10,... | collective-permute-start | bytes 3145736 | tf_op jit(solution)/shard_map/ppermute | solution.py:41
  629.7 0.9 copy-start.5
  630.6 12.7 %copy-start.7 = (f32[1,2048]{1,0:T(1,128)S(1)}, f32[1,2048]{1,0:T(1,128)}, u32[]{:S(2)}) copy-start(f32[1,2048]{1,0:T(1,128)} %get-tuple-element.110) | copy-start | bytes 24580
  644.0 2.6 copy-start.2
  649.2 216.0 %reduce-scatter.2.cloned.1.call-start = ((), (), s32[]{:S(2)}) async-start(), calls=%async_computation.1 | async-start | bytes 18874368 | tf_op jit(solution)/shard_map/reduce_scatter | solution.py:974
  649.9 35.8 %collective-permute-start.10 = (f32[2,2048]{1,0:T(2,128)S(1)}, f32[2,2048]{1,0:T(2,128)S(1)}, u32[]{:S(2)}, u32[]{:S(2)}) collective-permute-start(f32[2,2048]{1,0:T(2,128)S(1)} %pad_maximum_fusion.4), channel_id=1, source_target_pairs={{0,6},{1,7},{2,4},{3,5},{4,2},{5,3},{6,0},{7,1},{8,14},{9,15},{10,... | collective-permute-start | bytes 49160 | tf_op jit(solution)/shard_map/ppermute | solution.py:41
  651.6 34.1 %collective-permute-start.8 = (f32[2,2048]{1,0:T(2,128)S(1)}, f32[2,2048]{1,0:T(2,128)S(1)}, u32[]{:S(2)}, u32[]{:S(2)}) collective-permute-start(f32[2,2048]{1,0:T(2,128)S(1)} %pad_maximum_fusion.4), channel_id=1, source_target_pairs={{0,2},{1,3},{2,0},{3,1},{4,6},{5,7},{6,4},{7,5},{8,10},{9,11},{10,... | collective-permute-start | bytes 49160 | tf_op jit(solution)/shard_map/ppermute | solution.py:41
  651.9 33.8 %collective-permute-start.9 = (f32[2,2048]{1,0:T(2,128)S(1)}, f32[2,2048]{1,0:T(2,128)S(1)}, u32[]{:S(2)}, u32[]{:S(2)}) collective-permute-start(f32[2,2048]{1,0:T(2,128)S(1)} %pad_maximum_fusion.4), channel_id=1, source_target_pairs={{0,4},{1,5},{2,6},{3,7},{4,0},{5,1},{6,2},{7,3},{8,12},{9,13},{10,... | collective-permute-start | bytes 49160 | tf_op jit(solution)/shard_map/ppermute | solution.py:41
  653.4 80.3 %collective-permute-start.12 = (f32[256,2048]{1,0:T(8,128)}, f32[256,2048]{1,0:T(8,128)}, u32[]{:S(2)}, u32[]{:S(2)}) collective-permute-start(f32[256,2048]{1,0:T(8,128)} %get-tuple-element.119), channel_id=1, source_target_pairs={{0,2},{1,3},{2,0},{3,1},{4,6},{5,7},{6,4},{7,5},{8,10},{9,11},{10,... | collective-permute-start | bytes 6291464 | tf_op jit(solution)/shard_map/ppermute | solution.py:41
  653.9 79.9 %collective-permute-start.13 = (f32[256,2048]{1,0:T(8,128)}, f32[256,2048]{1,0:T(8,128)}, u32[]{:S(2)}, u32[]{:S(2)}) collective-permute-start(f32[256,2048]{1,0:T(8,128)} %get-tuple-element.120), channel_id=1, source_target_pairs={{0,4},{1,5},{2,6},{3,7},{4,0},{5,1},{6,2},{7,3},{8,12},{9,13},{10,... | collective-permute-start | bytes 6291464 | tf_op jit(solution)/shard_map/ppermute | solution.py:41
  685.7 48.0 %collective-permute-start.11 = (f32[2,2048]{1,0:T(2,128)S(1)}, f32[2,2048]{1,0:T(2,128)S(1)}, u32[]{:S(2)}, u32[]{:S(2)}) collective-permute-start(f32[2,2048]{1,0:T(2,128)S(1)} %add_add_fusion), channel_id=1, source_target_pairs={{0,1},{1,0},{2,3},{3,2},{4,5},{5,4},{6,7},{7,6},{8,9},{9,8},{10,11... | collective-permute-start | bytes 49160 | tf_op jit(solution)/shard_map/ppermute | solution.py:41
  750.4 117.8 %copy-start.4 = (f32[2048,256]{1,0:T(8,128)S(1)}, f32[2048,256]{1,0:T(8,128)}, u32[]{:S(2)}) copy-start(f32[2048,256]{1,0:T(8,128)} %get-tuple-element.189) | copy-start | bytes 6291460
Sparse Core Ops, SparseCore 0:
  649.3 101.1 all-reduce.2
  754.5 110.6 reduce-scatter.1

commit v9 on v8

--- a/solution.py
+++ b/solution.py
@@ -372,9 +372,9 @@
     return (gelu * upper).astype(BF16), (d_act * upper * slope).astype(BF16), (d_act * gelu).astype(BF16)
 
 
-def gated_kernel(z_own, g_own, wg_hbm, wu_hbm, wd_hbm, z_all, g_all, act, d_gate, d_up,
-                 wg, wu, wd, z_buf, g_buf, outs, w_sem, in_sem, own_sem, out_sem, send, recv, send0, recv0, *, bn):
-    rows, _ = z_own.shape
+def gated_kernel(z_own, g_own, wg_hbm, wu_hbm, wd_hbm, z_all, g_all, act, d_gate, d_up, diag_in,
+                 wg, wu, wd, z_buf, g_buf, outs, st, from_core, far_send, far_recv, diag_send, diag_recv, w_sem, in_sem, own_sem, out_sem, send, recv, send0, recv0, *, bn):
+    rows, dim = z_own.shape
     width = wg_hbm.shape[1]
     steps = width // bn
     piece = rows // 4
@@ -449,6 +449,47 @@
         starts = [(1 - late) * (first * rows + i * piece) + late * base for i, base in enumerate((base_x, base_y, pair_x, pair_y))]
         return [pl.ds(pl.multiple_of(st, 16), piece) for st in starts]
 
+    def pass_on(u):
+        for path in range(2):
+            for a in range(2):
+                link_copy(u, path, a).wait_recv()
+                core_copy(u, path, a).start()
+
+    def far_copy(j):
+        return remote(st.at[0, j], from_core.at[j], far_send.at[j], far_recv.at[j], core)
+
+    def diag_copy(k, j):
+        half = rows // 2
+        return remote(st.at[1, j, pl.ds(k * half, half)], diag_in.at[k, :, pl.ds(pl.multiple_of(j * bn, 128), bn)],
+                      diag_send.at[k, j], diag_recv.at[k, j], (side, back)[k])
+
+    def down_diagonal():
+        for slot in range(2):
+            for cp in out_copies(slot, stage_rows(5), 0):
+                cp.wait()
+        loads = [pltpu.make_async_copy(act.at[pl.ds(pl.multiple_of(dev * rows, 16), rows)], bufs[a], in_sem.at[a, 0])
+                 for a, dev in enumerate((flip(corner, 1), corner))]
+        for cp in loads:
+            cp.start()
+
+        def theirs(j, carry):
+            st[0, j] = dot_nn(z_buf[...], wd[:, pl.ds(pl.multiple_of(j * bn, 128), bn)]).astype(BF16)
+            far_copy(j).start()
+            return carry
+
+        def mine(j, carry):
+            far_copy(j).wait_recv()
+            total = dot_nn(g_buf[...], wd[:, pl.ds(pl.multiple_of(j * bn, 128), bn)]) + from_core[j].astype(F32)
+            st[1, j] = total.astype(BF16)
+            for k in range(2):
+                diag_copy(k, j).start()
+            return carry
+
+        loads[0].wait()
+        lax.fori_loop(0, dim // bn, theirs, 0)
+        loads[1].wait()
+        lax.fori_loop(0, dim // bn, mine, 0)
+
     def compute(s):
         s_rows = stage_rows(s)
 
@@ -456,7 +497,7 @@
             step = s * steps + n
             slot = step % 2
 
-            @pl.when(step >= 2)
+            @pl.when((step >= 2) & (step // 2 != 6 * steps // 2))
             def _():
                 for cp in out_copies(slot, s_rows, n):
                     cp.wait()
@@ -465,6 +506,10 @@
             def _():
                 for cp in weight_copies(n):
                     cp.wait()
+
+            @pl.when((s == 6) & (n == steps - 1))
+            def _():
+                pass_on(5)
 
             cols = pl.ds(pl.multiple_of(n * bn, 128), bn)
             res = gated_tile(z_buf[...], g_buf[...], wg[:, cols], wu[:, cols], wd[cols, :])
@@ -494,10 +539,10 @@
         for u in range(6):
             @pl.when(s == u + 2)
             def _(u=u):
-                for path in range(2):
-                    for a in range(2):
-                        link_copy(u, path, a).wait_recv()
-                        core_copy(u, path, a).start()
+                if u < 5:
+                    pass_on(u)
+                if u == 4:
+                    down_diagonal()
                 if u < 2:
                     for path in range(2):
                         for a in range(2):
@@ -529,6 +574,11 @@
     for slot in range(2):
         for cp in out_copies(slot, last, 0):
             cp.wait()
+    for j in range(dim // bn):
+        far_copy(j).wait_send()
+        for k in range(2):
+            diag_copy(k, j).wait_send()
+            diag_copy(k, j).wait_recv()
     for a in range(2):
         own_copy(a).wait_send()
         for path in range(2):
@@ -547,20 +597,21 @@
     dma = pltpu.SemaphoreType.DMA
     return pl.pallas_call(
         functools.partial(gated_kernel, bn=bn),
-        out_shape=(gathered, gathered, made, made, made),
+        out_shape=(gathered, gathered, made, made, made, jax.ShapeDtypeStruct((2, rows // 2, dim), BF16)),
         in_specs=[anyspace] * 5,
-        out_specs=(anyspace,) * 5,
+        out_specs=(anyspace,) * 6,
         scratch_shapes=[pltpu.VMEM((dim, width), BF16), pltpu.VMEM((dim, width), BF16), pltpu.VMEM((width, dim), BF16),
                         pltpu.VMEM((rows, dim), BF16), pltpu.VMEM((rows, dim), BF16), pltpu.VMEM((2, 3, rows, bn), BF16),
-                        dma((3, width // bn)), dma((2, 4)), dma((4,)), dma((2, 3, 4)), dma((4, 6, 2)), dma((4, 6, 2)), dma((2,)), dma((2,))],
+                        pltpu.VMEM((2, dim // bn, rows, bn), BF16), pltpu.VMEM((dim // bn, rows, bn), BF16),
+                        dma((dim // bn,)), dma((dim // bn,)), dma((2, dim // bn)), dma((2, dim // bn)), dma((3, width // bn)), dma((2, 4)), dma((4,)), dma((2, 3, 4)), dma((4, 6, 2)), dma((4, 6, 2)), dma((2,)), dma((2,))],
         compiler_params=pltpu.CompilerParams(vmem_limit_bytes=67043328, collective_id=0, has_side_effects=True),
         cost_estimate=pl.CostEstimate(flops=6 * total * dim * width, bytes_accessed=200 << 20, transcendentals=total * width),
         name="gated",
     )(z_own, g_own, w_gate, w_up, w_down)
 
 
-def back_kernel(act, d_gate, d_up, z_all, wg_hbm, wu_hbm, wd_hbm, own_out, x_in, y_in, g_gate,
-                wa, wb, lhs, st, from_core, from_diag, own_st, z_sem, w_sem, l_sem, o_sem, c_send, c_recv, d_send, d_recv, f_send, f_recv, *, rows, bn):
+def back_kernel(act, d_gate, d_up, z_all, diag_in, wg_hbm, wu_hbm, wd_hbm, own_out, x_in, y_in, g_gate,
+                wa, wb, lhs, st, from_core, from_diag, own_st, in_sem, z_sem, w_sem, l_sem, o_sem, c_send, c_recv, d_send, d_recv, f_send, f_recv, *, rows, bn):
     dim, width = wg_hbm.shape
     steps = dim // bn
     half = rows // 2
@@ -604,10 +655,16 @@
             return dot_nn(lhs[slot, 0], wa[:width, cols(j)])
         return dot_nt(lhs[slot, 0], wb[cols(j), :]) + dot_nt(lhs[slot, 1], wa[cols(j), :])
 
-    for cp in lhs_copies(0, 0):
+    def diag_load(k, j):
+        return pltpu.make_async_copy(diag_in.at[k, :, cols(j)], from_diag.at[0, k, j], in_sem.at[k, j])
+
+    for cp in lhs_copies(0, 2):
         cp.start()
     for j in range(steps):
         weight_copy(0, j).start()
+    for k in range(2):
+        for j in range(steps):
+            diag_load(k, j).start()
     enter((core, side, back))
 
     def tiles(body):
@@ -628,7 +685,7 @@
                     cp.start()
 
             if phase == 0:
-                @pl.when(t == 1)
+                @pl.when(t == 3)
                 def _():
                     for j in range(steps):
                         weight_copy(1, j).start()
@@ -643,13 +700,13 @@
                 pair = pair_of(t)
 
                 def body(j):
-                    @pl.when(t == 0)
+                    @pl.when(t == (2 if phase == 0 else 0))
                     def _():
                         for k in ((0,) if phase == 0 else (1, 2)):
                             weight_copy(k, j).wait()
 
                     if phase == 0:
-                        @pl.when(t > 0)
+                        @pl.when(t > 2)
                         def _():
                             core_copy(0, j).wait_send()
                     else:
@@ -659,26 +716,26 @@
 
                 tiles(body)
 
-            @pl.when(t == 1)
-            def _():
-                def body(j):
-                    core_copy(0, j).wait_recv()
-                    if phase == 1:
+            if phase == 1:
+                @pl.when(t == 1)
+                def _():
+                    def body(j):
+                        core_copy(0, j).wait_recv()
+                        st[1, j] = (product(phase, 1, j) + from_core[0, j].astype(F32)).astype(BF16)
                         for k in range(2):
-                            diag_copy(0, k, j).wait_send()
-                    st[1, j] = (product(phase, 1, j) + from_core[0, j].astype(F32)).astype(BF16)
-                    for k in range(2):
-                        diag_copy(phase, k, j).start()
-
-                tiles(body)
+                            diag_copy(phase, k, j).start()
+
+                    tiles(body)
 
             for k in range(2):
                 @pl.when(t == 5 + k)
                 def _(k=k):
                     def body(j):
                         core_copy(1 + k, j).wait_recv()
-                        diag_copy(phase, 1 - k, j).wait_recv()
-                        if phase == 1:
+                        if phase == 0:
+                            diag_load(1 - k, j).wait()
+                        else:
+                            diag_copy(phase, 1 - k, j).wait_recv()
                             final_copy(0, k, j).wait_send()
                         total = product(phase, (5 + k) % 2, j) + from_core[1 + k, j].astype(F32)
                         came = from_diag[phase, 1 - k, j].astype(F32)
@@ -711,7 +768,7 @@
 
             return carry
 
-        lax.fori_loop(0, 8, step, 0)
+        lax.fori_loop(2 if phase == 0 else 0, 8, step, 0)
 
     def z_copy(j, c):
         return pltpu.make_async_copy(z_all.at[pl.ds(c * rows, rows), cols(j)], lhs.at[c // 2, c % 2, :, cols(j)], z_sem.at[j, c])
@@ -760,7 +817,7 @@
                 final_copy(phase, k, j).wait_recv()
 
 
-def back_layer(act, d_gate, d_up, z_all, w_gate, w_up, w_down, tp, bn=512):
+def back_layer(act, d_gate, d_up, z_all, diag_in, w_gate, w_up, w_down, tp, bn=512):
     total, width = act.shape
     dim = w_gate.shape[0]
     rows = total // tp
@@ -771,17 +828,17 @@
     return pl.pallas_call(
         functools.partial(back_kernel, rows=rows, bn=bn),
         out_shape=(jax.ShapeDtypeStruct((2, rows, dim), F32), came, came, jax.ShapeDtypeStruct((dim, width), F32)),
-        in_specs=[anyspace] * 7,
+        in_specs=[anyspace] * 8,
         out_specs=(anyspace,) * 4,
         scratch_shapes=[pltpu.VMEM((4 * rows, dim), BF16), pltpu.VMEM((dim, width), BF16), pltpu.VMEM((2, 2, rows, width), BF16),
                         pltpu.VMEM((4, steps, rows, bn), BF16), pltpu.VMEM((4, steps, rows, bn), BF16),
                         pltpu.VMEM((2, 2, steps, rows // 2, bn), BF16), pltpu.VMEM((2, rows, bn), F32),
-                        dma((steps, 4)), dma((3, steps)), dma((2, 2)), dma((2,)), dma((steps,)), dma((4, steps)),
+                        dma((2, steps)), dma((steps, 4)), dma((3, steps)), dma((2, 2)), dma((2,)), dma((steps,)), dma((4, steps)),
                         dma((2, steps)), dma((2, 2, steps)), dma((2, steps)), dma((2, 2, steps))],
         compiler_params=pltpu.CompilerParams(vmem_limit_bytes=67043328, collective_id=1, has_side_effects=True),
         cost_estimate=pl.CostEstimate(flops=6 * total * dim * width, bytes_accessed=200 << 20, transcendentals=0),
         name="back",
-    )(act, d_gate, d_up, z_all, w_gate, w_up, w_down)
+    )(act, d_gate, d_up, z_all, diag_in, w_gate, w_up, w_down)
 
 
 def norm_back(x, gain, d_out):
@@ -967,8 +1024,8 @@
             prefix_len, valid_len, k_pos, cos_own, sin_own, attn_norm, mlp_norm, hidden, w_query, w_key, w_value, w_out, batch, tp_size)
         wo_all = wo_all.reshape(tp_size * head_dim, dim)
 
-        gated_all, grad_all, act, d_gate, d_upper = gated_layer(gated_in, grad_out, w_gate, w_up, w_down, tp_size)
-        own_part, x_part, y_part, g_gate_part = back_layer(act, d_gate, d_upper, gated_all, w_gate, w_up, w_down, tp_size)
+        gated_all, grad_all, act, d_gate, d_upper, diag_in = gated_layer(gated_in, grad_out, w_gate, w_up, w_down, tp_size)
+        own_part, x_part, y_part, g_gate_part = back_layer(act, d_gate, d_upper, gated_all, diag_in, w_gate, w_up, w_down, tp_size)
         hidden_out, d_resid, g_mlp_norm_part, d_mixed, g_out_part = join_layer(
             own_part, x_part, y_part, resid, grad_out, mlp_norm, wo_all, mixed)
         g_out = lax.psum_scatter(g_out_part, "tp", scatter_dimension=0, tiled=True)

time: 884 us -> 878 us (level)
    pallas_call x1, Pallas kernels: 176 us -> 165 us  [back_layer(): pl.pallas_call(functools.partial(back_kernel, rows=rows, bn=bn), out_shap...]
where the time goes in v9:
time: 878 us; the launch traced here: 870 us
  Pallas kernels  658 us (75%)
  waiting for transfers between devices  134 us (15%)
  matrix products  19.5 us (2%)
  other arithmetic  16.1 us (2%)
  local copies, waits for them, and re-layouts  15.5 us (2%)
  between operations  14.5 us (2%)
  starting transfers between devices  12.1 us (1%)
    pallas_call x1, Pallas kernels, gated_layer(): pl.pallas_call(functools.partial(gated_kernel, bn=bn), out_shape=(gathere...  192 us
    pallas_call x1, Pallas kernels, back_layer(): pl.pallas_call(functools.partial(back_kernel, rows=rows, bn=bn), out_shap...  165 us
    reduce_scatter x1, waiting for transfers between devices, layer(): g_out = lax.psum_scatter(g_out_part, 'tp', scatter_dimension=0, tiled=True)  115 us
    pallas_call x1, Pallas kernels, front_layer(): pl.pallas_call(functools.partial(front_kernel, batch=batch), out_shape=(s...  102 us
    pallas_call x2, Pallas kernels, weight_grad(): pl.pallas_call(product_kernel, out_shape=jax.ShapeDtypeStruct((m, n), F32...  95.8 us
    pallas_call x1, Pallas kernels, attention_backward(): pl.pallas_call(attn_bwd_kernel, out_shape=(jax.ShapeDtypeStruct((heads, r...  32.5 us
    pallas_call x1, Pallas kernels, weight_grad_rest(): pl.pallas_call(rest_kernel, out_shape=jax.ShapeDtypeStruct((m, n), F32),...  30 us
    pallas_call x1, Pallas kernels, join_layer(): pl.pallas_call(functools.partial(join_kernel, joins=joins), out_shape=(ac...  28.2 us
  transfers between devices with their start and end apart: 16, of which 4 were waited for; matrix products, arithmetic and copies ran while one was open for 4% of the time, Pallas kernels for 14%

profile of v9, /device:TPU:0, one launch (start us, length us, event | category | flops | bytes accessed | tf_op | source)
XLA Modules:
  0.0 869.9 jit_solution(2615341231879443704)
XLA Ops:
  13.9 101.8 %front.1 = (bf16[576,2048]{1,0:T(8,128)(2,1)}, bf16[8,2048,256]{2,1,0:T(8,128)(2,1)}, bf16[8,256,2048]{2,1,0:T(8,128)(2,1)}, bf16[8,576,512]{2,1,0:T(8,128)(2,1)...) custom-call(s32[3]{0:T(128)} %prefix_ref.1, ...), custom_call_target="tpu_custom_call" | custom-call | flops 19327352832 | bytes 62914560 | tf_op jit(solution)/shard_map/front/pallas_call | solution.py:323
  115.6 192.3 %gated.1 = (bf16[4608,2048]{1,0:T(8,128)(2,1)}, bf16[4608,2048]{1,0:T(8,128)(2,1)}, bf16[4608,2048]{1,0:T(8,128)(2,1)}, bf16[4608,2048]{1,0:T(8,128)(2,1)}, bf16...) custom-call(bf16[576,2048]{1,0:T(8,128)(2,1)} %get-tuple-element.72.z_own, bf16[576,2048]{1,0:T(8,128)(2,1)} %bitcast.69, ...), custom_call_target="tpu_custom_call" | custom-call | flops 115964116992 | bytes 209715200 | tf_op jit(solution)/shard_map/gated/pallas_call | solution.py:598
  308.0 164.8 %back.1 = (f32[2,576,2048]{2,1,0:T(8,128)}, bf16[2,576,2048]{2,1,0:T(8,128)(2,1)}, bf16[2,576,2048]{2,1,0:T(8,128)(2,1)}, f32[2048,2048]{1,0:T(8,128)}) custom-call(bf16[4608,2048]{1,0:T(8,128)(2,1)} %get-tuple-element.100.act.a_ref, bf16[4608,2048]{1,0:T(8,128)(2,1)} %get-tuple-element.114.d_gate.b_ref, bf16[4608,2048]{1,0:T(8,128)(2,1)} %get-tuple-element.123.d_up.b_ref, ...), custom_call_target="tpu_custom_call" | custom-call | flops 115964116992 | bytes 209715200 | tf_op jit(solution)/shard_map/back/pallas_call | solution.py:828
  472.8 28.2 %join.1 = (bf16[576,2048]{1,0:T(8,128)(2,1)}, bf16[576,2048]{1,0:T(8,128)(2,1)}, f32[1,2048]{1,0:T(1,128)}, bf16[576,2048]{1,0:T(8,128)(2,1)}, f32[2048,2048]{1,0:T(8,128)}) custom-call(f32[2,576,2048]{2,1,0:T(8,128)} %get-tuple-element.78.own_ref, bf16[2,576,2048]{2,1,0:T(8,128)(2,1)} %get-tuple-element.79.x_ref, ...), custom_call_target="tpu_custom_call" | custom-call | flops 9663676416 | bytes 62914560 | tf_op jit(solution)/shard_map/join/pallas_call | solution.py:887
  501.0 32.5 %attn_bwd.1 = (bf16[8,576,256]{2,1,0:T(8,128)(2,1)}, bf16[4,576,512]{2,1,0:T(8,128)(2,1)}, bf16[4,576,512]{2,1,0:T(8,128)(2,1)}) custom-call(s32[11,3]{1,0:T(8,128)} %add_add_fusion.1.lens_ref, f32[192,128]{1,0:T(8,128)} %get-tuple-element.183.cos_ref, f32[192,128]{1,0:T(8,128)} %get-tuple-element.182.sin_ref, bf16[8,576,256]{2,1,0:T(8,128)(2,1)} %get-tuple-element.85.q_ref, ...), custom_call_target="tpu_custom_call" | custom-call | flops 18119393280 | bytes 20971520 | tf_op jit(solution)/shard_map/attn_bwd/pallas_call | solution.py:349
  533.6 5.7 fusion.1
  539.9 10.2 %convolution_bitcast_fusion.part_ref = f32[576,2048]{1,0:T(8,128)} fusion(bf16[8,576,256]{2,1,0:T(8,128)(2,1)S(1)} %copy-done.6, bf16[8,2048,256]{2,1,0:T(8,128)(2,1)} %get-tuple-element.93), kind=kOutput, calls=%fused_computation.1 | convolution fusion | flops 4831838208 | bytes 15466496 | tf_op jit(solution)/shard_map/hte,hde->td/dot_general | solution.py:1042
  550.2 1.7 convert_add_fusion
  554.1 6.8 collective-permute-done.1
  564.9 3.5 convolution_add_fusion
  568.5 1.9 slice_bitcast_fusion
  570.4 2.3 copy-done
  574.9 47.8 %weight_grad.2 = f32[2048,2048]{1,0:T(8,128)} custom-call(bf16[4608,2048]{1,0:T(8,128)(2,1)} %get-tuple-element.100.act.a_ref, bf16[4608,2048]{1,0:T(8,128)(2,1)} %get-tuple-element.101.b_ref), custom_call_target="tpu_custom_call" | custom-call | flops 38654705664 | bytes 115343360 | tf_op jit(solution)/shard_map/weight_grad/pallas_call | solution.py:962
  623.6 12.7 %finish.1 = (f32[2048,256]{1,0:T(8,128)}, f32[2048,256]{1,0:T(8,128)}, bf16[576,2048]{1,0:T(8,128)(2,1)}, f32[1,2048]{1,0:T(1,128)}) custom-call(f32[576,512]{1,0:T(8,128)} %get-tuple-element.177.kv_ref, bf16[576,512]{1,0:T(8,128)(2,1)} %collective-permute-done.3.side_ref, bf16[576,512]{1,0:T(8,128)(2,1)} %copy-done.5, ...), custom_call_target="tpu_custom_call" | custom-call | flops 2415919104 | bytes 25165824 | tf_op jit(solution)/shard_map/finish/pallas_call | solution.py:943
  637.1 2.6 bitcast_add_fusion.1
  639.6 2.5 pad_maximum_fusion
  644.3 1.7 collective-permute-start.8
  648.3 30.0 %weight_grad_rest.1 = f32[2048,2048]{1,0:T(8,128)} custom-call(s32[1]{0:T(128)} %constant.3.clone.1.at_ref, bf16[4608,2048]{1,0:T(8,128)(2,1)} %get-tuple-element.76.z_all.a_ref, bf16[4608,2048]{1,0:T(8,128)(2,1)} %get-tuple-element.114.d_gate.b_ref, f32[2048,2048]{1,0:T(8,128)} %get-tuple-element.115.part_ref), custom_call_target="tpu_custom_call" | custom-call | flops 19327352832 | bytes 83886080 | tf_op jit(solution)/shard_map/weight_grad_rest/pallas_call | solution.py:981
  678.4 48.0 %weight_grad.3 = f32[2048,2048]{1,0:T(8,128)} custom-call(bf16[4608,2048]{1,0:T(8,128)(2,1)} %get-tuple-element.76.z_all.a_ref, bf16[4608,2048]{1,0:T(8,128)(2,1)} %get-tuple-element.123.d_up.b_ref), custom_call_target="tpu_custom_call" | custom-call | flops 38654705664 | bytes 115343360 | tf_op jit(solution)/shard_map/weight_grad/pallas_call | solution.py:962
  726.4 3.4 fusion.4
  729.8 1.8 copy.30
  732.3 11.4 %all-reduce.3.cloned.1.call-done = (f32[2048,256]{1,0:T(8,128)}, f32[2048,256]{1,0:T(8,128)}) async-done(((f32[2048,256]{1,0:T(8,128)}, f32[2048,256]{1,0:T(8,128)}), (f32[2048,256]{1,0:T(8,128)}, f32[2048,256]{1,0:T(8,128)})) %all-reduce.3.cloned.1.call-update) | async-done | bytes 4194320 | tf_op jit(solution)/shard_map/psum | solution.py:1057
  743.7 114.8 %reduce-scatter.2.cloned.1.call-done = f32[256,2048]{1,0:T(8,128)} async-done(((f32[2048,2048]{1,0:T(8,128)}), f32[256,2048]{1,0:T(8,128)}) %reduce-scatter.2.cloned.1.call-update) | async-done | bytes 2097168 | tf_op jit(solution)/shard_map/reduce_scatter | solution.py:1031
  858.5 3.0 copy.33
  (69 shorter events, 23.7 us)
Async XLA Ops:
  7.2 736.5 %all-reduce.3.cloned.1.call-start = ((), (), s32[]{:S(2)}) async-start(), calls=%async_computation.2 | async-start | bytes 8388608 | tf_op jit(solution)/shard_map/psum | solution.py:1057
  533.6 5.8 collective-permute-start
  533.6 6.2 copy-start.6
  539.3 25.6 %collective-permute-start.5 = (f32[4,256,2048]{2,1,0:T(8,128)S(1)}, f32[4,256,2048]{2,1,0:T(8,128)S(1)}, u32[]{:S(2)}, u32[]{:S(2)}) collective-permute-start(f32[4,256,2048]{2,1,0:T(8,128)S(1)} %fusion.1), channel_id=1, source_target_pairs={{0,1},{1,0},{2,3},{3,2},{4,5},{5,4},{6,7},{7,6},{8,9},{9,8},{10,11... | collective-permute-start | bytes 25165832 | tf_op jit(solution)/shard_map/ppermute | solution.py:41
  539.9 10.3 %copy-start.3 = (bf16[4,576,512]{2,1,0:T(8,128)(2,1)S(1)}, bf16[4,576,512]{2,1,0:T(8,128)(2,1)}, u32[]{:S(2)}) copy-start(bf16[4,576,512]{2,1,0:T(8,128)(2,1)} %get-tuple-element.88) | copy-start | bytes 7077892
  552.0 9.0 %collective-permute-start.1 = (bf16[288,512]{1,0:T(8,128)(2,1)S(1)}, bf16[288,512]{1,0:T(8,128)(2,1)S(1)}, u32[]{:S(2)}, u32[]{:S(2)}) collective-permute-start(bf16[288,512]{1,0:T(8,128)(2,1)S(1)} %get-tuple-element.179), channel_id=1, source_target_pairs={{0,2},{1,3},{2,0},{3,1},{4,6},{5,7},{6,4},{7,5},{8,10},{9,11},{10,... | collective-permute-start | bytes 884744 | tf_op jit(solution)/shard_map/ppermute | solution.py:41
  552.5 8.7 collective-permute-start.2
  554.1 10.8 %copy-start.1 = (bf16[576,2048]{1,0:T(8,128)(2,1)S(1)}, bf16[576,2048]{1,0:T(8,128)(2,1)}, u32[]{:S(2)}) copy-start(bf16[576,2048]{1,0:T(8,128)(2,1)} %get-tuple-element.91.normed_ref) | copy-start | bytes 7077892
  562.1 60.6 %collective-permute-start.4 = (bf16[576,512]{1,0:T(8,128)(2,1)}, bf16[576,512]{1,0:T(8,128)(2,1)S(1)}, u32[]{:S(2)}, u32[]{:S(2)}) collective-permute-start(bf16[576,512]{1,0:T(8,128)(2,1)} %pad_maximum_fusion.3), channel_id=1, source_target_pairs={{0,4},{1,5},{2,6},{3,7},{4,0},{5,1},{6,2},{7,3},{8,12},{9,13},{10,... | collective-permute-start | bytes 1769480 | tf_op jit(solution)/shard_map/ppermute | solution.py:41
  564.6 58.2 %collective-permute-start.3 = (bf16[576,512]{1,0:T(8,128)(2,1)}, bf16[576,512]{1,0:T(8,128)(2,1)}, u32[]{:S(2)}, u32[]{:S(2)}) collective-permute-start(bf16[576,512]{1,0:T(8,128)(2,1)} %pad_maximum_fusion.2), channel_id=1, source_target_pairs={{0,2},{1,3},{2,0},{3,1},{4,6},{5,7},{6,4},{7,5},{8,10},{9,11},{10,... | collective-permute-start | bytes 1769480 | tf_op jit(solution)/shard_map/ppermute | solution.py:41
  568.5 4.2 copy-start
  572.7 50.1 %collective-permute-start.6 = (f32[128,2048]{1,0:T(8,128)}, f32[128,2048]{1,0:T(8,128)}, u32[]{:S(2)}, u32[]{:S(2)}) collective-permute-start(f32[128,2048]{1,0:T(8,128)} %get-tuple-element.173), channel_id=1, source_target_pairs={{0,2},{1,3},{2,0},{3,1},{4,6},{5,7},{6,4},{7,5},{8,10},{9,11},{10,... | collective-permute-start | bytes 3145736 | tf_op jit(solution)/shard_map/ppermute | solution.py:41
  574.4 48.4 %collective-permute-start.7 = (f32[128,2048]{1,0:T(8,128)}, f32[128,2048]{1,0:T(8,128)}, u32[]{:S(2)}, u32[]{:S(2)}) collective-permute-start(f32[128,2048]{1,0:T(8,128)} %get-tuple-element.172), channel_id=1, source_target_pairs={{0,4},{1,5},{2,6},{3,7},{4,0},{5,1},{6,2},{7,3},{8,12},{9,13},{10,... | collective-permute-start | bytes 3145736 | tf_op jit(solution)/shard_map/ppermute | solution.py:41
  622.8 0.9 copy-start.5
  623.6 12.7 %copy-start.7 = (f32[1,2048]{1,0:T(1,128)S(1)}, f32[1,2048]{1,0:T(1,128)}, u32[]{:S(2)}) copy-start(f32[1,2048]{1,0:T(1,128)} %get-tuple-element.112) | copy-start | bytes 24580
  637.1 2.6 copy-start.2
  642.2 216.3 %reduce-scatter.2.cloned.1.call-start = ((), (), s32[]{:S(2)}) async-start(), calls=%async_computation.1 | async-start | bytes 18874368 | tf_op jit(solution)/shard_map/reduce_scatter | solution.py:1031
  643.0 35.4 %collective-permute-start.10 = (f32[2,2048]{1,0:T(2,128)S(1)}, f32[2,2048]{1,0:T(2,128)S(1)}, u32[]{:S(2)}, u32[]{:S(2)}) collective-permute-start(f32[2,2048]{1,0:T(2,128)S(1)} %pad_maximum_fusion.4), channel_id=1, source_target_pairs={{0,6},{1,7},{2,4},{3,5},{4,2},{5,3},{6,0},{7,1},{8,14},{9,15},{10,... | collective-permute-start | bytes 49160 | tf_op jit(solution)/shard_map/ppermute | solution.py:41
  644.3 34.1 %collective-permute-start.8 = (f32[2,2048]{1,0:T(2,128)S(1)}, f32[2,2048]{1,0:T(2,128)S(1)}, u32[]{:S(2)}, u32[]{:S(2)}) collective-permute-start(f32[2,2048]{1,0:T(2,128)S(1)} %pad_maximum_fusion.4), channel_id=1, source_target_pairs={{0,2},{1,3},{2,0},{3,1},{4,6},{5,7},{6,4},{7,5},{8,10},{9,11},{10,... | collective-permute-start | bytes 49160 | tf_op jit(solution)/shard_map/ppermute | solution.py:41
  646.0 32.4 %collective-permute-start.9 = (f32[2,2048]{1,0:T(2,128)S(1)}, f32[2,2048]{1,0:T(2,128)S(1)}, u32[]{:S(2)}, u32[]{:S(2)}) collective-permute-start(f32[2,2048]{1,0:T(2,128)S(1)} %pad_maximum_fusion.4), channel_id=1, source_target_pairs={{0,4},{1,5},{2,6},{3,7},{4,0},{5,1},{6,2},{7,3},{8,12},{9,13},{10,... | collective-permute-start | bytes 49160 | tf_op jit(solution)/shard_map/ppermute | solution.py:41
  646.5 79.9 %collective-permute-start.12 = (f32[256,2048]{1,0:T(8,128)}, f32[256,2048]{1,0:T(8,128)}, u32[]{:S(2)}, u32[]{:S(2)}) collective-permute-start(f32[256,2048]{1,0:T(8,128)} %get-tuple-element.121), channel_id=1, source_target_pairs={{0,2},{1,3},{2,0},{3,1},{4,6},{5,7},{6,4},{7,5},{8,10},{9,11},{10,... | collective-permute-start | bytes 6291464 | tf_op jit(solution)/shard_map/ppermute | solution.py:41
  648.0 78.4 %collective-permute-start.13 = (f32[256,2048]{1,0:T(8,128)}, f32[256,2048]{1,0:T(8,128)}, u32[]{:S(2)}, u32[]{:S(2)}) collective-permute-start(f32[256,2048]{1,0:T(8,128)} %get-tuple-element.122), channel_id=1, source_target_pairs={{0,4},{1,5},{2,6},{3,7},{4,0},{5,1},{6,2},{7,3},{8,12},{9,13},{10,... | collective-permute-start | bytes 6291464 | tf_op jit(solution)/shard_map/ppermute | solution.py:41
  678.4 48.0 %collective-permute-start.11 = (f32[2,2048]{1,0:T(2,128)S(1)}, f32[2,2048]{1,0:T(2,128)S(1)}, u32[]{:S(2)}, u32[]{:S(2)}) collective-permute-start(f32[2,2048]{1,0:T(2,128)S(1)} %add_add_fusion), channel_id=1, source_target_pairs={{0,1},{1,0},{2,3},{3,2},{4,5},{5,4},{6,7},{7,6},{8,9},{9,8},{10,11... | collective-permute-start | bytes 49160 | tf_op jit(solution)/shard_map/ppermute | solution.py:41
  743.7 117.8 %copy-start.4 = (f32[2048,256]{1,0:T(8,128)S(1)}, f32[2048,256]{1,0:T(8,128)}, u32[]{:S(2)}) copy-start(f32[2048,256]{1,0:T(8,128)} %get-tuple-element.191) | copy-start | bytes 6291460
Sparse Core Ops, SparseCore 0:
  642.3 101.3 all-reduce.2
  747.8 110.6 reduce-scatter.1

commit v10 on v9

--- a/solution.py
+++ b/solution.py
@@ -118,9 +118,9 @@
                                         device_id={"tp": peer}, device_id_type=pl.DeviceIdType.MESH)
 
 
-def front_kernel(prefix_ref, valid_ref, kpos_ref, cos_ref, sin_ref, gain1_ref, gain2_ref, hidden, w_query, w_key, w_value, w_out,
-                 normed_out, wq_all, wo_all, kv_all, query_out, mixed_out, resid_out, gated_out,
-                 x_buf, n_buf, wkv, wq, wo, kv, q, probs, mix, acc, load, store, send, recv, *, batch):
+def front_kernel(prefix_ref, valid_ref, kpos_ref, cos_ref, sin_ref, gain1_ref, gain2_ref, hidden, grad, w_query, w_key, w_value, w_out,
+                 normed_out, wq_all, wo_all, kv_all, query_out, mixed_out, resid_out, gated_out, g_all,
+                 x_buf, n_buf, wkv, wq, wo, kv, q, probs, mix, acc, load, store, send, recv, early_send, early_recv, *, batch):
     rows, dim = x_buf.shape
     shard = rows // batch
     head_dim = w_key.shape[1]
@@ -144,6 +144,15 @@
 
     def to_core(a, k):
         return remote(bufs[a].at[k], bufs[a].at[near + k], send.at[a, 4 + k], recv.at[a, 4 + k], core)
+
+    piece = rows // 4
+
+    def early(k, onto_core):
+        shard_at = ((side, back)[k] if onto_core else me) * rows + 2 * k * piece
+        there = g_all.at[pl.ds(pl.multiple_of(shard_at, 16), piece)]
+        src = there if onto_core else grad.at[pl.ds(2 * k * piece, piece)]
+        at = 2 * int(onto_core) + k
+        return remote(src, there, early_send.at[at], early_recv.at[at], core if onto_core else (side, back)[k])
 
     loads = [pltpu.make_async_copy(src, dst, load.at[i]) for i, (src, dst) in enumerate((
         (w_query, wq.at[0]), (hidden, x_buf), (w_key, wkv.at[:, :head_dim]), (w_value, wkv.at[:, head_dim:]), (w_out, wo.at[0])))]
@@ -266,6 +275,8 @@
     for cp in mixed_stores:
         cp.start()
     pass_on(2)
+    for k in range(2):
+        early(k, False).start()
 
     def project(k, first):
         def step(n, carry):
@@ -284,6 +295,9 @@
     pass_last(2)
     project(3, False)
     stores["wo"].start()
+    for k in range(2):
+        early(k, False).wait_recv()
+        early(k, True).start()
     stores["normed"].wait()
 
     def norm2(i, carry):
@@ -299,6 +313,10 @@
         cp.wait()
     for name in ("wq", "wo", "kv", "query", "resid", "gated"):
         stores[name].wait()
+    for k in range(2):
+        early(k, False).wait_send()
+        early(k, True).wait_send()
+        early(k, True).wait_recv()
     for a in range(3):
         to_side(a).wait_send()
         to_back(a).wait_send()
@@ -308,7 +326,7 @@
             to_core(a, k).wait_send()
 
 
-def front_layer(prefix_len, valid_len, k_pos, cos_t, sin_t, attn_norm, mlp_norm, hidden, w_query, w_key, w_value, w_out, batch, tp):
+def front_layer(prefix_len, valid_len, k_pos, cos_t, sin_t, attn_norm, mlp_norm, hidden, grad, w_query, w_key, w_value, w_out, batch, tp):
     rows, dim = hidden.shape
     head_dim = w_key.shape[1]
     shard = rows // batch
@@ -323,18 +341,18 @@
     return pl.pallas_call(
         functools.partial(front_kernel, batch=batch),
         out_shape=(shape(rows, dim), shape(tp, dim, head_dim), shape(tp, head_dim, dim), shape(tp, rows, 2 * head_dim),
-                   shape(tp, rows, head_dim), shape(rows, tp * head_dim), shape(rows, dim), shape(rows, dim)),
-        in_specs=[pl.BlockSpec(memory_space=pltpu.SMEM)] * 2 + [vmem] * 5 + [anyspace] * 5,
-        out_specs=(anyspace,) * 8,
+                   shape(tp, rows, head_dim), shape(rows, tp * head_dim), shape(rows, dim), shape(rows, dim), shape(tp * rows, dim)),
+        in_specs=[pl.BlockSpec(memory_space=pltpu.SMEM)] * 2 + [vmem] * 5 + [anyspace] * 6,
+        out_specs=(anyspace,) * 9,
         scratch_shapes=[pltpu.VMEM((rows, dim), BF16), pltpu.VMEM((rows, dim), BF16), pltpu.VMEM((dim, 2 * head_dim), BF16),
                         pltpu.VMEM((tp, dim, head_dim), BF16), pltpu.VMEM((tp, head_dim, dim), BF16),
                         pltpu.VMEM((tp, rows, 2 * head_dim), BF16), pltpu.VMEM((tp, rows, head_dim), BF16),
                         pltpu.VMEM((2, tp // 2 * shard, total), BF16), pltpu.VMEM((rows, tp * head_dim), BF16), pltpu.VMEM((rows, dim), F32),
-                        dma((5,)), dma((15,)), dma((3, 8)), dma((3, 8))],
+                        dma((5,)), dma((15,)), dma((3, 8)), dma((3, 8)), dma((4,)), dma((4,))],
         compiler_params=pltpu.CompilerParams(vmem_limit_bytes=62 << 20, collective_id=2, has_side_effects=True),
         cost_estimate=pl.CostEstimate(flops=8 * rows * dim * tp * head_dim, bytes_accessed=60 << 20, transcendentals=tp * rows * total),
         name="front",
-    )(prefix_len, valid_len, k_pos, cos_t, sin_t, attn_norm.reshape(1, dim), mlp_norm.reshape(1, dim), hidden, w_query, w_key, w_value, w_out)
+    )(prefix_len, valid_len, k_pos, cos_t, sin_t, attn_norm.reshape(1, dim), mlp_norm.reshape(1, dim), hidden, grad, w_query, w_key, w_value, w_out)
 
 
 def attention_backward(lens, cos_t, sin_t, query, kv_all, d_mixed, batch, group=8):
@@ -372,7 +390,7 @@
     return (gelu * upper).astype(BF16), (d_act * upper * slope).astype(BF16), (d_act * gelu).astype(BF16)
 
 
-def gated_kernel(z_own, g_own, wg_hbm, wu_hbm, wd_hbm, z_all, g_all, act, d_gate, d_up, diag_in,
+def gated_kernel(z_own, g_own, g_early, wg_hbm, wu_hbm, wd_hbm, z_all, g_all, act, d_gate, d_up, diag_in,
                  wg, wu, wd, z_buf, g_buf, outs, st, from_core, far_send, far_recv, diag_send, diag_recv, w_sem, in_sem, own_sem, out_sem, send, recv, send0, recv0, *, bn):
     rows, dim = z_own.shape
     width = wg_hbm.shape[1]
@@ -428,7 +446,7 @@
     enter((core, side, back))
     for u in range(2):
         for path in range(2):
-            for a in range(2):
+            for a in ((0,) if u == 0 else (0, 1)):
                 link_copy(u, path, a).start()
         if u == 0:
             for a in range(2):
@@ -449,9 +467,12 @@
         starts = [(1 - late) * (first * rows + i * piece) + late * base for i, base in enumerate((base_x, base_y, pair_x, pair_y))]
         return [pl.ds(pl.multiple_of(st, 16), piece) for st in starts]
 
+    def kinds(u):
+        return (0,) if u == 0 else (0, 1)
+
     def pass_on(u):
         for path in range(2):
-            for a in range(2):
+            for a in kinds(u):
                 link_copy(u, path, a).wait_recv()
                 core_copy(u, path, a).start()
 
@@ -553,7 +574,7 @@
                             for a in range(2):
                                 link_copy(later, path, a).start()
                 for path in range(2):
-                    for a in range(2):
+                    for a in kinds(u):
                         core_copy(u, path, a).wait_recv()
 
         @pl.when(s >= 1)
@@ -582,12 +603,12 @@
     for a in range(2):
         own_copy(a).wait_send()
         for path in range(2):
-            for u in range(6):
+            for u in range(a, 6):
                 link_copy(u, path, a).wait_send()
                 core_copy(u, path, a).wait_send()
 
 
-def gated_layer(z_own, g_own, w_gate, w_up, w_down, tp, bn=512):
+def gated_layer(z_own, g_own, g_early, w_gate, w_up, w_down, tp, bn=512):
     rows, dim = z_own.shape
     width = w_gate.shape[1]
     total = rows * tp
@@ -598,8 +619,9 @@
     return pl.pallas_call(
         functools.partial(gated_kernel, bn=bn),
         out_shape=(gathered, gathered, made, made, made, jax.ShapeDtypeStruct((2, rows // 2, dim), BF16)),
-        in_specs=[anyspace] * 5,
+        in_specs=[anyspace] * 6,
         out_specs=(anyspace,) * 6,
+        input_output_aliases={2: 1},
         scratch_shapes=[pltpu.VMEM((dim, width), BF16), pltpu.VMEM((dim, width), BF16), pltpu.VMEM((width, dim), BF16),
                         pltpu.VMEM((rows, dim), BF16), pltpu.VMEM((rows, dim), BF16), pltpu.VMEM((2, 3, rows, bn), BF16),
                         pltpu.VMEM((2, dim // bn, rows, bn), BF16), pltpu.VMEM((dim // bn, rows, bn), BF16),
@@ -607,7 +629,7 @@
         compiler_params=pltpu.CompilerParams(vmem_limit_bytes=67043328, collective_id=0, has_side_effects=True),
         cost_estimate=pl.CostEstimate(flops=6 * total * dim * width, bytes_accessed=200 << 20, transcendentals=total * width),
         name="gated",
-    )(z_own, g_own, w_gate, w_up, w_down)
+    )(z_own, g_own, g_early, w_gate, w_up, w_down)
 
 
 def back_kernel(act, d_gate, d_up, z_all, diag_in, wg_hbm, wu_hbm, wd_hbm, own_out, x_in, y_in, g_gate,
@@ -620,12 +642,14 @@
     def cols(j):
         return pl.ds(pl.multiple_of(j * bn, 128), bn)
 
-    def pair_of(t):
-        return ((t + 5) // 7) * ((t + 1) % 3 + 1)
+    def shard_of(phase, t):
+        if phase == 0:
+            return 1 + t // 2, 1 - t % 2
+        ge = [(t + 8 - k) // 8 for k in range(8)]
+        return ge[2] + ge[3] - ge[5] + 2 * ge[6], 1 - ge[1] + ge[2] - ge[4] + ge[6] - ge[7]
 
     def lhs_copies(phase, t):
-        pair = pair_of(t)
-        theirs = 1 - t // 5 - ((t + 6) // 7 - (t + 5) // 7)
+        pair, theirs = shard_of(phase, t)
         dev = me + (1 - pair // 2) * (side - me) + (1 - pair % 2) * (back - me)
         dev = dev + theirs * (flip(dev, 1) - dev)
         src = pl.ds(pl.multiple_of(dev * rows, 16), rows)
@@ -658,7 +682,7 @@
     def diag_load(k, j):
         return pltpu.make_async_copy(diag_in.at[k, :, cols(j)], from_diag.at[0, k, j], in_sem.at[k, j])
 
-    for cp in lhs_copies(0, 2):
+    for cp in lhs_copies(0, 0):
         cp.start()
     for j in range(steps):
         weight_copy(0, j).start()
@@ -679,34 +703,38 @@
             for cp in lhs_copies(phase, t):
                 cp.wait()
 
-            @pl.when(t < 7)
+            last = 5 if phase == 0 else 7
+
+            @pl.when(t < last)
             def _():
                 for cp in lhs_copies(phase, t + 1):
                     cp.start()
 
             if phase == 0:
-                @pl.when(t == 3)
+                @pl.when(t == 1)
                 def _():
                     for j in range(steps):
                         weight_copy(1, j).start()
 
-                @pl.when(t == 7)
+                @pl.when(t == last)
                 def _():
                     for cp in lhs_copies(1, 0):
                         cp.start()
 
-            @pl.when((t == 0) | ((t >= 2) & (t <= 4)))
+            theirs = (t % 2 == 0) if phase == 0 else ((t % 6 == 0) | (t // 2 == 1))
+
+            @pl.when(theirs)
             def _():
-                pair = pair_of(t)
+                pair = shard_of(phase, t)[0]
 
                 def body(j):
-                    @pl.when(t == (2 if phase == 0 else 0))
+                    @pl.when(t == 0)
                     def _():
                         for k in ((0,) if phase == 0 else (1, 2)):
                             weight_copy(k, j).wait()
 
                     if phase == 0:
-                        @pl.when(t > 2)
+                        @pl.when(t > 0)
                         def _():
                             core_copy(0, j).wait_send()
                     else:
@@ -728,7 +756,7 @@
                     tiles(body)
 
             for k in range(2):
-                @pl.when(t == 5 + k)
+                @pl.when(t == (1 + 2 * k if phase == 0 else 5 - k))
                 def _(k=k):
                     def body(j):
                         core_copy(1 + k, j).wait_recv()
@@ -737,7 +765,7 @@
                         else:
                             diag_copy(phase, 1 - k, j).wait_recv()
                             final_copy(0, k, j).wait_send()
-                        total = product(phase, (5 + k) % 2, j) + from_core[1 + k, j].astype(F32)
+                        total = product(phase, 1 if phase == 0 else 1 - k, j) + from_core[1 + k, j].astype(F32)
                         came = from_diag[phase, 1 - k, j].astype(F32)
                         split = slice(half, rows) if k == 0 else slice(0, half)
                         rest = slice(0, half) if k == 0 else slice(half, rows)
@@ -747,7 +775,7 @@
 
                     tiles(body)
 
-            @pl.when(t == 7)
+            @pl.when(t == last)
             def _():
                 def body(j):
                     core_copy(3, j).wait_recv()
@@ -768,20 +796,22 @@
 
             return carry
 
-        lax.fori_loop(2 if phase == 0 else 0, 8, step, 0)
+        lax.fori_loop(0, 6 if phase == 0 else 8, step, 0)
+
+    first = z_all.shape[0] - 2 * rows
 
     def z_copy(j, c):
-        return pltpu.make_async_copy(z_all.at[pl.ds(c * rows, rows), cols(j)], lhs.at[c // 2, c % 2, :, cols(j)], z_sem.at[j, c])
+        return pltpu.make_async_copy(z_all.at[pl.ds(first + c * rows, rows), cols(j)], lhs.at[0, c, :, cols(j)], z_sem.at[j, c])
 
     def gate_copy(j):
-        return pltpu.make_async_copy(d_gate.at[pl.ds(0, 4 * rows), cols(j)], wa.at[:, cols(j)], w_sem.at[0, j])
+        return pltpu.make_async_copy(d_gate.at[pl.ds(first, 2 * rows), cols(j)], wa.at[pl.ds(0, 2 * rows), cols(j)], w_sem.at[0, j])
 
     def grad_copy(i, j):
         slot = j % 2
         return pltpu.make_async_copy(own_st.at[slot, pl.ds(0, bn)], g_gate.at[cols(i), cols(j)], o_sem.at[slot])
 
     for j in range(steps):
-        for c in range(4):
+        for c in range(2):
             z_copy(j, c).start()
         gate_copy(j).start()
 
@@ -794,14 +824,14 @@
 
         @pl.when(j == 0)
         def _():
-            for c in range(4):
+            for c in range(2):
                 z_copy(i, c).wait()
 
         @pl.when(step >= 2)
         def _():
             grad_copy(i, j).wait()
 
-        own_st[j % 2, :bn] = dot_tn(lhs[:, :, :, cols(i)].reshape(4 * rows, bn), wa[:, cols(j)])
+        own_st[j % 2, :bn] = dot_tn(lhs[0, :, :, cols(i)].reshape(2 * rows, bn), wa[:2 * rows, cols(j)])
         grad_copy(i, j).start()
         return carry
 
@@ -830,10 +860,10 @@
         out_shape=(jax.ShapeDtypeStruct((2, rows, dim), F32), came, came, jax.ShapeDtypeStruct((dim, width), F32)),
         in_specs=[anyspace] * 8,
         out_specs=(anyspace,) * 4,
-        scratch_shapes=[pltpu.VMEM((4 * rows, dim), BF16), pltpu.VMEM((dim, width), BF16), pltpu.VMEM((2, 2, rows, width), BF16),
+        scratch_shapes=[pltpu.VMEM((width, dim), BF16), pltpu.VMEM((dim, width), BF16), pltpu.VMEM((2, 2, rows, width), BF16),
                         pltpu.VMEM((4, steps, rows, bn), BF16), pltpu.VMEM((4, steps, rows, bn), BF16),
                         pltpu.VMEM((2, 2, steps, rows // 2, bn), BF16), pltpu.VMEM((2, rows, bn), F32),
-                        dma((2, steps)), dma((steps, 4)), dma((3, steps)), dma((2, 2)), dma((2,)), dma((steps,)), dma((4, steps)),
+                        dma((2, steps)), dma((steps, 2)), dma((3, steps)), dma((2, 2)), dma((2,)), dma((steps,)), dma((4, steps)),
                         dma((2, steps)), dma((2, 2, steps)), dma((2, steps)), dma((2, 2, steps))],
         compiler_params=pltpu.CompilerParams(vmem_limit_bytes=67043328, collective_id=1, has_side_effects=True),
         cost_estimate=pl.CostEstimate(flops=6 * total * dim * width, bytes_accessed=200 << 20, transcendentals=0),
@@ -971,24 +1001,23 @@
     )(a, b)
 
 
-def rest_kernel(at_ref, a_ref, b_ref, part_ref, o_ref):
+def rest_kernel(a_ref, b_ref, part_ref, o_ref):
     o_ref[...] = part_ref[...] + dot_tn(a_ref[...], b_ref[...])
 
 
-def weight_grad_rest(a, b, part, block, count, bm=1024, bn=512):
+def weight_grad_rest(a, b, part, count, bm=1024, bn=512):
     m, n = part.shape
-    out = pl.BlockSpec((bm, bn), lambda i, j, at: (i, j))
+    out = pl.BlockSpec((bm, bn), lambda i, j: (i, j))
     return pl.pallas_call(
         rest_kernel,
         out_shape=jax.ShapeDtypeStruct((m, n), F32),
-        grid_spec=pltpu.PrefetchScalarGridSpec(
-            num_scalar_prefetch=1, grid=(m // bm, n // bn),
-            in_specs=[pl.BlockSpec((count, bm), lambda i, j, at: (at[0], i)), pl.BlockSpec((count, bn), lambda i, j, at: (at[0], j)), out],
-            out_specs=out),
+        grid=(m // bm, n // bn),
+        in_specs=[pl.BlockSpec((count, bm), lambda i, j: (0, i)), pl.BlockSpec((count, bn), lambda i, j: (0, j)), out],
+        out_specs=out,
         compiler_params=pltpu.CompilerParams(dimension_semantics=("arbitrary", "arbitrary"), vmem_limit_bytes=62 << 20),
         cost_estimate=pl.CostEstimate(flops=2 * count * m * n, bytes_accessed=80 << 20, transcendentals=0),
         name="weight_grad_rest",
-    )(jnp.asarray(block, jnp.int32).reshape(1), a, b, part)
+    )(a, b, part)
 
 
 def hop_diagonal(diag):
@@ -1020,11 +1049,11 @@
         cos_own, sin_own = rope_tables(me * shard + jnp.arange(shard), head_dim)
         hidden = hidden.reshape(rows, dim)
         grad_out = grad_out.reshape(rows, dim)
-        normed, wq_all, wo_all, kv_all, query, mixed, resid, gated_in = front_layer(
-            prefix_len, valid_len, k_pos, cos_own, sin_own, attn_norm, mlp_norm, hidden, w_query, w_key, w_value, w_out, batch, tp_size)
+        normed, wq_all, wo_all, kv_all, query, mixed, resid, gated_in, grad_early = front_layer(
+            prefix_len, valid_len, k_pos, cos_own, sin_own, attn_norm, mlp_norm, hidden, grad_out, w_query, w_key, w_value, w_out, batch, tp_size)
         wo_all = wo_all.reshape(tp_size * head_dim, dim)
 
-        gated_all, grad_all, act, d_gate, d_upper, diag_in = gated_layer(gated_in, grad_out, w_gate, w_up, w_down, tp_size)
+        gated_all, grad_all, act, d_gate, d_upper, diag_in = gated_layer(gated_in, grad_out, grad_early, w_gate, w_up, w_down, tp_size)
         own_part, x_part, y_part, g_gate_part = back_layer(act, d_gate, d_upper, gated_all, diag_in, w_gate, w_up, w_down, tp_size)
         hidden_out, d_resid, g_mlp_norm_part, d_mixed, g_out_part = join_layer(
             own_part, x_part, y_part, resid, grad_out, mlp_norm, wo_all, mixed)
@@ -1058,7 +1087,7 @@
         last_side = swap(q_next[0], 2)
         q_last = (last_side, swap(q_next[1], 4))
         norms_near = [swap(norms, bit) for bit in (2, 4, 6)]
-        g_gate = weight_grad_rest(gated_all, d_gate, g_gate_part, 1, 4 * rows)
+        g_gate = weight_grad_rest(gated_all, d_gate, g_gate_part, 6 * rows)
         norms_near, g_gate, d_upper = lax.optimization_barrier((norms_near, g_gate, d_upper))
         norms = norms + norms_near[0] + norms_near[1] + norms_near[2]
         norms, d_upper = lax.optimization_barrier((norms, d_upper))

time: 878 us -> 871 us (level)
  waiting for transfers between devices: 134 us -> 124 us
    pallas_call x1, Pallas kernels: 165 us -> 151 us  [back_layer(): pl.pallas_call(functools.partial(back_kernel, rows=rows, bn=bn), out_shap...]
    psum x1, waiting for transfers between devices: 11.4 us -> 0.24 us  [layer(): g_key, g_value = lax.psum((g_key_part, g_value_part), 'tp')]
    pallas_call x1, Pallas kernels: 30 us -> 40.7 us  [weight_grad_rest(): pl.pallas_call(rest_kernel, out_shape=jax.ShapeDtypeStruct((m, n), F32),...]
    pallas_call x1, Pallas kernels: 102 us -> 111 us  [front_layer(): pl.pallas_call(functools.partial(front_kernel, batch=batch), out_shape=(s...]
  transfers between devices with their start and end apart: 16 -> 16, of which waited for: 4 -> 4; matrix products, arithmetic and copies ran while one was open for 4% -> 4% of each run, Pallas kernels for 14% -> 16%
where the time goes in v10:
time: 871 us; the launch traced here: 863 us
  Pallas kernels  661 us (76%)
  waiting for transfers between devices  124 us (14%)
  matrix products  19.5 us (2%)
  other arithmetic  16.2 us (2%)
  local copies, waits for them, and re-layouts  15.5 us (2%)
  between operations  14.5 us (2%)
  starting transfers between devices  12.4 us (1%)
    pallas_call x1, Pallas kernels, gated_layer(): pl.pallas_call(functools.partial(gated_kernel, bn=bn), out_shape=(gathere...  189 us
    pallas_call x1, Pallas kernels, back_layer(): pl.pallas_call(functools.partial(back_kernel, rows=rows, bn=bn), out_shap...  151 us
    reduce_scatter x1, waiting for transfers between devices, layer(): g_out = lax.psum_scatter(g_out_part, 'tp', scatter_dimension=0, tiled=True)  115 us
    pallas_call x1, Pallas kernels, front_layer(): pl.pallas_call(functools.partial(front_kernel, batch=batch), out_shape=(s...  111 us
    pallas_call x2, Pallas kernels, weight_grad(): pl.pallas_call(product_kernel, out_shape=jax.ShapeDtypeStruct((m, n), F32...  95.7 us
    pallas_call x1, Pallas kernels, weight_grad_rest(): pl.pallas_call(rest_kernel, out_shape=jax.ShapeDtypeStruct((m, n), F32),...  40.7 us
    pallas_call x1, Pallas kernels, attention_backward(): pl.pallas_call(attn_bwd_kernel, out_shape=(jax.ShapeDtypeStruct((heads, r...  32.5 us
    pallas_call x1, Pallas kernels, join_layer(): pl.pallas_call(functools.partial(join_kernel, joins=joins), out_shape=(ac...  28.2 us
  transfers between devices with their start and end apart: 16, of which 4 were waited for; matrix products, arithmetic and copies ran while one was open for 4% of the time, Pallas kernels for 16%

profile of v10, /device:TPU:0, one launch (start us, length us, event | category | flops | bytes accessed | tf_op | source)
XLA Modules:
  0.0 863.0 jit_solution(10895522362865324722)
XLA Ops:
  13.9 110.8 %front.1 = (bf16[576,2048]{1,0:T(8,128)(2,1)}, bf16[8,2048,256]{2,1,0:T(8,128)(2,1)}, bf16[8,256,2048]{2,1,0:T(8,128)(2,1)}, bf16[8,576,512]{2,1,0:T(8,128)(2,1)...) custom-call(s32[3]{0:T(128)} %prefix_ref.1, ...), custom_call_target="tpu_custom_call" | custom-call | flops 19327352832 | bytes 62914560 | tf_op jit(solution)/shard_map/front/pallas_call | solution.py:341
  124.6 189.0 %gated.1 = (bf16[4608,2048]{1,0:T(8,128)(2,1)}, bf16[4608,2048]{1,0:T(8,128)(2,1)}, bf16[4608,2048]{1,0:T(8,128)(2,1)}, bf16[4608,2048]{1,0:T(8,128)(2,1)}, bf16...) custom-call(bf16[576,2048]{1,0:T(8,128)(2,1)} %get-tuple-element.73.z_own, ...), custom_call_target="tpu_custom_call", output_to_operand_aliasing={{1}: (2, {})} | custom-call | flops 115964116992 | bytes 209715200 | tf_op jit(solution)/shard_map/gated/pallas_call | solution.py:619
  313.7 151.4 %back.1 = (f32[2,576,2048]{2,1,0:T(8,128)}, bf16[2,576,2048]{2,1,0:T(8,128)(2,1)}, bf16[2,576,2048]{2,1,0:T(8,128)(2,1)}, f32[2048,2048]{1,0:T(8,128)}) custom-call(bf16[4608,2048]{1,0:T(8,128)(2,1)} %get-tuple-element.102.act.a_ref, bf16[4608,2048]{1,0:T(8,128)(2,1)} %get-tuple-element.116.d_gate.b_ref, bf16[4608,2048]{1,0:T(8,128)(2,1)} %get-tuple-element.125.d_up.b_ref, ...), custom_call_target="tpu_custom_call" | custom-call | flops 115964116992 | bytes 209715200 | tf_op jit(solution)/shard_map/back/pallas_call | solution.py:858
  465.0 28.2 %join.1 = (bf16[576,2048]{1,0:T(8,128)(2,1)}, bf16[576,2048]{1,0:T(8,128)(2,1)}, f32[1,2048]{1,0:T(1,128)}, bf16[576,2048]{1,0:T(8,128)(2,1)}, f32[2048,2048]{1,0:T(8,128)}) custom-call(f32[2,576,2048]{2,1,0:T(8,128)} %get-tuple-element.80.own_ref, bf16[2,576,2048]{2,1,0:T(8,128)(2,1)} %get-tuple-element.81.x_ref, ...), custom_call_target="tpu_custom_call" | custom-call | flops 9663676416 | bytes 62914560 | tf_op jit(solution)/shard_map/join/pallas_call | solution.py:917
  493.3 32.5 %attn_bwd.1 = (bf16[8,576,256]{2,1,0:T(8,128)(2,1)}, bf16[4,576,512]{2,1,0:T(8,128)(2,1)}, bf16[4,576,512]{2,1,0:T(8,128)(2,1)}) custom-call(s32[11,3]{1,0:T(8,128)} %add_add_fusion.1.lens_ref, f32[192,128]{1,0:T(8,128)} %get-tuple-element.185.cos_ref, f32[192,128]{1,0:T(8,128)} %get-tuple-element.184.sin_ref, bf16[8,576,256]{2,1,0:T(8,128)(2,1)} %get-tuple-element.87.q_ref, ...), custom_call_target="tpu_custom_call" | custom-call | flops 18119393280 | bytes 20971520 | tf_op jit(solution)/shard_map/attn_bwd/pallas_call | solution.py:367
  525.9 5.7 fusion.1
  532.2 10.2 %convolution_bitcast_fusion.part_ref = f32[576,2048]{1,0:T(8,128)} fusion(bf16[8,576,256]{2,1,0:T(8,128)(2,1)S(1)} %copy-done.6, bf16[8,2048,256]{2,1,0:T(8,128)(2,1)} %get-tuple-element.95), kind=kOutput, calls=%fused_computation.1 | convolution fusion | flops 4831838208 | bytes 15466496 | tf_op jit(solution)/shard_map/hte,hde->td/dot_general | solution.py:1071
  542.4 1.7 convert_add_fusion
  544.2 1.8 collective-permute-start.1
  546.5 6.8 collective-permute-done.1
  558.6 3.5 convolution_add_fusion
  562.1 1.9 slice_bitcast_fusion
  564.1 2.3 copy-done
  566.8 1.7 collective-permute-start.7
  568.5 48.0 %weight_grad.2 = f32[2048,2048]{1,0:T(8,128)} custom-call(bf16[4608,2048]{1,0:T(8,128)(2,1)} %get-tuple-element.102.act.a_ref, bf16[4608,2048]{1,0:T(8,128)(2,1)} %get-tuple-element.103.b_ref), custom_call_target="tpu_custom_call" | custom-call | flops 38654705664 | bytes 115343360 | tf_op jit(solution)/shard_map/weight_grad/pallas_call | solution.py:992
  617.3 12.7 %finish.1 = (f32[2048,256]{1,0:T(8,128)}, f32[2048,256]{1,0:T(8,128)}, bf16[576,2048]{1,0:T(8,128)(2,1)}, f32[1,2048]{1,0:T(1,128)}) custom-call(f32[576,512]{1,0:T(8,128)} %get-tuple-element.179.kv_ref, bf16[576,512]{1,0:T(8,128)(2,1)} %collective-permute-done.3.side_ref, bf16[576,512]{1,0:T(8,128)(2,1)} %copy-done.5, ...), custom_call_target="tpu_custom_call" | custom-call | flops 2415919104 | bytes 25165824 | tf_op jit(solution)/shard_map/finish/pallas_call | solution.py:973
  630.8 2.6 bitcast_add_fusion.1
  633.3 2.5 pad_maximum_fusion
  642.1 40.7 %weight_grad_rest.1 = f32[2048,2048]{1,0:T(8,128)} custom-call(bf16[4608,2048]{1,0:T(8,128)(2,1)} %get-tuple-element.78.z_all.a_ref, bf16[4608,2048]{1,0:T(8,128)(2,1)} %get-tuple-element.116.d_gate.b_ref, f32[2048,2048]{1,0:T(8,128)} %get-tuple-element.117.part_ref), custom_call_target="tpu_custom_call" | custom-call | flops 28991029248 | bytes 83886080 | tf_op jit(solution)/shard_map/weight_grad_rest/pallas_call | solution.py:1011
  682.9 47.7 %weight_grad.3 = f32[2048,2048]{1,0:T(8,128)} custom-call(bf16[4608,2048]{1,0:T(8,128)(2,1)} %get-tuple-element.78.z_all.a_ref, bf16[4608,2048]{1,0:T(8,128)(2,1)} %get-tuple-element.125.d_up.b_ref), custom_call_target="tpu_custom_call" | custom-call | flops 38654705664 | bytes 115343360 | tf_op jit(solution)/shard_map/weight_grad/pallas_call | solution.py:992
  730.7 3.4 fusion.4
  734.1 1.8 copy.31
  736.8 114.8 %reduce-scatter.2.cloned.1.call-done = f32[256,2048]{1,0:T(8,128)} async-done(((f32[2048,2048]{1,0:T(8,128)}), f32[256,2048]{1,0:T(8,128)}) %reduce-scatter.2.cloned.1.call-update) | async-done | bytes 2097168 | tf_op jit(solution)/shard_map/reduce_scatter | solution.py:1060
  851.6 3.0 copy.35
  (69 shorter events, 23.5 us)
Async XLA Ops:
  7.2 729.6 %all-reduce.3.cloned.1.call-start = ((), (), s32[]{:S(2)}) async-start(), calls=%async_computation.2 | async-start | bytes 8388608 | tf_op jit(solution)/shard_map/psum | solution.py:1086
  525.8 5.8 collective-permute-start
  525.9 6.2 copy-start.6
  531.6 27.0 %collective-permute-start.5 = (f32[4,256,2048]{2,1,0:T(8,128)S(1)}, f32[4,256,2048]{2,1,0:T(8,128)S(1)}, u32[]{:S(2)}, u32[]{:S(2)}) collective-permute-start(f32[4,256,2048]{2,1,0:T(8,128)S(1)} %fusion.1), channel_id=1, source_target_pairs={{0,1},{1,0},{2,3},{3,2},{4,5},{5,4},{6,7},{7,6},{8,9},{9,8},{10,11... | collective-permute-start | bytes 25165832 | tf_op jit(solution)/shard_map/ppermute | solution.py:41
  532.2 10.3 %copy-start.3 = (bf16[4,576,512]{2,1,0:T(8,128)(2,1)S(1)}, bf16[4,576,512]{2,1,0:T(8,128)(2,1)}, u32[]{:S(2)}) copy-start(bf16[4,576,512]{2,1,0:T(8,128)(2,1)} %get-tuple-element.90) | copy-start | bytes 7077892
  544.2 9.0 %collective-permute-start.1 = (bf16[288,512]{1,0:T(8,128)(2,1)S(1)}, bf16[288,512]{1,0:T(8,128)(2,1)S(1)}, u32[]{:S(2)}, u32[]{:S(2)}) collective-permute-start(bf16[288,512]{1,0:T(8,128)(2,1)S(1)} %get-tuple-element.181), channel_id=1, source_target_pairs={{0,2},{1,3},{2,0},{3,1},{4,6},{5,7},{6,4},{7,5},{8,10},{9,11},{10,... | collective-permute-start | bytes 884744 | tf_op jit(solution)/shard_map/ppermute | solution.py:41
  546.0 8.7 %collective-permute-start.2 = (bf16[288,512]{1,0:T(8,128)(2,1)S(1)}, bf16[288,512]{1,0:T(8,128)(2,1)S(1)}, u32[]{:S(2)}, u32[]{:S(2)}) collective-permute-start(bf16[288,512]{1,0:T(8,128)(2,1)S(1)} %get-tuple-element.180), channel_id=1, source_target_pairs={{0,4},{1,5},{2,6},{3,7},{4,0},{5,1},{6,2},{7,3},{8,12},{9,13},{10,... | collective-permute-start | bytes 884744 | tf_op jit(solution)/shard_map/ppermute | solution.py:41
  546.5 12.1 %copy-start.1 = (bf16[576,2048]{1,0:T(8,128)(2,1)S(1)}, bf16[576,2048]{1,0:T(8,128)(2,1)}, u32[]{:S(2)}) copy-start(bf16[576,2048]{1,0:T(8,128)(2,1)} %get-tuple-element.93.normed_ref) | copy-start | bytes 7077892
  555.7 60.8 %collective-permute-start.4 = (bf16[576,512]{1,0:T(8,128)(2,1)}, bf16[576,512]{1,0:T(8,128)(2,1)S(1)}, u32[]{:S(2)}, u32[]{:S(2)}) collective-permute-start(bf16[576,512]{1,0:T(8,128)(2,1)} %pad_maximum_fusion.3), channel_id=1, source_target_pairs={{0,4},{1,5},{2,6},{3,7},{4,0},{5,1},{6,2},{7,3},{8,12},{9,13},{10,... | collective-permute-start | bytes 1769480 | tf_op jit(solution)/shard_map/ppermute | solution.py:41
  557.0 59.5 %collective-permute-start.3 = (bf16[576,512]{1,0:T(8,128)(2,1)}, bf16[576,512]{1,0:T(8,128)(2,1)}, u32[]{:S(2)}, u32[]{:S(2)}) collective-permute-start(bf16[576,512]{1,0:T(8,128)(2,1)} %pad_maximum_fusion.2), channel_id=1, source_target_pairs={{0,2},{1,3},{2,0},{3,1},{4,6},{5,7},{6,4},{7,5},{8,10},{9,11},{10,... | collective-permute-start | bytes 1769480 | tf_op jit(solution)/shard_map/ppermute | solution.py:41
  562.1 4.2 copy-start
  566.4 50.1 %collective-permute-start.6 = (f32[128,2048]{1,0:T(8,128)}, f32[128,2048]{1,0:T(8,128)}, u32[]{:S(2)}, u32[]{:S(2)}) collective-permute-start(f32[128,2048]{1,0:T(8,128)} %get-tuple-element.175), channel_id=1, source_target_pairs={{0,2},{1,3},{2,0},{3,1},{4,6},{5,7},{6,4},{7,5},{8,10},{9,11},{10,... | collective-permute-start | bytes 3145736 | tf_op jit(solution)/shard_map/ppermute | solution.py:41
  566.8 49.7 %collective-permute-start.7 = (f32[128,2048]{1,0:T(8,128)}, f32[128,2048]{1,0:T(8,128)}, u32[]{:S(2)}, u32[]{:S(2)}) collective-permute-start(f32[128,2048]{1,0:T(8,128)} %get-tuple-element.174), channel_id=1, source_target_pairs={{0,4},{1,5},{2,6},{3,7},{4,0},{5,1},{6,2},{7,3},{8,12},{9,13},{10,... | collective-permute-start | bytes 3145736 | tf_op jit(solution)/shard_map/ppermute | solution.py:41
  616.5 0.9 copy-start.5
  617.3 12.7 %copy-start.7 = (f32[1,2048]{1,0:T(1,128)S(1)}, f32[1,2048]{1,0:T(1,128)}, u32[]{:S(2)}) copy-start(f32[1,2048]{1,0:T(1,128)} %get-tuple-element.114) | copy-start | bytes 24580
  630.7 2.6 copy-start.2
  635.9 215.7 %reduce-scatter.2.cloned.1.call-start = ((), (), s32[]{:S(2)}) async-start(), calls=%async_computation.1 | async-start | bytes 18874368 | tf_op jit(solution)/shard_map/reduce_scatter | solution.py:1060
  636.7 46.2 %collective-permute-start.10 = (f32[2,2048]{1,0:T(2,128)S(1)}, f32[2,2048]{1,0:T(2,128)S(1)}, u32[]{:S(2)}, u32[]{:S(2)}) collective-permute-start(f32[2,2048]{1,0:T(2,128)S(1)} %pad_maximum_fusion.4), channel_id=1, source_target_pairs={{0,6},{1,7},{2,4},{3,5},{4,2},{5,3},{6,0},{7,1},{8,14},{9,15},{10,... | collective-permute-start | bytes 49160 | tf_op jit(solution)/shard_map/ppermute | solution.py:41
  638.1 44.8 %collective-permute-start.8 = (f32[2,2048]{1,0:T(2,128)S(1)}, f32[2,2048]{1,0:T(2,128)S(1)}, u32[]{:S(2)}, u32[]{:S(2)}) collective-permute-start(f32[2,2048]{1,0:T(2,128)S(1)} %pad_maximum_fusion.4), channel_id=1, source_target_pairs={{0,2},{1,3},{2,0},{3,1},{4,6},{5,7},{6,4},{7,5},{8,10},{9,11},{10,... | collective-permute-start | bytes 49160 | tf_op jit(solution)/shard_map/ppermute | solution.py:41
  638.5 44.4 %collective-permute-start.9 = (f32[2,2048]{1,0:T(2,128)S(1)}, f32[2,2048]{1,0:T(2,128)S(1)}, u32[]{:S(2)}, u32[]{:S(2)}) collective-permute-start(f32[2,2048]{1,0:T(2,128)S(1)} %pad_maximum_fusion.4), channel_id=1, source_target_pairs={{0,4},{1,5},{2,6},{3,7},{4,0},{5,1},{6,2},{7,3},{8,12},{9,13},{10,... | collective-permute-start | bytes 49160 | tf_op jit(solution)/shard_map/ppermute | solution.py:41
  640.2 90.5 %collective-permute-start.12 = (f32[256,2048]{1,0:T(8,128)}, f32[256,2048]{1,0:T(8,128)}, u32[]{:S(2)}, u32[]{:S(2)}) collective-permute-start(f32[256,2048]{1,0:T(8,128)} %get-tuple-element.123), channel_id=1, source_target_pairs={{0,2},{1,3},{2,0},{3,1},{4,6},{5,7},{6,4},{7,5},{8,10},{9,11},{10,... | collective-permute-start | bytes 6291464 | tf_op jit(solution)/shard_map/ppermute | solution.py:41
  640.5 90.2 %collective-permute-start.13 = (f32[256,2048]{1,0:T(8,128)}, f32[256,2048]{1,0:T(8,128)}, u32[]{:S(2)}, u32[]{:S(2)}) collective-permute-start(f32[256,2048]{1,0:T(8,128)} %get-tuple-element.124), channel_id=1, source_target_pairs={{0,4},{1,5},{2,6},{3,7},{4,0},{5,1},{6,2},{7,3},{8,12},{9,13},{10,... | collective-permute-start | bytes 6291464 | tf_op jit(solution)/shard_map/ppermute | solution.py:41
  682.9 47.8 %collective-permute-start.11 = (f32[2,2048]{1,0:T(2,128)S(1)}, f32[2,2048]{1,0:T(2,128)S(1)}, u32[]{:S(2)}, u32[]{:S(2)}) collective-permute-start(f32[2,2048]{1,0:T(2,128)S(1)} %add_add_fusion), channel_id=1, source_target_pairs={{0,1},{1,0},{2,3},{3,2},{4,5},{5,4},{6,7},{7,6},{8,9},{9,8},{10,11... | collective-permute-start | bytes 49160 | tf_op jit(solution)/shard_map/ppermute | solution.py:41
  736.8 117.8 %copy-start.4 = (f32[2048,256]{1,0:T(8,128)S(1)}, f32[2048,256]{1,0:T(8,128)}, u32[]{:S(2)}) copy-start(f32[2048,256]{1,0:T(8,128)} %get-tuple-element.193) | copy-start | bytes 6291460
Sparse Core Ops, SparseCore 0:
  636.0 100.7 all-reduce.2
  740.9 110.6 reduce-scatter.1

commit v11 on v10

--- a/solution.py
+++ b/solution.py
@@ -118,9 +118,9 @@
                                         device_id={"tp": peer}, device_id_type=pl.DeviceIdType.MESH)
 
 
-def front_kernel(prefix_ref, valid_ref, kpos_ref, cos_ref, sin_ref, gain1_ref, gain2_ref, hidden, grad, w_query, w_key, w_value, w_out,
-                 normed_out, wq_all, wo_all, kv_all, query_out, mixed_out, resid_out, gated_out, g_all,
-                 x_buf, n_buf, wkv, wq, wo, kv, q, probs, mix, acc, load, store, send, recv, early_send, early_recv, *, batch):
+def front_kernel(prefix_ref, valid_ref, kpos_ref, cos_ref, sin_ref, gain1_ref, gain2_ref, hidden, w_query, w_key, w_value, w_out,
+                 normed_out, wq_all, wo_all, kv_all, query_out, mixed_out, resid_out, gated_out,
+                 x_buf, n_buf, wkv, wq, wo, kv, q, probs, mix, acc, load, store, send, recv, *, batch):
     rows, dim = x_buf.shape
     shard = rows // batch
     head_dim = w_key.shape[1]
@@ -144,15 +144,6 @@
 
     def to_core(a, k):
         return remote(bufs[a].at[k], bufs[a].at[near + k], send.at[a, 4 + k], recv.at[a, 4 + k], core)
-
-    piece = rows // 4
-
-    def early(k, onto_core):
-        shard_at = ((side, back)[k] if onto_core else me) * rows + 2 * k * piece
-        there = g_all.at[pl.ds(pl.multiple_of(shard_at, 16), piece)]
-        src = there if onto_core else grad.at[pl.ds(2 * k * piece, piece)]
-        at = 2 * int(onto_core) + k
-        return remote(src, there, early_send.at[at], early_recv.at[at], core if onto_core else (side, back)[k])
 
     loads = [pltpu.make_async_copy(src, dst, load.at[i]) for i, (src, dst) in enumerate((
         (w_query, wq.at[0]), (hidden, x_buf), (w_key, wkv.at[:, :head_dim]), (w_value, wkv.at[:, head_dim:]), (w_out, wo.at[0])))]
@@ -275,8 +266,6 @@
     for cp in mixed_stores:
         cp.start()
     pass_on(2)
-    for k in range(2):
-        early(k, False).start()
 
     def project(k, first):
         def step(n, carry):
@@ -295,9 +284,6 @@
     pass_last(2)
     project(3, False)
     stores["wo"].start()
-    for k in range(2):
-        early(k, False).wait_recv()
-        early(k, True).start()
     stores["normed"].wait()
 
     def norm2(i, carry):
@@ -313,10 +299,6 @@
         cp.wait()
     for name in ("wq", "wo", "kv", "query", "resid", "gated"):
         stores[name].wait()
-    for k in range(2):
-        early(k, False).wait_send()
-        early(k, True).wait_send()
-        early(k, True).wait_recv()
     for a in range(3):
         to_side(a).wait_send()
         to_back(a).wait_send()
@@ -326,7 +308,7 @@
             to_core(a, k).wait_send()
 
 
-def front_layer(prefix_len, valid_len, k_pos, cos_t, sin_t, attn_norm, mlp_norm, hidden, grad, w_query, w_key, w_value, w_out, batch, tp):
+def front_layer(prefix_len, valid_len, k_pos, cos_t, sin_t, attn_norm, mlp_norm, hidden, w_query, w_key, w_value, w_out, batch, tp):
     rows, dim = hidden.shape
     head_dim = w_key.shape[1]
     shard = rows // batch
@@ -341,18 +323,18 @@
     return pl.pallas_call(
         functools.partial(front_kernel, batch=batch),
         out_shape=(shape(rows, dim), shape(tp, dim, head_dim), shape(tp, head_dim, dim), shape(tp, rows, 2 * head_dim),
-                   shape(tp, rows, head_dim), shape(rows, tp * head_dim), shape(rows, dim), shape(rows, dim), shape(tp * rows, dim)),
-        in_specs=[pl.BlockSpec(memory_space=pltpu.SMEM)] * 2 + [vmem] * 5 + [anyspace] * 6,
-        out_specs=(anyspace,) * 9,
+                   shape(tp, rows, head_dim), shape(rows, tp * head_dim), shape(rows, dim), shape(rows, dim)),
+        in_specs=[pl.BlockSpec(memory_space=pltpu.SMEM)] * 2 + [vmem] * 5 + [anyspace] * 5,
+        out_specs=(anyspace,) * 8,
         scratch_shapes=[pltpu.VMEM((rows, dim), BF16), pltpu.VMEM((rows, dim), BF16), pltpu.VMEM((dim, 2 * head_dim), BF16),
                         pltpu.VMEM((tp, dim, head_dim), BF16), pltpu.VMEM((tp, head_dim, dim), BF16),
                         pltpu.VMEM((tp, rows, 2 * head_dim), BF16), pltpu.VMEM((tp, rows, head_dim), BF16),
                         pltpu.VMEM((2, tp // 2 * shard, total), BF16), pltpu.VMEM((rows, tp * head_dim), BF16), pltpu.VMEM((rows, dim), F32),
-                        dma((5,)), dma((15,)), dma((3, 8)), dma((3, 8)), dma((4,)), dma((4,))],
+                        dma((5,)), dma((15,)), dma((3, 8)), dma((3, 8))],
         compiler_params=pltpu.CompilerParams(vmem_limit_bytes=62 << 20, collective_id=2, has_side_effects=True),
         cost_estimate=pl.CostEstimate(flops=8 * rows * dim * tp * head_dim, bytes_accessed=60 << 20, transcendentals=tp * rows * total),
         name="front",
-    )(prefix_len, valid_len, k_pos, cos_t, sin_t, attn_norm.reshape(1, dim), mlp_norm.reshape(1, dim), hidden, grad, w_query, w_key, w_value, w_out)
+    )(prefix_len, valid_len, k_pos, cos_t, sin_t, attn_norm.reshape(1, dim), mlp_norm.reshape(1, dim), hidden, w_query, w_key, w_value, w_out)
 
 
 def attention_backward(lens, cos_t, sin_t, query, kv_all, d_mixed, batch, group=8):
@@ -390,7 +372,7 @@
     return (gelu * upper).astype(BF16), (d_act * upper * slope).astype(BF16), (d_act * gelu).astype(BF16)
 
 
-def gated_kernel(z_own, g_own, g_early, wg_hbm, wu_hbm, wd_hbm, z_all, g_all, act, d_gate, d_up, diag_in,
+def gated_kernel(z_own, g_own, wg_hbm, wu_hbm, wd_hbm, z_all, g_all, act, d_gate, d_up, diag_in,
                  wg, wu, wd, z_buf, g_buf, outs, st, from_core, far_send, far_recv, diag_send, diag_recv, w_sem, in_sem, own_sem, out_sem, send, recv, send0, recv0, *, bn):
     rows, dim = z_own.shape
     width = wg_hbm.shape[1]
@@ -446,7 +428,7 @@
     enter((core, side, back))
     for u in range(2):
         for path in range(2):
-            for a in ((0,) if u == 0 else (0, 1)):
+            for a in range(2):
                 link_copy(u, path, a).start()
         if u == 0:
             for a in range(2):
@@ -467,14 +449,16 @@
         starts = [(1 - late) * (first * rows + i * piece) + late * base for i, base in enumerate((base_x, base_y, pair_x, pair_y))]
         return [pl.ds(pl.multiple_of(st, 16), piece) for st in starts]
 
-    def kinds(u):
-        return (0,) if u == 0 else (0, 1)
-
     def pass_on(u):
         for path in range(2):
-            for a in kinds(u):
+            for a in range(2):
                 link_copy(u, path, a).wait_recv()
                 core_copy(u, path, a).start()
+        later = (2,) if u == 0 else (3, 4, 5) if u == 1 else ()
+        for v in later:
+            for path in range(2):
+                for a in range(2):
+                    link_copy(v, path, a).start()
 
     def far_copy(j):
         return remote(st.at[0, j], from_core.at[j], far_send.at[j], far_recv.at[j], core)
@@ -528,9 +512,10 @@
                 for cp in weight_copies(n):
                     cp.wait()
 
-            @pl.when((s == 6) & (n == steps - 1))
-            def _():
-                pass_on(5)
+            for u in range(6):
+                @pl.when((s == u + 1) & (n == steps - 1))
+                def _(u=u):
+                    pass_on(u)
 
             cols = pl.ds(pl.multiple_of(n * bn, 128), bn)
             res = gated_tile(z_buf[...], g_buf[...], wg[:, cols], wu[:, cols], wd[cols, :])
@@ -560,21 +545,10 @@
         for u in range(6):
             @pl.when(s == u + 2)
             def _(u=u):
-                if u < 5:
-                    pass_on(u)
                 if u == 4:
                     down_diagonal()
-                if u < 2:
-                    for path in range(2):
-                        for a in range(2):
-                            link_copy(u + 2, path, a).start()
-                if u == 1:
-                    for later in (4, 5):
-                        for path in range(2):
-                            for a in range(2):
-                                link_copy(later, path, a).start()
                 for path in range(2):
-                    for a in kinds(u):
+                    for a in range(2):
                         core_copy(u, path, a).wait_recv()
 
         @pl.when(s >= 1)
@@ -603,12 +577,12 @@
     for a in range(2):
         own_copy(a).wait_send()
         for path in range(2):
-            for u in range(a, 6):
+            for u in range(6):
                 link_copy(u, path, a).wait_send()
                 core_copy(u, path, a).wait_send()
 
 
-def gated_layer(z_own, g_own, g_early, w_gate, w_up, w_down, tp, bn=512):
+def gated_layer(z_own, g_own, w_gate, w_up, w_down, tp, bn=512):
     rows, dim = z_own.shape
     width = w_gate.shape[1]
     total = rows * tp
@@ -619,9 +593,8 @@
     return pl.pallas_call(
         functools.partial(gated_kernel, bn=bn),
         out_shape=(gathered, gathered, made, made, made, jax.ShapeDtypeStruct((2, rows // 2, dim), BF16)),
-        in_specs=[anyspace] * 6,
+        in_specs=[anyspace] * 5,
         out_specs=(anyspace,) * 6,
-        input_output_aliases={2: 1},
         scratch_shapes=[pltpu.VMEM((dim, width), BF16), pltpu.VMEM((dim, width), BF16), pltpu.VMEM((width, dim), BF16),
                         pltpu.VMEM((rows, dim), BF16), pltpu.VMEM((rows, dim), BF16), pltpu.VMEM((2, 3, rows, bn), BF16),
                         pltpu.VMEM((2, dim // bn, rows, bn), BF16), pltpu.VMEM((dim // bn, rows, bn), BF16),
@@ -629,7 +602,7 @@
         compiler_params=pltpu.CompilerParams(vmem_limit_bytes=67043328, collective_id=0, has_side_effects=True),
         cost_estimate=pl.CostEstimate(flops=6 * total * dim * width, bytes_accessed=200 << 20, transcendentals=total * width),
         name="gated",
-    )(z_own, g_own, g_early, w_gate, w_up, w_down)
+    )(z_own, g_own, w_gate, w_up, w_down)
 
 
 def back_kernel(act, d_gate, d_up, z_all, diag_in, wg_hbm, wu_hbm, wd_hbm, own_out, x_in, y_in, g_gate,
@@ -1049,11 +1022,11 @@
         cos_own, sin_own = rope_tables(me * shard + jnp.arange(shard), head_dim)
         hidden = hidden.reshape(rows, dim)
         grad_out = grad_out.reshape(rows, dim)
-        normed, wq_all, wo_all, kv_all, query, mixed, resid, gated_in, grad_early = front_layer(
-            prefix_len, valid_len, k_pos, cos_own, sin_own, attn_norm, mlp_norm, hidden, grad_out, w_query, w_key, w_value, w_out, batch, tp_size)
+        normed, wq_all, wo_all, kv_all, query, mixed, resid, gated_in = front_layer(
+            prefix_len, valid_len, k_pos, cos_own, sin_own, attn_norm, mlp_norm, hidden, w_query, w_key, w_value, w_out, batch, tp_size)
         wo_all = wo_all.reshape(tp_size * head_dim, dim)
 
-        gated_all, grad_all, act, d_gate, d_upper, diag_in = gated_layer(gated_in, grad_out, grad_early, w_gate, w_up, w_down, tp_size)
+        gated_all, grad_all, act, d_gate, d_upper, diag_in = gated_layer(gated_in, grad_out, w_gate, w_up, w_down, tp_size)
         own_part, x_part, y_part, g_gate_part = back_layer(act, d_gate, d_upper, gated_all, diag_in, w_gate, w_up, w_down, tp_size)
         hidden_out, d_resid, g_mlp_norm_part, d_mixed, g_out_part = join_layer(
             own_part, x_part, y_part, resid, grad_out, mlp_norm, wo_all, mixed)

time: 871 us -> 863 us (level)
    pallas_call x1, Pallas kernels: 111 us -> 102 us  [front_layer(): pl.pallas_call(functools.partial(front_kernel, batch=batch), out_shape=(s...]
where the time goes in v11:
time: 863 us; the launch traced here: 855 us
  Pallas kernels  654 us (76%)
  waiting for transfers between devices  123 us (14%)
  matrix products  19.5 us (2%)
  other arithmetic  16.2 us (2%)
  local copies, waits for them, and re-layouts  15.5 us (2%)
  between operations  14.5 us (2%)
  starting transfers between devices  12.6 us (1%)
    pallas_call x1, Pallas kernels, gated_layer(): pl.pallas_call(functools.partial(gated_kernel, bn=bn), out_shape=(gathere...  190 us
    pallas_call x1, Pallas kernels, back_layer(): pl.pallas_call(functools.partial(back_kernel, rows=rows, bn=bn), out_shap...  152 us
    reduce_scatter x1, waiting for transfers between devices, layer(): g_out = lax.psum_scatter(g_out_part, 'tp', scatter_dimension=0, tiled=True)  115 us
    pallas_call x1, Pallas kernels, front_layer(): pl.pallas_call(functools.partial(front_kernel, batch=batch), out_shape=(s...  102 us
    pallas_call x2, Pallas kernels, weight_grad(): pl.pallas_call(product_kernel, out_shape=jax.ShapeDtypeStruct((m, n), F32...  95.6 us
    pallas_call x1, Pallas kernels, weight_grad_rest(): pl.pallas_call(rest_kernel, out_shape=jax.ShapeDtypeStruct((m, n), F32),...  40.7 us
    pallas_call x1, Pallas kernels, attention_backward(): pl.pallas_call(attn_bwd_kernel, out_shape=(jax.ShapeDtypeStruct((heads, r...  32.5 us
    pallas_call x1, Pallas kernels, join_layer(): pl.pallas_call(functools.partial(join_kernel, joins=joins), out_shape=(ac...  28.2 us
  transfers between devices with their start and end apart: 16, of which 4 were waited for; matrix products, arithmetic and copies ran while one was open for 4% of the time, Pallas kernels for 16%

profile of v11, /device:TPU:0, one launch (start us, length us, event | category | flops | bytes accessed | tf_op | source)
XLA Modules:
  0.0 855.3 jit_solution(3264371648121656656)
XLA Ops:
  13.9 101.8 %front.1 = (bf16[576,2048]{1,0:T(8,128)(2,1)}, bf16[8,2048,256]{2,1,0:T(8,128)(2,1)}, bf16[8,256,2048]{2,1,0:T(8,128)(2,1)}, bf16[8,576,512]{2,1,0:T(8,128)(2,1)...) custom-call(s32[3]{0:T(128)} %prefix_ref.1, ...), custom_call_target="tpu_custom_call" | custom-call | flops 19327352832 | bytes 62914560 | tf_op jit(solution)/shard_map/front/pallas_call | solution.py:323
  115.6 190.1 %gated.1 = (bf16[4608,2048]{1,0:T(8,128)(2,1)}, bf16[4608,2048]{1,0:T(8,128)(2,1)}, bf16[4608,2048]{1,0:T(8,128)(2,1)}, bf16[4608,2048]{1,0:T(8,128)(2,1)}, bf16...) custom-call(bf16[576,2048]{1,0:T(8,128)(2,1)} %get-tuple-element.72.z_own, bf16[576,2048]{1,0:T(8,128)(2,1)} %bitcast.69, ...), custom_call_target="tpu_custom_call" | custom-call | flops 115964116992 | bytes 209715200 | tf_op jit(solution)/shard_map/gated/pallas_call | solution.py:593
  305.7 152.1 %back.1 = (f32[2,576,2048]{2,1,0:T(8,128)}, bf16[2,576,2048]{2,1,0:T(8,128)(2,1)}, bf16[2,576,2048]{2,1,0:T(8,128)(2,1)}, f32[2048,2048]{1,0:T(8,128)}) custom-call(bf16[4608,2048]{1,0:T(8,128)(2,1)} %get-tuple-element.100.act.a_ref, bf16[4608,2048]{1,0:T(8,128)(2,1)} %get-tuple-element.114.d_gate.b_ref, bf16[4608,2048]{1,0:T(8,128)(2,1)} %get-tuple-element.123.d_up.b_ref, ...), custom_call_target="tpu_custom_call" | custom-call | flops 115964116992 | bytes 209715200 | tf_op jit(solution)/shard_map/back/pallas_call | solution.py:831
  457.9 28.2 %join.1 = (bf16[576,2048]{1,0:T(8,128)(2,1)}, bf16[576,2048]{1,0:T(8,128)(2,1)}, f32[1,2048]{1,0:T(1,128)}, bf16[576,2048]{1,0:T(8,128)(2,1)}, f32[2048,2048]{1,0:T(8,128)}) custom-call(f32[2,576,2048]{2,1,0:T(8,128)} %get-tuple-element.78.own_ref, bf16[2,576,2048]{2,1,0:T(8,128)(2,1)} %get-tuple-element.79.x_ref, ...), custom_call_target="tpu_custom_call" | custom-call | flops 9663676416 | bytes 62914560 | tf_op jit(solution)/shard_map/join/pallas_call | solution.py:890
  486.1 32.5 %attn_bwd.1 = (bf16[8,576,256]{2,1,0:T(8,128)(2,1)}, bf16[4,576,512]{2,1,0:T(8,128)(2,1)}, bf16[4,576,512]{2,1,0:T(8,128)(2,1)}) custom-call(s32[11,3]{1,0:T(8,128)} %add_add_fusion.1.lens_ref, f32[192,128]{1,0:T(8,128)} %get-tuple-element.183.cos_ref, f32[192,128]{1,0:T(8,128)} %get-tuple-element.182.sin_ref, bf16[8,576,256]{2,1,0:T(8,128)(2,1)} %get-tuple-element.85.q_ref, ...), custom_call_target="tpu_custom_call" | custom-call | flops 18119393280 | bytes 20971520 | tf_op jit(solution)/shard_map/attn_bwd/pallas_call | solution.py:349
  518.7 5.7 fusion.1
  525.0 10.2 %convolution_bitcast_fusion.part_ref = f32[576,2048]{1,0:T(8,128)} fusion(bf16[8,576,256]{2,1,0:T(8,128)(2,1)S(1)} %copy-done.6, bf16[8,2048,256]{2,1,0:T(8,128)(2,1)} %get-tuple-element.93), kind=kOutput, calls=%fused_computation.1 | convolution fusion | flops 4831838208 | bytes 15466496 | tf_op jit(solution)/shard_map/hte,hde->td/dot_general | solution.py:1044
  535.3 1.7 convert_add_fusion
  537.9 1.3 collective-permute-start.2
  539.4 6.6 collective-permute-done.1
  550.6 3.5 convolution_add_fusion
  554.2 1.9 slice_bitcast_fusion
  556.1 2.3 copy-done
  560.4 47.8 %weight_grad.2 = f32[2048,2048]{1,0:T(8,128)} custom-call(bf16[4608,2048]{1,0:T(8,128)(2,1)} %get-tuple-element.100.act.a_ref, bf16[4608,2048]{1,0:T(8,128)(2,1)} %get-tuple-element.101.b_ref), custom_call_target="tpu_custom_call" | custom-call | flops 38654705664 | bytes 115343360 | tf_op jit(solution)/shard_map/weight_grad/pallas_call | solution.py:965
  609.1 12.7 %finish.1 = (f32[2048,256]{1,0:T(8,128)}, f32[2048,256]{1,0:T(8,128)}, bf16[576,2048]{1,0:T(8,128)(2,1)}, f32[1,2048]{1,0:T(1,128)}) custom-call(f32[576,512]{1,0:T(8,128)} %get-tuple-element.177.kv_ref, bf16[576,512]{1,0:T(8,128)(2,1)} %collective-permute-done.3.side_ref, bf16[576,512]{1,0:T(8,128)(2,1)} %copy-done.5, ...), custom_call_target="tpu_custom_call" | custom-call | flops 2415919104 | bytes 25165824 | tf_op jit(solution)/shard_map/finish/pallas_call | solution.py:946
  622.5 2.6 bitcast_add_fusion.1
  625.1 2.5 pad_maximum_fusion
  628.4 1.5 collective-permute-start.10
  634.0 40.7 %weight_grad_rest.1 = f32[2048,2048]{1,0:T(8,128)} custom-call(bf16[4608,2048]{1,0:T(8,128)(2,1)} %get-tuple-element.76.z_all.a_ref, bf16[4608,2048]{1,0:T(8,128)(2,1)} %get-tuple-element.114.d_gate.b_ref, f32[2048,2048]{1,0:T(8,128)} %get-tuple-element.115.part_ref), custom_call_target="tpu_custom_call" | custom-call | flops 28991029248 | bytes 83886080 | tf_op jit(solution)/shard_map/weight_grad_rest/pallas_call | solution.py:984
  674.8 47.7 %weight_grad.3 = f32[2048,2048]{1,0:T(8,128)} custom-call(bf16[4608,2048]{1,0:T(8,128)(2,1)} %get-tuple-element.76.z_all.a_ref, bf16[4608,2048]{1,0:T(8,128)(2,1)} %get-tuple-element.123.d_up.b_ref), custom_call_target="tpu_custom_call" | custom-call | flops 38654705664 | bytes 115343360 | tf_op jit(solution)/shard_map/weight_grad/pallas_call | solution.py:965
  722.6 3.5 fusion.4
  726.0 1.8 copy.30
  729.1 114.8 %reduce-scatter.2.cloned.1.call-done = f32[256,2048]{1,0:T(8,128)} async-done(((f32[2048,2048]{1,0:T(8,128)}), f32[256,2048]{1,0:T(8,128)}) %reduce-scatter.2.cloned.1.call-update) | async-done | bytes 2097168 | tf_op jit(solution)/shard_map/reduce_scatter | solution.py:1033
  843.8 3.0 copy.33
  (69 shorter events, 23.8 us)
Async XLA Ops:
  7.2 721.9 %all-reduce.3.cloned.1.call-start = ((), (), s32[]{:S(2)}) async-start(), calls=%async_computation.2 | async-start | bytes 8388608 | tf_op jit(solution)/shard_map/psum | solution.py:1059
  518.7 5.8 collective-permute-start
  518.7 6.2 copy-start.6
  524.4 26.2 %collective-permute-start.5 = (f32[4,256,2048]{2,1,0:T(8,128)S(1)}, f32[4,256,2048]{2,1,0:T(8,128)S(1)}, u32[]{:S(2)}, u32[]{:S(2)}) collective-permute-start(f32[4,256,2048]{2,1,0:T(8,128)S(1)} %fusion.1), channel_id=1, source_target_pairs={{0,1},{1,0},{2,3},{3,2},{4,5},{5,4},{6,7},{7,6},{8,9},{9,8},{10,11... | collective-permute-start | bytes 25165832 | tf_op jit(solution)/shard_map/ppermute | solution.py:41
  525.0 10.3 %copy-start.3 = (bf16[4,576,512]{2,1,0:T(8,128)(2,1)S(1)}, bf16[4,576,512]{2,1,0:T(8,128)(2,1)}, u32[]{:S(2)}) copy-start(bf16[4,576,512]{2,1,0:T(8,128)(2,1)} %get-tuple-element.88) | copy-start | bytes 7077892
  537.1 9.0 %collective-permute-start.1 = (bf16[288,512]{1,0:T(8,128)(2,1)S(1)}, bf16[288,512]{1,0:T(8,128)(2,1)S(1)}, u32[]{:S(2)}, u32[]{:S(2)}) collective-permute-start(bf16[288,512]{1,0:T(8,128)(2,1)S(1)} %get-tuple-element.179), channel_id=1, source_target_pairs={{0,2},{1,3},{2,0},{3,1},{4,6},{5,7},{6,4},{7,5},{8,10},{9,11},{10,... | collective-permute-start | bytes 884744 | tf_op jit(solution)/shard_map/ppermute | solution.py:41
  537.9 8.7 %collective-permute-start.2 = (bf16[288,512]{1,0:T(8,128)(2,1)S(1)}, bf16[288,512]{1,0:T(8,128)(2,1)S(1)}, u32[]{:S(2)}, u32[]{:S(2)}) collective-permute-start(bf16[288,512]{1,0:T(8,128)(2,1)S(1)} %get-tuple-element.178), channel_id=1, source_target_pairs={{0,4},{1,5},{2,6},{3,7},{4,0},{5,1},{6,2},{7,3},{8,12},{9,13},{10,... | collective-permute-start | bytes 884744 | tf_op jit(solution)/shard_map/ppermute | solution.py:41
  539.4 11.2 %copy-start.1 = (bf16[576,2048]{1,0:T(8,128)(2,1)S(1)}, bf16[576,2048]{1,0:T(8,128)(2,1)}, u32[]{:S(2)}) copy-start(bf16[576,2048]{1,0:T(8,128)(2,1)} %get-tuple-element.91.normed_ref) | copy-start | bytes 7077892
  547.6 60.6 %collective-permute-start.4 = (bf16[576,512]{1,0:T(8,128)(2,1)}, bf16[576,512]{1,0:T(8,128)(2,1)S(1)}, u32[]{:S(2)}, u32[]{:S(2)}) collective-permute-start(bf16[576,512]{1,0:T(8,128)(2,1)} %pad_maximum_fusion.3), channel_id=1, source_target_pairs={{0,4},{1,5},{2,6},{3,7},{4,0},{5,1},{6,2},{7,3},{8,12},{9,13},{10,... | collective-permute-start | bytes 1769480 | tf_op jit(solution)/shard_map/ppermute | solution.py:41
  549.9 58.3 %collective-permute-start.3 = (bf16[576,512]{1,0:T(8,128)(2,1)}, bf16[576,512]{1,0:T(8,128)(2,1)}, u32[]{:S(2)}, u32[]{:S(2)}) collective-permute-start(bf16[576,512]{1,0:T(8,128)(2,1)} %pad_maximum_fusion.2), channel_id=1, source_target_pairs={{0,2},{1,3},{2,0},{3,1},{4,6},{5,7},{6,4},{7,5},{8,10},{9,11},{10,... | collective-permute-start | bytes 1769480 | tf_op jit(solution)/shard_map/ppermute | solution.py:41
  554.2 4.2 copy-start
  558.4 49.8 %collective-permute-start.6 = (f32[128,2048]{1,0:T(8,128)}, f32[128,2048]{1,0:T(8,128)}, u32[]{:S(2)}, u32[]{:S(2)}) collective-permute-start(f32[128,2048]{1,0:T(8,128)} %get-tuple-element.173), channel_id=1, source_target_pairs={{0,2},{1,3},{2,0},{3,1},{4,6},{5,7},{6,4},{7,5},{8,10},{9,11},{10,... | collective-permute-start | bytes 3145736 | tf_op jit(solution)/shard_map/ppermute | solution.py:41
  559.7 48.5 %collective-permute-start.7 = (f32[128,2048]{1,0:T(8,128)}, f32[128,2048]{1,0:T(8,128)}, u32[]{:S(2)}, u32[]{:S(2)}) collective-permute-start(f32[128,2048]{1,0:T(8,128)} %get-tuple-element.172), channel_id=1, source_target_pairs={{0,4},{1,5},{2,6},{3,7},{4,0},{5,1},{6,2},{7,3},{8,12},{9,13},{10,... | collective-permute-start | bytes 3145736 | tf_op jit(solution)/shard_map/ppermute | solution.py:41
  608.2 0.9 copy-start.5
  609.1 12.7 %copy-start.7 = (f32[1,2048]{1,0:T(1,128)S(1)}, f32[1,2048]{1,0:T(1,128)}, u32[]{:S(2)}) copy-start(f32[1,2048]{1,0:T(1,128)} %get-tuple-element.112) | copy-start | bytes 24580
  622.5 2.6 copy-start.2
  627.7 216.2 %reduce-scatter.2.cloned.1.call-start = ((), (), s32[]{:S(2)}) async-start(), calls=%async_computation.1 | async-start | bytes 18874368 | tf_op jit(solution)/shard_map/reduce_scatter | solution.py:1033
  628.4 46.3 %collective-permute-start.10 = (f32[2,2048]{1,0:T(2,128)S(1)}, f32[2,2048]{1,0:T(2,128)S(1)}, u32[]{:S(2)}, u32[]{:S(2)}) collective-permute-start(f32[2,2048]{1,0:T(2,128)S(1)} %pad_maximum_fusion.4), channel_id=1, source_target_pairs={{0,6},{1,7},{2,4},{3,5},{4,2},{5,3},{6,0},{7,1},{8,14},{9,15},{10,... | collective-permute-start | bytes 49160 | tf_op jit(solution)/shard_map/ppermute | solution.py:41
  630.0 44.8 %collective-permute-start.8 = (f32[2,2048]{1,0:T(2,128)S(1)}, f32[2,2048]{1,0:T(2,128)S(1)}, u32[]{:S(2)}, u32[]{:S(2)}) collective-permute-start(f32[2,2048]{1,0:T(2,128)S(1)} %pad_maximum_fusion.4), channel_id=1, source_target_pairs={{0,2},{1,3},{2,0},{3,1},{4,6},{5,7},{6,4},{7,5},{8,10},{9,11},{10,... | collective-permute-start | bytes 49160 | tf_op jit(solution)/shard_map/ppermute | solution.py:41
  631.3 43.5 %collective-permute-start.9 = (f32[2,2048]{1,0:T(2,128)S(1)}, f32[2,2048]{1,0:T(2,128)S(1)}, u32[]{:S(2)}, u32[]{:S(2)}) collective-permute-start(f32[2,2048]{1,0:T(2,128)S(1)} %pad_maximum_fusion.4), channel_id=1, source_target_pairs={{0,4},{1,5},{2,6},{3,7},{4,0},{5,1},{6,2},{7,3},{8,12},{9,13},{10,... | collective-permute-start | bytes 49160 | tf_op jit(solution)/shard_map/ppermute | solution.py:41
  631.9 90.6 %collective-permute-start.12 = (f32[256,2048]{1,0:T(8,128)}, f32[256,2048]{1,0:T(8,128)}, u32[]{:S(2)}, u32[]{:S(2)}) collective-permute-start(f32[256,2048]{1,0:T(8,128)} %get-tuple-element.121), channel_id=1, source_target_pairs={{0,2},{1,3},{2,0},{3,1},{4,6},{5,7},{6,4},{7,5},{8,10},{9,11},{10,... | collective-permute-start | bytes 6291464 | tf_op jit(solution)/shard_map/ppermute | solution.py:41
  633.1 89.5 %collective-permute-start.13 = (f32[256,2048]{1,0:T(8,128)}, f32[256,2048]{1,0:T(8,128)}, u32[]{:S(2)}, u32[]{:S(2)}) collective-permute-start(f32[256,2048]{1,0:T(8,128)} %get-tuple-element.122), channel_id=1, source_target_pairs={{0,4},{1,5},{2,6},{3,7},{4,0},{5,1},{6,2},{7,3},{8,12},{9,13},{10,... | collective-permute-start | bytes 6291464 | tf_op jit(solution)/shard_map/ppermute | solution.py:41
  674.8 47.8 %collective-permute-start.11 = (f32[2,2048]{1,0:T(2,128)S(1)}, f32[2,2048]{1,0:T(2,128)S(1)}, u32[]{:S(2)}, u32[]{:S(2)}) collective-permute-start(f32[2,2048]{1,0:T(2,128)S(1)} %add_add_fusion), channel_id=1, source_target_pairs={{0,1},{1,0},{2,3},{3,2},{4,5},{5,4},{6,7},{7,6},{8,9},{9,8},{10,11... | collective-permute-start | bytes 49160 | tf_op jit(solution)/shard_map/ppermute | solution.py:41
  729.1 117.8 %copy-start.4 = (f32[2048,256]{1,0:T(8,128)S(1)}, f32[2048,256]{1,0:T(8,128)}, u32[]{:S(2)}) copy-start(f32[2048,256]{1,0:T(8,128)} %get-tuple-element.191) | copy-start | bytes 6291460
Sparse Core Ops, SparseCore 0:
  627.8 101.2 all-reduce.2
  733.2 110.6 reduce-scatter.1

commit v12 on v11

--- a/solution.py
+++ b/solution.py
@@ -901,8 +901,8 @@
     )(own_part, x_part, y_part, resid, grad_out, gain.reshape(1, dim), wo_all, mixed)
 
 
-def finish_kernel(kv_ref, side_ref, back_ref, cos_ref, sin_ref, normed_ref, wk_ref, wv_ref, part_ref, hidden_ref, d_resid_ref, gain_ref,
-                  g_key_ref, g_value_ref, out_ref, g_gain_ref):
+def finish_kernel(kv_ref, side_ref, back_ref, cos_ref, sin_ref, normed_ref, wk_ref, wv_ref, part_ref, hidden_ref, d_resid_ref, gain_ref, mlp_ref,
+                  g_key_ref, g_value_ref, out_ref):
     head_dim = wk_ref.shape[1]
     half_dim = head_dim // 2
     d_kv = (kv_ref[...] + side_ref[...].astype(F32) + back_ref[...].astype(F32)).astype(BF16)
@@ -916,21 +916,27 @@
     g_key = dot_tn(normed_ref[...], d_key)
     g_value = dot_tn(normed_ref[...], d_value)
     g_gain = jnp.sum(terms, axis=0, keepdims=True)
+    dim = g_key.shape[0]
+    lines = dim // head_dim
 
     @pl.when(pl.program_id(0) == 0)
     def _():
         g_key_ref[...] = g_key
-        g_value_ref[...] = g_value
-        g_gain_ref[...] = g_gain
+        g_value_ref[:dim] = g_value
+        for r in range(lines):
+            part = slice(r * head_dim, (r + 1) * head_dim)
+            g_value_ref[dim + r:dim + r + 1] = g_gain[:, part]
+            g_value_ref[dim + lines + r:dim + lines + r + 1] = mlp_ref[:, part]
 
     @pl.when(pl.program_id(0) > 0)
     def _():
         g_key_ref[...] += g_key
-        g_value_ref[...] += g_value
-        g_gain_ref[...] += g_gain
-
-
-def finish_layer(kv_own, kv_side, kv_back, cos_t, sin_t, normed, w_key, w_value, part, hidden, d_resid, gain):
+        g_value_ref[:dim] += g_value
+        for r in range(lines):
+            g_value_ref[dim + r:dim + r + 1] += g_gain[:, r * head_dim:(r + 1) * head_dim]
+
+
+def finish_layer(kv_own, kv_side, kv_back, cos_t, sin_t, normed, w_key, w_value, part, hidden, d_resid, gain, g_mlp_norm):
     rows, dim = hidden.shape
     shard, half_dim = cos_t.shape
     head_dim = w_key.shape[1]
@@ -945,14 +951,14 @@
     grad = jax.ShapeDtypeStruct((dim, head_dim), F32)
     return pl.pallas_call(
         finish_kernel,
-        out_shape=(grad, grad, jax.ShapeDtypeStruct((rows, dim), BF16), jax.ShapeDtypeStruct((1, dim), F32)),
+        out_shape=(grad, jax.ShapeDtypeStruct((dim + 2 * dim // head_dim, head_dim), F32), jax.ShapeDtypeStruct((rows, dim), BF16)),
         grid=(rows // shard,),
-        in_specs=[kv, kv, kv, table, table, act, weight, weight, act, act, act, one],
-        out_specs=(weight, weight, act, one),
+        in_specs=[kv, kv, kv, table, table, act, weight, weight, act, act, act, one, one],
+        out_specs=(weight, whole(dim + 2 * dim // head_dim, head_dim), act),
         compiler_params=pltpu.CompilerParams(dimension_semantics=("arbitrary",), vmem_limit_bytes=62 << 20),
         cost_estimate=pl.CostEstimate(flops=8 * rows * dim * head_dim, bytes_accessed=24 << 20, transcendentals=rows),
         name="finish",
-    )(kv_own, kv_side, kv_back, cos_t, sin_t, normed, w_key, w_value, part, hidden, d_resid, gain.reshape(1, dim))
+    )(kv_own, kv_side, kv_back, cos_t, sin_t, normed, w_key, w_value, part, hidden, d_resid, gain.reshape(1, dim), g_mlp_norm)
 
 
 def product_kernel(a_ref, b_ref, o_ref):
@@ -1052,24 +1058,21 @@
         g_down = weight_grad(act, grad_all)
         kv_last, q_came, g_down = lax.optimization_barrier((kv_last, q_came, g_down))
         q_next = hop_near(g_query_sum[1], g_query_sum[2], *q_came)
-        g_key_part, g_value_part, grad_hidden, g_attn_norm_part = finish_layer(
-            kv_own, kv_last[0], kv_last[1], cos_own, sin_own, normed, w_key, w_value, d_normed_q, hidden, d_resid, attn_norm)
-        norms = jnp.concatenate([g_attn_norm_part, g_mlp_norm_part])
-        q_next, g_key_part, g_value_part, norms, d_gate = lax.optimization_barrier((q_next, g_key_part, g_value_part, norms, d_gate))
-        g_key, g_value = lax.psum((g_key_part, g_value_part), "tp")
+        g_key_part, g_value_part, grad_hidden = finish_layer(
+            kv_own, kv_last[0], kv_last[1], cos_own, sin_own, normed, w_key, w_value, d_normed_q, hidden, d_resid, attn_norm, g_mlp_norm_part)
+        parts = (g_key_part, g_value_part)
+        q_next, parts, d_gate = lax.optimization_barrier((q_next, parts, d_gate))
+        g_key, g_value = lax.psum(parts, "tp")
         last_side = swap(q_next[0], 2)
         q_last = (last_side, swap(q_next[1], 4))
-        norms_near = [swap(norms, bit) for bit in (2, 4, 6)]
         g_gate = weight_grad_rest(gated_all, d_gate, g_gate_part, 6 * rows)
-        norms_near, g_gate, d_upper = lax.optimization_barrier((norms_near, g_gate, d_upper))
-        norms = norms + norms_near[0] + norms_near[1] + norms_near[2]
-        norms, d_upper = lax.optimization_barrier((norms, d_upper))
-        norms_core = swap(norms, 1)
+        d_upper, g_gate = lax.optimization_barrier((d_upper, g_gate))
         g_up = weight_grad(gated_all, d_upper)
-        norms_core, q_last, g_up = lax.optimization_barrier((norms_core, q_last, g_up))
-        g_norms = norms + norms_core
+        q_last, g_up = lax.optimization_barrier((q_last, g_up))
         g_query = (g_query_sum[0] + q_last[0] + q_last[1]).T
+        g_attn_norm, g_mlp_norm = g_value[dim:].reshape(2, dim)
+        g_value = g_value[:dim]
         full = (batch, shard, dim)
-        return (hidden_out.reshape(full), grad_hidden.reshape(full), g_norms[0], g_query, g_key, g_value, g_out, g_norms[1], g_gate, g_up, g_down)
+        return (hidden_out.reshape(full), grad_hidden.reshape(full), g_attn_norm, g_query, g_key, g_value, g_out, g_mlp_norm, g_gate, g_up, g_down)
 
     return jax.shard_map(layer, mesh=mesh, in_specs=in_specs, out_specs=out_specs, check_vma=False)

time: 863 us -> 854 us (0.990)
    reduce_scatter x1, waiting for transfers between devices: 115 us -> 88.9 us  [layer(): g_out = lax.psum_scatter(g_out_part, 'tp', scatter_dimension=0, tiled=True)]
    ppermute x14 -> x10, waiting for transfers between devices: 7.26 us -> 26.2 us  [swap(): return lax.ppermute(x, 'tp', [(t, t ^ bit) for t in range(8)])]
  transfers between devices with their start and end apart: 16 -> 12, of which waited for: 4 -> 5; matrix products, arithmetic and copies ran while one was open for 4% -> 4% of each run, Pallas kernels for 16% -> 16%
where the time goes in v12:
time: 854 us; the launch traced here: 846 us
  Pallas kernels  655 us (77%)
  waiting for transfers between devices  116 us (14%)
  matrix products  19.5 us (2%)
  other arithmetic  16.6 us (2%)
  local copies, waits for them, and re-layouts  16.5 us (2%)
  between operations  14.5 us (2%)
    pallas_call x1, Pallas kernels, gated_layer(): pl.pallas_call(functools.partial(gated_kernel, bn=bn), out_shape=(gathere...  190 us
    pallas_call x1, Pallas kernels, back_layer(): pl.pallas_call(functools.partial(back_kernel, rows=rows, bn=bn), out_shap...  152 us
    pallas_call x1, Pallas kernels, front_layer(): pl.pallas_call(functools.partial(front_kernel, batch=batch), out_shape=(s...  102 us
    pallas_call x2, Pallas kernels, weight_grad(): pl.pallas_call(product_kernel, out_shape=jax.ShapeDtypeStruct((m, n), F32...  95.7 us
    reduce_scatter x1, waiting for transfers between devices, layer(): g_out = lax.psum_scatter(g_out_part, 'tp', scatter_dimension=0, tiled=True)  88.9 us
    pallas_call x1, Pallas kernels, weight_grad_rest(): pl.pallas_call(rest_kernel, out_shape=jax.ShapeDtypeStruct((m, n), F32),...  41.6 us
    pallas_call x1, Pallas kernels, attention_backward(): pl.pallas_call(attn_bwd_kernel, out_shape=(jax.ShapeDtypeStruct((heads, r...  32.5 us
    pallas_call x1, Pallas kernels, join_layer(): pl.pallas_call(functools.partial(join_kernel, joins=joins), out_shape=(ac...  28.3 us
  transfers between devices with their start and end apart: 12, of which 5 were waited for; matrix products, arithmetic and copies ran while one was open for 4% of the time, Pallas kernels for 16%

profile of v12, /device:TPU:0, one launch (start us, length us, event | category | flops | bytes accessed | tf_op | source)
XLA Modules:
  0.0 846.0 jit_solution(459993138719935413)
XLA Ops:
  12.5 1.3 add_add_fusion.lens_ref
  13.8 101.7 %front.1 = (bf16[576,2048]{1,0:T(8,128)(2,1)}, bf16[8,2048,256]{2,1,0:T(8,128)(2,1)}, bf16[8,256,2048]{2,1,0:T(8,128)(2,1)}, bf16[8,576,512]{2,1,0:T(8,128)(2,1)...) custom-call(s32[3]{0:T(128)} %prefix_ref.1, ...), custom_call_target="tpu_custom_call" | custom-call | flops 19327352832 | bytes 62914560 | tf_op jit(solution)/shard_map/front/pallas_call | solution.py:323
  115.6 190.0 %gated.1 = (bf16[4608,2048]{1,0:T(8,128)(2,1)}, bf16[4608,2048]{1,0:T(8,128)(2,1)}, bf16[4608,2048]{1,0:T(8,128)(2,1)}, bf16[4608,2048]{1,0:T(8,128)(2,1)}, bf16...) custom-call(bf16[576,2048]{1,0:T(8,128)(2,1)} %get-tuple-element.64.z_own, bf16[576,2048]{1,0:T(8,128)(2,1)} %bitcast.73, ...), custom_call_target="tpu_custom_call" | custom-call | flops 115964116992 | bytes 209715200 | tf_op jit(solution)/shard_map/gated/pallas_call | solution.py:593
  305.6 152.3 %back.1 = (f32[2,576,2048]{2,1,0:T(8,128)}, bf16[2,576,2048]{2,1,0:T(8,128)(2,1)}, bf16[2,576,2048]{2,1,0:T(8,128)(2,1)}, f32[2048,2048]{1,0:T(8,128)}) custom-call(bf16[4608,2048]{1,0:T(8,128)(2,1)} %get-tuple-element.92.act.a_ref, bf16[4608,2048]{1,0:T(8,128)(2,1)} %get-tuple-element.107.d_gate.b_ref, bf16[4608,2048]{1,0:T(8,128)(2,1)} %get-tuple-element.109.d_up.b_ref, ...), custom_call_target="tpu_custom_call" | custom-call | flops 115964116992 | bytes 209715200 | tf_op jit(solution)/shard_map/back/pallas_call | solution.py:831
  457.9 28.3 %join.1 = (bf16[576,2048]{1,0:T(8,128)(2,1)}, bf16[576,2048]{1,0:T(8,128)(2,1)}, f32[1,2048]{1,0:T(1,128)}, bf16[576,2048]{1,0:T(8,128)(2,1)}, f32[2048,2048]{1,0:T(8,128)}) custom-call(f32[2,576,2048]{2,1,0:T(8,128)} %get-tuple-element.70.own_ref, bf16[2,576,2048]{2,1,0:T(8,128)(2,1)} %get-tuple-element.71.x_ref, ...), custom_call_target="tpu_custom_call" | custom-call | flops 9663676416 | bytes 62914560 | tf_op jit(solution)/shard_map/join/pallas_call | solution.py:890
  486.1 32.5 %attn_bwd.1 = (bf16[8,576,256]{2,1,0:T(8,128)(2,1)}, bf16[4,576,512]{2,1,0:T(8,128)(2,1)}, bf16[4,576,512]{2,1,0:T(8,128)(2,1)}) custom-call(s32[11,3]{1,0:T(8,128)} %add_add_fusion.lens_ref, f32[192,128]{1,0:T(8,128)} %get-tuple-element.167.cos_ref, f32[192,128]{1,0:T(8,128)} %get-tuple-element.166.sin_ref, bf16[8,576,256]{2,1,0:T(8,128)(2,1)} %get-tuple-element.77.q_ref, ...), custom_call_target="tpu_custom_call" | custom-call | flops 18119393280 | bytes 20971520 | tf_op jit(solution)/shard_map/attn_bwd/pallas_call | solution.py:349
  518.7 5.7 fusion.1
  525.0 10.2 %convolution_bitcast_fusion.part_ref = f32[576,2048]{1,0:T(8,128)} fusion(bf16[8,576,256]{2,1,0:T(8,128)(2,1)S(1)} %copy-done.6, bf16[8,2048,256]{2,1,0:T(8,128)(2,1)} %get-tuple-element.85), kind=kOutput, calls=%fused_computation.1 | convolution fusion | flops 4831838208 | bytes 15466496 | tf_op jit(solution)/shard_map/hte,hde->td/dot_general | solution.py:1050
  535.3 1.7 convert_add_fusion
  539.0 7.0 collective-permute-done.1
  550.5 3.5 convolution_add_fusion
  554.0 1.9 slice_bitcast_fusion
  555.9 2.3 copy-done
  560.3 47.9 %weight_grad.2 = f32[2048,2048]{1,0:T(8,128)} custom-call(bf16[4608,2048]{1,0:T(8,128)(2,1)} %get-tuple-element.92.act.a_ref, bf16[4608,2048]{1,0:T(8,128)(2,1)} %get-tuple-element.93.b_ref), custom_call_target="tpu_custom_call" | custom-call | flops 38654705664 | bytes 115343360 | tf_op jit(solution)/shard_map/weight_grad/pallas_call | solution.py:971
  608.2 2.7 bitcast_add_fusion.1
  611.0 2.5 pad_maximum_fusion
  613.5 12.7 %finish.1 = (f32[2048,256]{1,0:T(8,128)}, f32[2064,256]{1,0:T(8,128)}, bf16[576,2048]{1,0:T(8,128)(2,1)}) custom-call(f32[576,512]{1,0:T(8,128)} %get-tuple-element.161.kv_ref, bf16[576,512]{1,0:T(8,128)(2,1)} %collective-permute-done.3.side_ref, bf16[576,512]{1,0:T(8,128)(2,1)} %copy-done.5, f32[192,128]{1,0:T(8,128)} %get-tuple-element.167.cos_ref, ...), custom_call_target="tpu_custom_call" | custom-call | flops 2415919104 | bytes 25165824 | tf_op jit(solution)/shard_map/finish/pallas_call | solution.py:952
  627.0 41.6 %weight_grad_rest.1 = f32[2048,2048]{1,0:T(8,128)} custom-call(bf16[4608,2048]{1,0:T(8,128)(2,1)} %get-tuple-element.68.z_all.a_ref, bf16[4608,2048]{1,0:T(8,128)(2,1)} %get-tuple-element.107.d_gate.b_ref, f32[2048,2048]{1,0:T(8,128)} %get-tuple-element.108.part_ref), custom_call_target="tpu_custom_call" | custom-call | flops 28991029248 | bytes 83886080 | tf_op jit(solution)/shard_map/weight_grad_rest/pallas_call | solution.py:990
  670.3 47.9 %weight_grad.3 = f32[2048,2048]{1,0:T(8,128)} custom-call(bf16[4608,2048]{1,0:T(8,128)(2,1)} %get-tuple-element.68.z_all.a_ref, bf16[4608,2048]{1,0:T(8,128)(2,1)} %get-tuple-element.109.d_up.b_ref), custom_call_target="tpu_custom_call" | custom-call | flops 38654705664 | bytes 115343360 | tf_op jit(solution)/shard_map/weight_grad/pallas_call | solution.py:971
  718.2 17.8 %collective-permute-done.8 = f32[256,2048]{1,0:T(8,128)} collective-permute-done((f32[256,2048]{1,0:T(8,128)}, f32[256,2048]{1,0:T(8,128)}, u32[]{:S(2)}, u32[]{:S(2)}) %collective-permute-start.8) | collective-permute-done | bytes 2097184 | tf_op jit(solution)/shard_map/ppermute | solution.py:41
  736.9 4.5 fusion.4
  741.4 1.8 copy.30
  743.2 3.6 slice.166
  748.7 88.9 %reduce-scatter.2.cloned.1.call-done = f32[256,2048]{1,0:T(8,128)} async-done(((f32[2048,2048]{1,0:T(8,128)}), f32[256,2048]{1,0:T(8,128)}) %reduce-scatter.2.cloned.1.call-update) | async-done | bytes 2097168 | tf_op jit(solution)/shard_map/reduce_scatter | solution.py:1039
  (58 shorter events, 21.1 us)
Async XLA Ops:
  7.2 736.0 %all-reduce.3.cloned.1.call-start = ((), (), s32[]{:S(2)}) async-start(), calls=%async_computation.2 | async-start | bytes 8421376 | tf_op jit(solution)/shard_map/psum | solution.py:1065
  518.7 5.8 collective-permute-start
  518.7 6.2 copy-start.6
  524.4 26.1 %collective-permute-start.5 = (f32[4,256,2048]{2,1,0:T(8,128)S(1)}, f32[4,256,2048]{2,1,0:T(8,128)S(1)}, u32[]{:S(2)}, u32[]{:S(2)}) collective-permute-start(f32[4,256,2048]{2,1,0:T(8,128)S(1)} %fusion.1), channel_id=1, source_target_pairs={{0,1},{1,0},{2,3},{3,2},{4,5},{5,4},{6,7},{7,6},{8,9},{9,8},{10,11... | collective-permute-start | bytes 25165832 | tf_op jit(solution)/shard_map/ppermute | solution.py:41
  525.0 10.3 %copy-start.3 = (bf16[4,576,512]{2,1,0:T(8,128)(2,1)S(1)}, bf16[4,576,512]{2,1,0:T(8,128)(2,1)}, u32[]{:S(2)}) copy-start(bf16[4,576,512]{2,1,0:T(8,128)(2,1)} %get-tuple-element.80) | copy-start | bytes 7077892
  537.1 9.0 %collective-permute-start.1 = (bf16[288,512]{1,0:T(8,128)(2,1)S(1)}, bf16[288,512]{1,0:T(8,128)(2,1)S(1)}, u32[]{:S(2)}, u32[]{:S(2)}) collective-permute-start(bf16[288,512]{1,0:T(8,128)(2,1)S(1)} %get-tuple-element.165), channel_id=1, source_target_pairs={{0,2},{1,3},{2,0},{3,1},{4,6},{5,7},{6,4},{7,5},{8,10},{9,11},{10,... | collective-permute-start | bytes 884744 | tf_op jit(solution)/shard_map/ppermute | solution.py:41
  537.9 8.7 %collective-permute-start.2 = (bf16[288,512]{1,0:T(8,128)(2,1)S(1)}, bf16[288,512]{1,0:T(8,128)(2,1)S(1)}, u32[]{:S(2)}, u32[]{:S(2)}) collective-permute-start(bf16[288,512]{1,0:T(8,128)(2,1)S(1)} %get-tuple-element.164), channel_id=1, source_target_pairs={{0,4},{1,5},{2,6},{3,7},{4,0},{5,1},{6,2},{7,3},{8,12},{9,13},{10,... | collective-permute-start | bytes 884744 | tf_op jit(solution)/shard_map/ppermute | solution.py:41
  539.0 11.4 %copy-start.1 = (bf16[576,2048]{1,0:T(8,128)(2,1)S(1)}, bf16[576,2048]{1,0:T(8,128)(2,1)}, u32[]{:S(2)}) copy-start(bf16[576,2048]{1,0:T(8,128)(2,1)} %get-tuple-element.83.normed_ref) | copy-start | bytes 7077892
  547.5 60.7 %collective-permute-start.4 = (bf16[576,512]{1,0:T(8,128)(2,1)}, bf16[576,512]{1,0:T(8,128)(2,1)S(1)}, u32[]{:S(2)}, u32[]{:S(2)}) collective-permute-start(bf16[576,512]{1,0:T(8,128)(2,1)} %pad_maximum_fusion.3), channel_id=1, source_target_pairs={{0,4},{1,5},{2,6},{3,7},{4,0},{5,1},{6,2},{7,3},{8,12},{9,13},{10,... | collective-permute-start | bytes 1769480 | tf_op jit(solution)/shard_map/ppermute | solution.py:41
  549.5 58.7 %collective-permute-start.3 = (bf16[576,512]{1,0:T(8,128)(2,1)}, bf16[576,512]{1,0:T(8,128)(2,1)}, u32[]{:S(2)}, u32[]{:S(2)}) collective-permute-start(bf16[576,512]{1,0:T(8,128)(2,1)} %pad_maximum_fusion.2), channel_id=1, source_target_pairs={{0,2},{1,3},{2,0},{3,1},{4,6},{5,7},{6,4},{7,5},{8,10},{9,11},{10,... | collective-permute-start | bytes 1769480 | tf_op jit(solution)/shard_map/ppermute | solution.py:41
  554.0 4.2 copy-start
  558.3 49.9 %collective-permute-start.6 = (f32[128,2048]{1,0:T(8,128)}, f32[128,2048]{1,0:T(8,128)}, u32[]{:S(2)}, u32[]{:S(2)}) collective-permute-start(f32[128,2048]{1,0:T(8,128)} %get-tuple-element.157), channel_id=1, source_target_pairs={{0,2},{1,3},{2,0},{3,1},{4,6},{5,7},{6,4},{7,5},{8,10},{9,11},{10,... | collective-permute-start | bytes 3145736 | tf_op jit(solution)/shard_map/ppermute | solution.py:41
  559.4 48.9 %collective-permute-start.7 = (f32[128,2048]{1,0:T(8,128)}, f32[128,2048]{1,0:T(8,128)}, u32[]{:S(2)}, u32[]{:S(2)}) collective-permute-start(f32[128,2048]{1,0:T(8,128)} %get-tuple-element.156), channel_id=1, source_target_pairs={{0,4},{1,5},{2,6},{3,7},{4,0},{5,1},{6,2},{7,3},{8,12},{9,13},{10,... | collective-permute-start | bytes 3145736 | tf_op jit(solution)/shard_map/ppermute | solution.py:41
  608.2 2.8 copy-start.2
  608.2 2.8 copy-start.5
  626.2 211.4 %reduce-scatter.2.cloned.1.call-start = ((), (), s32[]{:S(2)}) async-start(), calls=%async_computation.1 | async-start | bytes 18874368 | tf_op jit(solution)/shard_map/reduce_scatter | solution.py:1039
  668.6 67.4 %collective-permute-start.8 = (f32[256,2048]{1,0:T(8,128)}, f32[256,2048]{1,0:T(8,128)}, u32[]{:S(2)}, u32[]{:S(2)}) collective-permute-start(f32[256,2048]{1,0:T(8,128)} %get-tuple-element.105), channel_id=1, source_target_pairs={{0,2},{1,3},{2,0},{3,1},{4,6},{5,7},{6,4},{7,5},{8,10},{9,11},{10,... | collective-permute-start | bytes 6291464 | tf_op jit(solution)/shard_map/ppermute | solution.py:41
  669.8 67.1 %collective-permute-start.9 = (f32[256,2048]{1,0:T(8,128)}, f32[256,2048]{1,0:T(8,128)}, u32[]{:S(2)}, u32[]{:S(2)}) collective-permute-start(f32[256,2048]{1,0:T(8,128)} %get-tuple-element.106), channel_id=1, source_target_pairs={{0,4},{1,5},{2,6},{3,7},{4,0},{5,1},{6,2},{7,3},{8,12},{9,13},{10,... | collective-permute-start | bytes 6291464 | tf_op jit(solution)/shard_map/ppermute | solution.py:41
  743.2 94.4 %copy-start.4 = (f32[2048,256]{1,0:T(8,128)S(1)}, f32[2048,256]{1,0:T(8,128)}, u32[]{:S(2)}) copy-start(f32[2048,256]{1,0:T(8,128)} %get-tuple-element.174) | copy-start | bytes 6291460
Sparse Core Ops, SparseCore 0:
  626.4 96.4 all-reduce.2
  727.0 110.5 reduce-scatter.1
